TPU v7x, 256 devices: a whole 4x4x8 slice. The times are simulated.
256 devices in a mesh: gx: 4 (over x_lo, core), gy: 16 (over z, x_hi), gz: 4 (over y).
Axes of the slice: x: 4 (x_hi: 2, x_lo: 2; x = x_hi * 2 + x_lo), y: 4, z: 8, core: 2. Of those that a mesh axis runs over, the one named last changes fastest.
Arguments:
- fields: float32 [5, 64, 128, 512], P(None, 'gz', 'gy', 'gx'), may hold values from -4 to 4
- radius: float32 [8, 64, 128, 512], P(None, 'gz', 'gy', 'gx'), may hold values from 0.4 to 1.5
- weight: float32 [8, 64, 128, 512], P(None, 'gz', 'gy', 'gx'), may hold values from 0.05 to 0.5
- column: int32 [8, 64, 128, 512], P(None, 'gz', 'gy', 'gx'), may hold values from 0 to 127
- counts: int32 [64, 128, 512], P('gz', 'gy', 'gx'), may hold values from 1 to 8
- fall_depth: int32 [8, 64, 128, 4], P(None, 'gz', 'gy', 'gx'), may hold values from 0 to 8, as said below
Outputs:
- new_fields: float32 [5, 64, 128, 512], P(None, 'gz', 'gy', 'gx')
- moments: float32 [3, 64, 128, 512], P(None, 'gz', 'gy', 'gx')
Inputs may be any that keep to these rules, and one draw needn't show every extreme that they name: The droplet in slot s of cell (k, j, i) sits in x cell (i // 128) * 128 + column[s, k, j, i]. Slots s < counts[k, j, i] hold live droplets. The droplets of slot s in cells (k, j, b * 128) to (k, j, (b + 1) * 128 - 1) fall together by fall_depth[s, k, j, b] levels, never below the lowest level: fall_depth[s, k, j, b] <= k; 8 is reached in every draw.
All inputs are finite; a program needn't handle non-finite values. Where the computation divides by a largest or mean magnitude, that divisor is 1e-20 or more.
Results may differ from a plain program's by a relative error of at most 0.00021.
Values sent between devices are 32-bit elements; how exact they have to be, the bound alone decides.
No kernel may reach another device: no remote copies, remote signals or barrier semaphores. Data moves between devices by JAX's collectives and lax.ppermute only.
A program may use at most 64 MiB of HBM per device.

v0:
```python
import jax
import jax.numpy as jnp
from jax import lax
from jax.experimental import pallas as pl
from jax.experimental.pallas import tpu as pltpu
from jax.sharding import PartitionSpec as P

NS = 4
FMAX = 8
GRID_AXES = ("gx", "gy", "gz")

sound_speed = 10.0
buoyancy = 0.5
courant_goal = 0.6
growth = 0.3

LEVELS, ROWS, COLS = 16, 8, 128
TALL, WIDE = 24, 256
REACH = 7
DEPTH = LEVELS + 2 * REACH
EDGE = 8
F32 = jnp.float32
ANY = pltpu.VMEM


def lanes(shape):
    return lax.broadcasted_iota(jnp.int32, shape, len(shape) - 1)


def pack_columns(own, above, below, to_left, to_right):
    blocks = (own, above, below)
    lane = lanes((ROWS, COLS))

    def one(k, _):
        left = jnp.zeros((ROWS, COLS), F32)
        right = jnp.zeros((ROWS, COLS), F32)
        for tile in range(3):
            for field in range(5):
                start = tile * 40 + field * EDGE
                here = (lane >= start) & (lane < start + EDGE)
                value = blocks[tile][field, k]
                first = pltpu.roll(value, start, 1) if start else value
                last = pltpu.roll(value, (start + EDGE) % COLS, 1)
                left = jnp.where(here, first, left)
                right = jnp.where(here, last, right)
        to_left[k] = left
        to_right[k] = right
        return 0

    lax.fori_loop(0, LEVELS, one, 0)


def halo_columns(from_right, from_left, tile, field):
    start = tile * 40 + field * EDGE
    right = pltpu.roll(from_right, COLS - start, 1) if start else from_right
    left = pltpu.roll(from_left, (COLS - EDGE - start) % COLS, 1)
    return jnp.where(lanes((ROWS, COLS)) < COLS // 2, right, left)


def pack_levels(reach):
    def kernel(own, above, below, from_right, from_left, to_down, to_up):
        for a in range(reach):
            for out, k in ((to_down, a), (to_up, LEVELS - reach + a)):
                for tile, block in enumerate((own, above, below)):
                    for field in range(5):
                        out[a, field * 3 + tile] = block[field, k]
                out[a, 15] = from_right[k]
                out[a, 16] = from_left[k]

    return kernel


def assemble(refs, ext, reach, place, last):
    own, above, below, from_right, from_left, from_up, from_down = refs
    blocks = (own, above, below)

    def middle(k, _):
        right, left = from_right[k], from_left[k]
        for field in range(5):
            for tile in range(3):
                at = pl.ds(tile * ROWS, ROWS)
                ext[field, REACH + k, at, 0:COLS] = blocks[tile][field, k]
                ext[field, REACH + k, at, COLS:WIDE] = halo_columns(right, left, tile, field)
        return 0

    lax.fori_loop(0, LEVELS, middle, 0)
    for message, first, there in (
        (from_down, REACH - reach, place > 0),
        (from_up, REACH + LEVELS, place < last),
    ):
        keep = jnp.where(there, 1.0, 0.0).astype(F32)

        def outer(a, _, message=message, first=first, keep=keep):
            right, left = message[a, 15], message[a, 16]
            for field in range(5):
                for tile in range(3):
                    at = pl.ds(tile * ROWS, ROWS)
                    ext[field, first + a, at, 0:COLS] = message[a, field * 3 + tile] * keep
                    ext[field, first + a, at, COLS:WIDE] = (
                        halo_columns(right, left, tile, field) * keep
                    )
            return 0

        lax.fori_loop(0, reach, outer, 0)


def shift(value, by, axis):
    return pltpu.roll(value, (-by) % value.shape[axis], axis)


def face_flux(q, wind):
    central = 37.0 * (q[2] + q[3]) - 8.0 * (q[1] + q[4]) + (q[0] + q[5])
    upwind = 10.0 * (q[3] - q[2]) - 5.0 * (q[4] - q[1]) + (q[5] - q[0])
    return wind * central - jnp.abs(wind) * upwind


def flat_flux(q, wind, axis):
    flux = face_flux([shift(q, by, axis) if by else q for by in range(-2, 4)], wind)
    return flux - shift(flux, -1, axis)


def level_flux(read, wind, l):
    return face_flux([read(l + by) for by in range(-2, 4)], wind)


def in_domain(l, place, last, lid):
    g = place * LEVELS + l - REACH
    top = (last + 1) * LEVELS - (1 if lid else 0)
    return jnp.where((g >= 0) & (g < top), 1.0, 0.0).astype(F32)


def first_rates(
    place_ref, own, above, below, from_right, from_left, from_up, from_down, ext, rate
):
    place, last = place_ref[0], place_ref[1]
    assemble(
        (own, above, below, from_right, from_left, from_up, from_down), ext, REACH, place, last
    )

    @pl.when(place == last)
    def _():
        ext[4, REACH + LEVELS - 1] = jnp.zeros((TALL, WIDE), F32)

    read_c = lambda l: ext[0, l]
    read_p = lambda l: ext[1, l]

    def one(l, carry):
        low_c, low_p = carry
        u, v, w = ext[2, l], ext[3, l], ext[4, l]
        high_c = level_flux(read_c, w, l)
        high_p = level_flux(read_p, w, l)
        c, p = ext[0, l], ext[1, l]
        rate[0, l] = -(flat_flux(c, u, 1) + flat_flux(c, v, 0) + (high_c - low_c)) / 60.0
        rate[1, l] = -(flat_flux(p, u, 1) + flat_flux(p, v, 0) + (high_p - low_p)) / 60.0
        return high_c, high_p

    start = REACH - 4
    w = ext[4, start - 1]
    lax.fori_loop(
        start,
        REACH + LEVELS + 4,
        one,
        (level_flux(read_c, w, start - 1), level_flux(read_p, w, start - 1)),
    )


def acoustic(p, u, v, w, read_c, rate, step, first, count, place, last, out=None):
    pull = step * sound_speed

    def wind_w(l, p_here):
        lift = (buoyancy * 0.5) * (read_c(l) + read_c(l + 1))
        return (w[0](l) + step * lift - pull * (p[0](l + 1) - p_here)) * in_domain(
            l, place, last, True
        )

    def one(l, w_low):
        p_here = p[0](l)
        w_new = wind_w(l, p_here)
        u_new = u[0](l) - pull * (shift(p_here, 1, 1) - p_here)
        v_new = v[0](l) - pull * (shift(p_here, 1, 0) - p_here)
        divergence = (
            (u_new - shift(u_new, -1, 1)) + (v_new - shift(v_new, -1, 0)) + (w_new - w_low)
        )
        p_new = (p_here + step * rate(l) - pull * divergence) * in_domain(l, place, last, False)
        p[1](l, p_new)
        u[1](l, u_new)
        v[1](l, v_new)
        w[1](l, w_new)
        return w_new

    w_low = wind_w(first - 1, p[0](first - 1))
    w[1](first - 1, w_low)
    lax.fori_loop(first, first + count, one, w_low)


def access(ref, *lead):
    def read(l):
        return ref[(*lead, l)]

    def write(l, value):
        ref[(*lead, l)] = value

    return read, write


def own_write(ref, field):
    def write(l, value):
        if not isinstance(l, int):
            ref[field, l - REACH] = value[0:ROWS, 0:COLS]

    return write


def tracer_rate(ext, l, low):
    c_all, v = ext[0, l], ext[3, l]
    rows = flat_flux(c_all[:, 0:COLS], v[:, 0:COLS], 0)[0:ROWS]
    cols = flat_flux(ext[0, l, 0:ROWS, :], ext[2, l, 0:ROWS, :], 1)[:, 0:COLS]
    high = tracer_high(ext, l)
    return -(rows + cols + (high - low)) / 60.0, high


def tracer_high(ext, l):
    return level_flux(lambda m: ext[0, m, 0:ROWS, 0:COLS], ext[4, l, 0:ROWS, 0:COLS], l)


def pressure_rates(ext, rate, first, count):
    read_p = lambda l: ext[1, l]

    def one(l, low):
        p = ext[1, l]
        high = level_flux(read_p, ext[4, l], l)
        rate[l] = -(flat_flux(p, ext[2, l], 1) + flat_flux(p, ext[3, l], 0) + (high - low)) / 60.0
        return high

    lax.fori_loop(first, first + count, one, level_flux(read_p, ext[4, first - 1], first - 1))


def two_sections(place_ref, speed, start, rate0, s2, dt_out, s1, rate1, fast):
    place, last = place_ref[0], place_ref[1]
    dt = courant_goal / (1.0 + jnp.max(speed[...]))
    dt_out[0] = dt
    third = dt * (1.0 / 3.0)

    def tracer(l, _):
        s1[0, l] = (start[0, l] + third * rate0[0, l]) * in_domain(l, place, last, False)
        return 0

    lax.fori_loop(REACH - 4, REACH + LEVELS + 4, tracer, 0)
    acoustic(
        (access(start, 1)[0], access(s1, 1)[1]),
        (access(start, 2)[0], access(s1, 2)[1]),
        (access(start, 3)[0], access(s1, 3)[1]),
        (access(start, 4)[0], access(s1, 4)[1]),
        access(start, 0)[0],
        access(rate0, 1)[0],
        third,
        REACH - 4,
        LEVELS + 8,
        place,
        last,
    )
    half = dt * 0.5

    def own_tracer(l, low):
        tendency, high = tracer_rate(s1, l, low)
        s2[0, l - REACH] = start[0, l, 0:ROWS, 0:COLS] + half * tendency
        return high

    lax.fori_loop(REACH, REACH + LEVELS, own_tracer, tracer_high(s1, REACH - 1))
    pressure_rates(s1, rate1, REACH - 1, LEVELS + 2)
    step = half / (NS // 2)
    acoustic(
        (access(start, 1)[0], access(fast, 0)[1]),
        (access(start, 2)[0], access(fast, 1)[1]),
        (access(start, 3)[0], access(fast, 2)[1]),
        (access(start, 4)[0], access(fast, 3)[1]),
        access(s1, 0)[0],
        access(rate1)[0],
        step,
        REACH - 1,
        LEVELS + 2,
        place,
        last,
    )
    acoustic(
        (access(fast, 0)[0], own_write(s2, 1)),
        (access(fast, 1)[0], own_write(s2, 2)),
        (access(fast, 2)[0], own_write(s2, 3)),
        (access(fast, 3)[0], own_write(s2, 4)),
        access(s1, 0)[0],
        access(rate1)[0],
        step,
        REACH,
        LEVELS,
        place,
        last,
    )


def last_tracer(
    place_ref,
    dt_ref,
    own,
    above,
    below,
    from_right,
    from_left,
    from_up,
    from_down,
    fields,
    by_depth,
    ext,
    tracer,
    landed,
    fallen,
    total,
):
    place, last = place_ref[0], place_ref[1]
    dt = dt_ref[0]
    assemble((own, above, below, from_right, from_left, from_up, from_down), ext, 6, place, last)
    total[...] = jnp.zeros(total.shape, F32)

    def one(l, low):
        k = l - REACH
        tendency, high = tracer_rate(ext, l, low)
        c = fields[0, k] + dt * tendency
        tracer[k] = c
        grown = jnp.exp(growth * c)
        weights = (None, grown, grown * jnp.exp((0.5 * growth) * c))
        for depth in range(FMAX + 1):
            for moment in range(3):
                value = by_depth[k, depth, moment]
                if moment:
                    value = value * weights[moment]
                total[moment, k + FMAX - depth] += value
        return high

    lax.fori_loop(REACH, REACH + LEVELS, one, tracer_high(ext, REACH - 1))
    landed[...] = total[:, FMAX:]
    fallen[...] = total[:, 0:FMAX]


def last_section(place_ref, dt_ref, ext, start, tracer, out, rate, fast):
    place, last = place_ref[0], place_ref[1]
    step = dt_ref[0] / NS
    pressure_rates(ext, rate, REACH - 3, LEVELS + 6)
    out[0] = tracer[...]
    for repeat in range(NS):
        reads = [access(start, f + 1)[0] if repeat == 0 else access(fast, f)[0] for f in range(4)]
        writes = [
            own_write(out, f + 1) if repeat == NS - 1 else access(fast, f)[1] for f in range(4)
        ]
        acoustic(
            (reads[0], writes[0]),
            (reads[1], writes[1]),
            (reads[2], writes[2]),
            (reads[3], writes[3]),
            access(ext, 0)[0],
            access(rate)[0],
            step,
            REACH - 3 + repeat,
            LEVELS + 6 - 2 * repeat,
            place,
            last,
        )


def deposit(radius, weight, column, counts, fall_depth, out):
    slots, levels = radius.shape[0], radius.shape[1]
    target = lax.broadcasted_iota(jnp.int32, (COLS, COLS), 0)
    row = lax.broadcasted_iota(jnp.int32, (ROWS, COLS), 0)
    per_step = 4

    for k in range(levels):
        out[k] = jnp.zeros(out.shape[1:], F32)
        live = counts[k]

        def some(step, _, k=k, live=live):
            sums = [[None] * 3 for _ in range(FMAX + 1)]
            for part in range(per_step):
                s = step * per_step + part
                r = radius[s, k]
                number = jnp.where(s < live, weight[s, k], 0.0)
                area = number * r * r
                terms = []
                for t in (number, area, area * r):
                    high = t.astype(jnp.bfloat16).astype(F32)
                    terms += [high, t - high]
                cols = column[s, k]
                left, right = [], []
                for j in range(ROWS):
                    left.append(
                        jnp.concatenate([jnp.where(row == j, t, 0.0) for t in terms], axis=0)
                    )
                    right.append(jnp.where(cols[j : j + 1] == target, 1.0, 0.0).astype(F32))
                sent = lax.dot_general(
                    jnp.concatenate(left, axis=1),
                    jnp.concatenate(right, axis=1),
                    (((1,), (1,)), ((), ())),
                    preferred_element_type=F32,
                )
                depth = jnp.broadcast_to(fall_depth[s, k], (ROWS, COLS))
                for d in range(FMAX + 1):
                    falls = depth == d
                    for m in range(3):
                        both = sent[16 * m : 16 * m + 8] + sent[16 * m + 8 : 16 * m + 16]
                        value = jnp.where(falls, both, 0.0)
                        sums[d][m] = value if sums[d][m] is None else sums[d][m] + value
            for d in range(FMAX + 1):
                for m in range(3):
                    out[k, d, m] += sums[d][m]
            return 0

        lax.fori_loop(0, slots // per_step, some, 0)


def vmem(n):
    return [pl.BlockSpec(memory_space=pltpu.VMEM)] * n


def smem(n):
    return [pl.BlockSpec(memory_space=pltpu.SMEM)] * n


def shaped(*dims):
    return jax.ShapeDtypeStruct(dims, F32)


PARAMS = pltpu.CompilerParams(vmem_limit_bytes=60 * 1024 * 1024)


def call(kernel, name, ins, outs, scratch=(), out_specs=None, flops=None):
    return pl.pallas_call(
        kernel,
        name=name,
        in_specs=ins,
        out_specs=tuple(out_specs or vmem(len(outs))),
        out_shape=tuple(outs),
        scratch_shapes=list(scratch),
        compiler_params=PARAMS,
        cost_estimate=(
            pl.CostEstimate(flops=flops, bytes_accessed=0, transcendentals=0) if flops else None
        ),
    )


def both_ways(value, axis, low=None):
    count = lax.axis_size(axis)
    down = [((i + 1) % count, i) for i in range(count)]
    up = [(i, (i + 1) % count) for i in range(count)]
    return (
        lax.ppermute(value, axis, down),
        lax.ppermute(value if low is None else low, axis, up),
    )


def exchange(block, reach, after_rows=None):
    above, below = both_ways(block, "gy")
    if after_rows is not None:
        above, below, after_rows = lax.optimization_barrier((above, below, after_rows))
    to_left, to_right = call(
        pack_columns, "pack_columns", vmem(3), [shaped(LEVELS, ROWS, COLS)] * 2
    )(block, above, below)
    from_right, from_left = both_ways(to_left, "gx", to_right)
    to_down, to_up = call(
        pack_levels(reach), "pack_levels", vmem(5), [shaped(reach, 17, ROWS, COLS)] * 2
    )(block, above, below, from_right, from_left)
    from_up, from_down = both_ways(to_down, "gz", to_up)
    return above, below, from_right, from_left, from_up, from_down


def top_speed(fields, place, last):
    w = fields[4] * (
        (jnp.arange(LEVELS) < LEVELS - 1) | (place != last)
    ).astype(F32)[:, None, None]
    local = jnp.max(jnp.abs(fields[2]) + jnp.abs(fields[3]) + jnp.abs(w))
    devices = lax.axis_size(GRID_AXES)
    everywhere = jnp.broadcast_to(local, (devices, 1, COLS))
    return lax.all_to_all(everywhere, GRID_AXES, 0, 0)


def per_device(fields, radius, weight, column, counts, fall_depth):
    place = lax.axis_index("gz")
    last = lax.axis_size("gz") - 1
    where = jnp.stack([place, jnp.int32(last)]).astype(jnp.int32)

    chunk = 2
    by_depth = []
    for n in range(LEVELS // chunk):
        by_depth.append(
            pl.pallas_call(
                deposit,
                name="deposit",
                grid=(1,),
                in_specs=[
                    pl.BlockSpec((8, chunk, ROWS, COLS), lambda i, n=n: (0, n, 0, 0)),
                    pl.BlockSpec((8, chunk, ROWS, COLS), lambda i, n=n: (0, n, 0, 0)),
                    pl.BlockSpec((8, chunk, ROWS, COLS), lambda i, n=n: (0, n, 0, 0)),
                    pl.BlockSpec((chunk, ROWS, COLS), lambda i, n=n: (n, 0, 0)),
                    pl.BlockSpec((8, chunk, ROWS, 1), lambda i, n=n: (0, n, 0, 0)),
                ],
                out_specs=pl.BlockSpec(
                    (chunk, FMAX + 1, 3, ROWS, COLS), lambda i: (0, 0, 0, 0, 0)
                ),
                out_shape=shaped(chunk, FMAX + 1, 3, ROWS, COLS),
                compiler_params=PARAMS,
                cost_estimate=pl.CostEstimate(
                    flops=200_000_000, bytes_accessed=0, transcendentals=0
                ),
            )(radius, weight, column, counts, fall_depth)
        )
    by_depth = jnp.concatenate(by_depth, axis=0)

    speed = top_speed(fields, place, last)
    halos = exchange(fields, REACH)
    start, rate0 = call(
        first_rates,
        "first_rates",
        smem(1) + vmem(7),
        [shaped(5, DEPTH, TALL, WIDE), shaped(2, DEPTH, TALL, WIDE)],
    )(where, fields, *halos)
    s2, dt = call(
        two_sections,
        "two_sections",
        smem(1) + vmem(3),
        [shaped(5, LEVELS, ROWS, COLS), shaped(1)],
        scratch=[
            pltpu.VMEM((5, DEPTH, TALL, WIDE), F32),
            pltpu.VMEM((DEPTH, TALL, WIDE), F32),
            pltpu.VMEM((4, DEPTH, TALL, WIDE), F32),
        ],
        out_specs=vmem(1) + smem(1),
    )(where, speed, start, rate0)
    halos = exchange(s2, 6)
    ext, tracer, landed, fallen = call(
        last_tracer,
        "last_tracer",
        smem(2) + vmem(9),
        [
            shaped(5, DEPTH, TALL, WIDE),
            shaped(LEVELS, ROWS, COLS),
            shaped(3, LEVELS, ROWS, COLS),
            shaped(3, FMAX, ROWS, COLS),
        ],
        scratch=[pltpu.VMEM((3, LEVELS + FMAX, ROWS, COLS), F32)],
    )(where, dt, s2, *halos, fields, by_depth)
    count = lax.axis_size("gz")
    arrived = lax.ppermute(fallen, "gz", [((i + 1) % count, i) for i in range(count)])
    (new_fields,) = call(
        last_section,
        "last_section",
        smem(2) + vmem(3),
        [shaped(5, LEVELS, ROWS, COLS)],
        scratch=[
            pltpu.VMEM((DEPTH, TALL, WIDE), F32),
            pltpu.VMEM((4, DEPTH, TALL, WIDE), F32),
        ],
        flops=1_000_000_000,
    )(where, dt, ext, start, tracer)
    arrived = jnp.where(place == last, 0.0, arrived)
    moments = landed.at[:, LEVELS - FMAX :].add(arrived)
    return (new_fields, moments)


def solution(mesh):
    spread = P(None, "gz", "gy", "gx")
    return jax.shard_map(
        per_device,
        mesh=mesh,
        in_specs=(spread, spread, spread, spread, P("gz", "gy", "gx"), spread),
        out_specs=(spread, spread),
        check_vma=False,
    )
```

profile of v0, /device:TPU:4, one launch (start us, length us, event | category | flops | bytes accessed | tf_op | source)
XLA Modules:
  0.0 182.7 jit_solution(200207701510263073)
XLA Ops:
  4.3 14.7 %collective-permute-done.1.below = f32[5,16,8,128]{3,2,1,0:T(8,128)S(1)} collective-permute-done((f32[5,16,8,128]{3,2,1,0:T(8,128)}, f32[5,16,8,128]{3,2,1,0:T(8,128)S(1)}, u32[]{:S(2)}, u32[]{:S(2)}) %collective-permute-start.1) | collective-permute-done | bytes 327712 | tf_op jit(solution)/shard_map/ppermute | solution.py:453
  20.4 3.4 %pack_columns.2 = (f32[16,8,128]{2,1,0:T(8,128)}, f32[16,8,128]{2,1,0:T(8,128)}) custom-call(f32[5,16,8,128]{3,2,1,0:T(8,128)} %fields.1, f32[5,16,8,128]{3,2,1,0:T(8,128)} %copy-done.4, f32[5,16,8,128]{3,2,1,0:T(8,128)} %copy-done.3), custom_call_target="tpu_custom_call" | custom-call | tf_op jit(solution)/shard_map/pack_columns/pallas_call | solution.py:461
  26.0 2.1 %collective-permute-done.3.from_left = f32[16,8,128]{2,1,0:T(8,128)S(1)} collective-permute-done((f32[16,8,128]{2,1,0:T(8,128)}, f32[16,8,128]{2,1,0:T(8,128)S(1)}, u32[]{:S(2)}, u32[]{:S(2)}) %collective-permute-start.3) | collective-permute-done | bytes 65568 | tf_op jit(solution)/shard_map/ppermute | solution.py:453
  28.8 2.2 %pack_levels.2 = (f32[7,17,8,128]{3,2,1,0:T(8,128)}, f32[7,17,8,128]{3,2,1,0:T(8,128)}) custom-call(f32[5,16,8,128]{3,2,1,0:T(8,128)} %fields.1, f32[5,16,8,128]{3,2,1,0:T(8,128)} %copy-done.4, f32[5,16,8,128]{3,2,1,0:T(8,128)} %copy-done.3, f32[16,8,128]{2,1,0:T(8,128)} %copy-done.19, f32[16,8,128]{2,1,0:T(8,128)} %copy-done.20), custom_call_target="tpu_custom_call" | custom-call | tf_op jit(solution)/shard_map/pack_levels/pallas_call | solution.py:465
  31.0 3.0 %collective-permute-start.4 = (f32[7,17,8,128]{3,2,1,0:T(8,128)}, f32[7,17,8,128]{3,2,1,0:T(8,128)S(1)}, u32[]{:S(2)}, u32[]{:S(2)}) collective-permute-start(f32[7,17,8,128]{3,2,1,0:T(8,128)} %get-tuple-element.32), channel_id=1, source_target_pairs={{1,0},{2,1},{3,2},{0,3},{5,4},{6,5},{7,6},{4,7},{9,8},{10,9},{11,1... | collective-permute-start | bytes 1462280 | tf_op jit(solution)/shard_map/ppermute | solution.py:452
  36.2 14.7 %all-to-all-start = ((f32[256,1,128]{2,1,0:T(1,128)}), f32[256,1,128]{2,1,0:T(1,128)S(1)}, u32[]{:S(2)}, u32[]{:S(2)}) async-start(f32[256,1,128]{2,1,0:T(1,128)} %broadcast_in_dim.8), calls=%async_computation | async-start | bytes 262144 | tf_op jit(solution)/shard_map/all_to_all | solution.py:479
  52.1 3.5 %deposit.11 = f32[2,9,3,8,128]{4,3,2,1,0:T(8,128)} custom-call(f32[8,16,8,128]{3,2,1,0:T(8,128)} %radius.15, f32[8,16,8,128]{3,2,1,0:T(8,128)} %weight.15, s32[8,16,8,128]{3,2,1,0:T(8,128)} %column.15, s32[16,8,128]{2,1,0:T(8,128)} %counts.15, s32[8,16,8,1]{3,2,1,0:T(8,128)} %copy.8.fall_depth), custom_call_target="tpu_custom_call" | custom-call | flops 200000000 | tf_op jit(solution)/shard_map/deposit/pallas_call | solution.py:491
  55.6 3.6 %deposit.10 = f32[2,9,3,8,128]{4,3,2,1,0:T(8,128)} custom-call(f32[8,16,8,128]{3,2,1,0:T(8,128)} %radius.15, f32[8,16,8,128]{3,2,1,0:T(8,128)} %weight.15, s32[8,16,8,128]{3,2,1,0:T(8,128)} %column.15, s32[16,8,128]{2,1,0:T(8,128)} %counts.15, s32[8,16,8,1]{3,2,1,0:T(8,128)} %copy.8.fall_depth), custom_call_target="tpu_custom_call" | custom-call | flops 200000000 | tf_op jit(solution)/shard_map/deposit/pallas_call | solution.py:491
  59.2 3.6 %deposit.9 = f32[2,9,3,8,128]{4,3,2,1,0:T(8,128)} custom-call(f32[8,16,8,128]{3,2,1,0:T(8,128)} %radius.15, f32[8,16,8,128]{3,2,1,0:T(8,128)} %weight.15, s32[8,16,8,128]{3,2,1,0:T(8,128)} %column.15, s32[16,8,128]{2,1,0:T(8,128)} %counts.15, s32[8,16,8,1]{3,2,1,0:T(8,128)} %copy.8.fall_depth), custom_call_target="tpu_custom_call" | custom-call | flops 200000000 | tf_op jit(solution)/shard_map/deposit/pallas_call | solution.py:491
  62.8 3.5 %deposit.8 = f32[2,9,3,8,128]{4,3,2,1,0:T(8,128)} custom-call(f32[8,16,8,128]{3,2,1,0:T(8,128)} %radius.15, f32[8,16,8,128]{3,2,1,0:T(8,128)} %weight.15, s32[8,16,8,128]{3,2,1,0:T(8,128)} %column.15, s32[16,8,128]{2,1,0:T(8,128)} %counts.15, s32[8,16,8,1]{3,2,1,0:T(8,128)} %copy.8.fall_depth), custom_call_target="tpu_custom_call" | custom-call | flops 200000000 | tf_op jit(solution)/shard_map/deposit/pallas_call | solution.py:491
  68.6 12.3 %first_rates.1 = (f32[5,30,24,256]{3,2,1,0:T(8,128)}, f32[2,30,24,256]{3,2,1,0:T(8,128)}) custom-call(s32[2]{0:T(128)} %pad_add_fusion.place_ref, f32[5,16,8,128]{3,2,1,0:T(8,128)} %fields.1, f32[5,16,8,128]{3,2,1,0:T(8,128)} %copy-done.4, f32[5,16,8,128]{3,2,1,0:T(8,128)} %copy-done.3, f32[16,8,128]{2,1,0:T(8,128)} %copy-done.19, f32[16,8,128]{2,1,0:T(8,128)} %copy-done.20, ...), custom_call_target="tpu_custom_call" | custom-call | tf_op jit(solution)/shard_map/first_rates/pallas_call | solution.py:516
  81.6 18.5 %two_sections.1 = (f32[5,16,8,128]{3,2,1,0:T(8,128)}, f32[1]{0:T(128)}) custom-call(s32[2]{0:T(128)} %pad_add_fusion.place_ref, f32[256,1,128]{2,1,0:T(1,128)} %copy-done.12, f32[5,30,24,256]{3,2,1,0:T(8,128)} %get-tuple-element.34.start, f32[2,30,24,256]{3,2,1,0:T(8,128)} %get-tuple-element.35.rate0), custom_call_target="tpu_custom_call" | custom-call | tf_op jit(solution)/shard_map/two_sections/pallas_call | solution.py:522
  101.8 1.9 %collective-permute-start.6 = (f32[5,16,8,128]{3,2,1,0:T(8,128)}, f32[5,16,8,128]{3,2,1,0:T(8,128)S(1)}, u32[]{:S(2)}, u32[]{:S(2)}) collective-permute-start(f32[5,16,8,128]{3,2,1,0:T(8,128)} %get-tuple-element.37.own), channel_id=1, source_target_pairs={{4,0},{8,4},{12,8},{16,12},{20,16},{24,20},{28,24},{32,28},{36,32}... | collective-permute-start | bytes 983048 | tf_op jit(solution)/shard_map/ppermute | solution.py:452
  103.8 14.8 %collective-permute-done.7.below = f32[5,16,8,128]{3,2,1,0:T(8,128)S(1)} collective-permute-done((f32[5,16,8,128]{3,2,1,0:T(8,128)}, f32[5,16,8,128]{3,2,1,0:T(8,128)S(1)}, u32[]{:S(2)}, u32[]{:S(2)}) %collective-permute-start.7) | collective-permute-done | bytes 327712 | tf_op jit(solution)/shard_map/ppermute | solution.py:453
  120.1 3.4 %pack_columns.3 = (f32[16,8,128]{2,1,0:T(8,128)}, f32[16,8,128]{2,1,0:T(8,128)}) custom-call(f32[5,16,8,128]{3,2,1,0:T(8,128)} %get-tuple-element.37.own, f32[5,16,8,128]{3,2,1,0:T(8,128)} %copy-done.2, f32[5,16,8,128]{3,2,1,0:T(8,128)} %copy-done.1), custom_call_target="tpu_custom_call" | custom-call | tf_op jit(solution)/shard_map/pack_columns/pallas_call | solution.py:461
  124.1 3.6 %deposit.12 = f32[2,9,3,8,128]{4,3,2,1,0:T(8,128)} custom-call(f32[8,16,8,128]{3,2,1,0:T(8,128)} %radius.15, f32[8,16,8,128]{3,2,1,0:T(8,128)} %weight.15, s32[8,16,8,128]{3,2,1,0:T(8,128)} %column.15, s32[16,8,128]{2,1,0:T(8,128)} %counts.15, s32[8,16,8,1]{3,2,1,0:T(8,128)} %copy.8.fall_depth), custom_call_target="tpu_custom_call" | custom-call | flops 200000000 | tf_op jit(solution)/shard_map/deposit/pallas_call | solution.py:491
  128.9 2.2 %pack_levels.3 = (f32[6,17,8,128]{3,2,1,0:T(8,128)}, f32[6,17,8,128]{3,2,1,0:T(8,128)}) custom-call(f32[5,16,8,128]{3,2,1,0:T(8,128)} %get-tuple-element.37.own, f32[5,16,8,128]{3,2,1,0:T(8,128)} %copy-done.2, f32[5,16,8,128]{3,2,1,0:T(8,128)} %copy-done.1, f32[16,8,128]{2,1,0:T(8,128)} %copy-done.17, f32[16,8,128]{2,1,0:T(8,128)} %copy-done.18), custom_call_target="tpu_custom_call" | custom-call | tf_op jit(solution)/shard_map/pack_levels/pallas_call | solution.py:465
  131.1 2.8 %collective-permute-start.10 = (f32[6,17,8,128]{3,2,1,0:T(8,128)}, f32[6,17,8,128]{3,2,1,0:T(8,128)S(1)}, u32[]{:S(2)}, u32[]{:S(2)}) collective-permute-start(f32[6,17,8,128]{3,2,1,0:T(8,128)} %get-tuple-element.40), channel_id=1, source_target_pairs={{1,0},{2,1},{3,2},{0,3},{5,4},{6,5},{7,6},{4,7},{9,8},{10,9},{11,1... | collective-permute-start | bytes 1253384 | tf_op jit(solution)/shard_map/ppermute | solution.py:452
  134.8 3.6 %deposit.15 = f32[2,9,3,8,128]{4,3,2,1,0:T(8,128)} custom-call(f32[8,16,8,128]{3,2,1,0:T(8,128)} %radius.15, f32[8,16,8,128]{3,2,1,0:T(8,128)} %weight.15, s32[8,16,8,128]{3,2,1,0:T(8,128)} %column.15, s32[16,8,128]{2,1,0:T(8,128)} %counts.15, s32[8,16,8,1]{3,2,1,0:T(8,128)} %copy.8.fall_depth), custom_call_target="tpu_custom_call" | custom-call | flops 200000000 | tf_op jit(solution)/shard_map/deposit/pallas_call | solution.py:491
  138.4 3.6 %deposit.14 = f32[2,9,3,8,128]{4,3,2,1,0:T(8,128)} custom-call(f32[8,16,8,128]{3,2,1,0:T(8,128)} %radius.15, f32[8,16,8,128]{3,2,1,0:T(8,128)} %weight.15, s32[8,16,8,128]{3,2,1,0:T(8,128)} %column.15, s32[16,8,128]{2,1,0:T(8,128)} %counts.15, s32[8,16,8,1]{3,2,1,0:T(8,128)} %copy.8.fall_depth), custom_call_target="tpu_custom_call" | custom-call | flops 200000000 | tf_op jit(solution)/shard_map/deposit/pallas_call | solution.py:491
  141.9 3.6 %deposit.13 = f32[2,9,3,8,128]{4,3,2,1,0:T(8,128)} custom-call(f32[8,16,8,128]{3,2,1,0:T(8,128)} %radius.15, f32[8,16,8,128]{3,2,1,0:T(8,128)} %weight.15, s32[8,16,8,128]{3,2,1,0:T(8,128)} %column.15, s32[16,8,128]{2,1,0:T(8,128)} %counts.15, s32[8,16,8,1]{3,2,1,0:T(8,128)} %copy.8.fall_depth), custom_call_target="tpu_custom_call" | custom-call | flops 200000000 | tf_op jit(solution)/shard_map/deposit/pallas_call | solution.py:491
  148.1 10.3 %last_tracer.1 = (f32[5,30,24,256]{3,2,1,0:T(8,128)}, f32[16,8,128]{2,1,0:T(8,128)}, f32[3,16,8,128]{3,2,1,0:T(8,128)}, f32[3,8,8,128]{3,2,1,0:T(8,128)}) custom-call(s32[2]{0:T(128)} %pad_add_fusion.place_ref, f32[1]{0:T(128)} %get-tuple-element.36.dt_ref, f32[5,16,8,128]{3,2,1,0:T(8,128)} %get-tuple-element.37.own, f32[5,16,8,128]{3,2,1,0:T(8,128)} %copy-done.2, ...), custom_call_target="tpu_custom_call" | custom-call | tf_op jit(solution)/shard_map/last_tracer/pallas_call | solution.py:535
  158.4 3.2 %collective-permute-start.12 = (f32[3,8,8,128]{3,2,1,0:T(8,128)}, f32[3,8,8,128]{3,2,1,0:T(8,128)S(1)}, u32[]{:S(2)}, u32[]{:S(2)}) collective-permute-start(f32[3,8,8,128]{3,2,1,0:T(8,128)} %get-tuple-element.45), channel_id=1, source_target_pairs={{1,0},{2,1},{3,2},{0,3},{5,4},{6,5},{7,6},{4,7},{9,8},{10,9},{11,1... | collective-permute-start | bytes 294920 | tf_op jit(solution)/shard_map/ppermute | solution.py:548
  161.6 20.3 %last_section.1 = f32[5,16,8,128]{3,2,1,0:T(8,128)} custom-call(s32[2]{0:T(128)} %pad_add_fusion.place_ref, f32[1]{0:T(128)} %get-tuple-element.36.dt_ref, f32[5,30,24,256]{3,2,1,0:T(8,128)} %get-tuple-element.42.ext, f32[5,30,24,256]{3,2,1,0:T(8,128)} %get-tuple-element.34.start, f32[16,8,128]{2,1,0:T(8,128)} %get-tuple-element.43.tracer), custom_call_target="tpu_custom_call" | custom-call | flops 1000000000 | tf_op jit(solution)/shard_map/last_section/pallas_call | solution.py:549
  (82 shorter events, 23.4 us)
Async XLA Ops:
  0.6 33.4 %copy-start = (f32[5,16,8,128]{3,2,1,0:T(8,128)S(1)}, f32[5,16,8,128]{3,2,1,0:T(8,128)}, u32[]{:S(2)}) copy-start(f32[5,16,8,128]{3,2,1,0:T(8,128)} %fields.1) | copy-start | bytes 983044
  0.6 50.2 %copy-start.23 = (s32[8,16,8,1]{1,3,2,0:T(1,128)S(1)}, s32[8,16,8,1]{1,3,2,0:T(1,128)}, u32[]{:S(2)}) copy-start(s32[8,16,8,1]{1,3,2,0:T(1,128)} %param.13) | copy-start | bytes 12292
  0.7 18.3 %collective-permute-start.1 = (f32[5,16,8,128]{3,2,1,0:T(8,128)}, f32[5,16,8,128]{3,2,1,0:T(8,128)S(1)}, u32[]{:S(2)}, u32[]{:S(2)}) collective-permute-start(f32[5,16,8,128]{3,2,1,0:T(8,128)} %fields.1), channel_id=1, source_target_pairs={{0,4},{4,8},{8,12},{12,16},{16,20},{20,24},{24,28},{28,32},{32,36}... | collective-permute-start | bytes 983048 | tf_op jit(solution)/shard_map/ppermute | solution.py:453
  2.6 16.3 %collective-permute-start = (f32[5,16,8,128]{3,2,1,0:T(8,128)}, f32[5,16,8,128]{3,2,1,0:T(8,128)S(1)}, u32[]{:S(2)}, u32[]{:S(2)}) collective-permute-start(f32[5,16,8,128]{3,2,1,0:T(8,128)} %fields.1), channel_id=1, source_target_pairs={{4,0},{8,4},{12,8},{16,12},{20,16},{24,20},{28,24},{32,28},{36,32}... | collective-permute-start | bytes 983048 | tf_op jit(solution)/shard_map/ppermute | solution.py:452
  23.8 2.2 %collective-permute-start.2 = (f32[16,8,128]{2,1,0:T(8,128)}, f32[16,8,128]{2,1,0:T(8,128)S(1)}, u32[]{:S(2)}, u32[]{:S(2)}) collective-permute-start(f32[16,8,128]{2,1,0:T(8,128)} %get-tuple-element.30), channel_id=1, source_target_pairs={{64,0},{128,64},{192,128},{0,192},{65,1},{129,65},{193,129},{1,193... | collective-permute-start | bytes 196616 | tf_op jit(solution)/shard_map/ppermute | solution.py:452
  23.8 4.3 %collective-permute-start.3 = (f32[16,8,128]{2,1,0:T(8,128)}, f32[16,8,128]{2,1,0:T(8,128)S(1)}, u32[]{:S(2)}, u32[]{:S(2)}) collective-permute-start(f32[16,8,128]{2,1,0:T(8,128)} %get-tuple-element.31), channel_id=1, source_target_pairs={{0,64},{64,128},{128,192},{192,0},{1,65},{65,129},{129,193},{193,1... | collective-permute-start | bytes 196616 | tf_op jit(solution)/shard_map/ppermute | solution.py:453
  26.0 2.1 %copy-start.19 = (f32[16,8,128]{2,1,0:T(8,128)}, f32[16,8,128]{2,1,0:T(8,128)S(1)}, u32[]{:S(2)}) copy-start(f32[16,8,128]{2,1,0:T(8,128)S(1)} %collective-permute-done.2.from_right) | copy-start | bytes 196612
  31.0 36.0 %collective-permute-start.4 = (f32[7,17,8,128]{3,2,1,0:T(8,128)}, f32[7,17,8,128]{3,2,1,0:T(8,128)S(1)}, u32[]{:S(2)}, u32[]{:S(2)}) collective-permute-start(f32[7,17,8,128]{3,2,1,0:T(8,128)} %get-tuple-element.32), channel_id=1, source_target_pairs={{1,0},{2,1},{3,2},{0,3},{5,4},{6,5},{7,6},{4,7},{9,8},{10,9},{11,1... | collective-permute-start | bytes 1462280 | tf_op jit(solution)/shard_map/ppermute | solution.py:452
  34.0 33.0 %collective-permute-start.5 = (f32[7,17,8,128]{3,2,1,0:T(8,128)}, f32[7,17,8,128]{3,2,1,0:T(8,128)S(1)}, u32[]{:S(2)}, u32[]{:S(2)}) collective-permute-start(f32[7,17,8,128]{3,2,1,0:T(8,128)} %get-tuple-element.33), channel_id=1, source_target_pairs={{0,1},{1,2},{2,3},{3,0},{4,5},{5,6},{6,7},{7,4},{8,9},{9,10},{10,1... | collective-permute-start | bytes 1462280 | tf_op jit(solution)/shard_map/ppermute | solution.py:453
  36.2 44.7 %all-to-all-start = ((f32[256,1,128]{2,1,0:T(1,128)}), f32[256,1,128]{2,1,0:T(1,128)S(1)}, u32[]{:S(2)}, u32[]{:S(2)}) async-start(f32[256,1,128]{2,1,0:T(1,128)} %broadcast_in_dim.8), calls=%async_computation | async-start | bytes 262144 | tf_op jit(solution)/shard_map/all_to_all | solution.py:479
  81.6 22.2 %copy-start.9 = (f32[2,9,3,8,128]{4,3,2,1,0:T(8,128)S(1)}, f32[2,9,3,8,128]{4,3,2,1,0:T(8,128)}, u32[]{:S(2)}) copy-start(f32[2,9,3,8,128]{4,3,2,1,0:T(8,128)} %deposit.8) | copy-start | bytes 663556
  81.6 22.2 %copy-start.8 = (f32[2,9,3,8,128]{4,3,2,1,0:T(8,128)S(1)}, f32[2,9,3,8,128]{4,3,2,1,0:T(8,128)}, u32[]{:S(2)}) copy-start(f32[2,9,3,8,128]{4,3,2,1,0:T(8,128)} %deposit.9) | copy-start | bytes 663556
  81.6 22.2 %copy-start.7 = (f32[2,9,3,8,128]{4,3,2,1,0:T(8,128)S(1)}, f32[2,9,3,8,128]{4,3,2,1,0:T(8,128)}, u32[]{:S(2)}) copy-start(f32[2,9,3,8,128]{4,3,2,1,0:T(8,128)} %deposit.10) | copy-start | bytes 663556
  100.1 23.9 %copy-start.6 = (f32[2,9,3,8,128]{4,3,2,1,0:T(8,128)S(1)}, f32[2,9,3,8,128]{4,3,2,1,0:T(8,128)}, u32[]{:S(2)}) copy-start(f32[2,9,3,8,128]{4,3,2,1,0:T(8,128)} %deposit.11) | copy-start | bytes 663556
  100.1 18.5 %collective-permute-start.7 = (f32[5,16,8,128]{3,2,1,0:T(8,128)}, f32[5,16,8,128]{3,2,1,0:T(8,128)S(1)}, u32[]{:S(2)}, u32[]{:S(2)}) collective-permute-start(f32[5,16,8,128]{3,2,1,0:T(8,128)} %get-tuple-element.37.own), channel_id=1, source_target_pairs={{0,4},{4,8},{8,12},{12,16},{16,20},{20,24},{24,28},{28,32},{32,36}... | collective-permute-start | bytes 983048 | tf_op jit(solution)/shard_map/ppermute | solution.py:453
  101.8 16.9 %collective-permute-start.6 = (f32[5,16,8,128]{3,2,1,0:T(8,128)}, f32[5,16,8,128]{3,2,1,0:T(8,128)S(1)}, u32[]{:S(2)}, u32[]{:S(2)}) collective-permute-start(f32[5,16,8,128]{3,2,1,0:T(8,128)} %get-tuple-element.37.own), channel_id=1, source_target_pairs={{4,0},{8,4},{12,8},{16,12},{20,16},{24,20},{28,24},{32,28},{36,32}... | collective-permute-start | bytes 983048 | tf_op jit(solution)/shard_map/ppermute | solution.py:452
  123.5 4.1 %collective-permute-start.8 = (f32[16,8,128]{2,1,0:T(8,128)}, f32[16,8,128]{2,1,0:T(8,128)S(1)}, u32[]{:S(2)}, u32[]{:S(2)}) collective-permute-start(f32[16,8,128]{2,1,0:T(8,128)} %get-tuple-element.38), channel_id=1, source_target_pairs={{64,0},{128,64},{192,128},{0,192},{65,1},{129,65},{193,129},{1,193... | collective-permute-start | bytes 196616 | tf_op jit(solution)/shard_map/ppermute | solution.py:452
  123.6 4.3 %collective-permute-start.9 = (f32[16,8,128]{2,1,0:T(8,128)}, f32[16,8,128]{2,1,0:T(8,128)S(1)}, u32[]{:S(2)}, u32[]{:S(2)}) collective-permute-start(f32[16,8,128]{2,1,0:T(8,128)} %get-tuple-element.39), channel_id=1, source_target_pairs={{0,64},{64,128},{128,192},{192,0},{1,65},{65,129},{129,193},{193,1... | collective-permute-start | bytes 196616 | tf_op jit(solution)/shard_map/ppermute | solution.py:453
  131.1 15.5 %collective-permute-start.10 = (f32[6,17,8,128]{3,2,1,0:T(8,128)}, f32[6,17,8,128]{3,2,1,0:T(8,128)S(1)}, u32[]{:S(2)}, u32[]{:S(2)}) collective-permute-start(f32[6,17,8,128]{3,2,1,0:T(8,128)} %get-tuple-element.40), channel_id=1, source_target_pairs={{1,0},{2,1},{3,2},{0,3},{5,4},{6,5},{7,6},{4,7},{9,8},{10,9},{11,1... | collective-permute-start | bytes 1253384 | tf_op jit(solution)/shard_map/ppermute | solution.py:452
  133.8 13.5 %collective-permute-start.11 = (f32[6,17,8,128]{3,2,1,0:T(8,128)}, f32[6,17,8,128]{3,2,1,0:T(8,128)S(1)}, u32[]{:S(2)}, u32[]{:S(2)}) collective-permute-start(f32[6,17,8,128]{3,2,1,0:T(8,128)} %get-tuple-element.41), channel_id=1, source_target_pairs={{0,1},{1,2},{2,3},{3,0},{4,5},{5,6},{6,7},{7,4},{8,9},{9,10},{10,1... | collective-permute-start | bytes 1253384 | tf_op jit(solution)/shard_map/ppermute | solution.py:453
  141.9 4.6 %copy-start.11 = (f32[2,9,3,8,128]{4,3,2,1,0:T(8,128)S(1)}, f32[2,9,3,8,128]{4,3,2,1,0:T(8,128)}, u32[]{:S(2)}) copy-start(f32[2,9,3,8,128]{4,3,2,1,0:T(8,128)} %deposit.14) | copy-start | bytes 663556
  141.9 4.6 %copy-start.10 = (f32[2,9,3,8,128]{4,3,2,1,0:T(8,128)S(1)}, f32[2,9,3,8,128]{4,3,2,1,0:T(8,128)}, u32[]{:S(2)}) copy-start(f32[2,9,3,8,128]{4,3,2,1,0:T(8,128)} %deposit.15) | copy-start | bytes 663556
  158.4 23.6 %collective-permute-start.12 = (f32[3,8,8,128]{3,2,1,0:T(8,128)}, f32[3,8,8,128]{3,2,1,0:T(8,128)S(1)}, u32[]{:S(2)}, u32[]{:S(2)}) collective-permute-start(f32[3,8,8,128]{3,2,1,0:T(8,128)} %get-tuple-element.45), channel_id=1, source_target_pairs={{1,0},{2,1},{3,2},{0,3},{5,4},{6,5},{7,6},{4,7},{9,8},{10,9},{11,1... | collective-permute-start | bytes 294920 | tf_op jit(solution)/shard_map/ppermute | solution.py:548
  161.6 20.4 %copy-start.21 = (f32[3,16,8,128]{3,2,1,0:T(8,128)S(1)}, f32[3,16,8,128]{3,2,1,0:T(8,128)}, u32[]{:S(2)}) copy-start(f32[3,16,8,128]{3,2,1,0:T(8,128)} %get-tuple-element.44) | copy-start | bytes 589828
  (14 other events, 11.2 us)
where the time goes:
time: 186 us; the launch traced here: 183 us
  Pallas kernels  101 us (54%)
  waiting for transfers between devices  34.3 us (18%)
  starting transfers between devices  32 us (17%)
  local copies, waits for them, and re-layouts  12.9 us (7%)
    ppermute x6, waiting for transfers between devices, both_ways(): lax.ppermute(value if low is None else low, axis, up)  32.6 us
    pallas_call x8, Pallas kernels, per_device(): pl.pallas_call(deposit, name='deposit', grid=(1,), in_specs=[pl.BlockSpec...  28.5 us
    pallas_call x1, Pallas kernels, per_device(): call(last_section, 'last_section', smem(2) + vmem(3), [shaped(5, LEVELS,...  20.3 us
    pallas_call x1, Pallas kernels, per_device(): call(two_sections, 'two_sections', smem(1) + vmem(3), [shaped(5, LEVELS,...  18.5 us
    all_to_all x1, starting transfers between devices, top_speed(): return lax.all_to_all(everywhere, GRID_AXES, 0, 0)  14.7 us
    pallas_call x1, Pallas kernels, per_device(): call(first_rates, 'first_rates', smem(1) + vmem(7), [shaped(5, DEPTH, TAL...  12.3 us
    unnamed x56, local copies, waits for them, and re-layouts  11.5 us
    pallas_call x1, Pallas kernels, per_device(): call(last_tracer, 'last_tracer', smem(2) + vmem(9), [shaped(5, DEPTH, TAL...  10.3 us
  transfers between devices with their start and end apart: 14, of which 6 were waited for; matrix products, arithmetic and copies ran while one was open for 3% of the time, Pallas kernels for 33%

commit v1 on v0

v1 whole, which is shorter than its diff:
```python
import jax
import jax.numpy as jnp
from jax import lax
from jax.experimental import pallas as pl
from jax.experimental.pallas import tpu as pltpu
from jax.sharding import PartitionSpec as P

NS = 4
FMAX = 8
GRID_AXES = ("gx", "gy", "gz")

sound_speed = 10.0
buoyancy = 0.5
courant_goal = 0.6
growth = 0.3

LEVELS, ROWS, COLS = 16, 8, 128
WIDE = 2 * COLS
REACH = 7
DEPTH = LEVELS + 2 * REACH
EDGE = 8
F32 = jnp.float32
C, PR, U, V, W = range(5)


class Plan:
    def __init__(self, tall, reach, short):
        self.tiles = [
            (field, part)
            for field in range(5)
            for part in ("oab" if field in tall else "on")
        ]
        self.at = {tile: n for n, tile in enumerate(self.tiles)}
        self.tall, self.reach, self.short = tall, reach, short
        far = [t for t in self.tiles if t[0] in (C, PR)] if C in tall else [
            t for t in self.tiles if t[0] == PR
        ]
        self.carried = []
        for a in range(reach):
            names = self.tiles if a < short else far
            self.carried += [(a, self.at[t]) for t in names] + [(a, -1), (a, -2)]

    def rows(self, ref, field, l):
        return jnp.concatenate(
            [
                ref[self.at[field, part], l]
                for part in ("oab" if field in self.tall else "on")
            ],
            axis=0,
        )

    def sixteen(self, ref, field, l):
        value = self.rows(ref, field, l)
        return sixteen(value) if field in self.tall else value


def lanes(shape):
    return lax.broadcasted_iota(jnp.int32, shape, len(shape) - 1)


def lower_rows(shape):
    return lax.broadcasted_iota(jnp.int32, shape, 0) < ROWS // 2


def around(above, below):
    return jnp.where(lower_rows(above.shape), above, below)


def sixteen(value):
    return jnp.concatenate(
        [value[0:ROWS], around(value[ROWS : 2 * ROWS], value[2 * ROWS :])], axis=0
    )


def raw_tile(refs, field, part, k):
    own, above, below = refs
    if part == "o":
        return own[field, k]
    if part == "n":
        return around(above[field, k], below[field, k])
    return (above if part == "a" else below)[field, k]


SHARED = {C: (1, 0), U: (1, 1), V: (2, 0), W: (2, 1)}


def shared_rows(read):
    down, up = [read(PR)], [read(PR)]
    for first, second in ((C, U), (V, W)):
        one, other = read(first), pltpu.roll(read(second), ROWS // 2, 0)
        down.append(around(one, other))
        up.append(around(other, one))
    return down, up


def shared_tile(refs, field, part, k):
    own, above, below = refs
    if part == "o":
        return own[field, k]
    if part == "n":
        index, half = SHARED[field]
        if half == 0:
            return around(above[index, k], below[index, k])
        return pltpu.roll(around(below[index, k], above[index, k]), ROWS // 2, 0)
    return (above if part == "a" else below)[0, k]


FIRST = Plan((C, PR, V), 7, 5)
SECOND = Plan((PR,), 6, 4)
TILE_OF = {FIRST: raw_tile, SECOND: shared_tile}


def pack_columns(plan):
    def kernel(own, above, below, speed, to_left, to_right):
        lane = lanes((ROWS, COLS))

        def one(k, _):
            left = jnp.zeros((ROWS, COLS), F32)
            right = jnp.zeros((ROWS, COLS), F32)
            for n, (field, part) in enumerate(plan.tiles):
                start = n * EDGE
                here = (lane >= start) & (lane < start + EDGE)
                value = TILE_OF[plan]((own, above, below), field, part, k)
                first = pltpu.roll(value, start, 1) if start else value
                last = pltpu.roll(value, (start + EDGE) % COLS, 1)
                left = jnp.where(here, first, left)
                right = jnp.where(here, last, right)
            to_left[k] = left
            to_right[k] = right
            return 0

        def pair(i, _):
            one(2 * i, 0)
            return one(2 * i + 1, 0)

        lax.fori_loop(0, LEVELS // 2, pair, 0)

    return kernel


def halo_columns(from_right, from_left, n):
    start = n * EDGE
    right = pltpu.roll(from_right, COLS - start, 1) if start else from_right
    left = pltpu.roll(from_left, (COLS - EDGE - start) % COLS, 1)
    return jnp.where(lanes((ROWS, COLS)) < COLS // 2, right, left)


def pack_levels(plan):
    def kernel(own, above, below, from_right, from_left, to_down, to_up):
        for place, (a, n) in enumerate(plan.carried):
            for out, k in ((to_down, a), (to_up, LEVELS - 1 - a)):
                if n >= 0:
                    out[place] = TILE_OF[plan]((own, above, below), *plan.tiles[n], k)
                else:
                    out[place] = (from_right if n == -1 else from_left)[k]

    return kernel


def assemble(plan, refs, ext, place, last):
    own, above, below, from_right, from_left, from_up, from_down = refs

    def middle(k, _):
        right, left = from_right[k], from_left[k]
        for n, (field, part) in enumerate(plan.tiles):
            ext[n, REACH + k, :, 0:COLS] = TILE_OF[plan]((own, above, below), field, part, k)
            ext[n, REACH + k, :, COLS:WIDE] = halo_columns(right, left, n)
        return 0

    lax.fori_loop(0, LEVELS, middle, 0)
    columns = {}
    for index, (a, n) in enumerate(plan.carried):
        if n < 0:
            columns[a, n] = index
    for message, level, there in (
        (from_down, lambda a: REACH - 1 - a, place > 0),
        (from_up, lambda a: REACH + LEVELS + a, place < last),
    ):
        keep = jnp.where(there, 1.0, 0.0).astype(F32)
        for index, (a, n) in enumerate(plan.carried):
            if n >= 0:
                ext[n, level(a), :, 0:COLS] = message[index] * keep
                ext[n, level(a), :, COLS:WIDE] = (
                    halo_columns(message[columns[a, -1]], message[columns[a, -2]], n) * keep
                )


def shift(value, by, axis):
    return pltpu.roll(value, (-by) % value.shape[axis], axis)


def face_flux(q, wind):
    central = 37.0 * (q[2] + q[3]) - 8.0 * (q[1] + q[4]) + (q[0] + q[5])
    upwind = 10.0 * (q[3] - q[2]) - 5.0 * (q[4] - q[1]) + (q[5] - q[0])
    return wind * central - jnp.abs(wind) * upwind


def flat_flux(q, wind, axis):
    flux = face_flux([shift(q, by, axis) if by else q for by in range(-2, 4)], wind)
    return flux - shift(flux, -1, axis)


def rows_flux(q, wind):
    if wind.shape[0] == 24:
        return sixteen(flat_flux(q, wind, 0))
    if q.shape[0] == 24:
        flux = face_flux([sixteen(shift(q, by, 0) if by else q) for by in range(-2, 4)], wind)
        return flux - shift(flux, -1, 0)
    return flat_flux(q, wind, 0)


def level_flux(read, wind, l):
    return face_flux([read(l + by) for by in range(-2, 4)], wind)


def in_domain(l, place, last, lid):
    g = place * LEVELS + l - REACH
    top = (last + 1) * LEVELS - (1 if lid else 0)
    return jnp.where((g >= 0) & (g < top), 1.0, 0.0).astype(F32)


SIXTIETH = -1.0 / 60.0


def rates(plan, ext, fields, write, first, count):
    reads = [lambda l, f=f: plan.sixteen(ext, f, l) for f in fields]

    def one(l, lows):
        u, v, w = (
            plan.sixteen(ext, U, l),
            plan.rows(ext, V, l),
            plan.sixteen(ext, W, l),
        )
        highs = []
        for n, f in enumerate(fields):
            high = level_flux(reads[n], w, l)
            here = plan.rows(ext, f, l)
            cells = reads[n](l)
            total = flat_flux(cells, u, 1) + rows_flux(here, v) + (high - lows[n])
            write(n, l, total * SIXTIETH)
            highs.append(high)
        return tuple(highs)

    w = plan.sixteen(ext, W, first - 1)
    lax.fori_loop(
        first, first + count, one, tuple(level_flux(read, w, first - 1) for read in reads)
    )


def first_rates(
    place_ref, own, above, below, from_right, from_left, from_up, from_down, ext, rate
):
    place, last = place_ref[0], place_ref[1]
    assemble(
        FIRST, (own, above, below, from_right, from_left, from_up, from_down), ext, place, last
    )

    @pl.when(place == last)
    def _():
        for part in "on":
            ext[FIRST.at[W, part], REACH + LEVELS - 1] = jnp.zeros((ROWS, WIDE), F32)

    def write(n, l, value):
        rate[n, l] = value

    rates(FIRST, ext, (C, PR), write, REACH - 4, LEVELS + 8)


def acoustic(p, u, v, w, read_c, rate, step, first, count, place, last):
    pull = step * sound_speed

    def wind_w(l):
        lift = (buoyancy * 0.5) * (read_c(l) + read_c(l + 1))
        return (w[0](l) + step * lift - pull * (level(l + 1) - level(l))) * in_domain(
            l, place, last, True
        )

    def level(l):
        value = p[0](l)
        return sixteen(value) if value.shape[0] == 24 else value

    def one(l, w_low):
        tall = p[0](l)
        p_here = level(l)
        w_new = wind_w(l)
        u_new = u[0](l) - pull * (shift(p_here, 1, 1) - p_here)
        v_old = v[0](l)
        if v_old.shape[0] == 24:
            v_tall = v_old - pull * (shift(tall, 1, 0) - tall)
            v_new, v_flow = sixteen(v_tall), sixteen(v_tall - shift(v_tall, -1, 0))
        else:
            v_new = v_old - pull * (shift(p_here, 1, 0) - p_here)
            v_flow = v_new - shift(v_new, -1, 0)
        divergence = (u_new - shift(u_new, -1, 1)) + v_flow + (w_new - w_low)
        p_new = (p_here + step * rate(l) - pull * divergence) * in_domain(l, place, last, False)
        p[1](l, p_new)
        u[1](l, u_new)
        v[1](l, v_new)
        w[1](l, w_new)
        return w_new

    w_low = wind_w(first - 1)
    w[1](first - 1, w_low)
    lax.fori_loop(first, first + count, one, w_low)


def access(ref, *lead):
    def read(l):
        return ref[(*lead, l)]

    def write(l, value):
        ref[(*lead, l)] = value

    return read, write


def begin(start, field, tall=False):
    return lambda l: (FIRST.rows if tall else FIRST.sixteen)(start, field, l)


def own_write(ref, field):
    def write(l, value):
        if not isinstance(l, int):
            ref[field, l - REACH] = value[0:ROWS, 0:COLS]

    return write


def tracer_rate(tiles, winds, l, low):
    u, v, w = winds
    rows = flat_flux(tiles(l)[:, 0:COLS], v(l)[:, 0:COLS], 0)[0:ROWS]
    cols = flat_flux(tiles(l)[0:ROWS], u(l)[0:ROWS], 1)[:, 0:COLS]
    high = tracer_high(tiles, w, l)
    return (rows + cols + (high - low)) * SIXTIETH, high


def tracer_high(tiles, w, l):
    return level_flux(lambda m: tiles(m)[0:ROWS, 0:COLS], w(l)[0:ROWS, 0:COLS], l)


def two_sections(place_ref, speed, start, rate0, s2, down, up, dt_out, s1, rate1, fast):
    place, last = place_ref[0], place_ref[1]
    dt = courant_goal / (1.0 + jnp.max(speed[...]))
    dt_out[0] = dt
    third = dt * (1.0 / 3.0)

    def tracer(l, _):
        s1[C, l] = (FIRST.sixteen(start, C, l) + third * rate0[0, l]) * in_domain(
            l, place, last, False
        )
        return 0

    lax.fori_loop(REACH - 4, REACH + LEVELS + 4, tracer, 0)
    acoustic(
        (begin(start, PR, True), access(s1, PR)[1]),
        (begin(start, U), access(s1, U)[1]),
        (begin(start, V, True), access(s1, V)[1]),
        (begin(start, W), access(s1, W)[1]),
        begin(start, C),
        access(rate0, 1)[0],
        third,
        REACH - 4,
        LEVELS + 8,
        place,
        last,
    )
    half = dt * 0.5
    tiles = access(s1, C)[0]
    winds = [access(s1, f)[0] for f in (U, V, W)]

    def own_tracer(l, low):
        tendency, high = tracer_rate(tiles, winds, l, low)
        s2[C, l - REACH] = start[FIRST.at[C, "o"], l, :, 0:COLS] + half * tendency
        return high

    lax.fori_loop(REACH, REACH + LEVELS, own_tracer, tracer_high(tiles, winds[2], REACH - 1))

    def write(n, l, value):
        rate1[l] = value

    rates(SECTION, s1, (PR,), write, REACH - 1, LEVELS + 2)
    step = half / (NS // 2)
    acoustic(
        (begin(start, PR), access(fast, 0)[1]),
        (begin(start, U), access(fast, 1)[1]),
        (begin(start, V), access(fast, 2)[1]),
        (begin(start, W), access(fast, 3)[1]),
        access(s1, C)[0],
        access(rate1)[0],
        step,
        REACH - 1,
        LEVELS + 2,
        place,
        last,
    )
    acoustic(
        (access(fast, 0)[0], own_write(s2, PR)),
        (access(fast, 1)[0], own_write(s2, U)),
        (access(fast, 2)[0], own_write(s2, V)),
        (access(fast, 3)[0], own_write(s2, W)),
        access(s1, C)[0],
        access(rate1)[0],
        step,
        REACH,
        LEVELS,
        place,
        last,
    )

    def share(k, _):
        to_down, to_up = shared_rows(lambda f: s2[f, k])
        for n in range(3):
            down[n, k] = to_down[n]
            up[n, k] = to_up[n]
        return 0

    lax.fori_loop(0, LEVELS, share, 0)


class Whole:
    def rows(self, ref, field, l):
        return ref[field, l]

    sixteen = rows


SECTION = Whole()


def last_tracer(
    place_ref,
    dt_ref,
    own,
    above,
    below,
    from_right,
    from_left,
    from_up,
    from_down,
    fields,
    *rest,
):
    *chunks, ext, tracer, landed, fallen, total, by_depth, sem = rest
    place, last = place_ref[0], place_ref[1]
    dt = dt_ref[0]
    each = LEVELS // len(chunks)
    copies = [
        pltpu.make_async_copy(chunk, by_depth.at[pl.ds(n * each, each)], sem.at[n])
        for n, chunk in enumerate(chunks)
    ]
    for copy in copies:
        copy.start()
    assemble(
        SECOND, (own, above, below, from_right, from_left, from_up, from_down), ext, place, last
    )
    total[...] = jnp.zeros(total.shape, F32)
    for copy in copies:
        copy.wait()
    tiles = lambda l: SECOND.rows(ext, C, l)
    winds = [lambda l, f=f: SECOND.rows(ext, f, l) for f in (U, V, W)]

    def one(l, low):
        k = l - REACH
        tendency, high = tracer_rate(tiles, winds, l, low)
        c = fields[C, k] + dt * tendency
        tracer[k] = c
        grown = jnp.exp(growth * c)
        weights = (None, grown, grown * jnp.exp((0.5 * growth) * c))
        for depth in range(FMAX + 1):
            for moment in range(3):
                value = by_depth[k, depth, moment]
                if moment:
                    value = value * weights[moment]
                total[moment, k + FMAX - depth] += value
        return high

    lax.fori_loop(REACH, REACH + LEVELS, one, tracer_high(tiles, winds[2], REACH - 1))
    landed[...] = total[:, FMAX:]
    fallen[...] = total[:, 0:FMAX]


def last_section(place_ref, dt_ref, ext, start, tracer, out, rate, fast):
    place, last = place_ref[0], place_ref[1]
    step = dt_ref[0] / NS

    def write(n, l, value):
        rate[l] = value

    rates(SECOND, ext, (PR,), write, REACH - 3, LEVELS + 6)
    out[C] = tracer[...]
    names = (PR, U, V, W)
    for repeat in range(NS):
        reads = [
            begin(start, f) if repeat == 0 else access(fast, n)[0] for n, f in enumerate(names)
        ]
        writes = [
            own_write(out, f) if repeat == NS - 1 else access(fast, n)[1]
            for n, f in enumerate(names)
        ]
        acoustic(
            *zip(reads, writes),
            lambda l: SECOND.rows(ext, C, l),
            access(rate)[0],
            step,
            REACH - 3 + repeat,
            LEVELS + 6 - 2 * repeat,
            place,
            last,
        )


def deposit(radius, weight, column, counts, fall_depth, out):
    slots, levels = radius.shape[0], radius.shape[1]
    target = lax.broadcasted_iota(jnp.int32, (COLS, COLS), 0)
    row = lax.broadcasted_iota(jnp.int32, (ROWS, COLS), 0)
    per_step = 4

    for k in range(levels):
        out[k] = jnp.zeros(out.shape[1:], F32)
        live = counts[k]

        def some(step, _, k=k, live=live):
            sums = [[None] * 3 for _ in range(FMAX + 1)]
            for part in range(per_step):
                s = step * per_step + part
                r = radius[s, k]
                number = jnp.where(s < live, weight[s, k], 0.0)
                area = number * r * r
                terms = []
                for t in (number, area, area * r):
                    high = t.astype(jnp.bfloat16).astype(F32)
                    terms += [high, t - high]
                cols = column[s, k]
                left, right = [], []
                for j in range(ROWS):
                    left.append(
                        jnp.concatenate([jnp.where(row == j, t, 0.0) for t in terms], axis=0)
                    )
                    right.append(jnp.where(cols[j : j + 1] == target, 1.0, 0.0).astype(F32))
                sent = lax.dot_general(
                    jnp.concatenate(left, axis=1),
                    jnp.concatenate(right, axis=1),
                    (((1,), (1,)), ((), ())),
                    preferred_element_type=F32,
                )
                depth = jnp.broadcast_to(fall_depth[s, k], (ROWS, COLS))
                for d in range(FMAX + 1):
                    falls = depth == d
                    for m in range(3):
                        both = sent[16 * m : 16 * m + 8] + sent[16 * m + 8 : 16 * m + 16]
                        value = jnp.where(falls, both, 0.0)
                        sums[d][m] = value if sums[d][m] is None else sums[d][m] + value
            for d in range(FMAX + 1):
                for m in range(3):
                    out[k, d, m] += sums[d][m]
            return 0

        lax.fori_loop(0, slots // per_step, some, 0)


def vmem(n):
    return [pl.BlockSpec(memory_space=pltpu.VMEM)] * n


def smem(n):
    return [pl.BlockSpec(memory_space=pltpu.SMEM)] * n


def anywhere(n):
    return [pl.BlockSpec(memory_space=pl.ANY)] * n


def shaped(*dims):
    return jax.ShapeDtypeStruct(dims, F32)


def held(*dims):
    return pltpu.VMEM(dims, F32)


def call(kernel, name, ins, outs, scratch=(), out_specs=None, flops=None, grant=4):
    made = pl.pallas_call(
        kernel,
        name=name,
        in_specs=ins,
        out_specs=tuple(out_specs or vmem(len(outs))),
        out_shape=tuple(outs),
        scratch_shapes=list(scratch),
        compiler_params=pltpu.CompilerParams(vmem_limit_bytes=grant << 20),
        cost_estimate=(
            pl.CostEstimate(flops=flops, bytes_accessed=0, transcendentals=0) if flops else None
        ),
    )

    def run(*operands):
        return made(
            *(
                pltpu.with_memory_space_constraint(value, pltpu.VMEM)
                if spec.memory_space == pltpu.VMEM
                else value
                for spec, value in zip(ins, operands)
            )
        )

    return run


def both_ways(down, axis, up):
    count = lax.axis_size(axis)
    return (
        lax.ppermute(down, axis, [((i + 1) % count, i) for i in range(count)]),
        lax.ppermute(up, axis, [(i, (i + 1) % count) for i in range(count)]),
    )


def exchange(plan, own, down, up, token):
    above, below = both_ways(down, "gy", up)
    to_left, to_right = call(
        pack_columns(plan),
        "pack_columns",
        vmem(3) + anywhere(1),
        [held(LEVELS, ROWS, COLS)] * 2,
    )(own, above, below, token)
    from_right, from_left = both_ways(to_left, "gx", to_right)
    tiles = len(plan.carried)
    to_down, to_up = call(
        pack_levels(plan), "pack_levels", vmem(5), [held(tiles, ROWS, COLS)] * 2
    )(own, above, below, from_right, from_left)
    from_up, from_down = both_ways(to_down, "gz", to_up)
    return above, below, from_right, from_left, from_up, from_down


def top_speed(fields, place, last):
    w = fields[4] * (
        (jnp.arange(LEVELS) < LEVELS - 1) | (place != last)
    ).astype(F32)[:, None, None]
    local = jnp.max(jnp.abs(fields[2]) + jnp.abs(fields[3]) + jnp.abs(w))
    devices = lax.axis_size(GRID_AXES)
    everywhere = jnp.broadcast_to(local, (devices, 1, COLS))
    return lax.all_to_all(everywhere, GRID_AXES, 0, 0)


def droplets(radius, weight, column, counts, fall_depth, chunk):
    slots = radius.shape[0]
    made = []
    for n in range(LEVELS // chunk):
        whole = pl.BlockSpec((slots, chunk, ROWS, COLS), lambda i, n=n: (0, n, 0, 0))
        made.append(
            pl.pallas_call(
                deposit,
                name="deposit",
                grid=(1,),
                in_specs=[
                    whole,
                    whole,
                    whole,
                    pl.BlockSpec((chunk, ROWS, COLS), lambda i, n=n: (n, 0, 0)),
                    pl.BlockSpec((slots, chunk, ROWS, 1), lambda i, n=n: (0, n, 0, 0)),
                ],
                out_specs=pl.BlockSpec(
                    (chunk, FMAX + 1, 3, ROWS, COLS), lambda i: (0, 0, 0, 0, 0)
                ),
                out_shape=shaped(chunk, FMAX + 1, 3, ROWS, COLS),
                compiler_params=pltpu.CompilerParams(vmem_limit_bytes=12 << 20),
                cost_estimate=pl.CostEstimate(
                    flops=200_000_000, bytes_accessed=0, transcendentals=0
                ),
            )(radius, weight, column, counts, fall_depth)
        )
    return made


def per_device(fields, radius, weight, column, counts, fall_depth):
    place = lax.axis_index("gz")
    last = lax.axis_size("gz") - 1
    where = jnp.stack([place, jnp.int32(last)]).astype(jnp.int32)
    by_depth = droplets(radius, weight, column, counts, fall_depth, 2)
    speed = top_speed(fields, place, last)
    halos = exchange(FIRST, fields, fields, fields, speed)
    start, rate0 = call(
        first_rates,
        "first_rates",
        smem(1) + vmem(7),
        [held(len(FIRST.tiles), DEPTH, ROWS, WIDE), held(2, DEPTH, 2 * ROWS, WIDE)],
    )(where, fields, *halos)
    s2, down, up, dt = call(
        two_sections,
        "two_sections",
        smem(1) + vmem(3),
        [held(5, LEVELS, ROWS, COLS)] + [held(3, LEVELS, ROWS, COLS)] * 2 + [shaped(1)],
        scratch=[
            pltpu.VMEM((5, DEPTH, 2 * ROWS, WIDE), F32),
            pltpu.VMEM((DEPTH, 2 * ROWS, WIDE), F32),
            pltpu.VMEM((4, DEPTH, 2 * ROWS, WIDE), F32),
        ],
        out_specs=vmem(3) + smem(1),
        grant=10,
    )(where, speed, start, rate0)
    halos = exchange(SECOND, s2, down, up, speed)
    ext, tracer, landed, fallen = call(
        last_tracer,
        "last_tracer",
        smem(2) + vmem(8) + anywhere(len(by_depth)),
        [
            held(len(SECOND.tiles), DEPTH, ROWS, WIDE),
            held(LEVELS, ROWS, COLS),
            held(3, LEVELS, ROWS, COLS),
            held(3, FMAX, ROWS, COLS),
        ],
        scratch=[
            pltpu.VMEM((3, LEVELS + FMAX, ROWS, COLS), F32),
            pltpu.VMEM((LEVELS, FMAX + 1, 3, ROWS, COLS), F32),
            pltpu.SemaphoreType.DMA((len(by_depth),)),
        ],
    )(where, dt, s2, *halos, fields, *by_depth)
    count = lax.axis_size("gz")
    arrived = lax.ppermute(fallen, "gz", [((i + 1) % count, i) for i in range(count)])
    (new_fields,) = call(
        last_section,
        "last_section",
        smem(2) + vmem(3),
        [shaped(5, LEVELS, ROWS, COLS)],
        scratch=[
            pltpu.VMEM((DEPTH, 2 * ROWS, WIDE), F32),
            pltpu.VMEM((4, DEPTH, 2 * ROWS, WIDE), F32),
        ],
        flops=1_000_000_000,
        grant=8,
    )(where, dt, ext, start, tracer)
    arrived = jnp.where(place == last, 0.0, arrived)
    moments = landed.at[:, LEVELS - FMAX :].add(arrived)
    return (new_fields, moments)


def solution(mesh):
    spread = P(None, "gz", "gy", "gx")
    return jax.shard_map(
        per_device,
        mesh=mesh,
        in_specs=(spread, spread, spread, spread, P("gz", "gy", "gx"), spread),
        out_specs=(spread, spread),
        check_vma=False,
    )
```

time: 186 us -> 148 us (0.80); the launches traced: 183 us -> 147 us
  Pallas kernels: 101 us -> 68.1 us
  blocking collectives: 0 us -> 26.5 us
  starting transfers between devices: 32 us -> 15.9 us
  waiting for transfers between devices: 34.3 us -> 25.3 us
  local copies, waits for them, and re-layouts: 12.9 us -> 8.61 us
    pallas_call x16, Pallas kernels: 101 us -> 68.1 us  [the longest x8 52.8 us: run(): made(*(pltpu.with_memory_space_constraint(value, pltpu.VMEM) if spec.memo...]
    all_to_all x0 -> x1, blocking collectives: none -> 26.5 us  [top_speed(): return lax.all_to_all(everywhere, GRID_AXES, 0, 0)]
    all_to_all x1 -> x0, starting transfers between devices: 14.7 us -> none  [top_speed(): return lax.all_to_all(everywhere, GRID_AXES, 0, 0)]
    ppermute x12, waiting for transfers between devices: 34.3 us -> 25.3 us  [the longest x6 17.8 us: both_ways(): lax.ppermute(down, axis, [((i + 1) % count, i) for i in range(count)])]
    unnamed x56 -> x42, local copies, waits for them, and re-layouts: 11.5 us -> 7.9 us
  transfers between devices with their start and end apart: 14 -> 13, of which waited for: 6 -> 8; matrix products, arithmetic and copies ran while one was open for 3% -> 2% of each run, Pallas kernels for 33% -> 22%
where the time goes in v1:
time: 148 us; the launch traced here: 147 us
  Pallas kernels  68.1 us (46%)
  blocking collectives  26.5 us (18%)
  waiting for transfers between devices  25.3 us (17%)
  starting transfers between devices  15.9 us (11%)
  local copies, waits for them, and re-layouts  8.61 us (6%)
  other arithmetic  1.7 us (1%)
    pallas_call x8, Pallas kernels, run(): made(*(pltpu.with_memory_space_constraint(value, pltpu.VMEM) if spec.memo...  52.8 us
    all_to_all x1, blocking collectives, top_speed(): return lax.all_to_all(everywhere, GRID_AXES, 0, 0)  26.5 us
    ppermute x6, waiting for transfers between devices, both_ways(): lax.ppermute(down, axis, [((i + 1) % count, i) for i in range(count)])  17.8 us
    pallas_call x8, Pallas kernels, droplets(): pl.pallas_call(deposit, name='deposit', grid=(1,), in_specs=[whole, whole...  15.3 us
    ppermute x6, starting transfers between devices, both_ways(): lax.ppermute(down, axis, [((i + 1) % count, i) for i in range(count)])  7.95 us
    unnamed x42, local copies, waits for them, and re-layouts  7.9 us
    ppermute x6, waiting for transfers between devices, both_ways(): lax.ppermute(up, axis, [(i, (i + 1) % count) for i in range(count)])  7.53 us
    ppermute x6, starting transfers between devices, both_ways(): lax.ppermute(up, axis, [(i, (i + 1) % count) for i in range(count)])  5.92 us
  transfers between devices with their start and end apart: 13, of which 8 were waited for; matrix products, arithmetic and copies ran while one was open for 2% of the time, Pallas kernels for 22%

profile of v1, /device:TPU:4, one launch (start us, length us, event | category | flops | bytes accessed | tf_op | source)
XLA Modules:
  0.0 147.0 jit_solution(1825343166710863076)
XLA Ops:
  0.6 1.9 %collective-permute-start.1 = (f32[5,16,8,128]{3,2,1,0:T(8,128)}, f32[5,16,8,128]{3,2,1,0:T(8,128)S(1)}, u32[]{:S(2)}, u32[]{:S(2)}) collective-permute-start(f32[5,16,8,128]{3,2,1,0:T(8,128)} %fields.1), channel_id=1, source_target_pairs={{0,4},{4,8},{8,12},{12,16},{16,20},{20,24},{24,28},{28,32},{32,36}... | collective-permute-start | bytes 983048 | tf_op jit(solution)/shard_map/ppermute | solution.py:612
  2.6 1.7 %collective-permute-start = (f32[5,16,8,128]{3,2,1,0:T(8,128)}, f32[5,16,8,128]{3,2,1,0:T(8,128)S(1)}, u32[]{:S(2)}, u32[]{:S(2)}) collective-permute-start(f32[5,16,8,128]{3,2,1,0:T(8,128)} %fields.1), channel_id=1, source_target_pairs={{4,0},{8,4},{12,8},{16,12},{20,16},{24,20},{28,24},{32,28},{36,32}... | collective-permute-start | bytes 983048 | tf_op jit(solution)/shard_map/ppermute | solution.py:611
  6.6 26.5 %all_to_all.5.speed = f32[256,1,128]{2,1,0:T(1,128)S(1)} all-to-all(f32[256,1,128]{2,1,0:T(1,128)S(1)} %broadcast_in_dim.8), channel_id=1, replica_groups=mesh['gx'=4,'gy'=16,'gz'=4] {'gx','gy','gz'}, dimensions={0} | all-to-all | bytes 262144 | tf_op jit(solution)/shard_map/all_to_all | solution.py:640
  35.8 2.3 %collective-permute-done.2.from_right = f32[16,8,128]{2,1,0:T(8,128)S(1)} collective-permute-done((f32[16,8,128]{2,1,0:T(8,128)S(1)}, f32[16,8,128]{2,1,0:T(8,128)S(1)}, u32[]{:S(2)}, u32[]{:S(2)}) %collective-permute-start.2) | collective-permute-done | bytes 65568 | tf_op jit(solution)/shard_map/ppermute | solution.py:611
  41.7 7.5 %collective-permute-done.4.from_up = f32[91,8,128]{2,1,0:T(8,128)S(1)} collective-permute-done((f32[91,8,128]{2,1,0:T(8,128)S(1)}, f32[91,8,128]{2,1,0:T(8,128)S(1)}, u32[]{:S(2)}, u32[]{:S(2)}) %collective-permute-start.4) | collective-permute-done | bytes 372768 | tf_op jit(solution)/shard_map/ppermute | solution.py:611
  49.2 2.6 %collective-permute-done.5.from_down = f32[91,8,128]{2,1,0:T(8,128)S(1)} collective-permute-done((f32[91,8,128]{2,1,0:T(8,128)S(1)}, f32[91,8,128]{2,1,0:T(8,128)S(1)}, u32[]{:S(2)}, u32[]{:S(2)}) %collective-permute-start.5) | collective-permute-done | bytes 372768 | tf_op jit(solution)/shard_map/ppermute | solution.py:612
  52.8 7.2 %first_rates.1 = (f32[13,30,8,256]{3,2,1,0:T(8,128)S(1)}, f32[2,30,16,256]{3,2,1,0:T(8,128)S(1)}) custom-call(s32[2]{0:T(128)S(1)} %pad_add_fusion.place_ref, f32[5,16,8,128]{3,2,1,0:T(8,128)S(1)} %copy-done.6, f32[5,16,8,128]{3,2,1,0:T(8,128)S(1)} %collective-permute-done.above, f32[5,16,8,128]{3,2,1,0:T(8,128)S(1)} %collective-permute-done.1.below, ...), custom_call_target="tpu_custom_call" | custom-call | tf_op jit(solution)/shard_map/first_rates/pallas_call | solution.py:596
  60.1 15.9 %two_sections.1 = (f32[5,16,8,128]{3,2,1,0:T(8,128)S(1)}, f32[3,16,8,128]{3,2,1,0:T(8,128)S(1)}, f32[3,16,8,128]{3,2,1,0:T(8,128)S(1)}, f32[1]{0:T(128)}) custom-call(s32[2]{0:T(128)S(1)} %pad_add_fusion.place_ref, f32[256,1,128]{2,1,0:T(1,128)S(1)} %all_to_all.5.speed, f32[13,30,8,256]{3,2,1,0:T(8,128)S(1)} %get-tuple-element.36.start, ...), custom_call_target="tpu_custom_call" | custom-call | tf_op jit(solution)/shard_map/two_sections/pallas_call | solution.py:596
  76.1 3.0 %collective-permute-start.6 = (f32[3,16,8,128]{3,2,1,0:T(8,128)S(1)}, f32[3,16,8,128]{3,2,1,0:T(8,128)S(1)}, u32[]{:S(2)}, u32[]{:S(2)}) collective-permute-start(f32[3,16,8,128]{3,2,1,0:T(8,128)S(1)} %get-tuple-element.40), channel_id=1, source_target_pairs={{4,0},{8,4},{12,8},{16,12},{20,16},{24,20},{28,24},{32,28},{36,32}... | collective-permute-start | bytes 589832 | tf_op jit(solution)/shard_map/ppermute | solution.py:611
  80.6 6.0 %collective-permute-done.6.above = f32[3,16,8,128]{3,2,1,0:T(8,128)S(1)} collective-permute-done((f32[3,16,8,128]{3,2,1,0:T(8,128)S(1)}, f32[3,16,8,128]{3,2,1,0:T(8,128)S(1)}, u32[]{:S(2)}, u32[]{:S(2)}) %collective-permute-start.6) | collective-permute-done | bytes 196640 | tf_op jit(solution)/shard_map/ppermute | solution.py:611
  89.7 1.9 %collective-permute-done.8.from_right = f32[16,8,128]{2,1,0:T(8,128)S(1)} collective-permute-done((f32[16,8,128]{2,1,0:T(8,128)S(1)}, f32[16,8,128]{2,1,0:T(8,128)S(1)}, u32[]{:S(2)}, u32[]{:S(2)}) %collective-permute-start.8) | collective-permute-done | bytes 65568 | tf_op jit(solution)/shard_map/ppermute | solution.py:611
  91.6 1.9 %collective-permute-done.9.from_left = f32[16,8,128]{2,1,0:T(8,128)S(1)} collective-permute-done((f32[16,8,128]{2,1,0:T(8,128)S(1)}, f32[16,8,128]{2,1,0:T(8,128)S(1)}, u32[]{:S(2)}, u32[]{:S(2)}) %collective-permute-start.9) | collective-permute-done | bytes 65568 | tf_op jit(solution)/shard_map/ppermute | solution.py:612
  97.2 1.9 %deposit.15.rest_7_ = f32[2,9,3,8,128]{4,3,2,1,0:T(8,128)S(1)} custom-call(f32[8,16,8,128]{3,2,1,0:T(8,128)S(1)} %copy-done, f32[8,16,8,128]{3,2,1,0:T(8,128)S(1)} %copy-done.1, s32[8,16,8,128]{3,2,1,0:T(8,128)S(1)} %copy-done.2, s32[16,8,128]{2,1,0:T(8,128)S(1)} %copy-done.8, s32[8,16,8,1]{3,2,1,0:T(8,128)S(1)} %copy.8.fall_depth), custom_call_target="tpu_custom_call" | custom-call | flops 200000000 | tf_op jit(solution)/shard_map/deposit/pallas_call | solution.py:649
  99.1 1.9 %deposit.14.rest_6_ = f32[2,9,3,8,128]{4,3,2,1,0:T(8,128)S(1)} custom-call(f32[8,16,8,128]{3,2,1,0:T(8,128)S(1)} %copy-done, f32[8,16,8,128]{3,2,1,0:T(8,128)S(1)} %copy-done.1, s32[8,16,8,128]{3,2,1,0:T(8,128)S(1)} %copy-done.2, s32[16,8,128]{2,1,0:T(8,128)S(1)} %copy-done.8, s32[8,16,8,1]{3,2,1,0:T(8,128)S(1)} %copy.8.fall_depth), custom_call_target="tpu_custom_call" | custom-call | flops 200000000 | tf_op jit(solution)/shard_map/deposit/pallas_call | solution.py:649
  101.0 1.9 %deposit.13.rest_5_ = f32[2,9,3,8,128]{4,3,2,1,0:T(8,128)S(1)} custom-call(f32[8,16,8,128]{3,2,1,0:T(8,128)S(1)} %copy-done, f32[8,16,8,128]{3,2,1,0:T(8,128)S(1)} %copy-done.1, s32[8,16,8,128]{3,2,1,0:T(8,128)S(1)} %copy-done.2, s32[16,8,128]{2,1,0:T(8,128)S(1)} %copy-done.8, s32[8,16,8,1]{3,2,1,0:T(8,128)S(1)} %copy.8.fall_depth), custom_call_target="tpu_custom_call" | custom-call | flops 200000000 | tf_op jit(solution)/shard_map/deposit/pallas_call | solution.py:649
  103.0 1.9 %deposit.12.rest_4_ = f32[2,9,3,8,128]{4,3,2,1,0:T(8,128)S(1)} custom-call(f32[8,16,8,128]{3,2,1,0:T(8,128)S(1)} %copy-done, f32[8,16,8,128]{3,2,1,0:T(8,128)S(1)} %copy-done.1, s32[8,16,8,128]{3,2,1,0:T(8,128)S(1)} %copy-done.2, s32[16,8,128]{2,1,0:T(8,128)S(1)} %copy-done.8, s32[8,16,8,1]{3,2,1,0:T(8,128)S(1)} %copy.8.fall_depth), custom_call_target="tpu_custom_call" | custom-call | flops 200000000 | tf_op jit(solution)/shard_map/deposit/pallas_call | solution.py:649
  104.9 1.9 %deposit.11.rest_3_ = f32[2,9,3,8,128]{4,3,2,1,0:T(8,128)S(1)} custom-call(f32[8,16,8,128]{3,2,1,0:T(8,128)S(1)} %copy-done, f32[8,16,8,128]{3,2,1,0:T(8,128)S(1)} %copy-done.1, s32[8,16,8,128]{3,2,1,0:T(8,128)S(1)} %copy-done.2, s32[16,8,128]{2,1,0:T(8,128)S(1)} %copy-done.8, s32[8,16,8,1]{3,2,1,0:T(8,128)S(1)} %copy.8.fall_depth), custom_call_target="tpu_custom_call" | custom-call | flops 200000000 | tf_op jit(solution)/shard_map/deposit/pallas_call | solution.py:649
  106.8 1.9 %deposit.10.rest_2_ = f32[2,9,3,8,128]{4,3,2,1,0:T(8,128)S(1)} custom-call(f32[8,16,8,128]{3,2,1,0:T(8,128)S(1)} %copy-done, f32[8,16,8,128]{3,2,1,0:T(8,128)S(1)} %copy-done.1, s32[8,16,8,128]{3,2,1,0:T(8,128)S(1)} %copy-done.2, s32[16,8,128]{2,1,0:T(8,128)S(1)} %copy-done.8, s32[8,16,8,1]{3,2,1,0:T(8,128)S(1)} %copy.8.fall_depth), custom_call_target="tpu_custom_call" | custom-call | flops 200000000 | tf_op jit(solution)/shard_map/deposit/pallas_call | solution.py:649
  108.8 1.9 %deposit.9.rest_1_ = f32[2,9,3,8,128]{4,3,2,1,0:T(8,128)S(1)} custom-call(f32[8,16,8,128]{3,2,1,0:T(8,128)S(1)} %copy-done, f32[8,16,8,128]{3,2,1,0:T(8,128)S(1)} %copy-done.1, s32[8,16,8,128]{3,2,1,0:T(8,128)S(1)} %copy-done.2, s32[16,8,128]{2,1,0:T(8,128)S(1)} %copy-done.8, s32[8,16,8,1]{3,2,1,0:T(8,128)S(1)} %copy.8.fall_depth), custom_call_target="tpu_custom_call" | custom-call | flops 200000000 | tf_op jit(solution)/shard_map/deposit/pallas_call | solution.py:649
  110.7 1.9 %deposit.8.rest_0_ = f32[2,9,3,8,128]{4,3,2,1,0:T(8,128)S(1)} custom-call(f32[8,16,8,128]{3,2,1,0:T(8,128)S(1)} %copy-done, f32[8,16,8,128]{3,2,1,0:T(8,128)S(1)} %copy-done.1, s32[8,16,8,128]{3,2,1,0:T(8,128)S(1)} %copy-done.2, s32[16,8,128]{2,1,0:T(8,128)S(1)} %copy-done.8, s32[8,16,8,1]{3,2,1,0:T(8,128)S(1)} %copy.8.fall_depth), custom_call_target="tpu_custom_call" | custom-call | flops 200000000 | tf_op jit(solution)/shard_map/deposit/pallas_call | solution.py:649
  112.7 9.6 %last_tracer.1 = (f32[11,30,8,256]{3,2,1,0:T(8,128)S(1)}, f32[16,8,128]{2,1,0:T(8,128)S(1)}, f32[3,16,8,128]{3,2,1,0:T(8,128)S(1)}, f32[3,8,8,128]{3,2,1,0:T(8,128)}) custom-call(s32[2]{0:T(128)S(1)} %pad_add_fusion.place_ref, f32[1]{0:T(128)} %get-tuple-element.38.dt_ref, f32[5,16,8,128]{3,2,1,0:T(8,128)S(1)} %copy-done.10, ...), custom_call_target="tpu_custom_call" | custom-call | tf_op jit(solution)/shard_map/last_tracer/pallas_call | solution.py:596
  124.4 2.0 %collective-permute-start.12 = (f32[3,8,8,128]{3,2,1,0:T(8,128)}, f32[3,8,8,128]{3,2,1,0:T(8,128)S(1)}, u32[]{:S(2)}, u32[]{:S(2)}) collective-permute-start(f32[3,8,8,128]{3,2,1,0:T(8,128)} %get-tuple-element.49), channel_id=1, source_target_pairs={{1,0},{2,1},{3,2},{0,3},{5,4},{6,5},{7,6},{4,7},{9,8},{10,9},{11,1... | collective-permute-start | bytes 294920 | tf_op jit(solution)/shard_map/ppermute | solution.py:717
  126.4 1.8 %copy-done.12 = f32[11,30,8,256]{3,2,1,0:T(8,128)S(1)} copy-done((f32[11,30,8,256]{3,2,1,0:T(8,128)S(1)}, f32[11,30,8,256]{3,2,1,0:T(8,128)}, u32[]{:S(2)}) %copy-start.12) | copy-done | bytes 2703384
  129.0 17.2 %last_section.1 = f32[5,16,8,128]{3,2,1,0:T(8,128)} custom-call(s32[2]{0:T(128)S(1)} %pad_add_fusion.place_ref, f32[1]{0:T(128)} %get-tuple-element.38.dt_ref, f32[11,30,8,256]{3,2,1,0:T(8,128)S(1)} %copy-done.12, f32[13,30,8,256]{3,2,1,0:T(8,128)S(1)} %copy-done.4, f32[16,8,128]{2,1,0:T(8,128)S(1)} %copy-done.18), custom_call_target="tpu_custom_call" | custom-call | flops 1000000000 | tf_op jit(solution)/shard_map/last_section/pallas_call | solution.py:596
  (66 shorter events, 21.6 us)
Async XLA Ops:
  0.6 32.4 %collective-permute-start.1 = (f32[5,16,8,128]{3,2,1,0:T(8,128)}, f32[5,16,8,128]{3,2,1,0:T(8,128)S(1)}, u32[]{:S(2)}, u32[]{:S(2)}) collective-permute-start(f32[5,16,8,128]{3,2,1,0:T(8,128)} %fields.1), channel_id=1, source_target_pairs={{0,4},{4,8},{8,12},{12,16},{16,20},{20,24},{24,28},{28,32},{32,36}... | collective-permute-start | bytes 983048 | tf_op jit(solution)/shard_map/ppermute | solution.py:612
  2.6 30.5 %collective-permute-start = (f32[5,16,8,128]{3,2,1,0:T(8,128)}, f32[5,16,8,128]{3,2,1,0:T(8,128)S(1)}, u32[]{:S(2)}, u32[]{:S(2)}) collective-permute-start(f32[5,16,8,128]{3,2,1,0:T(8,128)} %fields.1), channel_id=1, source_target_pairs={{4,0},{8,4},{12,8},{16,12},{20,16},{24,20},{28,24},{32,28},{36,32}... | collective-permute-start | bytes 983048 | tf_op jit(solution)/shard_map/ppermute | solution.py:611
  35.0 3.1 %collective-permute-start.2 = (f32[16,8,128]{2,1,0:T(8,128)S(1)}, f32[16,8,128]{2,1,0:T(8,128)S(1)}, u32[]{:S(2)}, u32[]{:S(2)}) collective-permute-start(f32[16,8,128]{2,1,0:T(8,128)S(1)} %get-tuple-element.32), channel_id=1, source_target_pairs={{64,0},{128,64},{192,128},{0,192},{65,1},{129,65},{193,129},{1,193... | collective-permute-start | bytes 196616 | tf_op jit(solution)/shard_map/ppermute | solution.py:611
  35.8 3.7 %collective-permute-start.3 = (f32[16,8,128]{2,1,0:T(8,128)S(1)}, f32[16,8,128]{2,1,0:T(8,128)S(1)}, u32[]{:S(2)}, u32[]{:S(2)}) collective-permute-start(f32[16,8,128]{2,1,0:T(8,128)S(1)} %get-tuple-element.33), channel_id=1, source_target_pairs={{0,64},{64,128},{128,192},{192,0},{1,65},{65,129},{129,193},{193,1... | collective-permute-start | bytes 196616 | tf_op jit(solution)/shard_map/ppermute | solution.py:612
  39.5 9.7 %collective-permute-start.4 = (f32[91,8,128]{2,1,0:T(8,128)S(1)}, f32[91,8,128]{2,1,0:T(8,128)S(1)}, u32[]{:S(2)}, u32[]{:S(2)}) collective-permute-start(f32[91,8,128]{2,1,0:T(8,128)S(1)} %get-tuple-element.34), channel_id=1, source_target_pairs={{1,0},{2,1},{3,2},{0,3},{5,4},{6,5},{7,6},{4,7},{9,8},{10,9},{11,1... | collective-permute-start | bytes 1118216 | tf_op jit(solution)/shard_map/ppermute | solution.py:611
  40.8 11.1 %collective-permute-start.5 = (f32[91,8,128]{2,1,0:T(8,128)S(1)}, f32[91,8,128]{2,1,0:T(8,128)S(1)}, u32[]{:S(2)}, u32[]{:S(2)}) collective-permute-start(f32[91,8,128]{2,1,0:T(8,128)S(1)} %get-tuple-element.35), channel_id=1, source_target_pairs={{0,1},{1,2},{2,3},{3,0},{4,5},{5,6},{6,7},{7,4},{8,9},{9,10},{10,1... | collective-permute-start | bytes 1118216 | tf_op jit(solution)/shard_map/ppermute | solution.py:612
  60.0 35.1 %copy-start.3 = (f32[13,30,8,256]{3,2,1,0:T(8,128)}, f32[13,30,8,256]{3,2,1,0:T(8,128)S(1)}, u32[]{:S(2)}) copy-start(f32[13,30,8,256]{3,2,1,0:T(8,128)S(1)} %get-tuple-element.36.start) | copy-start | bytes 9584644
  60.1 36.6 %copy-start.19 = (s32[8,16,8,1]{1,3,2,0:T(1,128)S(1)}, s32[8,16,8,1]{1,3,2,0:T(1,128)}, u32[]{:S(2)}) copy-start(s32[8,16,8,1]{1,3,2,0:T(1,128)} %param.13) | copy-start | bytes 12292
  60.1 37.1 %copy-start = (f32[8,16,8,128]{3,2,1,0:T(8,128)S(1)}, f32[8,16,8,128]{3,2,1,0:T(8,128)}, u32[]{:S(2)}) copy-start(f32[8,16,8,128]{3,2,1,0:T(8,128)} %radius.15) | copy-start | bytes 1572868
  60.1 37.1 %copy-start.1 = (f32[8,16,8,128]{3,2,1,0:T(8,128)S(1)}, f32[8,16,8,128]{3,2,1,0:T(8,128)}, u32[]{:S(2)}) copy-start(f32[8,16,8,128]{3,2,1,0:T(8,128)} %weight.15) | copy-start | bytes 1572868
  60.1 37.1 %copy-start.2 = (s32[8,16,8,128]{3,2,1,0:T(8,128)S(1)}, s32[8,16,8,128]{3,2,1,0:T(8,128)}, u32[]{:S(2)}) copy-start(s32[8,16,8,128]{3,2,1,0:T(8,128)} %column.15) | copy-start | bytes 1572868
  60.1 37.1 %copy-start.8 = (s32[16,8,128]{2,1,0:T(8,128)S(1)}, s32[16,8,128]{2,1,0:T(8,128)}, u32[]{:S(2)}) copy-start(s32[16,8,128]{2,1,0:T(8,128)} %counts.15) | copy-start | bytes 196612
  76.1 19.1 %copy-start.9 = (f32[5,16,8,128]{3,2,1,0:T(8,128)}, f32[5,16,8,128]{3,2,1,0:T(8,128)S(1)}, u32[]{:S(2)}) copy-start(f32[5,16,8,128]{3,2,1,0:T(8,128)S(1)} %get-tuple-element.39.own) | copy-start | bytes 983044
  76.1 10.5 %collective-permute-start.6 = (f32[3,16,8,128]{3,2,1,0:T(8,128)S(1)}, f32[3,16,8,128]{3,2,1,0:T(8,128)S(1)}, u32[]{:S(2)}, u32[]{:S(2)}) collective-permute-start(f32[3,16,8,128]{3,2,1,0:T(8,128)S(1)} %get-tuple-element.40), channel_id=1, source_target_pairs={{4,0},{8,4},{12,8},{16,12},{20,16},{24,20},{28,24},{32,28},{36,32}... | collective-permute-start | bytes 589832 | tf_op jit(solution)/shard_map/ppermute | solution.py:611
  79.1 9.1 %collective-permute-start.7 = (f32[3,16,8,128]{3,2,1,0:T(8,128)S(1)}, f32[3,16,8,128]{3,2,1,0:T(8,128)S(1)}, u32[]{:S(2)}, u32[]{:S(2)}) collective-permute-start(f32[3,16,8,128]{3,2,1,0:T(8,128)S(1)} %get-tuple-element.41), channel_id=1, source_target_pairs={{0,4},{4,8},{8,12},{12,16},{16,20},{20,24},{24,28},{28,32},{32,36}... | collective-permute-start | bytes 589832 | tf_op jit(solution)/shard_map/ppermute | solution.py:612
  86.6 8.6 %copy-start.13 = (f32[3,16,8,128]{3,2,1,0:T(8,128)}, f32[3,16,8,128]{3,2,1,0:T(8,128)S(1)}, u32[]{:S(2)}) copy-start(f32[3,16,8,128]{3,2,1,0:T(8,128)S(1)} %collective-permute-done.6.above) | copy-start | bytes 589828
  88.2 7.0 %copy-start.15 = (f32[3,16,8,128]{3,2,1,0:T(8,128)}, f32[3,16,8,128]{3,2,1,0:T(8,128)S(1)}, u32[]{:S(2)}) copy-start(f32[3,16,8,128]{3,2,1,0:T(8,128)S(1)} %collective-permute-done.7.below) | copy-start | bytes 589828
  89.1 2.5 %collective-permute-start.8 = (f32[16,8,128]{2,1,0:T(8,128)S(1)}, f32[16,8,128]{2,1,0:T(8,128)S(1)}, u32[]{:S(2)}, u32[]{:S(2)}) collective-permute-start(f32[16,8,128]{2,1,0:T(8,128)S(1)} %get-tuple-element.42), channel_id=1, source_target_pairs={{64,0},{128,64},{192,128},{0,192},{65,1},{129,65},{193,129},{1,193... | collective-permute-start | bytes 196616 | tf_op jit(solution)/shard_map/ppermute | solution.py:611
  89.6 4.0 %collective-permute-start.9 = (f32[16,8,128]{2,1,0:T(8,128)S(1)}, f32[16,8,128]{2,1,0:T(8,128)S(1)}, u32[]{:S(2)}, u32[]{:S(2)}) collective-permute-start(f32[16,8,128]{2,1,0:T(8,128)S(1)} %get-tuple-element.43), channel_id=1, source_target_pairs={{0,64},{64,128},{128,192},{192,0},{1,65},{65,129},{129,193},{193,1... | collective-permute-start | bytes 196616 | tf_op jit(solution)/shard_map/ppermute | solution.py:612
  94.4 18.3 %collective-permute-start.10 = (f32[62,8,128]{2,1,0:T(8,128)}, f32[62,8,128]{2,1,0:T(8,128)}, u32[]{:S(2)}, u32[]{:S(2)}) collective-permute-start(f32[62,8,128]{2,1,0:T(8,128)} %get-tuple-element.44), channel_id=1, source_target_pairs={{1,0},{2,1},{3,2},{0,3},{5,4},{6,5},{7,6},{4,7},{9,8},{10,9},{11,1... | collective-permute-start | bytes 761864 | tf_op jit(solution)/shard_map/ppermute | solution.py:611
  95.2 17.5 %collective-permute-start.11 = (f32[62,8,128]{2,1,0:T(8,128)}, f32[62,8,128]{2,1,0:T(8,128)}, u32[]{:S(2)}, u32[]{:S(2)}) collective-permute-start(f32[62,8,128]{2,1,0:T(8,128)} %get-tuple-element.45), channel_id=1, source_target_pairs={{0,1},{1,2},{2,3},{3,0},{4,5},{5,6},{6,7},{7,4},{8,9},{9,10},{10,1... | collective-permute-start | bytes 761864 | tf_op jit(solution)/shard_map/ppermute | solution.py:612
  106.8 5.9 %copy-start.7 = (f32[5,16,8,128]{3,2,1,0:T(8,128)S(1)}, f32[5,16,8,128]{3,2,1,0:T(8,128)}, u32[]{:S(2)}) copy-start(f32[5,16,8,128]{3,2,1,0:T(8,128)} %fields.1) | copy-start | bytes 983044
  112.6 13.8 %copy-start.4 = (f32[13,30,8,256]{3,2,1,0:T(8,128)S(1)}, f32[13,30,8,256]{3,2,1,0:T(8,128)}, u32[]{:S(2)}) copy-start(f32[13,30,8,256]{3,2,1,0:T(8,128)} %copy-done.3) | copy-start | bytes 9584644
  124.4 21.8 %collective-permute-start.12 = (f32[3,8,8,128]{3,2,1,0:T(8,128)}, f32[3,8,8,128]{3,2,1,0:T(8,128)S(1)}, u32[]{:S(2)}, u32[]{:S(2)}) collective-permute-start(f32[3,8,8,128]{3,2,1,0:T(8,128)} %get-tuple-element.49), channel_id=1, source_target_pairs={{1,0},{2,1},{3,2},{0,3},{5,4},{6,5},{7,6},{4,7},{9,8},{10,9},{11,1... | collective-permute-start | bytes 294920 | tf_op jit(solution)/shard_map/ppermute | solution.py:717
  (9 other events, 24.3 us)

commit v2 on v1

--- a/solution.py
+++ b/solution.py
@@ -7,6 +7,7 @@
 
 NS = 4
 FMAX = 8
+EARLY = 5
 GRID_AXES = ("gx", "gy", "gz")
 
 sound_speed = 10.0
@@ -111,7 +112,8 @@
 
 
 def pack_columns(plan):
-    def kernel(own, above, below, speed, to_left, to_right):
+    def kernel(own, above, below, *rest):
+        to_left, to_right = rest[-2:]
         lane = lanes((ROWS, COLS))
 
         def one(k, _):
@@ -160,14 +162,15 @@
 def assemble(plan, refs, ext, place, last):
     own, above, below, from_right, from_left, from_up, from_down = refs
 
-    def middle(k, _):
-        right, left = from_right[k], from_left[k]
-        for n, (field, part) in enumerate(plan.tiles):
-            ext[n, REACH + k, :, 0:COLS] = TILE_OF[plan]((own, above, below), field, part, k)
-            ext[n, REACH + k, :, COLS:WIDE] = halo_columns(right, left, n)
+    def middle(levels, _):
+        for k in levels:
+            right, left = from_right[k], from_left[k]
+            for n, (field, part) in enumerate(plan.tiles):
+                ext[n, REACH + k, :, 0:COLS] = TILE_OF[plan]((own, above, below), field, part, k)
+                ext[n, REACH + k, :, COLS:WIDE] = halo_columns(right, left, n)
         return 0
 
-    lax.fori_loop(0, LEVELS, middle, 0)
+    sweep(0, LEVELS, 4, middle)
     columns = {}
     for index, (a, n) in enumerate(plan.carried):
         if n < 0:
@@ -222,33 +225,47 @@
 SIXTIETH = -1.0 / 60.0
 
 
-def rates(plan, ext, fields, write, first, count):
+def sweep(first, count, most, body, carry=0):
+    size = max(n for n in range(1, most + 1) if count % n == 0)
+
+    def run(i, carry):
+        start = first + i * size
+        return body([start + n for n in range(size)], carry)
+
+    return lax.fori_loop(0, count // size, run, carry)
+
+
+def rates(plan, ext, fields, write, first, count, most):
     reads = [lambda l, f=f: plan.sixteen(ext, f, l) for f in fields]
 
-    def one(l, lows):
-        u, v, w = (
-            plan.sixteen(ext, U, l),
-            plan.rows(ext, V, l),
-            plan.sixteen(ext, W, l),
-        )
-        highs = []
-        for n, f in enumerate(fields):
-            high = level_flux(reads[n], w, l)
-            here = plan.rows(ext, f, l)
-            cells = reads[n](l)
-            total = flat_flux(cells, u, 1) + rows_flux(here, v) + (high - lows[n])
-            write(n, l, total * SIXTIETH)
-            highs.append(high)
-        return tuple(highs)
+    def some(levels, lows):
+        results = []
+        for l in levels:
+            u, v, w = (
+                plan.sixteen(ext, U, l),
+                plan.rows(ext, V, l),
+                plan.sixteen(ext, W, l),
+            )
+            highs = []
+            for n, f in enumerate(fields):
+                high = level_flux(reads[n], w, l)
+                here = plan.rows(ext, f, l)
+                total = (
+                    flat_flux(reads[n](l), u, 1) + rows_flux(here, v) + (high - lows[n])
+                )
+                results.append((n, l, total * SIXTIETH))
+                highs.append(high)
+            lows = tuple(highs)
+        for result in results:
+            write(*result)
+        return lows
 
     w = plan.sixteen(ext, W, first - 1)
-    lax.fori_loop(
-        first, first + count, one, tuple(level_flux(read, w, first - 1) for read in reads)
-    )
+    sweep(first, count, most, some, tuple(level_flux(read, w, first - 1) for read in reads))
 
 
 def first_rates(
-    place_ref, own, above, below, from_right, from_left, from_up, from_down, ext, rate
+    place_ref, own, above, below, from_right, from_left, from_up, from_down, speed, ext, rate
 ):
     place, last = place_ref[0], place_ref[1]
     assemble(
@@ -263,45 +280,50 @@
     def write(n, l, value):
         rate[n, l] = value
 
-    rates(FIRST, ext, (C, PR), write, REACH - 4, LEVELS + 8)
+    rates(FIRST, ext, (C, PR), write, REACH - 4, LEVELS + 8, 2)
 
 
 def acoustic(p, u, v, w, read_c, rate, step, first, count, place, last):
     pull = step * sound_speed
 
-    def wind_w(l):
-        lift = (buoyancy * 0.5) * (read_c(l) + read_c(l + 1))
-        return (w[0](l) + step * lift - pull * (level(l + 1) - level(l))) * in_domain(
-            l, place, last, True
-        )
-
-    def level(l):
-        value = p[0](l)
+    def level(value):
         return sixteen(value) if value.shape[0] == 24 else value
 
-    def one(l, w_low):
-        tall = p[0](l)
-        p_here = level(l)
-        w_new = wind_w(l)
-        u_new = u[0](l) - pull * (shift(p_here, 1, 1) - p_here)
-        v_old = v[0](l)
-        if v_old.shape[0] == 24:
-            v_tall = v_old - pull * (shift(tall, 1, 0) - tall)
-            v_new, v_flow = sixteen(v_tall), sixteen(v_tall - shift(v_tall, -1, 0))
-        else:
-            v_new = v_old - pull * (shift(p_here, 1, 0) - p_here)
-            v_flow = v_new - shift(v_new, -1, 0)
-        divergence = (u_new - shift(u_new, -1, 1)) + v_flow + (w_new - w_low)
-        p_new = (p_here + step * rate(l) - pull * divergence) * in_domain(l, place, last, False)
-        p[1](l, p_new)
-        u[1](l, u_new)
-        v[1](l, v_new)
-        w[1](l, w_new)
-        return w_new
-
-    w_low = wind_w(first - 1)
-    w[1](first - 1, w_low)
-    lax.fori_loop(first, first + count, one, w_low)
+    def wind_w(l, lift_low, lift_high, p_here, p_above):
+        lift = (buoyancy * 0.5) * (lift_low + lift_high)
+        return (w[0](l) + step * lift - pull * (p_above - p_here)) * in_domain(l, place, last, True)
+
+    def some(levels, w_low):
+        talls = [p[0](l) for l in (*levels, levels[-1] + 1)]
+        cells = [level(value) for value in talls]
+        warm = [read_c(l) for l in (*levels, levels[-1] + 1)]
+        results = []
+        for n, l in enumerate(levels):
+            p_here = cells[n]
+            w_new = wind_w(l, warm[n], warm[n + 1], p_here, cells[n + 1])
+            u_new = u[0](l) - pull * (shift(p_here, 1, 1) - p_here)
+            v_old = v[0](l)
+            if v_old.shape[0] == 24:
+                v_tall = v_old - pull * (shift(talls[n], 1, 0) - talls[n])
+                v_new, v_flow = sixteen(v_tall), sixteen(v_tall - shift(v_tall, -1, 0))
+            else:
+                v_new = v_old - pull * (shift(p_here, 1, 0) - p_here)
+                v_flow = v_new - shift(v_new, -1, 0)
+            divergence = (u_new - shift(u_new, -1, 1)) + v_flow + (w_new - w_low)
+            p_new = (p_here + step * rate(l) - pull * divergence) * in_domain(
+                l, place, last, False
+            )
+            results.append((l, p_new, u_new, v_new, w_new))
+            w_low = w_new
+        for l, *news in results:
+            for target, value in zip((p, u, v, w), news):
+                target[1](l, value)
+        return w_low
+
+    low = first - 1
+    w_low = wind_w(low, read_c(low), read_c(first), level(p[0](low)), level(p[0](first)))
+    w[1](low, w_low)
+    sweep(first, count, 6, some, w_low)
 
 
 def access(ref, *lead):
@@ -344,13 +366,14 @@
     dt_out[0] = dt
     third = dt * (1.0 / 3.0)
 
-    def tracer(l, _):
-        s1[C, l] = (FIRST.sixteen(start, C, l) + third * rate0[0, l]) * in_domain(
-            l, place, last, False
-        )
+    def tracer(levels, _):
+        for l in levels:
+            s1[C, l] = (FIRST.sixteen(start, C, l) + third * rate0[0, l]) * in_domain(
+                l, place, last, False
+            )
         return 0
 
-    lax.fori_loop(REACH - 4, REACH + LEVELS + 4, tracer, 0)
+    sweep(REACH - 4, LEVELS + 8, 4, tracer)
     acoustic(
         (begin(start, PR, True), access(s1, PR)[1]),
         (begin(start, U), access(s1, U)[1]),
@@ -368,17 +391,21 @@
     tiles = access(s1, C)[0]
     winds = [access(s1, f)[0] for f in (U, V, W)]
 
-    def own_tracer(l, low):
-        tendency, high = tracer_rate(tiles, winds, l, low)
-        s2[C, l - REACH] = start[FIRST.at[C, "o"], l, :, 0:COLS] + half * tendency
-        return high
-
-    lax.fori_loop(REACH, REACH + LEVELS, own_tracer, tracer_high(tiles, winds[2], REACH - 1))
+    def own_tracer(levels, low):
+        results = []
+        for l in levels:
+            tendency, low = tracer_rate(tiles, winds, l, low)
+            results.append(start[FIRST.at[C, "o"], l, :, 0:COLS] + half * tendency)
+        for l, value in zip(levels, results):
+            s2[C, l - REACH] = value
+        return low
+
+    sweep(REACH, LEVELS, 4, own_tracer, tracer_high(tiles, winds[2], REACH - 1))
 
     def write(n, l, value):
         rate1[l] = value
 
-    rates(SECTION, s1, (PR,), write, REACH - 1, LEVELS + 2)
+    rates(SECTION, s1, (PR,), write, REACH - 1, LEVELS + 2, 3)
     step = half / (NS // 2)
     acoustic(
         (begin(start, PR), access(fast, 0)[1]),
@@ -407,14 +434,15 @@
         last,
     )
 
-    def share(k, _):
-        to_down, to_up = shared_rows(lambda f: s2[f, k])
-        for n in range(3):
-            down[n, k] = to_down[n]
-            up[n, k] = to_up[n]
+    def share(levels, _):
+        made = [shared_rows(lambda f, k=k: s2[f, k]) for k in levels]
+        for k, (to_down, to_up) in zip(levels, made):
+            for n in range(3):
+                down[n, k] = to_down[n]
+                up[n, k] = to_up[n]
         return 0
 
-    lax.fori_loop(0, LEVELS, share, 0)
+    sweep(0, LEVELS, 4, share)
 
 
 class Whole:
@@ -437,10 +465,10 @@
     from_left,
     from_up,
     from_down,
-    fields,
+    start,
     *rest,
 ):
-    *chunks, ext, tracer, landed, fallen, total, by_depth, sem = rest
+    *chunks, ext, tracer, landed, fallen, factor, by_depth, sem = rest
     place, last = place_ref[0], place_ref[1]
     dt = dt_ref[0]
     each = LEVELS // len(chunks)
@@ -453,30 +481,39 @@
     assemble(
         SECOND, (own, above, below, from_right, from_left, from_up, from_down), ext, place, last
     )
-    total[...] = jnp.zeros(total.shape, F32)
+    tiles = lambda l: SECOND.rows(ext, C, l)
+    winds = [lambda l, f=f: SECOND.rows(ext, f, l) for f in (U, V, W)]
+
+    def some(levels, low):
+        results = []
+        for l in levels:
+            tendency, low = tracer_rate(tiles, winds, l, low)
+            c = start[FIRST.at[C, "o"], l, :, 0:COLS] + dt * tendency
+            grown = jnp.exp(growth * c)
+            results.append((c, grown, grown * jnp.exp((0.5 * growth) * c)))
+        for l, (c, second, third) in zip(levels, results):
+            tracer[l - REACH] = c
+            factor[0, l - REACH] = second
+            factor[1, l - REACH] = third
+        return low
+
+    sweep(REACH, LEVELS, 4, some, tracer_high(tiles, winds[2], REACH - 1))
     for copy in copies:
         copy.wait()
-    tiles = lambda l: SECOND.rows(ext, C, l)
-    winds = [lambda l, f=f: SECOND.rows(ext, f, l) for f in (U, V, W)]
-
-    def one(l, low):
-        k = l - REACH
-        tendency, high = tracer_rate(tiles, winds, l, low)
-        c = fields[C, k] + dt * tendency
-        tracer[k] = c
-        grown = jnp.exp(growth * c)
-        weights = (None, grown, grown * jnp.exp((0.5 * growth) * c))
-        for depth in range(FMAX + 1):
-            for moment in range(3):
-                value = by_depth[k, depth, moment]
-                if moment:
-                    value = value * weights[moment]
-                total[moment, k + FMAX - depth] += value
-        return high
-
-    lax.fori_loop(REACH, REACH + LEVELS, one, tracer_high(tiles, winds[2], REACH - 1))
-    landed[...] = total[:, FMAX:]
-    fallen[...] = total[:, 0:FMAX]
+    for target in range(-FMAX, LEVELS):
+        for moment in range(3):
+            total = None
+            for depth in range(FMAX + 1):
+                k = target + depth
+                if 0 <= k < LEVELS:
+                    value = by_depth[k, depth, moment]
+                    if moment:
+                        value = value * factor[moment - 1, k]
+                    total = value if total is None else total + value
+            if target < 0:
+                fallen[moment, target + FMAX] = total
+            else:
+                landed[moment, target] = total
 
 
 def last_section(place_ref, dt_ref, ext, start, tracer, out, rate, fast):
@@ -486,7 +523,7 @@
     def write(n, l, value):
         rate[l] = value
 
-    rates(SECOND, ext, (PR,), write, REACH - 3, LEVELS + 6)
+    rates(SECOND, ext, (PR,), write, REACH - 3, LEVELS + 6, 2)
     out[C] = tracer[...]
     names = (PR, U, V, W)
     for repeat in range(NS):
@@ -613,14 +650,14 @@
     )
 
 
-def exchange(plan, own, down, up, token):
+def exchange(plan, own, down, up, tokens=()):
     above, below = both_ways(down, "gy", up)
     to_left, to_right = call(
         pack_columns(plan),
         "pack_columns",
-        vmem(3) + anywhere(1),
+        vmem(3) + anywhere(len(tokens)),
         [held(LEVELS, ROWS, COLS)] * 2,
-    )(own, above, below, token)
+    )(own, above, below, *tokens)
     from_right, from_left = both_ways(to_left, "gx", to_right)
     tiles = len(plan.carried)
     to_down, to_up = call(
@@ -630,14 +667,16 @@
     return above, below, from_right, from_left, from_up, from_down
 
 
-def top_speed(fields, place, last):
-    w = fields[4] * (
-        (jnp.arange(LEVELS) < LEVELS - 1) | (place != last)
-    ).astype(F32)[:, None, None]
-    local = jnp.max(jnp.abs(fields[2]) + jnp.abs(fields[3]) + jnp.abs(w))
-    devices = lax.axis_size(GRID_AXES)
-    everywhere = jnp.broadcast_to(local, (devices, 1, COLS))
-    return lax.all_to_all(everywhere, GRID_AXES, 0, 0)
+def prepare(place_ref, fields, own, speed):
+    own[...] = fields[...]
+    keep = jnp.where(place_ref[0] == place_ref[1], 0.0, 1.0).astype(F32)
+    most = jnp.zeros((ROWS, COLS), F32)
+    for k in range(LEVELS):
+        w = jnp.abs(fields[W, k])
+        if k == LEVELS - 1:
+            w = w * keep
+        most = jnp.maximum(most, jnp.abs(fields[U, k]) + jnp.abs(fields[V, k]) + w)
+    speed[...] = jnp.broadcast_to(jnp.max(most), speed.shape)
 
 
 def droplets(radius, weight, column, counts, fall_depth, chunk):
@@ -675,14 +714,25 @@
     last = lax.axis_size("gz") - 1
     where = jnp.stack([place, jnp.int32(last)]).astype(jnp.int32)
     by_depth = droplets(radius, weight, column, counts, fall_depth, 2)
-    speed = top_speed(fields, place, last)
-    halos = exchange(FIRST, fields, fields, fields, speed)
+    devices = lax.axis_size(GRID_AXES)
+    own, speed = pl.pallas_call(
+        prepare,
+        name="prepare",
+        in_specs=smem(1) + vmem(1),
+        out_specs=tuple(vmem(2)),
+        out_shape=(held(5, LEVELS, ROWS, COLS), shaped(devices, 1, COLS)),
+        compiler_params=pltpu.CompilerParams(vmem_limit_bytes=4 << 20),
+    )(where, fields)
+    early = EARLY
+    halos = exchange(FIRST, own, fields, fields, by_depth[:early])
+    speed, _ = lax.optimization_barrier((speed, halos[2]))
+    speed = lax.all_to_all(speed, GRID_AXES, 0, 0)
     start, rate0 = call(
         first_rates,
         "first_rates",
-        smem(1) + vmem(7),
+        smem(1) + vmem(7) + anywhere(1),
         [held(len(FIRST.tiles), DEPTH, ROWS, WIDE), held(2, DEPTH, 2 * ROWS, WIDE)],
-    )(where, fields, *halos)
+    )(where, own, *halos, speed)
     s2, down, up, dt = call(
         two_sections,
         "two_sections",
@@ -696,7 +746,7 @@
         out_specs=vmem(3) + smem(1),
         grant=10,
     )(where, speed, start, rate0)
-    halos = exchange(SECOND, s2, down, up, speed)
+    halos = exchange(SECOND, s2, down, up, by_depth[early:])
     ext, tracer, landed, fallen = call(
         last_tracer,
         "last_tracer",
@@ -708,11 +758,11 @@
             held(3, FMAX, ROWS, COLS),
         ],
         scratch=[
-            pltpu.VMEM((3, LEVELS + FMAX, ROWS, COLS), F32),
+            pltpu.VMEM((2, LEVELS, ROWS, COLS), F32),
             pltpu.VMEM((LEVELS, FMAX + 1, 3, ROWS, COLS), F32),
             pltpu.SemaphoreType.DMA((len(by_depth),)),
         ],
-    )(where, dt, s2, *halos, fields, *by_depth)
+    )(where, dt, s2, *halos, start, *by_depth)
     count = lax.axis_size("gz")
     arrived = lax.ppermute(fallen, "gz", [((i + 1) % count, i) for i in range(count)])
     (new_fields,) = call(

time: 148 us -> 112 us (0.76)
  Pallas kernels: 68.1 us -> 41.8 us
  waiting for transfers between devices: 25.3 us -> 17.9 us
  other arithmetic: 1.7 us -> 0.1 us
    pallas_call x8, Pallas kernels: 52.8 us -> 25.7 us  [run(): made(*(pltpu.with_memory_space_constraint(value, pltpu.VMEM) if spec.memo...]
    ppermute x6, waiting for transfers between devices: 17.8 us -> 9.31 us  [both_ways(): lax.ppermute(down, axis, [((i + 1) % count, i) for i in range(count)])]
    ppermute x1, starting transfers between devices: 1.99 us -> 0.36 us  [per_device(): lax.ppermute(fallen, 'gz', [((i + 1) % count, i) for i in range(count)])]
    reduce_max x1 -> x0, other arithmetic: 1.6 us -> none  [top_speed(): local = jnp.max(jnp.abs(fields[2]) + jnp.abs(fields[3]) + jnp.abs(w))]
    ppermute x6, starting transfers between devices: 7.95 us -> 9.53 us  [both_ways(): lax.ppermute(down, axis, [((i + 1) % count, i) for i in range(count)])]
    unnamed x42 -> x24, local copies, waits for them, and re-layouts: 7.9 us -> 8.74 us
  transfers between devices with their start and end apart: 13 -> 13, of which waited for: 8 -> 8; matrix products, arithmetic and copies ran while one was open for 2% -> 1% of each run, Pallas kernels for 22% -> 21%
where the time goes in v2:
time: 112 us; the launch traced here: 111 us
  Pallas kernels  41.8 us (37%)
  blocking collectives  26.2 us (23%)
  waiting for transfers between devices  17.9 us (16%)
  starting transfers between devices  15.4 us (14%)
  local copies, waits for them, and re-layouts  8.74 us (8%)
    all_to_all x1, blocking collectives, per_device(): speed = lax.all_to_all(speed, GRID_AXES, 0, 0)  26.2 us
    pallas_call x8, Pallas kernels, run(): made(*(pltpu.with_memory_space_constraint(value, pltpu.VMEM) if spec.memo...  25.7 us
    pallas_call x8, Pallas kernels, droplets(): pl.pallas_call(deposit, name='deposit', grid=(1,), in_specs=[whole, whole...  15.3 us
    ppermute x6, starting transfers between devices, both_ways(): lax.ppermute(down, axis, [((i + 1) % count, i) for i in range(count)])  9.53 us
    ppermute x6, waiting for transfers between devices, both_ways(): lax.ppermute(down, axis, [((i + 1) % count, i) for i in range(count)])  9.31 us
    unnamed x24, local copies, waits for them, and re-layouts  8.74 us
    ppermute x6, waiting for transfers between devices, both_ways(): lax.ppermute(up, axis, [(i, (i + 1) % count) for i in range(count)])  8.54 us
    ppermute x6, starting transfers between devices, both_ways(): lax.ppermute(up, axis, [(i, (i + 1) % count) for i in range(count)])  5.49 us
  transfers between devices with their start and end apart: 13, of which 8 were waited for; matrix products, arithmetic and copies ran while one was open for 1% of the time, Pallas kernels for 21%

profile of v2, /device:TPU:4, one launch (start us, length us, event | category | flops | bytes accessed | tf_op | source)
XLA Modules:
  0.0 110.9 jit_solution(10787503709686898366)
XLA Ops:
  0.6 1.9 %collective-permute-start.1 = (f32[5,16,8,128]{3,2,1,0:T(8,128)}, f32[5,16,8,128]{3,2,1,0:T(8,128)S(1)}, u32[]{:S(2)}, u32[]{:S(2)}) collective-permute-start(f32[5,16,8,128]{3,2,1,0:T(8,128)} %fields.1), channel_id=1, source_target_pairs={{0,4},{4,8},{8,12},{12,16},{16,20},{20,24},{24,28},{28,32},{32,36}... | collective-permute-start | bytes 983048 | tf_op jit(solution)/shard_map/ppermute | solution.py:649
  2.6 1.7 %collective-permute-start = (f32[5,16,8,128]{3,2,1,0:T(8,128)}, f32[5,16,8,128]{3,2,1,0:T(8,128)S(1)}, u32[]{:S(2)}, u32[]{:S(2)}) collective-permute-start(f32[5,16,8,128]{3,2,1,0:T(8,128)} %fields.1), channel_id=1, source_target_pairs={{4,0},{8,4},{12,8},{16,12},{20,16},{24,20},{28,24},{32,28},{36,32}... | collective-permute-start | bytes 983048 | tf_op jit(solution)/shard_map/ppermute | solution.py:648
  11.2 1.9 %deposit.12.rest_4_ = f32[2,9,3,8,128]{4,3,2,1,0:T(8,128)S(1)} custom-call(f32[8,16,8,128]{3,2,1,0:T(8,128)S(1)} %copy-done, f32[8,16,8,128]{3,2,1,0:T(8,128)S(1)} %copy-done.2, s32[8,16,8,128]{3,2,1,0:T(8,128)S(1)} %copy-done.4, s32[16,8,128]{2,1,0:T(8,128)S(1)} %copy-done.8, s32[8,16,8,1]{3,2,1,0:T(8,128)S(1)} %copy.8.fall_depth), custom_call_target="tpu_custom_call" | custom-call | flops 200000000 | tf_op jit(solution)/shard_map/deposit/pallas_call | solution.py:688
  13.2 1.9 %deposit.11.rest_3_ = f32[2,9,3,8,128]{4,3,2,1,0:T(8,128)S(1)} custom-call(f32[8,16,8,128]{3,2,1,0:T(8,128)S(1)} %copy-done, f32[8,16,8,128]{3,2,1,0:T(8,128)S(1)} %copy-done.2, s32[8,16,8,128]{3,2,1,0:T(8,128)S(1)} %copy-done.4, s32[16,8,128]{2,1,0:T(8,128)S(1)} %copy-done.8, s32[8,16,8,1]{3,2,1,0:T(8,128)S(1)} %copy.8.fall_depth), custom_call_target="tpu_custom_call" | custom-call | flops 200000000 | tf_op jit(solution)/shard_map/deposit/pallas_call | solution.py:688
  15.1 1.9 %deposit.10.rest_2_ = f32[2,9,3,8,128]{4,3,2,1,0:T(8,128)S(1)} custom-call(f32[8,16,8,128]{3,2,1,0:T(8,128)S(1)} %copy-done, f32[8,16,8,128]{3,2,1,0:T(8,128)S(1)} %copy-done.2, s32[8,16,8,128]{3,2,1,0:T(8,128)S(1)} %copy-done.4, s32[16,8,128]{2,1,0:T(8,128)S(1)} %copy-done.8, s32[8,16,8,1]{3,2,1,0:T(8,128)S(1)} %copy.8.fall_depth), custom_call_target="tpu_custom_call" | custom-call | flops 200000000 | tf_op jit(solution)/shard_map/deposit/pallas_call | solution.py:688
  17.0 1.9 %deposit.9.rest_1_ = f32[2,9,3,8,128]{4,3,2,1,0:T(8,128)S(1)} custom-call(f32[8,16,8,128]{3,2,1,0:T(8,128)S(1)} %copy-done, f32[8,16,8,128]{3,2,1,0:T(8,128)S(1)} %copy-done.2, s32[8,16,8,128]{3,2,1,0:T(8,128)S(1)} %copy-done.4, s32[16,8,128]{2,1,0:T(8,128)S(1)} %copy-done.8, s32[8,16,8,1]{3,2,1,0:T(8,128)S(1)} %copy.8.fall_depth), custom_call_target="tpu_custom_call" | custom-call | flops 200000000 | tf_op jit(solution)/shard_map/deposit/pallas_call | solution.py:688
  18.9 1.9 %deposit.8.rest_0_ = f32[2,9,3,8,128]{4,3,2,1,0:T(8,128)S(1)} custom-call(f32[8,16,8,128]{3,2,1,0:T(8,128)S(1)} %copy-done, f32[8,16,8,128]{3,2,1,0:T(8,128)S(1)} %copy-done.2, s32[8,16,8,128]{3,2,1,0:T(8,128)S(1)} %copy-done.4, s32[16,8,128]{2,1,0:T(8,128)S(1)} %copy-done.8, s32[8,16,8,1]{3,2,1,0:T(8,128)S(1)} %copy.8.fall_depth), custom_call_target="tpu_custom_call" | custom-call | flops 200000000 | tf_op jit(solution)/shard_map/deposit/pallas_call | solution.py:688
  23.9 2.2 %collective-permute-done.3.from_left = f32[16,8,128]{2,1,0:T(8,128)S(1)} collective-permute-done((f32[16,8,128]{2,1,0:T(8,128)S(1)}, f32[16,8,128]{2,1,0:T(8,128)S(1)}, u32[]{:S(2)}, u32[]{:S(2)}) %collective-permute-start.3) | collective-permute-done | bytes 65568 | tf_op jit(solution)/shard_map/ppermute | solution.py:649
  26.1 3.1 %collective-permute-start.4 = (f32[91,8,128]{2,1,0:T(8,128)S(1)}, f32[91,8,128]{2,1,0:T(8,128)S(1)}, u32[]{:S(2)}, u32[]{:S(2)}) collective-permute-start(f32[91,8,128]{2,1,0:T(8,128)S(1)} %get-tuple-element.40), channel_id=1, source_target_pairs={{1,0},{2,1},{3,2},{0,3},{5,4},{6,5},{7,6},{4,7},{9,8},{10,9},{11,1... | collective-permute-start | bytes 1118216 | tf_op jit(solution)/shard_map/ppermute | solution.py:648
  29.2 26.2 %all_to_all.5.speed = f32[256,1,128]{2,1,0:T(1,128)S(1)} all-to-all(f32[256,1,128]{2,1,0:T(1,128)S(1)} %get-tuple-element.38), channel_id=1, replica_groups=mesh['gx'=4,'gy'=16,'gz'=4] {'gx','gy','gz'}, dimensions={0} | all-to-all | bytes 262144 | tf_op jit(solution)/shard_map/all_to_all | solution.py:729
  55.5 5.3 %first_rates.1 = (f32[13,30,8,256]{3,2,1,0:T(8,128)S(1)}, f32[2,30,16,256]{3,2,1,0:T(8,128)S(1)}) custom-call(s32[2]{0:T(128)S(1)} %pad_add_fusion.place_ref, f32[5,16,8,128]{3,2,1,0:T(8,128)S(1)} %get-tuple-element.36.own, f32[5,16,8,128]{3,2,1,0:T(8,128)S(1)} %collective-permute-done.above, f32[5,16,8,128]{3,2,1,0:T(8,128)S(1)} %collective-permute-done.1.below, ...), custom_call_target="tpu_custom_call" | custom-call | tf_op jit(solution)/shard_map/first_rates/pallas_call | solution.py:633
  60.7 5.5 %two_sections.1 = (f32[5,16,8,128]{3,2,1,0:T(8,128)S(1)}, f32[3,16,8,128]{3,2,1,0:T(8,128)S(1)}, f32[3,16,8,128]{3,2,1,0:T(8,128)S(1)}, f32[1]{0:T(128)}) custom-call(s32[2]{0:T(128)S(1)} %pad_add_fusion.place_ref, f32[256,1,128]{2,1,0:T(1,128)S(1)} %all_to_all.5.speed, f32[13,30,8,256]{3,2,1,0:T(8,128)S(1)} %get-tuple-element.42.start, ...), custom_call_target="tpu_custom_call" | custom-call | tf_op jit(solution)/shard_map/two_sections/pallas_call | solution.py:633
  66.2 2.2 %collective-permute-start.6 = (f32[3,16,8,128]{3,2,1,0:T(8,128)S(1)}, f32[3,16,8,128]{3,2,1,0:T(8,128)S(1)}, u32[]{:S(2)}, u32[]{:S(2)}) collective-permute-start(f32[3,16,8,128]{3,2,1,0:T(8,128)S(1)} %get-tuple-element.46), channel_id=1, source_target_pairs={{4,0},{8,4},{12,8},{16,12},{20,16},{24,20},{28,24},{32,28},{36,32}... | collective-permute-start | bytes 589832 | tf_op jit(solution)/shard_map/ppermute | solution.py:648
  68.5 2.3 %collective-permute-start.7 = (f32[3,16,8,128]{3,2,1,0:T(8,128)S(1)}, f32[3,16,8,128]{3,2,1,0:T(8,128)S(1)}, u32[]{:S(2)}, u32[]{:S(2)}) collective-permute-start(f32[3,16,8,128]{3,2,1,0:T(8,128)S(1)} %get-tuple-element.47), channel_id=1, source_target_pairs={{0,4},{4,8},{8,12},{12,16},{16,20},{20,24},{24,28},{28,32},{32,36}... | collective-permute-start | bytes 589832 | tf_op jit(solution)/shard_map/ppermute | solution.py:649
  70.7 1.9 %deposit.15.rest_2_.rest_7_ = f32[2,9,3,8,128]{4,3,2,1,0:T(8,128)S(1)} custom-call(f32[8,16,8,128]{3,2,1,0:T(8,128)S(1)} %copy-done.1, f32[8,16,8,128]{3,2,1,0:T(8,128)S(1)} %copy-done.3, s32[8,16,8,128]{3,2,1,0:T(8,128)S(1)} %copy-done.5, s32[16,8,128]{2,1,0:T(8,128)S(1)} %copy-done.9, s32[8,16,8,1]{3,2,1,0:T(8,128)S(1)} %copy.8.fall_depth), custom_call_target="tpu_custom_call" | custom-call | flops 200000000 | tf_op jit(solution)/shard_map/deposit/pallas_call | solution.py:688
  72.7 1.9 %deposit.14.rest_1_.rest_6_ = f32[2,9,3,8,128]{4,3,2,1,0:T(8,128)S(1)} custom-call(f32[8,16,8,128]{3,2,1,0:T(8,128)S(1)} %copy-done.1, f32[8,16,8,128]{3,2,1,0:T(8,128)S(1)} %copy-done.3, s32[8,16,8,128]{3,2,1,0:T(8,128)S(1)} %copy-done.5, s32[16,8,128]{2,1,0:T(8,128)S(1)} %copy-done.9, s32[8,16,8,1]{3,2,1,0:T(8,128)S(1)} %copy.8.fall_depth), custom_call_target="tpu_custom_call" | custom-call | flops 200000000 | tf_op jit(solution)/shard_map/deposit/pallas_call | solution.py:688
  74.6 1.9 %deposit.13.rest_0_.rest_5_ = f32[2,9,3,8,128]{4,3,2,1,0:T(8,128)S(1)} custom-call(f32[8,16,8,128]{3,2,1,0:T(8,128)S(1)} %copy-done.1, f32[8,16,8,128]{3,2,1,0:T(8,128)S(1)} %copy-done.3, s32[8,16,8,128]{3,2,1,0:T(8,128)S(1)} %copy-done.5, s32[16,8,128]{2,1,0:T(8,128)S(1)} %copy-done.9, s32[8,16,8,1]{3,2,1,0:T(8,128)S(1)} %copy.8.fall_depth), custom_call_target="tpu_custom_call" | custom-call | flops 200000000 | tf_op jit(solution)/shard_map/deposit/pallas_call | solution.py:688
  76.9 2.5 %collective-permute-done.7.below = f32[3,16,8,128]{3,2,1,0:T(8,128)S(1)} collective-permute-done((f32[3,16,8,128]{3,2,1,0:T(8,128)S(1)}, f32[3,16,8,128]{3,2,1,0:T(8,128)S(1)}, u32[]{:S(2)}, u32[]{:S(2)}) %collective-permute-start.7) | collective-permute-done | bytes 196640 | tf_op jit(solution)/shard_map/ppermute | solution.py:649
  81.4 2.5 %collective-permute-done.8.from_right = f32[16,8,128]{2,1,0:T(8,128)S(1)} collective-permute-done((f32[16,8,128]{2,1,0:T(8,128)S(1)}, f32[16,8,128]{2,1,0:T(8,128)S(1)}, u32[]{:S(2)}, u32[]{:S(2)}) %collective-permute-start.8) | collective-permute-done | bytes 65568 | tf_op jit(solution)/shard_map/ppermute | solution.py:648
  87.3 5.0 %collective-permute-done.10.from_up = f32[62,8,128]{2,1,0:T(8,128)S(1)} collective-permute-done((f32[62,8,128]{2,1,0:T(8,128)S(1)}, f32[62,8,128]{2,1,0:T(8,128)S(1)}, u32[]{:S(2)}, u32[]{:S(2)}) %collective-permute-start.10) | collective-permute-done | bytes 253984 | tf_op jit(solution)/shard_map/ppermute | solution.py:648
  92.2 2.7 %collective-permute-done.11.from_down = f32[62,8,128]{2,1,0:T(8,128)S(1)} collective-permute-done((f32[62,8,128]{2,1,0:T(8,128)S(1)}, f32[62,8,128]{2,1,0:T(8,128)S(1)}, u32[]{:S(2)}, u32[]{:S(2)}) %collective-permute-start.11) | collective-permute-done | bytes 253984 | tf_op jit(solution)/shard_map/ppermute | solution.py:649
  94.9 5.4 %last_tracer.1 = (f32[11,30,8,256]{3,2,1,0:T(8,128)S(1)}, f32[16,8,128]{2,1,0:T(8,128)S(1)}, f32[3,16,8,128]{3,2,1,0:T(8,128)S(1)}, f32[3,8,8,128]{3,2,1,0:T(8,128)S(1)}) custom-call(s32[2]{0:T(128)S(1)} %pad_add_fusion.place_ref, f32[1]{0:T(128)} %get-tuple-element.44.dt_ref, f32[5,16,8,128]{3,2,1,0:T(8,128)S(1)} %get-tuple-element.45.own, ...), custom_call_target="tpu_custom_call" | custom-call | tf_op jit(solution)/shard_map/last_tracer/pallas_call | solution.py:633
  100.6 1.9 %copy-done.7 = f32[13,30,8,256]{3,2,1,0:T(8,128)S(1)} copy-done((f32[13,30,8,256]{3,2,1,0:T(8,128)S(1)}, f32[13,30,8,256]{3,2,1,0:T(8,128)}, u32[]{:S(2)}) %copy-start.7) | copy-done | bytes 3194904
  102.5 7.6 %last_section.1 = f32[5,16,8,128]{3,2,1,0:T(8,128)} custom-call(s32[2]{0:T(128)S(1)} %pad_add_fusion.place_ref, f32[1]{0:T(128)} %get-tuple-element.44.dt_ref, f32[11,30,8,256]{3,2,1,0:T(8,128)S(1)} %get-tuple-element.52.ext, f32[13,30,8,256]{3,2,1,0:T(8,128)S(1)} %copy-done.7, f32[16,8,128]{2,1,0:T(8,128)S(1)} %get-tuple-element.53.tracer), custom_call_target="tpu_custom_call" | custom-call | flops 1000000000 | tf_op jit(solution)/shard_map/last_section/pallas_call | solution.py:633
  (46 shorter events, 17.0 us)
Async XLA Ops:
  0.6 20.2 %collective-permute-start.1 = (f32[5,16,8,128]{3,2,1,0:T(8,128)}, f32[5,16,8,128]{3,2,1,0:T(8,128)S(1)}, u32[]{:S(2)}, u32[]{:S(2)}) collective-permute-start(f32[5,16,8,128]{3,2,1,0:T(8,128)} %fields.1), channel_id=1, source_target_pairs={{0,4},{4,8},{8,12},{12,16},{16,20},{20,24},{24,28},{28,32},{32,36}... | collective-permute-start | bytes 983048 | tf_op jit(solution)/shard_map/ppermute | solution.py:649
  2.6 18.3 %collective-permute-start = (f32[5,16,8,128]{3,2,1,0:T(8,128)}, f32[5,16,8,128]{3,2,1,0:T(8,128)S(1)}, u32[]{:S(2)}, u32[]{:S(2)}) collective-permute-start(f32[5,16,8,128]{3,2,1,0:T(8,128)} %fields.1), channel_id=1, source_target_pairs={{4,0},{8,4},{12,8},{16,12},{20,16},{24,20},{28,24},{32,28},{36,32}... | collective-permute-start | bytes 983048 | tf_op jit(solution)/shard_map/ppermute | solution.py:648
  4.3 1.0 copy-start.10
  7.3 1.0 copy-start
  8.3 1.0 copy-start.2
  9.3 1.0 copy-start.4
  10.4 0.8 copy-start.8
  21.9 2.1 %collective-permute-start.2 = (f32[16,8,128]{2,1,0:T(8,128)S(1)}, f32[16,8,128]{2,1,0:T(8,128)S(1)}, u32[]{:S(2)}, u32[]{:S(2)}) collective-permute-start(f32[16,8,128]{2,1,0:T(8,128)S(1)} %get-tuple-element.37), channel_id=1, source_target_pairs={{64,0},{128,64},{192,128},{0,192},{65,1},{129,65},{193,129},{1,193... | collective-permute-start | bytes 196616 | tf_op jit(solution)/shard_map/ppermute | solution.py:648
  22.0 4.1 %collective-permute-start.3 = (f32[16,8,128]{2,1,0:T(8,128)S(1)}, f32[16,8,128]{2,1,0:T(8,128)S(1)}, u32[]{:S(2)}, u32[]{:S(2)}) collective-permute-start(f32[16,8,128]{2,1,0:T(8,128)S(1)} %get-tuple-element.39), channel_id=1, source_target_pairs={{0,64},{64,128},{128,192},{192,0},{1,65},{65,129},{129,193},{193,1... | collective-permute-start | bytes 196616 | tf_op jit(solution)/shard_map/ppermute | solution.py:649
  26.1 29.3 %collective-permute-start.4 = (f32[91,8,128]{2,1,0:T(8,128)S(1)}, f32[91,8,128]{2,1,0:T(8,128)S(1)}, u32[]{:S(2)}, u32[]{:S(2)}) collective-permute-start(f32[91,8,128]{2,1,0:T(8,128)S(1)} %get-tuple-element.40), channel_id=1, source_target_pairs={{1,0},{2,1},{3,2},{0,3},{5,4},{6,5},{7,6},{4,7},{9,8},{10,9},{11,1... | collective-permute-start | bytes 1118216 | tf_op jit(solution)/shard_map/ppermute | solution.py:648
  29.2 26.2 %collective-permute-start.5 = (f32[91,8,128]{2,1,0:T(8,128)S(1)}, f32[91,8,128]{2,1,0:T(8,128)S(1)}, u32[]{:S(2)}, u32[]{:S(2)}) collective-permute-start(f32[91,8,128]{2,1,0:T(8,128)S(1)} %get-tuple-element.41), channel_id=1, source_target_pairs={{0,1},{1,2},{2,3},{3,0},{4,5},{5,6},{6,7},{7,4},{8,9},{9,10},{10,1... | collective-permute-start | bytes 1118216 | tf_op jit(solution)/shard_map/ppermute | solution.py:649
  55.4 15.3 %copy-start.1 = (f32[8,16,8,128]{3,2,1,0:T(8,128)S(1)}, f32[8,16,8,128]{3,2,1,0:T(8,128)}, u32[]{:S(2)}) copy-start(f32[8,16,8,128]{3,2,1,0:T(8,128)} %radius.15) | copy-start | bytes 1572868
  55.4 15.3 %copy-start.3 = (f32[8,16,8,128]{3,2,1,0:T(8,128)S(1)}, f32[8,16,8,128]{3,2,1,0:T(8,128)}, u32[]{:S(2)}) copy-start(f32[8,16,8,128]{3,2,1,0:T(8,128)} %weight.15) | copy-start | bytes 1572868
  55.4 15.3 %copy-start.5 = (s32[8,16,8,128]{3,2,1,0:T(8,128)S(1)}, s32[8,16,8,128]{3,2,1,0:T(8,128)}, u32[]{:S(2)}) copy-start(s32[8,16,8,128]{3,2,1,0:T(8,128)} %column.15) | copy-start | bytes 1572868
  55.4 15.3 %copy-start.9 = (s32[16,8,128]{2,1,0:T(8,128)S(1)}, s32[16,8,128]{2,1,0:T(8,128)}, u32[]{:S(2)}) copy-start(s32[16,8,128]{2,1,0:T(8,128)} %counts.15) | copy-start | bytes 196612
  60.7 34.2 %copy-start.6 = (f32[13,30,8,256]{3,2,1,0:T(8,128)}, f32[13,30,8,256]{3,2,1,0:T(8,128)S(1)}, u32[]{:S(2)}) copy-start(f32[13,30,8,256]{3,2,1,0:T(8,128)S(1)} %get-tuple-element.42.start) | copy-start | bytes 9584644
  66.2 10.7 %collective-permute-start.6 = (f32[3,16,8,128]{3,2,1,0:T(8,128)S(1)}, f32[3,16,8,128]{3,2,1,0:T(8,128)S(1)}, u32[]{:S(2)}, u32[]{:S(2)}) collective-permute-start(f32[3,16,8,128]{3,2,1,0:T(8,128)S(1)} %get-tuple-element.46), channel_id=1, source_target_pairs={{4,0},{8,4},{12,8},{16,12},{20,16},{24,20},{28,24},{32,28},{36,32}... | collective-permute-start | bytes 589832 | tf_op jit(solution)/shard_map/ppermute | solution.py:648
  68.5 10.9 %collective-permute-start.7 = (f32[3,16,8,128]{3,2,1,0:T(8,128)S(1)}, f32[3,16,8,128]{3,2,1,0:T(8,128)S(1)}, u32[]{:S(2)}, u32[]{:S(2)}) collective-permute-start(f32[3,16,8,128]{3,2,1,0:T(8,128)S(1)} %get-tuple-element.47), channel_id=1, source_target_pairs={{0,4},{4,8},{8,12},{12,16},{16,20},{20,24},{24,28},{28,32},{32,36}... | collective-permute-start | bytes 589832 | tf_op jit(solution)/shard_map/ppermute | solution.py:649
  80.3 3.6 %collective-permute-start.8 = (f32[16,8,128]{2,1,0:T(8,128)S(1)}, f32[16,8,128]{2,1,0:T(8,128)S(1)}, u32[]{:S(2)}, u32[]{:S(2)}) collective-permute-start(f32[16,8,128]{2,1,0:T(8,128)S(1)} %get-tuple-element.48), channel_id=1, source_target_pairs={{64,0},{128,64},{192,128},{0,192},{65,1},{129,65},{193,129},{1,193... | collective-permute-start | bytes 196616 | tf_op jit(solution)/shard_map/ppermute | solution.py:648
  81.4 3.7 %collective-permute-start.9 = (f32[16,8,128]{2,1,0:T(8,128)S(1)}, f32[16,8,128]{2,1,0:T(8,128)S(1)}, u32[]{:S(2)}, u32[]{:S(2)}) collective-permute-start(f32[16,8,128]{2,1,0:T(8,128)S(1)} %get-tuple-element.49), channel_id=1, source_target_pairs={{0,64},{64,128},{128,192},{192,0},{1,65},{65,129},{129,193},{193,1... | collective-permute-start | bytes 196616 | tf_op jit(solution)/shard_map/ppermute | solution.py:649
  85.2 7.1 %collective-permute-start.10 = (f32[62,8,128]{2,1,0:T(8,128)S(1)}, f32[62,8,128]{2,1,0:T(8,128)S(1)}, u32[]{:S(2)}, u32[]{:S(2)}) collective-permute-start(f32[62,8,128]{2,1,0:T(8,128)S(1)} %get-tuple-element.50), channel_id=1, source_target_pairs={{1,0},{2,1},{3,2},{0,3},{5,4},{6,5},{7,6},{4,7},{9,8},{10,9},{11,1... | collective-permute-start | bytes 761864 | tf_op jit(solution)/shard_map/ppermute | solution.py:648
  86.4 8.5 %collective-permute-start.11 = (f32[62,8,128]{2,1,0:T(8,128)S(1)}, f32[62,8,128]{2,1,0:T(8,128)S(1)}, u32[]{:S(2)}, u32[]{:S(2)}) collective-permute-start(f32[62,8,128]{2,1,0:T(8,128)S(1)} %get-tuple-element.51), channel_id=1, source_target_pairs={{0,1},{1,2},{2,3},{3,0},{4,5},{5,6},{6,7},{7,4},{8,9},{9,10},{10,1... | collective-permute-start | bytes 761864 | tf_op jit(solution)/shard_map/ppermute | solution.py:649
  100.3 9.9 %collective-permute-start.12 = (f32[3,8,8,128]{3,2,1,0:T(8,128)S(1)}, f32[3,8,8,128]{3,2,1,0:T(8,128)S(1)}, u32[]{:S(2)}, u32[]{:S(2)}) collective-permute-start(f32[3,8,8,128]{3,2,1,0:T(8,128)S(1)} %get-tuple-element.55), channel_id=1, source_target_pairs={{1,0},{2,1},{3,2},{0,3},{5,4},{6,5},{7,6},{4,7},{9,8},{10,9},{11,1... | collective-permute-start | bytes 294920 | tf_op jit(solution)/shard_map/ppermute | solution.py:767
  100.6 1.9 %copy-start.7 = (f32[13,30,8,256]{3,2,1,0:T(8,128)S(1)}, f32[13,30,8,256]{3,2,1,0:T(8,128)}, u32[]{:S(2)}) copy-start(f32[13,30,8,256]{3,2,1,0:T(8,128)} %copy-done.6) | copy-start | bytes 9584644

commit v3 on v2

--- a/solution.py
+++ b/solution.py
@@ -7,7 +7,7 @@
 
 NS = 4
 FMAX = 8
-EARLY = 5
+EARLY, LATE = 4, 7
 GRID_AXES = ("gx", "gy", "gz")
 
 sound_speed = 10.0
@@ -25,21 +25,21 @@
 
 
 class Plan:
-    def __init__(self, tall, reach, short):
+    def __init__(self, tall, reach, sent):
+        self.tall, self.reach = tall, reach
         self.tiles = [
             (field, part)
             for field in range(5)
             for part in ("oab" if field in tall else "on")
         ]
         self.at = {tile: n for n, tile in enumerate(self.tiles)}
-        self.tall, self.reach, self.short = tall, reach, short
-        far = [t for t in self.tiles if t[0] in (C, PR)] if C in tall else [
-            t for t in self.tiles if t[0] == PR
-        ]
         self.carried = []
         for a in range(reach):
-            names = self.tiles if a < short else far
-            self.carried += [(a, self.at[t]) for t in names] + [(a, -1), (a, -2)]
+            for field in range(5):
+                for part in sent[field][a] if a < len(sent[field]) else "":
+                    self.carried.append((a, (field, part), 0))
+            if a < reach - 1:
+                self.carried += [(a, None, 0), (a, None, 1)]
 
     def rows(self, ref, field, l):
         return jnp.concatenate(
@@ -98,6 +98,8 @@
     own, above, below = refs
     if part == "o":
         return own[field, k]
+    if part == "n" and field == PR:
+        return around(above[0, k], below[0, k])
     if part == "n":
         index, half = SHARED[field]
         if half == 0:
@@ -106,8 +108,29 @@
     return (above if part == "a" else below)[0, k]
 
 
-FIRST = Plan((C, PR, V), 7, 5)
-SECOND = Plan((PR,), 6, 4)
+THREE, TWO, ONE = "oab", "on", "o"
+FIRST = Plan(
+    (C, PR, V),
+    7,
+    {
+        C: [THREE] + [TWO] * 4 + [ONE],
+        PR: [THREE] * 2 + [TWO] * 4 + [ONE],
+        U: [TWO] * 4,
+        V: [TWO] * 4,
+        W: [TWO] * 4 + [ONE],
+    },
+)
+SECOND = Plan(
+    (PR,),
+    6,
+    {
+        C: [TWO] * 3 + [ONE],
+        PR: [THREE] + [TWO] * 4 + [ONE],
+        U: [TWO] * 3,
+        V: [TWO] * 3,
+        W: [TWO] * 3 + [ONE],
+    },
+)
 TILE_OF = {FIRST: raw_tile, SECOND: shared_tile}
 
 
@@ -149,18 +172,18 @@
 
 def pack_levels(plan):
     def kernel(own, above, below, from_right, from_left, to_down, to_up):
-        for place, (a, n) in enumerate(plan.carried):
+        for index, (a, tile, side) in enumerate(plan.carried):
             for out, k in ((to_down, a), (to_up, LEVELS - 1 - a)):
-                if n >= 0:
-                    out[place] = TILE_OF[plan]((own, above, below), *plan.tiles[n], k)
+                if tile:
+                    out[index] = TILE_OF[plan]((own, above, below), *tile, k)
                 else:
-                    out[place] = (from_right if n == -1 else from_left)[k]
+                    out[index] = (from_left if side else from_right)[k]
 
     return kernel
 
 
-def assemble(plan, refs, ext, place, last):
-    own, above, below, from_right, from_left, from_up, from_down = refs
+def place_own(plan, refs, ext):
+    own, above, below, from_right, from_left = refs
 
     def middle(levels, _):
         for k in levels:
@@ -171,21 +194,27 @@
         return 0
 
     sweep(0, LEVELS, 4, middle)
-    columns = {}
-    for index, (a, n) in enumerate(plan.carried):
-        if n < 0:
-            columns[a, n] = index
+
+
+def place_halo(plan, from_up, from_down, ext, place, last):
+    columns = {(a, side): i for i, (a, tile, side) in enumerate(plan.carried) if not tile}
     for message, level, there in (
         (from_down, lambda a: REACH - 1 - a, place > 0),
         (from_up, lambda a: REACH + LEVELS + a, place < last),
     ):
         keep = jnp.where(there, 1.0, 0.0).astype(F32)
-        for index, (a, n) in enumerate(plan.carried):
-            if n >= 0:
-                ext[n, level(a), :, 0:COLS] = message[index] * keep
-                ext[n, level(a), :, COLS:WIDE] = (
-                    halo_columns(message[columns[a, -1]], message[columns[a, -2]], n) * keep
-                )
+        for index, (a, tile, _) in enumerate(plan.carried):
+            if not tile:
+                continue
+            field, part = tile
+            value = message[index] * keep
+            for kept in "ab" if part == "n" and field in plan.tall else part:
+                n = plan.at[field, kept]
+                ext[n, level(a), :, 0:COLS] = value
+                if (a, 0) in columns:
+                    ext[n, level(a), :, COLS:WIDE] = (
+                        halo_columns(message[columns[a, 0]], message[columns[a, 1]], n) * keep
+                    )
 
 
 def shift(value, by, axis):
@@ -235,52 +264,69 @@
     return lax.fori_loop(0, count // size, run, carry)
 
 
-def rates(plan, ext, fields, write, first, count, most):
+def flat_part(plan, ext, field, l):
+    return flat_flux(plan.sixteen(ext, field, l), plan.sixteen(ext, U, l), 1) + rows_flux(
+        plan.rows(ext, field, l), plan.rows(ext, V, l)
+    )
+
+
+def flat_own(plan, ext, fields, flat):
+    def some(levels, _):
+        results = [(n, l, flat_part(plan, ext, f, l)) for l in levels for n, f in enumerate(fields)]
+        for n, l, value in results:
+            flat[n, l - REACH] = value
+        return 0
+
+    sweep(REACH, LEVELS, 2, some)
+
+
+def rates(plan, ext, fields, write, around_own, most, flat=None):
     reads = [lambda l, f=f: plan.sixteen(ext, f, l) for f in fields]
 
-    def some(levels, lows):
+    def some(levels, lows, flat=None):
         results = []
         for l in levels:
-            u, v, w = (
-                plan.sixteen(ext, U, l),
-                plan.rows(ext, V, l),
-                plan.sixteen(ext, W, l),
-            )
+            w = plan.sixteen(ext, W, l)
             highs = []
             for n, f in enumerate(fields):
                 high = level_flux(reads[n], w, l)
-                here = plan.rows(ext, f, l)
-                total = (
-                    flat_flux(reads[n](l), u, 1) + rows_flux(here, v) + (high - lows[n])
-                )
-                results.append((n, l, total * SIXTIETH))
+                level = flat[n, l - REACH] if flat is not None else flat_part(plan, ext, f, l)
+                results.append((n, l, (level + (high - lows[n])) * SIXTIETH))
                 highs.append(high)
             lows = tuple(highs)
         for result in results:
             write(*result)
         return lows
 
+    first = REACH - around_own
     w = plan.sixteen(ext, W, first - 1)
-    sweep(first, count, most, some, tuple(level_flux(read, w, first - 1) for read in reads))
-
-
-def first_rates(
-    place_ref, own, above, below, from_right, from_left, from_up, from_down, speed, ext, rate
-):
-    place, last = place_ref[0], place_ref[1]
-    assemble(
-        FIRST, (own, above, below, from_right, from_left, from_up, from_down), ext, place, last
-    )
-
-    @pl.when(place == last)
+    lows = tuple(level_flux(read, w, first - 1) for read in reads)
+    if flat is None:
+        sweep(first, LEVELS + 2 * around_own, most, some, lows)
+        return
+    lows = sweep(first, around_own, most, some, lows)
+    lows = sweep(REACH, LEVELS, 4, lambda levels, c: some(levels, c, flat), lows)
+    sweep(REACH + LEVELS, around_own, most, some, lows)
+
+
+def first_own(place_ref, own, above, below, from_right, from_left, ext, flat):
+    place_own(FIRST, (own, above, below, from_right, from_left), ext)
+
+    @pl.when(place_ref[0] == place_ref[1])
     def _():
         for part in "on":
             ext[FIRST.at[W, part], REACH + LEVELS - 1] = jnp.zeros((ROWS, WIDE), F32)
 
+    flat_own(FIRST, ext, (C, PR), flat)
+
+
+def first_rates(place_ref, ext_in, flat, from_up, from_down, speed, ext, rate):
+    place_halo(FIRST, from_up, from_down, ext, place_ref[0], place_ref[1])
+
     def write(n, l, value):
         rate[n, l] = value
 
-    rates(FIRST, ext, (C, PR), write, REACH - 4, LEVELS + 8, 2)
+    rates(FIRST, ext, (C, PR), write, 4, 2, flat)
 
 
 def acoustic(p, u, v, w, read_c, rate, step, first, count, place, last):
@@ -348,12 +394,9 @@
     return write
 
 
-def tracer_rate(tiles, winds, l, low):
-    u, v, w = winds
+def tracer_flat(tiles, u, v, l):
     rows = flat_flux(tiles(l)[:, 0:COLS], v(l)[:, 0:COLS], 0)[0:ROWS]
-    cols = flat_flux(tiles(l)[0:ROWS], u(l)[0:ROWS], 1)[:, 0:COLS]
-    high = tracer_high(tiles, w, l)
-    return (rows + cols + (high - low)) * SIXTIETH, high
+    return rows + flat_flux(tiles(l)[0:ROWS], u(l)[0:ROWS], 1)[:, 0:COLS]
 
 
 def tracer_high(tiles, w, l):
@@ -394,7 +437,9 @@
     def own_tracer(levels, low):
         results = []
         for l in levels:
-            tendency, low = tracer_rate(tiles, winds, l, low)
+            high = tracer_high(tiles, winds[2], l)
+            tendency = (tracer_flat(tiles, *winds[:2], l) + (high - low)) * SIXTIETH
+            low = high
             results.append(start[FIRST.at[C, "o"], l, :, 0:COLS] + half * tendency)
         for l, value in zip(levels, results):
             s2[C, l - REACH] = value
@@ -405,7 +450,7 @@
     def write(n, l, value):
         rate1[l] = value
 
-    rates(SECTION, s1, (PR,), write, REACH - 1, LEVELS + 2, 3)
+    rates(SECTION, s1, (PR,), write, 1, 3)
     step = half / (NS // 2)
     acoustic(
         (begin(start, PR), access(fast, 0)[1]),
@@ -455,21 +500,22 @@
 SECTION = Whole()
 
 
-def last_tracer(
-    place_ref,
-    dt_ref,
-    own,
-    above,
-    below,
-    from_right,
-    from_left,
-    from_up,
-    from_down,
-    start,
-    *rest,
-):
+def second_own(own, above, below, from_right, from_left, ext, flat, tracer):
+    place_own(SECOND, (own, above, below, from_right, from_left), ext)
+    flat_own(SECOND, ext, (PR,), flat)
+    tiles, u, v = (lambda l, f=f: SECOND.rows(ext, f, l) for f in (C, U, V))
+
+    def some(levels, _):
+        results = [tracer_flat(tiles, u, v, l) for l in levels]
+        for l, value in zip(levels, results):
+            tracer[l - REACH] = value
+        return 0
+
+    sweep(REACH, LEVELS, 4, some)
+
+
+def last_tracer(place_ref, dt_ref, ext_in, flat_tracer, from_up, from_down, initial, *rest):
     *chunks, ext, tracer, landed, fallen, factor, by_depth, sem = rest
-    place, last = place_ref[0], place_ref[1]
     dt = dt_ref[0]
     each = LEVELS // len(chunks)
     copies = [
@@ -478,17 +524,17 @@
     ]
     for copy in copies:
         copy.start()
-    assemble(
-        SECOND, (own, above, below, from_right, from_left, from_up, from_down), ext, place, last
-    )
+    place_halo(SECOND, from_up, from_down, ext, place_ref[0], place_ref[1])
     tiles = lambda l: SECOND.rows(ext, C, l)
-    winds = [lambda l, f=f: SECOND.rows(ext, f, l) for f in (U, V, W)]
+    w = lambda l: SECOND.rows(ext, W, l)
 
     def some(levels, low):
         results = []
         for l in levels:
-            tendency, low = tracer_rate(tiles, winds, l, low)
-            c = start[FIRST.at[C, "o"], l, :, 0:COLS] + dt * tendency
+            high = tracer_high(tiles, w, l)
+            tendency = (flat_tracer[l - REACH] + (high - low)) * SIXTIETH
+            low = high
+            c = initial[C, l - REACH] + dt * tendency
             grown = jnp.exp(growth * c)
             results.append((c, grown, grown * jnp.exp((0.5 * growth) * c)))
         for l, (c, second, third) in zip(levels, results):
@@ -497,7 +543,7 @@
             factor[1, l - REACH] = third
         return low
 
-    sweep(REACH, LEVELS, 4, some, tracer_high(tiles, winds[2], REACH - 1))
+    sweep(REACH, LEVELS, 4, some, tracer_high(tiles, w, REACH - 1))
     for copy in copies:
         copy.wait()
     for target in range(-FMAX, LEVELS):
@@ -516,15 +562,18 @@
                 landed[moment, target] = total
 
 
-def last_section(place_ref, dt_ref, ext, start, tracer, out, rate, fast):
+def last_section(place_ref, dt_ref, ext, flat, start_far, tracer, out, rate, fast, start, sem):
     place, last = place_ref[0], place_ref[1]
     step = dt_ref[0] / NS
+    copy = pltpu.make_async_copy(start_far, start, sem)
+    copy.start()
 
     def write(n, l, value):
         rate[l] = value
 
-    rates(SECOND, ext, (PR,), write, REACH - 3, LEVELS + 6, 2)
+    rates(SECOND, ext, (PR,), write, 3, 3, flat)
     out[C] = tracer[...]
+    copy.wait()
     names = (PR, U, V, W)
     for repeat in range(NS):
         reads = [
@@ -615,7 +664,7 @@
     return pltpu.VMEM(dims, F32)
 
 
-def call(kernel, name, ins, outs, scratch=(), out_specs=None, flops=None, grant=4):
+def call(kernel, name, ins, outs, scratch=(), out_specs=None, flops=None, grant=4, alias=None):
     made = pl.pallas_call(
         kernel,
         name=name,
@@ -623,6 +672,7 @@
         out_specs=tuple(out_specs or vmem(len(outs))),
         out_shape=tuple(outs),
         scratch_shapes=list(scratch),
+        input_output_aliases=alias or {},
         compiler_params=pltpu.CompilerParams(vmem_limit_bytes=grant << 20),
         cost_estimate=(
             pl.CostEstimate(flops=flops, bytes_accessed=0, transcendentals=0) if flops else None
@@ -723,16 +773,23 @@
         out_shape=(held(5, LEVELS, ROWS, COLS), shaped(devices, 1, COLS)),
         compiler_params=pltpu.CompilerParams(vmem_limit_bytes=4 << 20),
     )(where, fields)
-    early = EARLY
-    halos = exchange(FIRST, own, fields, fields, by_depth[:early])
-    speed, _ = lax.optimization_barrier((speed, halos[2]))
+    *near, from_up, from_down = exchange(FIRST, own, fields, fields, by_depth[:EARLY])
+    ext = held(len(FIRST.tiles), DEPTH, ROWS, WIDE)
+    start, flat = call(
+        first_own,
+        "first_own",
+        smem(1) + vmem(5),
+        [ext, held(2, LEVELS, 2 * ROWS, WIDE)],
+    )(where, own, *near)
+    speed, flat = lax.optimization_barrier((speed, flat))
     speed = lax.all_to_all(speed, GRID_AXES, 0, 0)
     start, rate0 = call(
         first_rates,
         "first_rates",
-        smem(1) + vmem(7) + anywhere(1),
-        [held(len(FIRST.tiles), DEPTH, ROWS, WIDE), held(2, DEPTH, 2 * ROWS, WIDE)],
-    )(where, own, *halos, speed)
+        smem(1) + vmem(4) + anywhere(1),
+        [ext, held(2, DEPTH, 2 * ROWS, WIDE)],
+        alias={1: 0},
+    )(where, start, flat, from_up, from_down, speed)
     s2, down, up, dt = call(
         two_sections,
         "two_sections",
@@ -746,13 +803,21 @@
         out_specs=vmem(3) + smem(1),
         grant=10,
     )(where, speed, start, rate0)
-    halos = exchange(SECOND, s2, down, up, by_depth[early:])
-    ext, tracer, landed, fallen = call(
+    *near, from_up, from_down = exchange(SECOND, s2, down, up, by_depth[EARLY:LATE])
+    ext = held(len(SECOND.tiles), DEPTH, ROWS, WIDE)
+    around_s2, flat, flat_tracer = call(
+        second_own,
+        "second_own",
+        vmem(5),
+        [ext, held(1, LEVELS, 2 * ROWS, WIDE), held(LEVELS, ROWS, COLS)],
+        flops=1_000_000_000,
+    )(s2, *near)
+    around_s2, tracer, landed, fallen = call(
         last_tracer,
         "last_tracer",
-        smem(2) + vmem(8) + anywhere(len(by_depth)),
+        smem(2) + vmem(5) + anywhere(len(by_depth)),
         [
-            held(len(SECOND.tiles), DEPTH, ROWS, WIDE),
+            ext,
             held(LEVELS, ROWS, COLS),
             held(3, LEVELS, ROWS, COLS),
             held(3, FMAX, ROWS, COLS),
@@ -762,21 +827,24 @@
             pltpu.VMEM((LEVELS, FMAX + 1, 3, ROWS, COLS), F32),
             pltpu.SemaphoreType.DMA((len(by_depth),)),
         ],
-    )(where, dt, s2, *halos, start, *by_depth)
+        alias={2: 0},
+    )(where, dt, around_s2, flat_tracer, from_up, from_down, own, *by_depth)
     count = lax.axis_size("gz")
     arrived = lax.ppermute(fallen, "gz", [((i + 1) % count, i) for i in range(count)])
     (new_fields,) = call(
         last_section,
         "last_section",
-        smem(2) + vmem(3),
+        smem(2) + vmem(2) + anywhere(1) + vmem(1),
         [shaped(5, LEVELS, ROWS, COLS)],
         scratch=[
             pltpu.VMEM((DEPTH, 2 * ROWS, WIDE), F32),
             pltpu.VMEM((4, DEPTH, 2 * ROWS, WIDE), F32),
+            pltpu.VMEM((len(FIRST.tiles), DEPTH, ROWS, WIDE), F32),
+            pltpu.SemaphoreType.DMA,
         ],
         flops=1_000_000_000,
-        grant=8,
-    )(where, dt, ext, start, tracer)
+        grant=12,
+    )(where, dt, around_s2, flat, start, tracer)
     arrived = jnp.where(place == last, 0.0, arrived)
     moments = landed.at[:, LEVELS - FMAX :].add(arrived)
     return (new_fields, moments)

time: 112 us -> 111 us (level)
  waiting for transfers between devices: 17.9 us -> 11.7 us
  local copies, waits for them, and re-layouts: 8.74 us -> 11.1 us
  Pallas kernels: 41.8 us -> 43.4 us
    ppermute x6, waiting for transfers between devices: 9.31 us -> 4.32 us  [both_ways(): lax.ppermute(down, axis, [((i + 1) % count, i) for i in range(count)])]
    unnamed x24 -> x36, local copies, waits for them, and re-layouts: 8.74 us -> 11.1 us
    pallas_call x8 -> x10, Pallas kernels: 25.7 us -> 27.3 us  [run(): made(*(pltpu.with_memory_space_constraint(value, pltpu.VMEM) if spec.memo...]
  transfers between devices with their start and end apart: 13 -> 13, of which waited for: 8 -> 7; matrix products, arithmetic and copies ran while one was open for 1% -> 1% of each run, Pallas kernels for 21% -> 26%
where the time goes in v3:
time: 111 us
  Pallas kernels  43.4 us (39%)
  blocking collectives  26.3 us (24%)
  starting transfers between devices  16 us (14%)
  waiting for transfers between devices  11.7 us (11%)
  local copies, waits for them, and re-layouts  11.1 us (10%)
    pallas_call x10, Pallas kernels, run(): made(*(pltpu.with_memory_space_constraint(value, pltpu.VMEM) if spec.memo...  27.3 us
    all_to_all x1, blocking collectives, per_device(): speed = lax.all_to_all(speed, GRID_AXES, 0, 0)  26.3 us
    pallas_call x8, Pallas kernels, droplets(): pl.pallas_call(deposit, name='deposit', grid=(1,), in_specs=[whole, whole...  15.3 us
    unnamed x36, local copies, waits for them, and re-layouts  11.1 us
    ppermute x6, starting transfers between devices, both_ways(): lax.ppermute(down, axis, [((i + 1) % count, i) for i in range(count)])  9.53 us
    ppermute x6, waiting for transfers between devices, both_ways(): lax.ppermute(up, axis, [(i, (i + 1) % count) for i in range(count)])  7.42 us
    ppermute x6, starting transfers between devices, both_ways(): lax.ppermute(up, axis, [(i, (i + 1) % count) for i in range(count)])  5.49 us
    ppermute x6, waiting for transfers between devices, both_ways(): lax.ppermute(down, axis, [((i + 1) % count, i) for i in range(count)])  4.32 us
  transfers between devices with their start and end apart: 13, of which 7 were waited for; matrix products, arithmetic and copies ran while one was open for 1% of the time, Pallas kernels for 26%

profile of v3, /device:TPU:4, one launch (start us, length us, event | category | flops | bytes accessed | tf_op | source)
XLA Modules:
  0.0 110.6 jit_solution(943752962280639474)
XLA Ops:
  0.6 1.9 %collective-permute-start.1 = (f32[5,16,8,128]{3,2,1,0:T(8,128)}, f32[5,16,8,128]{3,2,1,0:T(8,128)S(1)}, u32[]{:S(2)}, u32[]{:S(2)}) collective-permute-start(f32[5,16,8,128]{3,2,1,0:T(8,128)} %fields.1), channel_id=1, source_target_pairs={{0,4},{4,8},{8,12},{12,16},{16,20},{20,24},{24,28},{28,32},{32,36}... | collective-permute-start | bytes 983048 | tf_op jit(solution)/shard_map/ppermute | solution.py:699
  2.6 1.7 %collective-permute-start = (f32[5,16,8,128]{3,2,1,0:T(8,128)}, f32[5,16,8,128]{3,2,1,0:T(8,128)S(1)}, u32[]{:S(2)}, u32[]{:S(2)}) collective-permute-start(f32[5,16,8,128]{3,2,1,0:T(8,128)} %fields.1), channel_id=1, source_target_pairs={{4,0},{8,4},{12,8},{16,12},{20,16},{24,20},{28,24},{32,28},{36,32}... | collective-permute-start | bytes 983048 | tf_op jit(solution)/shard_map/ppermute | solution.py:698
  11.3 1.9 %deposit.11.rest_3_ = f32[2,9,3,8,128]{4,3,2,1,0:T(8,128)S(1)} custom-call(f32[8,16,8,128]{3,2,1,0:T(8,128)S(1)} %copy-done, f32[8,16,8,128]{3,2,1,0:T(8,128)S(1)} %copy-done.2, s32[8,16,8,128]{3,2,1,0:T(8,128)S(1)} %copy-done.4, s32[16,8,128]{2,1,0:T(8,128)S(1)} %copy-done.12, s32[8,16,8,1]{3,2,1,0:T(8,128)S(1)} %copy.10.fall_depth), custom_call_target="tpu_custom_call" | custom-call | flops 200000000 | tf_op jit(solution)/shard_map/deposit/pallas_call | solution.py:738
  13.2 1.9 %deposit.10.rest_2_ = f32[2,9,3,8,128]{4,3,2,1,0:T(8,128)S(1)} custom-call(f32[8,16,8,128]{3,2,1,0:T(8,128)S(1)} %copy-done, f32[8,16,8,128]{3,2,1,0:T(8,128)S(1)} %copy-done.2, s32[8,16,8,128]{3,2,1,0:T(8,128)S(1)} %copy-done.4, s32[16,8,128]{2,1,0:T(8,128)S(1)} %copy-done.12, s32[8,16,8,1]{3,2,1,0:T(8,128)S(1)} %copy.10.fall_depth), custom_call_target="tpu_custom_call" | custom-call | flops 200000000 | tf_op jit(solution)/shard_map/deposit/pallas_call | solution.py:738
  15.1 1.9 %deposit.9.rest_1_ = f32[2,9,3,8,128]{4,3,2,1,0:T(8,128)S(1)} custom-call(f32[8,16,8,128]{3,2,1,0:T(8,128)S(1)} %copy-done, f32[8,16,8,128]{3,2,1,0:T(8,128)S(1)} %copy-done.2, s32[8,16,8,128]{3,2,1,0:T(8,128)S(1)} %copy-done.4, s32[16,8,128]{2,1,0:T(8,128)S(1)} %copy-done.12, s32[8,16,8,1]{3,2,1,0:T(8,128)S(1)} %copy.10.fall_depth), custom_call_target="tpu_custom_call" | custom-call | flops 200000000 | tf_op jit(solution)/shard_map/deposit/pallas_call | solution.py:738
  17.0 1.9 %deposit.8.rest_0_ = f32[2,9,3,8,128]{4,3,2,1,0:T(8,128)S(1)} custom-call(f32[8,16,8,128]{3,2,1,0:T(8,128)S(1)} %copy-done, f32[8,16,8,128]{3,2,1,0:T(8,128)S(1)} %copy-done.2, s32[8,16,8,128]{3,2,1,0:T(8,128)S(1)} %copy-done.4, s32[16,8,128]{2,1,0:T(8,128)S(1)} %copy-done.12, s32[8,16,8,1]{3,2,1,0:T(8,128)S(1)} %copy.10.fall_depth), custom_call_target="tpu_custom_call" | custom-call | flops 200000000 | tf_op jit(solution)/shard_map/deposit/pallas_call | solution.py:738
  22.0 2.2 %collective-permute-done.3.from_left = f32[16,8,128]{2,1,0:T(8,128)S(1)} collective-permute-done((f32[16,8,128]{2,1,0:T(8,128)S(1)}, f32[16,8,128]{2,1,0:T(8,128)S(1)}, u32[]{:S(2)}, u32[]{:S(2)}) %collective-permute-start.3) | collective-permute-done | bytes 65568 | tf_op jit(solution)/shard_map/ppermute | solution.py:699
  24.2 3.1 %collective-permute-start.4 = (f32[64,8,128]{2,1,0:T(8,128)S(1)}, f32[64,8,128]{2,1,0:T(8,128)S(1)}, u32[]{:S(2)}, u32[]{:S(2)}) collective-permute-start(f32[64,8,128]{2,1,0:T(8,128)S(1)} %get-tuple-element.49), channel_id=1, source_target_pairs={{1,0},{2,1},{3,2},{0,3},{5,4},{6,5},{7,6},{4,7},{9,8},{10,9},{11,1... | collective-permute-start | bytes 786440 | tf_op jit(solution)/shard_map/ppermute | solution.py:698
  27.3 3.3 %first_own.1 = (f32[13,30,8,256]{3,2,1,0:T(8,128)S(1)}, f32[2,16,16,256]{3,2,1,0:T(8,128)S(1)}) custom-call(s32[2]{0:T(128)S(1)} %pad_add_fusion.place_ref, f32[5,16,8,128]{3,2,1,0:T(8,128)S(1)} %get-tuple-element.42.own.initial, f32[5,16,8,128]{3,2,1,0:T(8,128)S(1)} %collective-permute-done.above, f32[5,16,8,128]{3,2,1,0:T(8,128)S(1)} %collective-permute-done.1.below, ...), custom_call_target="tpu_custom_call" | custom-call | tf_op jit(solution)/shard_map/first_own/pallas_call | solution.py:683
  30.7 26.3 %all_to_all.5.speed = f32[256,1,128]{2,1,0:T(1,128)S(1)} all-to-all(f32[256,1,128]{2,1,0:T(1,128)S(1)} %get-tuple-element.46), channel_id=1, replica_groups=mesh['gx'=4,'gy'=16,'gz'=4] {'gx','gy','gz'}, dimensions={0} | all-to-all | bytes 262144 | tf_op jit(solution)/shard_map/all_to_all | solution.py:785
  57.0 2.5 %first_rates.1 = (f32[13,30,8,256]{3,2,1,0:T(8,128)S(1)}, f32[2,30,16,256]{3,2,1,0:T(8,128)S(1)}) custom-call(s32[2]{0:T(128)S(1)} %pad_add_fusion.place_ref, f32[13,30,8,256]{3,2,1,0:T(8,128)S(1)} %get-tuple-element.47.ext_in, f32[2,16,16,256]{3,2,1,0:T(8,128)S(1)} %get-tuple-element.48.flat, ...), custom_call_target="tpu_custom_call", output_to_operand_aliasing={{0}: (1, {})} | custom-call | tf_op jit(solution)/shard_map/first_rates/pallas_call | solution.py:683
  59.5 5.5 %two_sections.1 = (f32[5,16,8,128]{3,2,1,0:T(8,128)S(1)}, f32[3,16,8,128]{3,2,1,0:T(8,128)S(1)}, f32[3,16,8,128]{3,2,1,0:T(8,128)S(1)}, f32[1]{0:T(128)}) custom-call(s32[2]{0:T(128)S(1)} %pad_add_fusion.place_ref, f32[256,1,128]{2,1,0:T(1,128)S(1)} %all_to_all.5.speed, f32[13,30,8,256]{3,2,1,0:T(8,128)S(1)} %get-tuple-element.51.start.start_far, ...), custom_call_target="tpu_custom_call" | custom-call | tf_op jit(solution)/shard_map/two_sections/pallas_call | solution.py:683
  65.0 2.2 %collective-permute-start.6 = (f32[3,16,8,128]{3,2,1,0:T(8,128)S(1)}, f32[3,16,8,128]{3,2,1,0:T(8,128)S(1)}, u32[]{:S(2)}, u32[]{:S(2)}) collective-permute-start(f32[3,16,8,128]{3,2,1,0:T(8,128)S(1)} %get-tuple-element.55), channel_id=1, source_target_pairs={{4,0},{8,4},{12,8},{16,12},{20,16},{24,20},{28,24},{32,28},{36,32}... | collective-permute-start | bytes 589832 | tf_op jit(solution)/shard_map/ppermute | solution.py:698
  67.2 2.3 %collective-permute-start.7 = (f32[3,16,8,128]{3,2,1,0:T(8,128)S(1)}, f32[3,16,8,128]{3,2,1,0:T(8,128)S(1)}, u32[]{:S(2)}, u32[]{:S(2)}) collective-permute-start(f32[3,16,8,128]{3,2,1,0:T(8,128)S(1)} %get-tuple-element.56), channel_id=1, source_target_pairs={{0,4},{4,8},{8,12},{12,16},{16,20},{20,24},{24,28},{28,32},{32,36}... | collective-permute-start | bytes 589832 | tf_op jit(solution)/shard_map/ppermute | solution.py:699
  69.5 1.9 %deposit.14.rest_2_.rest_6_ = f32[2,9,3,8,128]{4,3,2,1,0:T(8,128)S(1)} custom-call(f32[8,16,8,128]{3,2,1,0:T(8,128)S(1)} %copy-done.1, f32[8,16,8,128]{3,2,1,0:T(8,128)S(1)} %copy-done.3, s32[8,16,8,128]{3,2,1,0:T(8,128)S(1)} %copy-done.5, s32[16,8,128]{2,1,0:T(8,128)S(1)} %copy-done.13, s32[8,16,8,1]{3,2,1,0:T(8,128)S(1)} %copy.10.fall_depth), custom_call_target="tpu_custom_call" | custom-call | flops 200000000 | tf_op jit(solution)/shard_map/deposit/pallas_call | solution.py:738
  71.5 1.9 %deposit.13.rest_1_.rest_5_ = f32[2,9,3,8,128]{4,3,2,1,0:T(8,128)S(1)} custom-call(f32[8,16,8,128]{3,2,1,0:T(8,128)S(1)} %copy-done.1, f32[8,16,8,128]{3,2,1,0:T(8,128)S(1)} %copy-done.3, s32[8,16,8,128]{3,2,1,0:T(8,128)S(1)} %copy-done.5, s32[16,8,128]{2,1,0:T(8,128)S(1)} %copy-done.13, s32[8,16,8,1]{3,2,1,0:T(8,128)S(1)} %copy.10.fall_depth), custom_call_target="tpu_custom_call" | custom-call | flops 200000000 | tf_op jit(solution)/shard_map/deposit/pallas_call | solution.py:738
  73.4 1.9 %deposit.12.rest_0_.rest_4_ = f32[2,9,3,8,128]{4,3,2,1,0:T(8,128)S(1)} custom-call(f32[8,16,8,128]{3,2,1,0:T(8,128)S(1)} %copy-done.1, f32[8,16,8,128]{3,2,1,0:T(8,128)S(1)} %copy-done.3, s32[8,16,8,128]{3,2,1,0:T(8,128)S(1)} %copy-done.5, s32[16,8,128]{2,1,0:T(8,128)S(1)} %copy-done.13, s32[8,16,8,1]{3,2,1,0:T(8,128)S(1)} %copy.10.fall_depth), custom_call_target="tpu_custom_call" | custom-call | flops 200000000 | tf_op jit(solution)/shard_map/deposit/pallas_call | solution.py:738
  75.7 2.5 %collective-permute-done.7.below = f32[3,16,8,128]{3,2,1,0:T(8,128)S(1)} collective-permute-done((f32[3,16,8,128]{3,2,1,0:T(8,128)S(1)}, f32[3,16,8,128]{3,2,1,0:T(8,128)S(1)}, u32[]{:S(2)}, u32[]{:S(2)}) %collective-permute-start.7) | collective-permute-done | bytes 196640 | tf_op jit(solution)/shard_map/ppermute | solution.py:699
  80.2 2.5 %collective-permute-done.8.from_right = f32[16,8,128]{2,1,0:T(8,128)S(1)} collective-permute-done((f32[16,8,128]{2,1,0:T(8,128)S(1)}, f32[16,8,128]{2,1,0:T(8,128)S(1)}, u32[]{:S(2)}, u32[]{:S(2)}) %collective-permute-start.8) | collective-permute-done | bytes 65568 | tf_op jit(solution)/shard_map/ppermute | solution.py:698
  86.1 1.9 %deposit.15.rest_7_ = f32[2,9,3,8,128]{4,3,2,1,0:T(8,128)S(1)} custom-call(f32[8,16,8,128]{3,2,1,0:T(8,128)S(1)} %copy-done.1, f32[8,16,8,128]{3,2,1,0:T(8,128)S(1)} %copy-done.3, s32[8,16,8,128]{3,2,1,0:T(8,128)S(1)} %copy-done.5, s32[16,8,128]{2,1,0:T(8,128)S(1)} %copy-done.13, s32[8,16,8,1]{3,2,1,0:T(8,128)S(1)} %copy.10.fall_depth), custom_call_target="tpu_custom_call" | custom-call | flops 200000000 | tf_op jit(solution)/shard_map/deposit/pallas_call | solution.py:738
  88.0 2.9 %second_own.1 = (f32[11,30,8,256]{3,2,1,0:T(8,128)S(1)}, f32[1,16,16,256]{3,2,1,0:T(8,128)S(1)}, f32[16,8,128]{2,1,0:T(8,128)S(1)}) custom-call(f32[5,16,8,128]{3,2,1,0:T(8,128)S(1)} %get-tuple-element.54.own, f32[3,16,8,128]{3,2,1,0:T(8,128)S(1)} %collective-permute-done.6.above, f32[3,16,8,128]{3,2,1,0:T(8,128)S(1)} %collective-permute-done.7.below, ...), custom_call_target="tpu_custom_call" | custom-call | flops 1000000000 | tf_op jit(solution)/shard_map/second_own/pallas_call | solution.py:683
  92.5 4.6 %last_tracer.1 = (f32[11,30,8,256]{3,2,1,0:T(8,128)S(1)}, f32[16,8,128]{2,1,0:T(8,128)S(1)}, f32[3,16,8,128]{3,2,1,0:T(8,128)S(1)}, f32[3,8,8,128]{3,2,1,0:T(8,128)}) custom-call(s32[2]{0:T(128)S(1)} %pad_add_fusion.place_ref, f32[1]{0:T(128)} %get-tuple-element.53.dt_ref, ...), custom_call_target="tpu_custom_call", output_to_operand_aliasing={{0}: (2, {})} | custom-call | tf_op jit(solution)/shard_map/last_tracer/pallas_call | solution.py:683
  99.7 1.8 %copy-done.9 = f32[11,30,8,256]{3,2,1,0:T(8,128)S(1)} copy-done((f32[11,30,8,256]{3,2,1,0:T(8,128)S(1)}, f32[11,30,8,256]{3,2,1,0:T(8,128)}, u32[]{:S(2)}) %copy-start.9) | copy-done | bytes 2703384
  102.4 6.6 %last_section.1 = f32[5,16,8,128]{3,2,1,0:T(8,128)} custom-call(s32[2]{0:T(128)S(1)} %pad_add_fusion.place_ref, f32[1]{0:T(128)} %get-tuple-element.53.dt_ref, f32[11,30,8,256]{3,2,1,0:T(8,128)S(1)} %copy-done.9, f32[1,16,16,256]{3,2,1,0:T(8,128)S(1)} %copy-done.16, f32[13,30,8,256]{3,2,1,0:T(8,128)S(1)} %copy-done.7, f32[16,8,128]{2,1,0:T(8,128)S(1)} %get-tuple-element.65.tracer), custom_call_target="tpu_custom_call" | custom-call | flops 1000000000 | tf_op jit(solution)/shard_map/last_section/pallas_call | solution.py:683
  (60 shorter events, 22.5 us)
Async XLA Ops:
  0.6 18.3 %collective-permute-start.1 = (f32[5,16,8,128]{3,2,1,0:T(8,128)}, f32[5,16,8,128]{3,2,1,0:T(8,128)S(1)}, u32[]{:S(2)}, u32[]{:S(2)}) collective-permute-start(f32[5,16,8,128]{3,2,1,0:T(8,128)} %fields.1), channel_id=1, source_target_pairs={{0,4},{4,8},{8,12},{12,16},{16,20},{20,24},{24,28},{28,32},{32,36}... | collective-permute-start | bytes 983048 | tf_op jit(solution)/shard_map/ppermute | solution.py:699
  2.6 16.4 %collective-permute-start = (f32[5,16,8,128]{3,2,1,0:T(8,128)}, f32[5,16,8,128]{3,2,1,0:T(8,128)S(1)}, u32[]{:S(2)}, u32[]{:S(2)}) collective-permute-start(f32[5,16,8,128]{3,2,1,0:T(8,128)} %fields.1), channel_id=1, source_target_pairs={{4,0},{8,4},{12,8},{16,12},{20,16},{24,20},{28,24},{32,28},{36,32}... | collective-permute-start | bytes 983048 | tf_op jit(solution)/shard_map/ppermute | solution.py:698
  6.1 21.3 %copy-start.10 = (f32[5,16,8,128]{3,2,1,0:T(8,128)}, f32[5,16,8,128]{3,2,1,0:T(8,128)S(1)}, u32[]{:S(2)}) copy-start(f32[5,16,8,128]{3,2,1,0:T(8,128)S(1)} %get-tuple-element.42.own.initial) | copy-start | bytes 983044
  20.0 2.1 %collective-permute-start.2 = (f32[16,8,128]{2,1,0:T(8,128)S(1)}, f32[16,8,128]{2,1,0:T(8,128)S(1)}, u32[]{:S(2)}, u32[]{:S(2)}) collective-permute-start(f32[16,8,128]{2,1,0:T(8,128)S(1)} %get-tuple-element.43), channel_id=1, source_target_pairs={{64,0},{128,64},{192,128},{0,192},{65,1},{129,65},{193,129},{1,193... | collective-permute-start | bytes 196616 | tf_op jit(solution)/shard_map/ppermute | solution.py:698
  20.1 4.1 %collective-permute-start.3 = (f32[16,8,128]{2,1,0:T(8,128)S(1)}, f32[16,8,128]{2,1,0:T(8,128)S(1)}, u32[]{:S(2)}, u32[]{:S(2)}) collective-permute-start(f32[16,8,128]{2,1,0:T(8,128)S(1)} %get-tuple-element.44), channel_id=1, source_target_pairs={{0,64},{64,128},{128,192},{192,0},{1,65},{65,129},{129,193},{193,1... | collective-permute-start | bytes 196616 | tf_op jit(solution)/shard_map/ppermute | solution.py:699
  24.2 32.8 %collective-permute-start.4 = (f32[64,8,128]{2,1,0:T(8,128)S(1)}, f32[64,8,128]{2,1,0:T(8,128)S(1)}, u32[]{:S(2)}, u32[]{:S(2)}) collective-permute-start(f32[64,8,128]{2,1,0:T(8,128)S(1)} %get-tuple-element.49), channel_id=1, source_target_pairs={{1,0},{2,1},{3,2},{0,3},{5,4},{6,5},{7,6},{4,7},{9,8},{10,9},{11,1... | collective-permute-start | bytes 786440 | tf_op jit(solution)/shard_map/ppermute | solution.py:698
  27.3 29.7 %collective-permute-start.5 = (f32[64,8,128]{2,1,0:T(8,128)S(1)}, f32[64,8,128]{2,1,0:T(8,128)S(1)}, u32[]{:S(2)}, u32[]{:S(2)}) collective-permute-start(f32[64,8,128]{2,1,0:T(8,128)S(1)} %get-tuple-element.50), channel_id=1, source_target_pairs={{0,1},{1,2},{2,3},{3,0},{4,5},{5,6},{6,7},{7,4},{8,9},{9,10},{10,1... | collective-permute-start | bytes 786440 | tf_op jit(solution)/shard_map/ppermute | solution.py:699
  59.5 12.0 %copy-start.6 = (f32[13,30,8,256]{3,2,1,0:T(8,128)}, f32[13,30,8,256]{3,2,1,0:T(8,128)S(1)}, u32[]{:S(2)}) copy-start(f32[13,30,8,256]{3,2,1,0:T(8,128)S(1)} %get-tuple-element.51.start.start_far) | copy-start | bytes 9584644
  59.5 10.0 %copy-start.1 = (f32[8,16,8,128]{3,2,1,0:T(8,128)S(1)}, f32[8,16,8,128]{3,2,1,0:T(8,128)}, u32[]{:S(2)}) copy-start(f32[8,16,8,128]{3,2,1,0:T(8,128)} %radius.15) | copy-start | bytes 1572868
  59.5 10.0 %copy-start.3 = (f32[8,16,8,128]{3,2,1,0:T(8,128)S(1)}, f32[8,16,8,128]{3,2,1,0:T(8,128)}, u32[]{:S(2)}) copy-start(f32[8,16,8,128]{3,2,1,0:T(8,128)} %weight.15) | copy-start | bytes 1572868
  59.5 10.0 %copy-start.5 = (s32[8,16,8,128]{3,2,1,0:T(8,128)S(1)}, s32[8,16,8,128]{3,2,1,0:T(8,128)}, u32[]{:S(2)}) copy-start(s32[8,16,8,128]{3,2,1,0:T(8,128)} %column.15) | copy-start | bytes 1572868
  59.5 10.0 %copy-start.13 = (s32[16,8,128]{2,1,0:T(8,128)S(1)}, s32[16,8,128]{2,1,0:T(8,128)}, u32[]{:S(2)}) copy-start(s32[16,8,128]{2,1,0:T(8,128)} %counts.15) | copy-start | bytes 196612
  65.0 10.7 %collective-permute-start.6 = (f32[3,16,8,128]{3,2,1,0:T(8,128)S(1)}, f32[3,16,8,128]{3,2,1,0:T(8,128)S(1)}, u32[]{:S(2)}, u32[]{:S(2)}) collective-permute-start(f32[3,16,8,128]{3,2,1,0:T(8,128)S(1)} %get-tuple-element.55), channel_id=1, source_target_pairs={{4,0},{8,4},{12,8},{16,12},{20,16},{24,20},{28,24},{32,28},{36,32}... | collective-permute-start | bytes 589832 | tf_op jit(solution)/shard_map/ppermute | solution.py:698
  67.2 10.9 %collective-permute-start.7 = (f32[3,16,8,128]{3,2,1,0:T(8,128)S(1)}, f32[3,16,8,128]{3,2,1,0:T(8,128)S(1)}, u32[]{:S(2)}, u32[]{:S(2)}) collective-permute-start(f32[3,16,8,128]{3,2,1,0:T(8,128)S(1)} %get-tuple-element.56), channel_id=1, source_target_pairs={{0,4},{4,8},{8,12},{12,16},{16,20},{20,24},{24,28},{28,32},{32,36}... | collective-permute-start | bytes 589832 | tf_op jit(solution)/shard_map/ppermute | solution.py:699
  79.1 3.6 %collective-permute-start.8 = (f32[16,8,128]{2,1,0:T(8,128)S(1)}, f32[16,8,128]{2,1,0:T(8,128)S(1)}, u32[]{:S(2)}, u32[]{:S(2)}) collective-permute-start(f32[16,8,128]{2,1,0:T(8,128)S(1)} %get-tuple-element.57), channel_id=1, source_target_pairs={{64,0},{128,64},{192,128},{0,192},{65,1},{129,65},{193,129},{1,193... | collective-permute-start | bytes 196616 | tf_op jit(solution)/shard_map/ppermute | solution.py:698
  80.2 3.7 %collective-permute-start.9 = (f32[16,8,128]{2,1,0:T(8,128)S(1)}, f32[16,8,128]{2,1,0:T(8,128)S(1)}, u32[]{:S(2)}, u32[]{:S(2)}) collective-permute-start(f32[16,8,128]{2,1,0:T(8,128)S(1)} %get-tuple-element.58), channel_id=1, source_target_pairs={{0,64},{64,128},{128,192},{192,0},{1,65},{65,129},{129,193},{193,1... | collective-permute-start | bytes 196616 | tf_op jit(solution)/shard_map/ppermute | solution.py:699
  83.9 8.5 %copy-start.11 = (f32[5,16,8,128]{3,2,1,0:T(8,128)S(1)}, f32[5,16,8,128]{3,2,1,0:T(8,128)}, u32[]{:S(2)}) copy-start(f32[5,16,8,128]{3,2,1,0:T(8,128)} %copy-done.10) | copy-start | bytes 983044
  84.0 7.0 %collective-permute-start.10 = (f32[48,8,128]{2,1,0:T(8,128)S(1)}, f32[48,8,128]{2,1,0:T(8,128)S(1)}, u32[]{:S(2)}, u32[]{:S(2)}) collective-permute-start(f32[48,8,128]{2,1,0:T(8,128)S(1)} %get-tuple-element.61), channel_id=1, source_target_pairs={{1,0},{2,1},{3,2},{0,3},{5,4},{6,5},{7,6},{4,7},{9,8},{10,9},{11,1... | collective-permute-start | bytes 589832 | tf_op jit(solution)/shard_map/ppermute | solution.py:698
  85.2 7.3 %collective-permute-start.11 = (f32[48,8,128]{2,1,0:T(8,128)S(1)}, f32[48,8,128]{2,1,0:T(8,128)S(1)}, u32[]{:S(2)}, u32[]{:S(2)}) collective-permute-start(f32[48,8,128]{2,1,0:T(8,128)S(1)} %get-tuple-element.62), channel_id=1, source_target_pairs={{0,1},{1,2},{2,3},{3,0},{4,5},{5,6},{6,7},{7,4},{8,9},{9,10},{10,1... | collective-permute-start | bytes 589832 | tf_op jit(solution)/shard_map/ppermute | solution.py:699
  90.9 6.2 %copy-start.15 = (f32[1,16,16,256]{3,2,1,0:T(8,128)}, f32[1,16,16,256]{3,2,1,0:T(8,128)S(1)}, u32[]{:S(2)}) copy-start(f32[1,16,16,256]{3,2,1,0:T(8,128)S(1)} %get-tuple-element.64.flat) | copy-start | bytes 786436
  90.9 8.7 %copy-start.7 = (f32[13,30,8,256]{3,2,1,0:T(8,128)S(1)}, f32[13,30,8,256]{3,2,1,0:T(8,128)}, u32[]{:S(2)}) copy-start(f32[13,30,8,256]{3,2,1,0:T(8,128)} %copy-done.6) | copy-start | bytes 9584644
  97.1 1.5 %copy-start.8 = (f32[11,30,8,256]{3,2,1,0:T(8,128)}, f32[11,30,8,256]{3,2,1,0:T(8,128)S(1)}, u32[]{:S(2)}) copy-start(f32[11,30,8,256]{3,2,1,0:T(8,128)S(1)} %get-tuple-element.63.ext) | copy-start | bytes 8110084
  98.6 10.3 %collective-permute-start.12 = (f32[3,8,8,128]{3,2,1,0:T(8,128)}, f32[3,8,8,128]{3,2,1,0:T(8,128)}, u32[]{:S(2)}, u32[]{:S(2)}) collective-permute-start(f32[3,8,8,128]{3,2,1,0:T(8,128)} %get-tuple-element.67), channel_id=1, source_target_pairs={{1,0},{2,1},{3,2},{0,3},{5,4},{6,5},{7,6},{4,7},{9,8},{10,9},{11,1... | collective-permute-start | bytes 294920 | tf_op jit(solution)/shard_map/ppermute | solution.py:833
  99.7 1.8 %copy-start.9 = (f32[11,30,8,256]{3,2,1,0:T(8,128)S(1)}, f32[11,30,8,256]{3,2,1,0:T(8,128)}, u32[]{:S(2)}) copy-start(f32[11,30,8,256]{3,2,1,0:T(8,128)} %copy-done.8) | copy-start | bytes 8110084
  (6 other events, 5.9 us)

commit v4 on v3

--- a/solution.py
+++ b/solution.py
@@ -7,7 +7,6 @@
 
 NS = 4
 FMAX = 8
-EARLY, LATE = 4, 7
 GRID_AXES = ("gx", "gy", "gz")
 
 sound_speed = 10.0
@@ -320,7 +319,8 @@
     flat_own(FIRST, ext, (C, PR), flat)
 
 
-def first_rates(place_ref, ext_in, flat, from_up, from_down, speed, ext, rate):
+def first_rates(place_ref, ext_in, flat, from_up, from_down, *rest):
+    ext, rate = rest[-2:]
     place_halo(FIRST, from_up, from_down, ext, place_ref[0], place_ref[1])
 
     def write(n, l, value):
@@ -514,8 +514,10 @@
     sweep(REACH, LEVELS, 4, some)
 
 
-def last_tracer(place_ref, dt_ref, ext_in, flat_tracer, from_up, from_down, initial, *rest):
-    *chunks, ext, tracer, landed, fallen, factor, by_depth, sem = rest
+def last_tracer(
+    place_ref, dt_ref, ext_in, flat, flat_tracer, from_up, from_down, initial, *rest
+):
+    *chunks, ext, tracer, landed, fallen, rate, warm, factor, by_depth, sem = rest
     dt = dt_ref[0]
     each = LEVELS // len(chunks)
     copies = [
@@ -525,6 +527,18 @@
     for copy in copies:
         copy.start()
     place_halo(SECOND, from_up, from_down, ext, place_ref[0], place_ref[1])
+
+    def write(n, l, value):
+        rate[l] = value
+
+    rates(SECOND, ext, (PR,), write, 3, 3, flat)
+
+    def keep(levels, _):
+        for l in levels:
+            warm[l] = SECOND.rows(ext, C, l)
+        return 0
+
+    sweep(REACH - 4, LEVELS + 8, 4, keep)
     tiles = lambda l: SECOND.rows(ext, C, l)
     w = lambda l: SECOND.rows(ext, W, l)
 
@@ -562,18 +576,10 @@
                 landed[moment, target] = total
 
 
-def last_section(place_ref, dt_ref, ext, flat, start_far, tracer, out, rate, fast, start, sem):
+def last_section(place_ref, dt_ref, rate, warm, start, tracer, out, fast):
     place, last = place_ref[0], place_ref[1]
     step = dt_ref[0] / NS
-    copy = pltpu.make_async_copy(start_far, start, sem)
-    copy.start()
-
-    def write(n, l, value):
-        rate[l] = value
-
-    rates(SECOND, ext, (PR,), write, 3, 3, flat)
     out[C] = tracer[...]
-    copy.wait()
     names = (PR, U, V, W)
     for repeat in range(NS):
         reads = [
@@ -585,7 +591,7 @@
         ]
         acoustic(
             *zip(reads, writes),
-            lambda l: SECOND.rows(ext, C, l),
+            access(warm)[0],
             access(rate)[0],
             step,
             REACH - 3 + repeat,
@@ -593,6 +599,12 @@
             place,
             last,
         )
+
+
+def land(place_ref, landed, arrived, out):
+    keep = jnp.where(place_ref[0] < place_ref[1], 1.0, 0.0).astype(F32)
+    out[:, 0 : LEVELS - FMAX] = landed[:, 0 : LEVELS - FMAX]
+    out[:, LEVELS - FMAX :] = landed[:, LEVELS - FMAX :] + keep * arrived[...]
 
 
 def deposit(radius, weight, column, counts, fall_depth, out):
@@ -714,7 +726,7 @@
         pack_levels(plan), "pack_levels", vmem(5), [held(tiles, ROWS, COLS)] * 2
     )(own, above, below, from_right, from_left)
     from_up, from_down = both_ways(to_down, "gz", to_up)
-    return above, below, from_right, from_left, from_up, from_down
+    return above, below, from_right, from_left, from_up, from_down, to_down
 
 
 def prepare(place_ref, fields, own, speed):
@@ -729,10 +741,12 @@
     speed[...] = jnp.broadcast_to(jnp.max(most), speed.shape)
 
 
-def droplets(radius, weight, column, counts, fall_depth, chunk):
+def droplets(radius, weight, column, counts, fall_depth, chunk, numbers, after=None):
     slots = radius.shape[0]
+    if after is not None:
+        counts, _ = lax.optimization_barrier((counts, after))
     made = []
-    for n in range(LEVELS // chunk):
+    for n in numbers:
         whole = pl.BlockSpec((slots, chunk, ROWS, COLS), lambda i, n=n: (0, n, 0, 0))
         made.append(
             pl.pallas_call(
@@ -763,7 +777,9 @@
     place = lax.axis_index("gz")
     last = lax.axis_size("gz") - 1
     where = jnp.stack([place, jnp.int32(last)]).astype(jnp.int32)
-    by_depth = droplets(radius, weight, column, counts, fall_depth, 2)
+    def drops(numbers, after=None):
+        return droplets(radius, weight, column, counts, fall_depth, 2, numbers, after)
+
     devices = lax.axis_size(GRID_AXES)
     own, speed = pl.pallas_call(
         prepare,
@@ -773,7 +789,10 @@
         out_shape=(held(5, LEVELS, ROWS, COLS), shaped(devices, 1, COLS)),
         compiler_params=pltpu.CompilerParams(vmem_limit_bytes=4 << 20),
     )(where, fields)
-    *near, from_up, from_down = exchange(FIRST, own, fields, fields, by_depth[:EARLY])
+    early = drops(range(0, 2), speed)
+    speed = lax.all_to_all(speed, GRID_AXES, 0, 0)
+    *near, from_up, from_down, sent = exchange(FIRST, own, fields, fields, [speed, *early])
+    by_depth = drops(range(2, 3), sent)
     ext = held(len(FIRST.tiles), DEPTH, ROWS, WIDE)
     start, flat = call(
         first_own,
@@ -781,15 +800,13 @@
         smem(1) + vmem(5),
         [ext, held(2, LEVELS, 2 * ROWS, WIDE)],
     )(where, own, *near)
-    speed, flat = lax.optimization_barrier((speed, flat))
-    speed = lax.all_to_all(speed, GRID_AXES, 0, 0)
     start, rate0 = call(
         first_rates,
         "first_rates",
-        smem(1) + vmem(4) + anywhere(1),
+        smem(1) + vmem(4) + anywhere(len(by_depth)),
         [ext, held(2, DEPTH, 2 * ROWS, WIDE)],
         alias={1: 0},
-    )(where, start, flat, from_up, from_down, speed)
+    )(where, start, flat, from_up, from_down, *by_depth)
     s2, down, up, dt = call(
         two_sections,
         "two_sections",
@@ -803,7 +820,9 @@
         out_specs=vmem(3) + smem(1),
         grant=10,
     )(where, speed, start, rate0)
-    *near, from_up, from_down = exchange(SECOND, s2, down, up, by_depth[EARLY:LATE])
+    middle = drops(range(3, 7), s2)
+    *near, from_up, from_down, sent = exchange(SECOND, s2, down, up, middle)
+    by_depth = early + by_depth + middle + drops(range(7, 8), sent)
     ext = held(len(SECOND.tiles), DEPTH, ROWS, WIDE)
     around_s2, flat, flat_tracer = call(
         second_own,
@@ -812,15 +831,18 @@
         [ext, held(1, LEVELS, 2 * ROWS, WIDE), held(LEVELS, ROWS, COLS)],
         flops=1_000_000_000,
     )(s2, *near)
-    around_s2, tracer, landed, fallen = call(
+    rows = held(DEPTH, 2 * ROWS, WIDE)
+    _, tracer, landed, fallen, rate, warm = call(
         last_tracer,
         "last_tracer",
-        smem(2) + vmem(5) + anywhere(len(by_depth)),
+        smem(2) + vmem(6) + anywhere(len(by_depth)),
         [
             ext,
             held(LEVELS, ROWS, COLS),
             held(3, LEVELS, ROWS, COLS),
             held(3, FMAX, ROWS, COLS),
+            rows,
+            rows,
         ],
         scratch=[
             pltpu.VMEM((2, LEVELS, ROWS, COLS), F32),
@@ -828,25 +850,20 @@
             pltpu.SemaphoreType.DMA((len(by_depth),)),
         ],
         alias={2: 0},
-    )(where, dt, around_s2, flat_tracer, from_up, from_down, own, *by_depth)
+    )(where, dt, around_s2, flat, flat_tracer, from_up, from_down, own, *by_depth)
     count = lax.axis_size("gz")
     arrived = lax.ppermute(fallen, "gz", [((i + 1) % count, i) for i in range(count)])
     (new_fields,) = call(
         last_section,
         "last_section",
-        smem(2) + vmem(2) + anywhere(1) + vmem(1),
+        smem(2) + vmem(4),
         [shaped(5, LEVELS, ROWS, COLS)],
-        scratch=[
-            pltpu.VMEM((DEPTH, 2 * ROWS, WIDE), F32),
-            pltpu.VMEM((4, DEPTH, 2 * ROWS, WIDE), F32),
-            pltpu.VMEM((len(FIRST.tiles), DEPTH, ROWS, WIDE), F32),
-            pltpu.SemaphoreType.DMA,
-        ],
+        scratch=[pltpu.VMEM((4, DEPTH, 2 * ROWS, WIDE), F32)],
         flops=1_000_000_000,
-        grant=12,
-    )(where, dt, around_s2, flat, start, tracer)
-    arrived = jnp.where(place == last, 0.0, arrived)
-    moments = landed.at[:, LEVELS - FMAX :].add(arrived)
+    )(where, dt, rate, warm, start, tracer)
+    (moments,) = call(
+        land, "land", smem(1) + vmem(2), [shaped(3, LEVELS, ROWS, COLS)]
+    )(where, landed, arrived)
     return (new_fields, moments)
 
 

time: 111 us -> 99.1 us (0.89); the launches traced: 111 us -> 97.1 us
  blocking collectives: 26.3 us -> 0 us
  starting transfers between devices: 16 us -> 34.8 us
  local copies, waits for them, and re-layouts: 11.1 us -> 7.79 us
  waiting for transfers between devices: 11.7 us -> 9.11 us
    all_to_all x1 -> x0, blocking collectives: 26.3 us -> none  [per_device(): speed = lax.all_to_all(speed, GRID_AXES, 0, 0)]
    all_to_all x0 -> x1, starting transfers between devices: none -> 15.2 us  [per_device(): speed = lax.all_to_all(speed, GRID_AXES, 0, 0)]
    ppermute x6, waiting for transfers between devices: 7.42 us -> 2.85 us  [both_ways(): lax.ppermute(up, axis, [(i, (i + 1) % count) for i in range(count)])]
    ppermute x6, starting transfers between devices: 9.53 us -> 13.6 us  [both_ways(): lax.ppermute(down, axis, [((i + 1) % count, i) for i in range(count)])]
    unnamed x36 -> x25, local copies, waits for them, and re-layouts: 11.1 us -> 7.79 us
    ppermute x6, starting transfers between devices: 5.49 us -> 3.87 us  [both_ways(): lax.ppermute(up, axis, [(i, (i + 1) % count) for i in range(count)])]
    all_to_all x0 -> x1, waiting for transfers between devices: none -> 1.57 us  [per_device(): speed = lax.all_to_all(speed, GRID_AXES, 0, 0)]
    pallas_call x10 -> x11, Pallas kernels: 27.3 us -> 27.6 us  [run(): made(*(pltpu.with_memory_space_constraint(value, pltpu.VMEM) if spec.memo...]
  transfers between devices with their start and end apart: 13 -> 14, of which waited for: 7 -> 6; matrix products, arithmetic and copies ran while one was open for 1% -> 1% of each run, Pallas kernels for 26% -> 29%
where the time goes in v4:
time: 99.1 us; the launch traced here: 97.1 us
  Pallas kernels  44.4 us (45%)
  starting transfers between devices  34.8 us (35%)
  waiting for transfers between devices  9.11 us (9%)
  local copies, waits for them, and re-layouts  7.79 us (8%)
    pallas_call x11, Pallas kernels, run(): made(*(pltpu.with_memory_space_constraint(value, pltpu.VMEM) if spec.memo...  27.6 us
    pallas_call x8, Pallas kernels, droplets(): pl.pallas_call(deposit, name='deposit', grid=(1,), in_specs=[whole, whole...  15.3 us
    all_to_all x1, starting transfers between devices, per_device(): speed = lax.all_to_all(speed, GRID_AXES, 0, 0)  15.2 us
    ppermute x6, starting transfers between devices, both_ways(): lax.ppermute(down, axis, [((i + 1) % count, i) for i in range(count)])  13.6 us
    unnamed x25, local copies, waits for them, and re-layouts  7.79 us
    ppermute x6, waiting for transfers between devices, both_ways(): lax.ppermute(down, axis, [((i + 1) % count, i) for i in range(count)])  4.68 us
    ppermute x6, starting transfers between devices, both_ways(): lax.ppermute(up, axis, [(i, (i + 1) % count) for i in range(count)])  3.87 us
    ppermute x6, waiting for transfers between devices, both_ways(): lax.ppermute(up, axis, [(i, (i + 1) % count) for i in range(count)])  2.85 us
  transfers between devices with their start and end apart: 14, of which 6 were waited for; matrix products, arithmetic and copies ran while one was open for 1% of the time, Pallas kernels for 29%

profile of v4, /device:TPU:4, one launch (start us, length us, event | category | flops | bytes accessed | tf_op | source)
XLA Modules:
  0.0 97.1 jit_solution(15592421071201614968)
XLA Ops:
  0.6 1.9 %collective-permute-start.1 = (f32[5,16,8,128]{3,2,1,0:T(8,128)}, f32[5,16,8,128]{3,2,1,0:T(8,128)S(1)}, u32[]{:S(2)}, u32[]{:S(2)}) collective-permute-start(f32[5,16,8,128]{3,2,1,0:T(8,128)} %fields.1), channel_id=1, source_target_pairs={{0,4},{4,8},{8,12},{12,16},{16,20},{20,24},{24,28},{28,32},{32,36}... | collective-permute-start | bytes 983048 | tf_op jit(solution)/shard_map/ppermute | solution.py:711
  2.6 1.7 %collective-permute-start = (f32[5,16,8,128]{3,2,1,0:T(8,128)}, f32[5,16,8,128]{3,2,1,0:T(8,128)S(1)}, u32[]{:S(2)}, u32[]{:S(2)}) collective-permute-start(f32[5,16,8,128]{3,2,1,0:T(8,128)} %fields.1), channel_id=1, source_target_pairs={{4,0},{8,4},{12,8},{16,12},{20,16},{24,20},{28,24},{32,28},{36,32}... | collective-permute-start | bytes 983048 | tf_op jit(solution)/shard_map/ppermute | solution.py:710
  6.7 15.2 %all-to-all-start = ((f32[256,1,128]{2,1,0:T(1,128)}), f32[256,1,128]{2,1,0:T(1,128)S(1)}, u32[]{:S(2)}, u32[]{:S(2)}) async-start(f32[256,1,128]{2,1,0:T(1,128)} %get-tuple-element.32), calls=%async_computation | async-start | bytes 262144 | tf_op jit(solution)/shard_map/all_to_all | solution.py:793
  27.1 1.9 %deposit.9.rest_2_.rest_1_ = f32[2,9,3,8,128]{4,3,2,1,0:T(8,128)S(1)} custom-call(f32[8,16,8,128]{3,2,1,0:T(8,128)S(1)} %copy-done, f32[8,16,8,128]{3,2,1,0:T(8,128)S(1)} %copy-done.2, s32[8,16,8,128]{3,2,1,0:T(8,128)S(1)} %copy-done.4, s32[16,8,128]{2,1,0:T(8,128)S(1)} %copy-done.6, s32[8,16,8,1]{3,2,1,0:T(8,128)S(1)} %copy.10.fall_depth), custom_call_target="tpu_custom_call" | custom-call | flops 200000000 | tf_op jit(solution)/shard_map/deposit/pallas_call | solution.py:752
  29.1 1.9 %deposit.8.rest_1_.rest_0_ = f32[2,9,3,8,128]{4,3,2,1,0:T(8,128)S(1)} custom-call(f32[8,16,8,128]{3,2,1,0:T(8,128)S(1)} %copy-done, f32[8,16,8,128]{3,2,1,0:T(8,128)S(1)} %copy-done.2, s32[8,16,8,128]{3,2,1,0:T(8,128)S(1)} %copy-done.4, s32[16,8,128]{2,1,0:T(8,128)S(1)} %copy-done.6, s32[8,16,8,1]{3,2,1,0:T(8,128)S(1)} %copy.10.fall_depth), custom_call_target="tpu_custom_call" | custom-call | flops 200000000 | tf_op jit(solution)/shard_map/deposit/pallas_call | solution.py:752
  36.0 2.3 %collective-permute-done.2.from_right = f32[16,8,128]{2,1,0:T(8,128)S(1)} collective-permute-done((f32[16,8,128]{2,1,0:T(8,128)S(1)}, f32[16,8,128]{2,1,0:T(8,128)S(1)}, u32[]{:S(2)}, u32[]{:S(2)}) %collective-permute-start.2) | collective-permute-done | bytes 65568 | tf_op jit(solution)/shard_map/ppermute | solution.py:710
  40.4 2.7 %collective-permute-start.4 = (f32[64,8,128]{2,1,0:T(8,128)S(1)}, f32[64,8,128]{2,1,0:T(8,128)S(1)}, u32[]{:S(2)}, u32[]{:S(2)}) collective-permute-start(f32[64,8,128]{2,1,0:T(8,128)S(1)} %get-tuple-element.39), channel_id=1, source_target_pairs={{1,0},{2,1},{3,2},{0,3},{5,4},{6,5},{7,6},{4,7},{9,8},{10,9},{11,1... | collective-permute-start | bytes 786440 | tf_op jit(solution)/shard_map/ppermute | solution.py:710
  43.0 3.3 %first_own.1 = (f32[13,30,8,256]{3,2,1,0:T(8,128)S(1)}, f32[2,16,16,256]{3,2,1,0:T(8,128)S(1)}) custom-call(s32[2]{0:T(128)S(1)} %pad_add_fusion.place_ref, f32[5,16,8,128]{3,2,1,0:T(8,128)S(1)} %get-tuple-element.33.own.initial, f32[5,16,8,128]{3,2,1,0:T(8,128)S(1)} %collective-permute-done.above, f32[5,16,8,128]{3,2,1,0:T(8,128)S(1)} %collective-permute-done.1.below, ...), custom_call_target="tpu_custom_call" | custom-call | tf_op jit(solution)/shard_map/first_own/pallas_call | solution.py:695
  46.4 1.9 %deposit.10.rest_0_.rest_2_ = f32[2,9,3,8,128]{4,3,2,1,0:T(8,128)S(1)} custom-call(f32[8,16,8,128]{3,2,1,0:T(8,128)S(1)} %copy-done.1, f32[8,16,8,128]{3,2,1,0:T(8,128)S(1)} %copy-done.3, s32[8,16,8,128]{3,2,1,0:T(8,128)S(1)} %copy-done.5, s32[16,8,128]{2,1,0:T(8,128)S(1)} %copy-done.7, s32[8,16,8,1]{3,2,1,0:T(8,128)S(1)} %copy.10.fall_depth), custom_call_target="tpu_custom_call" | custom-call | flops 200000000 | tf_op jit(solution)/shard_map/deposit/pallas_call | solution.py:752
  48.4 2.5 %first_rates.1 = (f32[13,30,8,256]{3,2,1,0:T(8,128)S(1)}, f32[2,30,16,256]{3,2,1,0:T(8,128)S(1)}) custom-call(s32[2]{0:T(128)S(1)} %pad_add_fusion.place_ref, f32[13,30,8,256]{3,2,1,0:T(8,128)S(1)} %get-tuple-element.37.ext_in, f32[2,16,16,256]{3,2,1,0:T(8,128)S(1)} %get-tuple-element.38.flat, ...), custom_call_target="tpu_custom_call", output_to_operand_aliasing={{0}: (1, {})} | custom-call | tf_op jit(solution)/shard_map/first_rates/pallas_call | solution.py:695
  50.9 5.5 %two_sections.1 = (f32[5,16,8,128]{3,2,1,0:T(8,128)S(1)}, f32[3,16,8,128]{3,2,1,0:T(8,128)S(1)}, f32[3,16,8,128]{3,2,1,0:T(8,128)S(1)}, f32[1]{0:T(128)}) custom-call(s32[2]{0:T(128)S(1)} %pad_add_fusion.place_ref, f32[256,1,128]{2,1,0:T(1,128)S(1)} %all-to-all-done.rest_0_.speed, f32[13,30,8,256]{3,2,1,0:T(8,128)S(1)} %get-tuple-element.42.start, ...), custom_call_target="tpu_custom_call" | custom-call | tf_op jit(solution)/shard_map/two_sections/pallas_call | solution.py:695
  56.3 3.3 %collective-permute-start.6 = (f32[3,16,8,128]{3,2,1,0:T(8,128)S(1)}, f32[3,16,8,128]{3,2,1,0:T(8,128)S(1)}, u32[]{:S(2)}, u32[]{:S(2)}) collective-permute-start(f32[3,16,8,128]{3,2,1,0:T(8,128)S(1)} %get-tuple-element.46), channel_id=1, source_target_pairs={{4,0},{8,4},{12,8},{16,12},{20,16},{24,20},{28,24},{32,28},{36,32}... | collective-permute-start | bytes 589832 | tf_op jit(solution)/shard_map/ppermute | solution.py:710
  60.8 1.9 %deposit.14.rest_3_.rest_6_ = f32[2,9,3,8,128]{4,3,2,1,0:T(8,128)S(1)} custom-call(f32[8,16,8,128]{3,2,1,0:T(8,128)S(1)} %copy-done.1, f32[8,16,8,128]{3,2,1,0:T(8,128)S(1)} %copy-done.3, s32[8,16,8,128]{3,2,1,0:T(8,128)S(1)} %copy-done.5, s32[16,8,128]{2,1,0:T(8,128)S(1)} %copy-done.7, s32[8,16,8,1]{3,2,1,0:T(8,128)S(1)} %copy.10.fall_depth), custom_call_target="tpu_custom_call" | custom-call | flops 200000000 | tf_op jit(solution)/shard_map/deposit/pallas_call | solution.py:752
  62.8 1.9 %deposit.13.rest_2_.rest_5_ = f32[2,9,3,8,128]{4,3,2,1,0:T(8,128)S(1)} custom-call(f32[8,16,8,128]{3,2,1,0:T(8,128)S(1)} %copy-done.1, f32[8,16,8,128]{3,2,1,0:T(8,128)S(1)} %copy-done.3, s32[8,16,8,128]{3,2,1,0:T(8,128)S(1)} %copy-done.5, s32[16,8,128]{2,1,0:T(8,128)S(1)} %copy-done.7, s32[8,16,8,1]{3,2,1,0:T(8,128)S(1)} %copy.10.fall_depth), custom_call_target="tpu_custom_call" | custom-call | flops 200000000 | tf_op jit(solution)/shard_map/deposit/pallas_call | solution.py:752
  64.7 1.9 %deposit.12.rest_1_.rest_4_ = f32[2,9,3,8,128]{4,3,2,1,0:T(8,128)S(1)} custom-call(f32[8,16,8,128]{3,2,1,0:T(8,128)S(1)} %copy-done.1, f32[8,16,8,128]{3,2,1,0:T(8,128)S(1)} %copy-done.3, s32[8,16,8,128]{3,2,1,0:T(8,128)S(1)} %copy-done.5, s32[16,8,128]{2,1,0:T(8,128)S(1)} %copy-done.7, s32[8,16,8,1]{3,2,1,0:T(8,128)S(1)} %copy.10.fall_depth), custom_call_target="tpu_custom_call" | custom-call | flops 200000000 | tf_op jit(solution)/shard_map/deposit/pallas_call | solution.py:752
  66.6 1.9 %deposit.11.rest_0_.rest_3_ = f32[2,9,3,8,128]{4,3,2,1,0:T(8,128)S(1)} custom-call(f32[8,16,8,128]{3,2,1,0:T(8,128)S(1)} %copy-done.1, f32[8,16,8,128]{3,2,1,0:T(8,128)S(1)} %copy-done.3, s32[8,16,8,128]{3,2,1,0:T(8,128)S(1)} %copy-done.5, s32[16,8,128]{2,1,0:T(8,128)S(1)} %copy-done.7, s32[8,16,8,1]{3,2,1,0:T(8,128)S(1)} %copy.10.fall_depth), custom_call_target="tpu_custom_call" | custom-call | flops 200000000 | tf_op jit(solution)/shard_map/deposit/pallas_call | solution.py:752
  69.6 2.0 %collective-permute-start.8 = (f32[16,8,128]{2,1,0:T(8,128)S(1)}, f32[16,8,128]{2,1,0:T(8,128)S(1)}, u32[]{:S(2)}, u32[]{:S(2)}) collective-permute-start(f32[16,8,128]{2,1,0:T(8,128)S(1)} %get-tuple-element.49), channel_id=1, source_target_pairs={{64,0},{128,64},{192,128},{0,192},{65,1},{129,65},{193,129},{1,193... | collective-permute-start | bytes 196616 | tf_op jit(solution)/shard_map/ppermute | solution.py:710
  71.6 2.4 %collective-permute-done.8.from_right = f32[16,8,128]{2,1,0:T(8,128)S(1)} collective-permute-done((f32[16,8,128]{2,1,0:T(8,128)S(1)}, f32[16,8,128]{2,1,0:T(8,128)S(1)}, u32[]{:S(2)}, u32[]{:S(2)}) %collective-permute-start.8) | collective-permute-done | bytes 65568 | tf_op jit(solution)/shard_map/ppermute | solution.py:710
  75.4 3.2 %collective-permute-start.10 = (f32[48,8,128]{2,1,0:T(8,128)S(1)}, f32[48,8,128]{2,1,0:T(8,128)S(1)}, u32[]{:S(2)}, u32[]{:S(2)}) collective-permute-start(f32[48,8,128]{2,1,0:T(8,128)S(1)} %get-tuple-element.54), channel_id=1, source_target_pairs={{1,0},{2,1},{3,2},{0,3},{5,4},{6,5},{7,6},{4,7},{9,8},{10,9},{11,1... | collective-permute-start | bytes 589832 | tf_op jit(solution)/shard_map/ppermute | solution.py:710
  78.6 1.9 %deposit.15.rest_7_ = f32[2,9,3,8,128]{4,3,2,1,0:T(8,128)S(1)} custom-call(f32[8,16,8,128]{3,2,1,0:T(8,128)S(1)} %copy-done.1, f32[8,16,8,128]{3,2,1,0:T(8,128)S(1)} %copy-done.3, s32[8,16,8,128]{3,2,1,0:T(8,128)S(1)} %copy-done.5, s32[16,8,128]{2,1,0:T(8,128)S(1)} %copy-done.7, s32[8,16,8,1]{3,2,1,0:T(8,128)S(1)} %copy.10.fall_depth), custom_call_target="tpu_custom_call" | custom-call | flops 200000000 | tf_op jit(solution)/shard_map/deposit/pallas_call | solution.py:752
  80.6 2.9 %second_own.1 = (f32[11,30,8,256]{3,2,1,0:T(8,128)S(1)}, f32[1,16,16,256]{3,2,1,0:T(8,128)S(1)}, f32[16,8,128]{2,1,0:T(8,128)S(1)}) custom-call(f32[5,16,8,128]{3,2,1,0:T(8,128)S(1)} %get-tuple-element.45.own, f32[3,16,8,128]{3,2,1,0:T(8,128)S(1)} %collective-permute-done.6.above, f32[3,16,8,128]{3,2,1,0:T(8,128)S(1)} %collective-permute-done.7.below, ...), custom_call_target="tpu_custom_call" | custom-call | flops 1000000000 | tf_op jit(solution)/shard_map/second_own/pallas_call | solution.py:695
  83.5 4.7 %last_tracer.1 = (f32[11,30,8,256]{3,2,1,0:T(8,128)S(1)}, f32[16,8,128]{2,1,0:T(8,128)S(1)}, f32[3,16,8,128]{3,2,1,0:T(8,128)S(1)}, f32[3,8,8,128]{3,2,1,0:T(8,1...) custom-call(s32[2]{0:T(128)S(1)} %pad_add_fusion.place_ref, ...), custom_call_target="tpu_custom_call", output_to_operand_aliasing={{0}: (2, {})} | custom-call | tf_op jit(solution)/shard_map/last_tracer/pallas_call | solution.py:695
  88.2 2.1 %collective-permute-start.12 = (f32[3,8,8,128]{3,2,1,0:T(8,128)S(1)}, f32[3,8,8,128]{3,2,1,0:T(8,128)S(1)}, u32[]{:S(2)}, u32[]{:S(2)}) collective-permute-start(f32[3,8,8,128]{3,2,1,0:T(8,128)S(1)} %get-tuple-element.61), channel_id=1, source_target_pairs={{1,0},{2,1},{3,2},{0,3},{5,4},{6,5},{7,6},{4,7},{9,8},{10,9},{11,1... | collective-permute-start | bytes 294920 | tf_op jit(solution)/shard_map/ppermute | solution.py:855
  90.3 5.6 %last_section.1 = f32[5,16,8,128]{3,2,1,0:T(8,128)} custom-call(s32[2]{0:T(128)S(1)} %pad_add_fusion.place_ref, f32[1]{0:T(128)} %get-tuple-element.44.dt_ref, f32[30,16,256]{2,1,0:T(8,128)S(1)} %get-tuple-element.57.rate, f32[30,16,256]{2,1,0:T(8,128)S(1)} %get-tuple-element.58.warm, f32[13,30,8,256]{3,2,1,0:T(8,128)S(1)} %get-tuple-element.42.start, ...), custom_call_target="tpu_custom_call" | custom-call | flops 1000000000 | tf_op jit(solution)/shard_map/last_section/pallas_call | solution.py:695
  (50 shorter events, 19.6 us)
Async XLA Ops:
  0.6 32.7 %collective-permute-start.1 = (f32[5,16,8,128]{3,2,1,0:T(8,128)}, f32[5,16,8,128]{3,2,1,0:T(8,128)S(1)}, u32[]{:S(2)}, u32[]{:S(2)}) collective-permute-start(f32[5,16,8,128]{3,2,1,0:T(8,128)} %fields.1), channel_id=1, source_target_pairs={{0,4},{4,8},{8,12},{12,16},{16,20},{20,24},{24,28},{28,32},{32,36}... | collective-permute-start | bytes 983048 | tf_op jit(solution)/shard_map/ppermute | solution.py:711
  2.6 30.7 %collective-permute-start = (f32[5,16,8,128]{3,2,1,0:T(8,128)}, f32[5,16,8,128]{3,2,1,0:T(8,128)S(1)}, u32[]{:S(2)}, u32[]{:S(2)}) collective-permute-start(f32[5,16,8,128]{3,2,1,0:T(8,128)} %fields.1), channel_id=1, source_target_pairs={{4,0},{8,4},{12,8},{16,12},{20,16},{24,20},{28,24},{32,28},{36,32}... | collective-permute-start | bytes 983048 | tf_op jit(solution)/shard_map/ppermute | solution.py:710
  4.3 1.0 %copy-start.11 = (f32[5,16,8,128]{3,2,1,0:T(8,128)S(1)}, f32[5,16,8,128]{3,2,1,0:T(8,128)}, u32[]{:S(2)}) copy-start(f32[5,16,8,128]{3,2,1,0:T(8,128)} %fields.1) | copy-start | bytes 983044
  6.7 26.6 %all-to-all-start = ((f32[256,1,128]{2,1,0:T(1,128)}), f32[256,1,128]{2,1,0:T(1,128)S(1)}, u32[]{:S(2)}, u32[]{:S(2)}) async-start(f32[256,1,128]{2,1,0:T(1,128)} %get-tuple-element.32), calls=%async_computation | async-start | bytes 262144 | tf_op jit(solution)/shard_map/all_to_all | solution.py:793
  23.2 1.0 %copy-start = (f32[8,16,8,128]{3,2,1,0:T(8,128)S(1)}, f32[8,16,8,128]{3,2,1,0:T(8,128)}, u32[]{:S(2)}) copy-start(f32[8,16,8,128]{3,2,1,0:T(8,128)} %radius.15) | copy-start | bytes 1572868
  24.2 1.0 %copy-start.2 = (f32[8,16,8,128]{3,2,1,0:T(8,128)S(1)}, f32[8,16,8,128]{3,2,1,0:T(8,128)}, u32[]{:S(2)}) copy-start(f32[8,16,8,128]{3,2,1,0:T(8,128)} %weight.15) | copy-start | bytes 1572868
  25.2 1.0 %copy-start.4 = (s32[8,16,8,128]{3,2,1,0:T(8,128)S(1)}, s32[8,16,8,128]{3,2,1,0:T(8,128)}, u32[]{:S(2)}) copy-start(s32[8,16,8,128]{3,2,1,0:T(8,128)} %column.15) | copy-start | bytes 1572868
  29.0 17.3 %copy-start.1 = (f32[8,16,8,128]{3,2,1,0:T(8,128)S(1)}, f32[8,16,8,128]{3,2,1,0:T(8,128)}, u32[]{:S(2)}) copy-start(f32[8,16,8,128]{3,2,1,0:T(8,128)} %radius.15) | copy-start | bytes 1572868
  29.1 17.3 %copy-start.3 = (f32[8,16,8,128]{3,2,1,0:T(8,128)S(1)}, f32[8,16,8,128]{3,2,1,0:T(8,128)}, u32[]{:S(2)}) copy-start(f32[8,16,8,128]{3,2,1,0:T(8,128)} %weight.15) | copy-start | bytes 1572868
  29.1 17.3 %copy-start.5 = (s32[8,16,8,128]{3,2,1,0:T(8,128)S(1)}, s32[8,16,8,128]{3,2,1,0:T(8,128)}, u32[]{:S(2)}) copy-start(s32[8,16,8,128]{3,2,1,0:T(8,128)} %column.15) | copy-start | bytes 1572868
  29.1 17.3 %copy-start.7 = (s32[16,8,128]{2,1,0:T(8,128)S(1)}, s32[16,8,128]{2,1,0:T(8,128)}, u32[]{:S(2)}) copy-start(s32[16,8,128]{2,1,0:T(8,128)} %counts.7) | copy-start | bytes 196612
  33.3 0.9 copy-start.9
  35.2 3.1 %collective-permute-start.2 = (f32[16,8,128]{2,1,0:T(8,128)S(1)}, f32[16,8,128]{2,1,0:T(8,128)S(1)}, u32[]{:S(2)}, u32[]{:S(2)}) collective-permute-start(f32[16,8,128]{2,1,0:T(8,128)S(1)} %get-tuple-element.35), channel_id=1, source_target_pairs={{64,0},{128,64},{192,128},{0,192},{65,1},{129,65},{193,129},{1,193... | collective-permute-start | bytes 196616 | tf_op jit(solution)/shard_map/ppermute | solution.py:710
  36.0 3.7 %collective-permute-start.3 = (f32[16,8,128]{2,1,0:T(8,128)S(1)}, f32[16,8,128]{2,1,0:T(8,128)S(1)}, u32[]{:S(2)}, u32[]{:S(2)}) collective-permute-start(f32[16,8,128]{2,1,0:T(8,128)S(1)} %get-tuple-element.36), channel_id=1, source_target_pairs={{0,64},{64,128},{128,192},{192,0},{1,65},{65,129},{129,193},{193,1... | collective-permute-start | bytes 196616 | tf_op jit(solution)/shard_map/ppermute | solution.py:711
  39.7 8.6 %collective-permute-start.5 = (f32[64,8,128]{2,1,0:T(8,128)S(1)}, f32[64,8,128]{2,1,0:T(8,128)S(1)}, u32[]{:S(2)}, u32[]{:S(2)}) collective-permute-start(f32[64,8,128]{2,1,0:T(8,128)S(1)} %get-tuple-element.40), channel_id=1, source_target_pairs={{0,1},{1,2},{2,3},{3,0},{4,5},{5,6},{6,7},{7,4},{8,9},{9,10},{10,1... | collective-permute-start | bytes 786440 | tf_op jit(solution)/shard_map/ppermute | solution.py:711
  40.4 8.0 %collective-permute-start.4 = (f32[64,8,128]{2,1,0:T(8,128)S(1)}, f32[64,8,128]{2,1,0:T(8,128)S(1)}, u32[]{:S(2)}, u32[]{:S(2)}) collective-permute-start(f32[64,8,128]{2,1,0:T(8,128)S(1)} %get-tuple-element.39), channel_id=1, source_target_pairs={{1,0},{2,1},{3,2},{0,3},{5,4},{6,5},{7,6},{4,7},{9,8},{10,9},{11,1... | collective-permute-start | bytes 786440 | tf_op jit(solution)/shard_map/ppermute | solution.py:710
  56.3 12.2 %collective-permute-start.6 = (f32[3,16,8,128]{3,2,1,0:T(8,128)S(1)}, f32[3,16,8,128]{3,2,1,0:T(8,128)S(1)}, u32[]{:S(2)}, u32[]{:S(2)}) collective-permute-start(f32[3,16,8,128]{3,2,1,0:T(8,128)S(1)} %get-tuple-element.46), channel_id=1, source_target_pairs={{4,0},{8,4},{12,8},{16,12},{20,16},{24,20},{28,24},{32,28},{36,32}... | collective-permute-start | bytes 589832 | tf_op jit(solution)/shard_map/ppermute | solution.py:710
  59.6 9.1 %collective-permute-start.7 = (f32[3,16,8,128]{3,2,1,0:T(8,128)S(1)}, f32[3,16,8,128]{3,2,1,0:T(8,128)S(1)}, u32[]{:S(2)}, u32[]{:S(2)}) collective-permute-start(f32[3,16,8,128]{3,2,1,0:T(8,128)S(1)} %get-tuple-element.47), channel_id=1, source_target_pairs={{0,4},{4,8},{8,12},{12,16},{16,20},{20,24},{24,28},{28,32},{32,36}... | collective-permute-start | bytes 589832 | tf_op jit(solution)/shard_map/ppermute | solution.py:711
  69.6 4.4 %collective-permute-start.8 = (f32[16,8,128]{2,1,0:T(8,128)S(1)}, f32[16,8,128]{2,1,0:T(8,128)S(1)}, u32[]{:S(2)}, u32[]{:S(2)}) collective-permute-start(f32[16,8,128]{2,1,0:T(8,128)S(1)} %get-tuple-element.49), channel_id=1, source_target_pairs={{64,0},{128,64},{192,128},{0,192},{65,1},{129,65},{193,129},{1,193... | collective-permute-start | bytes 196616 | tf_op jit(solution)/shard_map/ppermute | solution.py:710
  71.6 3.7 %collective-permute-start.9 = (f32[16,8,128]{2,1,0:T(8,128)S(1)}, f32[16,8,128]{2,1,0:T(8,128)S(1)}, u32[]{:S(2)}, u32[]{:S(2)}) collective-permute-start(f32[16,8,128]{2,1,0:T(8,128)S(1)} %get-tuple-element.50), channel_id=1, source_target_pairs={{0,64},{64,128},{128,192},{192,0},{1,65},{65,129},{129,193},{193,1... | collective-permute-start | bytes 196616 | tf_op jit(solution)/shard_map/ppermute | solution.py:711
  75.3 8.2 %copy-start.10 = (f32[2,9,3,8,128]{4,3,2,1,0:T(8,128)S(1)}, f32[2,9,3,8,128]{4,3,2,1,0:T(8,128)}, u32[]{:S(2)}) copy-start(f32[2,9,3,8,128]{4,3,2,1,0:T(8,128)} %copy-done.8) | copy-start | bytes 663556
  75.3 8.2 %collective-permute-start.11 = (f32[48,8,128]{2,1,0:T(8,128)S(1)}, f32[48,8,128]{2,1,0:T(8,128)S(1)}, u32[]{:S(2)}, u32[]{:S(2)}) collective-permute-start(f32[48,8,128]{2,1,0:T(8,128)S(1)} %get-tuple-element.55), channel_id=1, source_target_pairs={{0,1},{1,2},{2,3},{3,0},{4,5},{5,6},{6,7},{7,4},{8,9},{9,10},{10,1... | collective-permute-start | bytes 589832 | tf_op jit(solution)/shard_map/ppermute | solution.py:711
  75.4 8.1 %collective-permute-start.10 = (f32[48,8,128]{2,1,0:T(8,128)S(1)}, f32[48,8,128]{2,1,0:T(8,128)S(1)}, u32[]{:S(2)}, u32[]{:S(2)}) collective-permute-start(f32[48,8,128]{2,1,0:T(8,128)S(1)} %get-tuple-element.54), channel_id=1, source_target_pairs={{1,0},{2,1},{3,2},{0,3},{5,4},{6,5},{7,6},{4,7},{9,8},{10,9},{11,1... | collective-permute-start | bytes 589832 | tf_op jit(solution)/shard_map/ppermute | solution.py:710
  88.2 7.6 %collective-permute-start.12 = (f32[3,8,8,128]{3,2,1,0:T(8,128)S(1)}, f32[3,8,8,128]{3,2,1,0:T(8,128)S(1)}, u32[]{:S(2)}, u32[]{:S(2)}) collective-permute-start(f32[3,8,8,128]{3,2,1,0:T(8,128)S(1)} %get-tuple-element.61), channel_id=1, source_target_pairs={{1,0},{2,1},{3,2},{0,3},{5,4},{6,5},{7,6},{4,7},{9,8},{10,9},{11,1... | collective-permute-start | bytes 294920 | tf_op jit(solution)/shard_map/ppermute | solution.py:855
  (2 other events, 1.5 us)

commit v5 on v4

--- a/solution.py
+++ b/solution.py
@@ -133,14 +133,20 @@
 TILE_OF = {FIRST: raw_tile, SECOND: shared_tile}
 
 
-def pack_columns(plan):
+SPARE = 104
+
+
+def pack_columns(plan, with_speed):
     def kernel(own, above, below, *rest):
         to_left, to_right = rest[-2:]
         lane = lanes((ROWS, COLS))
+        filler = jnp.zeros((ROWS, COLS), F32)
+        if with_speed:
+            filler = filler + jnp.max(rest[0][...])
 
         def one(k, _):
-            left = jnp.zeros((ROWS, COLS), F32)
-            right = jnp.zeros((ROWS, COLS), F32)
+            left = filler
+            right = filler
             for n, (field, part) in enumerate(plan.tiles):
                 start = n * EDGE
                 here = (lane >= start) & (lane < start + EDGE)
@@ -169,8 +175,16 @@
     return jnp.where(lanes((ROWS, COLS)) < COLS // 2, right, left)
 
 
-def pack_levels(plan):
-    def kernel(own, above, below, from_right, from_left, to_down, to_up):
+def pack_levels(plan, with_speed):
+    def kernel(own, above, below, from_right, from_left, *rest):
+        if with_speed:
+            speed, to_down, to_up, speeds = rest
+            near = jnp.maximum(from_right[0], from_left[0])
+            near = jnp.where(lanes((ROWS, COLS)) < SPARE, 0.0, near)
+            top = jnp.maximum(jnp.max(near), jnp.max(speed[...]))
+            speeds[...] = jnp.broadcast_to(top, speeds.shape)
+        else:
+            to_down, to_up = rest
         for index, (a, tile, side) in enumerate(plan.carried):
             for out, k in ((to_down, a), (to_up, LEVELS - 1 - a)):
                 if tile:
@@ -308,7 +322,8 @@
     sweep(REACH + LEVELS, around_own, most, some, lows)
 
 
-def first_own(place_ref, own, above, below, from_right, from_left, ext, flat):
+def first_own(place_ref, own, above, below, from_right, from_left, *rest):
+    ext, flat = rest[-2:]
     place_own(FIRST, (own, above, below, from_right, from_left), ext)
 
     @pl.when(place_ref[0] == place_ref[1])
@@ -319,8 +334,7 @@
     flat_own(FIRST, ext, (C, PR), flat)
 
 
-def first_rates(place_ref, ext_in, flat, from_up, from_down, *rest):
-    ext, rate = rest[-2:]
+def first_rates(place_ref, ext_in, flat, from_up, from_down, ext, rate):
     place_halo(FIRST, from_up, from_down, ext, place_ref[0], place_ref[1])
 
     def write(n, l, value):
@@ -712,21 +726,25 @@
     )
 
 
-def exchange(plan, own, down, up, tokens=()):
+def exchange(plan, own, down, up, tokens=(), speed=None):
     above, below = both_ways(down, "gy", up)
+    extra = [] if speed is None else [speed]
     to_left, to_right = call(
-        pack_columns(plan),
+        pack_columns(plan, bool(extra)),
         "pack_columns",
-        vmem(3) + anywhere(len(tokens)),
+        vmem(3 + len(extra)) + anywhere(len(tokens)),
         [held(LEVELS, ROWS, COLS)] * 2,
-    )(own, above, below, *tokens)
+    )(own, above, below, *extra, *tokens)
     from_right, from_left = both_ways(to_left, "gx", to_right)
     tiles = len(plan.carried)
-    to_down, to_up = call(
-        pack_levels(plan), "pack_levels", vmem(5), [held(tiles, ROWS, COLS)] * 2
-    )(own, above, below, from_right, from_left)
+    to_down, to_up, *speeds = call(
+        pack_levels(plan, bool(extra)),
+        "pack_levels",
+        vmem(5 + len(extra)),
+        [held(tiles, ROWS, COLS)] * 2 + [shaped(lax.axis_size("gy"), 1, COLS)] * len(extra),
+    )(own, above, below, from_right, from_left, *extra)
     from_up, from_down = both_ways(to_down, "gz", to_up)
-    return above, below, from_right, from_left, from_up, from_down, to_down
+    return above, below, from_right, from_left, from_up, from_down, to_down, *speeds
 
 
 def prepare(place_ref, fields, own, speed):
@@ -780,33 +798,35 @@
     def drops(numbers, after=None):
         return droplets(radius, weight, column, counts, fall_depth, 2, numbers, after)
 
-    devices = lax.axis_size(GRID_AXES)
     own, speed = pl.pallas_call(
         prepare,
         name="prepare",
         in_specs=smem(1) + vmem(1),
         out_specs=tuple(vmem(2)),
-        out_shape=(held(5, LEVELS, ROWS, COLS), shaped(devices, 1, COLS)),
+        out_shape=(held(5, LEVELS, ROWS, COLS), shaped(ROWS, COLS)),
         compiler_params=pltpu.CompilerParams(vmem_limit_bytes=4 << 20),
     )(where, fields)
-    early = drops(range(0, 2), speed)
-    speed = lax.all_to_all(speed, GRID_AXES, 0, 0)
-    *near, from_up, from_down, sent = exchange(FIRST, own, fields, fields, [speed, *early])
-    by_depth = drops(range(2, 3), sent)
+    pair = [(i, i ^ 1) for i in range(lax.axis_size("gx"))]
+    speed = jnp.maximum(speed, lax.ppermute(speed, "gx", pair))
+    speed = jnp.broadcast_to(speed[0:1], (lax.axis_size("gz"), 1, COLS))
+    speed = jnp.max(lax.all_to_all(speed, "gz", 0, 0), axis=0)
+    *near, from_up, from_down, sent, speed = exchange(FIRST, own, fields, fields, (), speed)
+    early = drops(range(0, 2), sent)
+    speed = lax.all_to_all(speed, "gy", 0, 0)
     ext = held(len(FIRST.tiles), DEPTH, ROWS, WIDE)
     start, flat = call(
         first_own,
         "first_own",
-        smem(1) + vmem(5),
+        smem(1) + vmem(5) + anywhere(1 + len(early)),
         [ext, held(2, LEVELS, 2 * ROWS, WIDE)],
-    )(where, own, *near)
+    )(where, own, *near, speed, *early)
     start, rate0 = call(
         first_rates,
         "first_rates",
-        smem(1) + vmem(4) + anywhere(len(by_depth)),
+        smem(1) + vmem(4),
         [ext, held(2, DEPTH, 2 * ROWS, WIDE)],
         alias={1: 0},
-    )(where, start, flat, from_up, from_down, *by_depth)
+    )(where, start, flat, from_up, from_down)
     s2, down, up, dt = call(
         two_sections,
         "two_sections",
@@ -820,9 +840,9 @@
         out_specs=vmem(3) + smem(1),
         grant=10,
     )(where, speed, start, rate0)
-    middle = drops(range(3, 7), s2)
+    middle = drops(range(2, 6), s2)
     *near, from_up, from_down, sent = exchange(SECOND, s2, down, up, middle)
-    by_depth = early + by_depth + middle + drops(range(7, 8), sent)
+    by_depth = early + middle + drops(range(6, 8), sent)
     ext = held(len(SECOND.tiles), DEPTH, ROWS, WIDE)
     around_s2, flat, flat_tracer = call(
         second_own,

time: 99.1 us -> 103 us (1.039); the launches traced: 97.1 us -> 102 us
  blocking collectives: 0 us -> 9.54 us
  starting transfers between devices: 34.8 us -> 28.6 us
  waiting for transfers between devices: 9.11 us -> 13.3 us
  local copies, waits for them, and re-layouts: 7.79 us -> 4.73 us
    all_to_all x0 -> x1, blocking collectives: none -> 9.54 us  [per_device(): speed = jnp.max(lax.all_to_all(speed, 'gz', 0, 0), axis=0)]
    ppermute x6, starting transfers between devices: 13.6 us -> 9.39 us  [both_ways(): lax.ppermute(down, axis, [((i + 1) % count, i) for i in range(count)])]
    ppermute x6, waiting for transfers between devices: 2.85 us -> 6.85 us  [both_ways(): lax.ppermute(up, axis, [(i, (i + 1) % count) for i in range(count)])]
    all_to_all x1, starting transfers between devices: 15.2 us -> 11.5 us  [per_device(): speed = lax.all_to_all(speed, 'gy', 0, 0)]
    unnamed x25 -> x21, local copies, waits for them, and re-layouts: 7.79 us -> 4.72 us
    ppermute x6, starting transfers between devices: 3.87 us -> 6.43 us  [both_ways(): lax.ppermute(up, axis, [(i, (i + 1) % count) for i in range(count)])]
    ppermute x6, waiting for transfers between devices: 4.68 us -> 2.81 us  [both_ways(): lax.ppermute(down, axis, [((i + 1) % count, i) for i in range(count)])]
    pallas_call x11, Pallas kernels: 27.6 us -> 28.9 us  [run(): made(*(pltpu.with_memory_space_constraint(value, pltpu.VMEM) if spec.memo...]
  transfers between devices with their start and end apart: 14 -> 15, of which waited for: 6 -> 7; matrix products, arithmetic and copies ran while one was open for 1% -> 1% of each run, Pallas kernels for 29% -> 27%
where the time goes in v5:
time: 103 us; the launch traced here: 102 us
  Pallas kernels  45 us (44%)
  starting transfers between devices  28.6 us (28%)
  waiting for transfers between devices  13.3 us (13%)
  blocking collectives  9.54 us (9%)
  local copies, waits for them, and re-layouts  4.73 us (5%)
    pallas_call x11, Pallas kernels, run(): made(*(pltpu.with_memory_space_constraint(value, pltpu.VMEM) if spec.memo...  28.9 us
    pallas_call x8, Pallas kernels, droplets(): pl.pallas_call(deposit, name='deposit', grid=(1,), in_specs=[whole, whole...  15.3 us
    all_to_all x1, starting transfers between devices, per_device(): speed = lax.all_to_all(speed, 'gy', 0, 0)  11.5 us
    all_to_all x1, blocking collectives, per_device(): speed = jnp.max(lax.all_to_all(speed, 'gz', 0, 0), axis=0)  9.54 us
    ppermute x6, starting transfers between devices, both_ways(): lax.ppermute(down, axis, [((i + 1) % count, i) for i in range(count)])  9.39 us
    ppermute x6, waiting for transfers between devices, both_ways(): lax.ppermute(up, axis, [(i, (i + 1) % count) for i in range(count)])  6.85 us
    ppermute x6, starting transfers between devices, both_ways(): lax.ppermute(up, axis, [(i, (i + 1) % count) for i in range(count)])  6.43 us
    unnamed x21, local copies, waits for them, and re-layouts  4.72 us
  transfers between devices with their start and end apart: 15, of which 7 were waited for; matrix products, arithmetic and copies ran while one was open for 1% of the time, Pallas kernels for 27%

profile of v5, /device:TPU:4, one launch (start us, length us, event | category | flops | bytes accessed | tf_op | source)
XLA Modules:
  0.0 102.1 jit_solution(16513784388259541917)
XLA Ops:
  0.7 1.9 %collective-permute-start.1 = (f32[5,16,8,128]{3,2,1,0:T(8,128)}, f32[5,16,8,128]{3,2,1,0:T(8,128)S(1)}, u32[]{:S(2)}, u32[]{:S(2)}) collective-permute-start(f32[5,16,8,128]{3,2,1,0:T(8,128)} %fields.1), channel_id=1, source_target_pairs={{0,4},{4,8},{8,12},{12,16},{16,20},{20,24},{24,28},{28,32},{32,36}... | collective-permute-start | bytes 983048 | tf_op jit(solution)/shard_map/ppermute | solution.py:725
  2.6 1.7 %collective-permute-start = (f32[5,16,8,128]{3,2,1,0:T(8,128)}, f32[5,16,8,128]{3,2,1,0:T(8,128)S(1)}, u32[]{:S(2)}, u32[]{:S(2)}) collective-permute-start(f32[5,16,8,128]{3,2,1,0:T(8,128)} %fields.1), channel_id=1, source_target_pairs={{4,0},{8,4},{12,8},{16,12},{20,16},{24,20},{28,24},{32,28},{36,32}... | collective-permute-start | bytes 983048 | tf_op jit(solution)/shard_map/ppermute | solution.py:724
  7.3 9.5 %all_to_all.10 = f32[4,1,128]{2,1,0:T(1,128)S(1)} all-to-all(f32[4,1,128]{2,1,0:T(1,128)S(1)} %broadcast_in_dim.3), channel_id=1, replica_groups=mesh['gx'=4,'gy'=16,'gz'=4] {'gz'}, dimensions={0} | all-to-all | bytes 4096 | tf_op jit(solution)/shard_map/all_to_all | solution.py:812
  16.8 2.1 %collective-permute-done.1.below = f32[5,16,8,128]{3,2,1,0:T(8,128)S(1)} collective-permute-done((f32[5,16,8,128]{3,2,1,0:T(8,128)}, f32[5,16,8,128]{3,2,1,0:T(8,128)S(1)}, u32[]{:S(2)}, u32[]{:S(2)}) %collective-permute-start.1) | collective-permute-done | bytes 327712 | tf_op jit(solution)/shard_map/ppermute | solution.py:725
  22.0 2.2 %collective-permute-done.4.from_left = f32[16,8,128]{2,1,0:T(8,128)S(1)} collective-permute-done((f32[16,8,128]{2,1,0:T(8,128)S(1)}, f32[16,8,128]{2,1,0:T(8,128)S(1)}, u32[]{:S(2)}, u32[]{:S(2)}) %collective-permute-start.4) | collective-permute-done | bytes 65568 | tf_op jit(solution)/shard_map/ppermute | solution.py:725
  29.5 11.5 %all-to-all-start.1 = ((f32[16,1,128]{2,1,0:T(1,128)}), f32[16,1,128]{2,1,0:T(1,128)S(1)}, u32[]{:S(2)}, u32[]{:S(2)}) async-start(f32[16,1,128]{2,1,0:T(1,128)} %get-tuple-element.36), calls=%async_computation.1 | async-start | bytes 16384 | tf_op jit(solution)/shard_map/all_to_all | solution.py:815
  41.9 1.9 %deposit.9.rest_2_.rest_1_ = f32[2,9,3,8,128]{4,3,2,1,0:T(8,128)S(1)} custom-call(f32[8,16,8,128]{3,2,1,0:T(8,128)S(1)} %copy-done, f32[8,16,8,128]{3,2,1,0:T(8,128)S(1)} %copy-done.1, s32[8,16,8,128]{3,2,1,0:T(8,128)S(1)} %copy-done.2, s32[16,8,128]{2,1,0:T(8,128)S(1)} %copy-done.3, s32[8,16,8,1]{3,2,1,0:T(8,128)S(1)} %copy.27.fall_depth), custom_call_target="tpu_custom_call" | custom-call | flops 200000000 | tf_op jit(solution)/shard_map/deposit/pallas_call | solution.py:770
  43.8 1.9 %deposit.8.rest_1_.rest_0_ = f32[2,9,3,8,128]{4,3,2,1,0:T(8,128)S(1)} custom-call(f32[8,16,8,128]{3,2,1,0:T(8,128)S(1)} %copy-done, f32[8,16,8,128]{3,2,1,0:T(8,128)S(1)} %copy-done.1, s32[8,16,8,128]{3,2,1,0:T(8,128)S(1)} %copy-done.2, s32[16,8,128]{2,1,0:T(8,128)S(1)} %copy-done.3, s32[8,16,8,1]{3,2,1,0:T(8,128)S(1)} %copy.27.fall_depth), custom_call_target="tpu_custom_call" | custom-call | flops 200000000 | tf_op jit(solution)/shard_map/deposit/pallas_call | solution.py:770
  45.8 2.5 %all-to-all-done.1.rest_0_.speed = f32[16,1,128]{2,1,0:T(1,128)S(1)} async-done(((f32[16,1,128]{2,1,0:T(1,128)}), f32[16,1,128]{2,1,0:T(1,128)S(1)}, u32[]{:S(2)}, u32[]{:S(2)}) %all-to-all-start.1) | async-done | bytes 8224 | tf_op jit(solution)/shard_map/all_to_all | solution.py:815
  49.9 3.3 %first_own.1 = (f32[13,30,8,256]{3,2,1,0:T(8,128)S(1)}, f32[2,16,16,256]{3,2,1,0:T(8,128)S(1)}) custom-call(s32[2]{0:T(128)S(1)} %pad_add_fusion.place_ref, f32[5,16,8,128]{3,2,1,0:T(8,128)S(1)} %get-tuple-element.32.own.initial, f32[5,16,8,128]{3,2,1,0:T(8,128)S(1)} %collective-permute-done.above, f32[5,16,8,128]{3,2,1,0:T(8,128)S(1)} %collective-permute-done.1.below, ...), custom_call_target="tpu_custom_call" | custom-call | tf_op jit(solution)/shard_map/first_own/pallas_call | solution.py:709
  53.3 3.0 %first_rates.1 = (f32[13,30,8,256]{3,2,1,0:T(8,128)S(1)}, f32[2,30,16,256]{3,2,1,0:T(8,128)S(1)}) custom-call(s32[2]{0:T(128)S(1)} %pad_add_fusion.place_ref, f32[13,30,8,256]{3,2,1,0:T(8,128)S(1)} %get-tuple-element.39.ext_in, f32[2,16,16,256]{3,2,1,0:T(8,128)S(1)} %get-tuple-element.40.flat, ...), custom_call_target="tpu_custom_call", output_to_operand_aliasing={{0}: (1, {})} | custom-call | tf_op jit(solution)/shard_map/first_rates/pallas_call | solution.py:709
  56.3 5.4 %two_sections.1 = (f32[5,16,8,128]{3,2,1,0:T(8,128)S(1)}, f32[3,16,8,128]{3,2,1,0:T(8,128)S(1)}, f32[3,16,8,128]{3,2,1,0:T(8,128)S(1)}, f32[1]{0:T(128)}) custom-call(s32[2]{0:T(128)S(1)} %pad_add_fusion.place_ref, f32[16,1,128]{2,1,0:T(1,128)S(1)} %all-to-all-done.1.rest_0_.speed, f32[13,30,8,256]{3,2,1,0:T(8,128)S(1)} %get-tuple-element.42.start, ...), custom_call_target="tpu_custom_call" | custom-call | tf_op jit(solution)/shard_map/two_sections/pallas_call | solution.py:709
  61.6 3.0 %collective-permute-start.7 = (f32[3,16,8,128]{3,2,1,0:T(8,128)S(1)}, f32[3,16,8,128]{3,2,1,0:T(8,128)S(1)}, u32[]{:S(2)}, u32[]{:S(2)}) collective-permute-start(f32[3,16,8,128]{3,2,1,0:T(8,128)S(1)} %get-tuple-element.46), channel_id=1, source_target_pairs={{4,0},{8,4},{12,8},{16,12},{20,16},{24,20},{28,24},{32,28},{36,32}... | collective-permute-start | bytes 589832 | tf_op jit(solution)/shard_map/ppermute | solution.py:724
  66.1 1.9 %deposit.13.rest_3_.rest_5_ = f32[2,9,3,8,128]{4,3,2,1,0:T(8,128)S(1)} custom-call(f32[8,16,8,128]{3,2,1,0:T(8,128)S(1)} %copy-done, f32[8,16,8,128]{3,2,1,0:T(8,128)S(1)} %copy-done.1, s32[8,16,8,128]{3,2,1,0:T(8,128)S(1)} %copy-done.2, s32[16,8,128]{2,1,0:T(8,128)S(1)} %copy-done.4, s32[8,16,8,1]{3,2,1,0:T(8,128)S(1)} %copy.27.fall_depth), custom_call_target="tpu_custom_call" | custom-call | flops 200000000 | tf_op jit(solution)/shard_map/deposit/pallas_call | solution.py:770
  68.1 1.9 %deposit.12.rest_2_.rest_4_ = f32[2,9,3,8,128]{4,3,2,1,0:T(8,128)S(1)} custom-call(f32[8,16,8,128]{3,2,1,0:T(8,128)S(1)} %copy-done, f32[8,16,8,128]{3,2,1,0:T(8,128)S(1)} %copy-done.1, s32[8,16,8,128]{3,2,1,0:T(8,128)S(1)} %copy-done.2, s32[16,8,128]{2,1,0:T(8,128)S(1)} %copy-done.4, s32[8,16,8,1]{3,2,1,0:T(8,128)S(1)} %copy.27.fall_depth), custom_call_target="tpu_custom_call" | custom-call | flops 200000000 | tf_op jit(solution)/shard_map/deposit/pallas_call | solution.py:770
  70.0 1.9 %deposit.11.rest_1_.rest_3_ = f32[2,9,3,8,128]{4,3,2,1,0:T(8,128)S(1)} custom-call(f32[8,16,8,128]{3,2,1,0:T(8,128)S(1)} %copy-done, f32[8,16,8,128]{3,2,1,0:T(8,128)S(1)} %copy-done.1, s32[8,16,8,128]{3,2,1,0:T(8,128)S(1)} %copy-done.2, s32[16,8,128]{2,1,0:T(8,128)S(1)} %copy-done.4, s32[8,16,8,1]{3,2,1,0:T(8,128)S(1)} %copy.27.fall_depth), custom_call_target="tpu_custom_call" | custom-call | flops 200000000 | tf_op jit(solution)/shard_map/deposit/pallas_call | solution.py:770
  71.9 1.9 %deposit.10.rest_0_.rest_2_ = f32[2,9,3,8,128]{4,3,2,1,0:T(8,128)S(1)} custom-call(f32[8,16,8,128]{3,2,1,0:T(8,128)S(1)} %copy-done, f32[8,16,8,128]{3,2,1,0:T(8,128)S(1)} %copy-done.1, s32[8,16,8,128]{3,2,1,0:T(8,128)S(1)} %copy-done.2, s32[16,8,128]{2,1,0:T(8,128)S(1)} %copy-done.4, s32[8,16,8,1]{3,2,1,0:T(8,128)S(1)} %copy.27.fall_depth), custom_call_target="tpu_custom_call" | custom-call | flops 200000000 | tf_op jit(solution)/shard_map/deposit/pallas_call | solution.py:770
  76.8 2.5 %collective-permute-done.10.from_left = f32[16,8,128]{2,1,0:T(8,128)S(1)} collective-permute-done((f32[16,8,128]{2,1,0:T(8,128)S(1)}, f32[16,8,128]{2,1,0:T(8,128)S(1)}, u32[]{:S(2)}, u32[]{:S(2)}) %collective-permute-start.10) | collective-permute-done | bytes 65568 | tf_op jit(solution)/shard_map/ppermute | solution.py:725
  79.8 2.9 %collective-permute-start.11 = (f32[48,8,128]{2,1,0:T(8,128)S(1)}, f32[48,8,128]{2,1,0:T(8,128)S(1)}, u32[]{:S(2)}, u32[]{:S(2)}) collective-permute-start(f32[48,8,128]{2,1,0:T(8,128)S(1)} %get-tuple-element.54), channel_id=1, source_target_pairs={{1,0},{2,1},{3,2},{0,3},{5,4},{6,5},{7,6},{4,7},{9,8},{10,9},{11,1... | collective-permute-start | bytes 589832 | tf_op jit(solution)/shard_map/ppermute | solution.py:724
  82.7 1.9 %deposit.15.rest_7_ = f32[2,9,3,8,128]{4,3,2,1,0:T(8,128)S(1)} custom-call(f32[8,16,8,128]{3,2,1,0:T(8,128)S(1)} %copy-done, f32[8,16,8,128]{3,2,1,0:T(8,128)S(1)} %copy-done.1, s32[8,16,8,128]{3,2,1,0:T(8,128)S(1)} %copy-done.2, s32[16,8,128]{2,1,0:T(8,128)S(1)} %copy-done.4, s32[8,16,8,1]{3,2,1,0:T(8,128)S(1)} %copy.27.fall_depth), custom_call_target="tpu_custom_call" | custom-call | flops 200000000 | tf_op jit(solution)/shard_map/deposit/pallas_call | solution.py:770
  84.6 1.9 %deposit.14.rest_6_ = f32[2,9,3,8,128]{4,3,2,1,0:T(8,128)S(1)} custom-call(f32[8,16,8,128]{3,2,1,0:T(8,128)S(1)} %copy-done, f32[8,16,8,128]{3,2,1,0:T(8,128)S(1)} %copy-done.1, s32[8,16,8,128]{3,2,1,0:T(8,128)S(1)} %copy-done.2, s32[16,8,128]{2,1,0:T(8,128)S(1)} %copy-done.4, s32[8,16,8,1]{3,2,1,0:T(8,128)S(1)} %copy.27.fall_depth), custom_call_target="tpu_custom_call" | custom-call | flops 200000000 | tf_op jit(solution)/shard_map/deposit/pallas_call | solution.py:770
  86.5 2.9 %second_own.1 = (f32[11,30,8,256]{3,2,1,0:T(8,128)S(1)}, f32[1,16,16,256]{3,2,1,0:T(8,128)S(1)}, f32[16,8,128]{2,1,0:T(8,128)S(1)}) custom-call(f32[5,16,8,128]{3,2,1,0:T(8,128)S(1)} %get-tuple-element.45.own, f32[3,16,8,128]{3,2,1,0:T(8,128)S(1)} %collective-permute-done.7.above, f32[3,16,8,128]{3,2,1,0:T(8,128)S(1)} %collective-permute-done.8.below, ...), custom_call_target="tpu_custom_call" | custom-call | flops 1000000000 | tf_op jit(solution)/shard_map/second_own/pallas_call | solution.py:709
  89.5 4.7 %last_tracer.1 = (f32[11,30,8,256]{3,2,1,0:T(8,128)S(1)}, f32[16,8,128]{2,1,0:T(8,128)S(1)}, f32[3,16,8,128]{3,2,1,0:T(8,128)S(1)}, f32[3,8,8,128]{3,2,1,0:T(8,1...) custom-call(s32[2]{0:T(128)S(1)} %pad_add_fusion.place_ref, ...), custom_call_target="tpu_custom_call", output_to_operand_aliasing={{0}: (2, {})} | custom-call | tf_op jit(solution)/shard_map/last_tracer/pallas_call | solution.py:709
  95.3 5.6 %last_section.1 = f32[5,16,8,128]{3,2,1,0:T(8,128)} custom-call(s32[2]{0:T(128)S(1)} %pad_add_fusion.place_ref, f32[1]{0:T(128)} %get-tuple-element.44.dt_ref, f32[30,16,256]{2,1,0:T(8,128)S(1)} %get-tuple-element.57.rate, f32[30,16,256]{2,1,0:T(8,128)S(1)} %get-tuple-element.58.warm, f32[13,30,8,256]{3,2,1,0:T(8,128)S(1)} %get-tuple-element.42.start, ...), custom_call_target="tpu_custom_call" | custom-call | flops 1000000000 | tf_op jit(solution)/shard_map/last_section/pallas_call | solution.py:709
  (53 shorter events, 21.1 us)
Async XLA Ops:
  0.6 40.4 %copy-start.2 = (s32[8,16,8,128]{3,2,1,0:T(8,128)S(1)}, s32[8,16,8,128]{3,2,1,0:T(8,128)}, u32[]{:S(2)}) copy-start(s32[8,16,8,128]{3,2,1,0:T(8,128)} %column.15) | copy-start | bytes 1572868
  0.6 40.4 %copy-start.1 = (f32[8,16,8,128]{3,2,1,0:T(8,128)S(1)}, f32[8,16,8,128]{3,2,1,0:T(8,128)}, u32[]{:S(2)}) copy-start(f32[8,16,8,128]{3,2,1,0:T(8,128)} %weight.15) | copy-start | bytes 1572868
  0.7 40.4 %copy-start = (f32[8,16,8,128]{3,2,1,0:T(8,128)S(1)}, f32[8,16,8,128]{3,2,1,0:T(8,128)}, u32[]{:S(2)}) copy-start(f32[8,16,8,128]{3,2,1,0:T(8,128)} %radius.15) | copy-start | bytes 1572868
  0.7 18.3 %collective-permute-start.1 = (f32[5,16,8,128]{3,2,1,0:T(8,128)}, f32[5,16,8,128]{3,2,1,0:T(8,128)S(1)}, u32[]{:S(2)}, u32[]{:S(2)}) collective-permute-start(f32[5,16,8,128]{3,2,1,0:T(8,128)} %fields.1), channel_id=1, source_target_pairs={{0,4},{4,8},{8,12},{12,16},{16,20},{20,24},{24,28},{28,32},{32,36}... | collective-permute-start | bytes 983048 | tf_op jit(solution)/shard_map/ppermute | solution.py:725
  2.6 16.3 %collective-permute-start = (f32[5,16,8,128]{3,2,1,0:T(8,128)}, f32[5,16,8,128]{3,2,1,0:T(8,128)S(1)}, u32[]{:S(2)}, u32[]{:S(2)}) collective-permute-start(f32[5,16,8,128]{3,2,1,0:T(8,128)} %fields.1), channel_id=1, source_target_pairs={{4,0},{8,4},{12,8},{16,12},{20,16},{24,20},{28,24},{32,28},{36,32}... | collective-permute-start | bytes 983048 | tf_op jit(solution)/shard_map/ppermute | solution.py:724
  4.3 1.0 copy-start.5
  6.0 1.3 %collective-permute-start.2 = (f32[8,128]{1,0:T(8,128)S(1)}, f32[8,128]{1,0:T(8,128)S(1)}, u32[]{:S(2)}, u32[]{:S(2)}) collective-permute-start(f32[8,128]{1,0:T(8,128)S(1)} %get-tuple-element.33), channel_id=1, source_target_pairs={{0,64},{64,0},{128,192},{192,128},{1,65},{65,1},{129,193},{193,129... | collective-permute-start | bytes 12296 | tf_op jit(solution)/shard_map/ppermute | solution.py:810
  20.0 2.0 %collective-permute-start.3 = (f32[16,8,128]{2,1,0:T(8,128)S(1)}, f32[16,8,128]{2,1,0:T(8,128)S(1)}, u32[]{:S(2)}, u32[]{:S(2)}) collective-permute-start(f32[16,8,128]{2,1,0:T(8,128)S(1)} %get-tuple-element.34), channel_id=1, source_target_pairs={{64,0},{128,64},{192,128},{0,192},{65,1},{129,65},{193,129},{1,193... | collective-permute-start | bytes 196616 | tf_op jit(solution)/shard_map/ppermute | solution.py:724
  20.1 4.1 %collective-permute-start.4 = (f32[16,8,128]{2,1,0:T(8,128)S(1)}, f32[16,8,128]{2,1,0:T(8,128)S(1)}, u32[]{:S(2)}, u32[]{:S(2)}) collective-permute-start(f32[16,8,128]{2,1,0:T(8,128)S(1)} %get-tuple-element.35), channel_id=1, source_target_pairs={{0,64},{64,128},{128,192},{192,0},{1,65},{65,129},{129,193},{193,1... | collective-permute-start | bytes 196616 | tf_op jit(solution)/shard_map/ppermute | solution.py:725
  22.0 4.6 %copy-start.6 = (f32[16,8,128]{2,1,0:T(8,128)}, f32[16,8,128]{2,1,0:T(8,128)S(1)}, u32[]{:S(2)}) copy-start(f32[16,8,128]{2,1,0:T(8,128)S(1)} %collective-permute-done.3.from_right) | copy-start | bytes 196612
  24.2 2.4 %copy-start.8 = (f32[16,8,128]{2,1,0:T(8,128)}, f32[16,8,128]{2,1,0:T(8,128)S(1)}, u32[]{:S(2)}) copy-start(f32[16,8,128]{2,1,0:T(8,128)S(1)} %collective-permute-done.4.from_left) | copy-start | bytes 196612
  25.1 28.2 %collective-permute-start.6 = (f32[64,8,128]{2,1,0:T(8,128)}, f32[64,8,128]{2,1,0:T(8,128)}, u32[]{:S(2)}, u32[]{:S(2)}) collective-permute-start(f32[64,8,128]{2,1,0:T(8,128)} %get-tuple-element.41), channel_id=1, source_target_pairs={{0,1},{1,2},{2,3},{3,0},{4,5},{5,6},{6,7},{7,4},{8,9},{9,10},{10,1... | collective-permute-start | bytes 786440 | tf_op jit(solution)/shard_map/ppermute | solution.py:725
  26.6 26.6 %collective-permute-start.5 = (f32[64,8,128]{2,1,0:T(8,128)}, f32[64,8,128]{2,1,0:T(8,128)}, u32[]{:S(2)}, u32[]{:S(2)}) collective-permute-start(f32[64,8,128]{2,1,0:T(8,128)} %get-tuple-element.37), channel_id=1, source_target_pairs={{1,0},{2,1},{3,2},{0,3},{5,4},{6,5},{7,6},{4,7},{9,8},{10,9},{11,1... | collective-permute-start | bytes 786440 | tf_op jit(solution)/shard_map/ppermute | solution.py:724
  29.5 18.7 %all-to-all-start.1 = ((f32[16,1,128]{2,1,0:T(1,128)}), f32[16,1,128]{2,1,0:T(1,128)S(1)}, u32[]{:S(2)}, u32[]{:S(2)}) async-start(f32[16,1,128]{2,1,0:T(1,128)} %get-tuple-element.36), calls=%async_computation.1 | async-start | bytes 16384 | tf_op jit(solution)/shard_map/all_to_all | solution.py:815
  41.1 0.8 copy-start.3
  48.2 0.8 copy-start.7
  53.2 12.9 %copy-start.4 = (s32[16,8,128]{2,1,0:T(8,128)S(1)}, s32[16,8,128]{2,1,0:T(8,128)}, u32[]{:S(2)}) copy-start(s32[16,8,128]{2,1,0:T(8,128)} %counts.7) | copy-start | bytes 196612
  61.6 12.2 %collective-permute-start.7 = (f32[3,16,8,128]{3,2,1,0:T(8,128)S(1)}, f32[3,16,8,128]{3,2,1,0:T(8,128)S(1)}, u32[]{:S(2)}, u32[]{:S(2)}) collective-permute-start(f32[3,16,8,128]{3,2,1,0:T(8,128)S(1)} %get-tuple-element.46), channel_id=1, source_target_pairs={{4,0},{8,4},{12,8},{16,12},{20,16},{24,20},{28,24},{32,28},{36,32}... | collective-permute-start | bytes 589832 | tf_op jit(solution)/shard_map/ppermute | solution.py:724
  64.7 9.2 %collective-permute-start.8 = (f32[3,16,8,128]{3,2,1,0:T(8,128)S(1)}, f32[3,16,8,128]{3,2,1,0:T(8,128)S(1)}, u32[]{:S(2)}, u32[]{:S(2)}) collective-permute-start(f32[3,16,8,128]{3,2,1,0:T(8,128)S(1)} %get-tuple-element.47), channel_id=1, source_target_pairs={{0,4},{4,8},{8,12},{12,16},{16,20},{20,24},{24,28},{28,32},{32,36}... | collective-permute-start | bytes 589832 | tf_op jit(solution)/shard_map/ppermute | solution.py:725
  74.8 2.0 %collective-permute-start.9 = (f32[16,8,128]{2,1,0:T(8,128)S(1)}, f32[16,8,128]{2,1,0:T(8,128)S(1)}, u32[]{:S(2)}, u32[]{:S(2)}) collective-permute-start(f32[16,8,128]{2,1,0:T(8,128)S(1)} %get-tuple-element.49), channel_id=1, source_target_pairs={{64,0},{128,64},{192,128},{0,192},{65,1},{129,65},{193,129},{1,193... | collective-permute-start | bytes 196616 | tf_op jit(solution)/shard_map/ppermute | solution.py:724
  74.9 4.4 %collective-permute-start.10 = (f32[16,8,128]{2,1,0:T(8,128)S(1)}, f32[16,8,128]{2,1,0:T(8,128)S(1)}, u32[]{:S(2)}, u32[]{:S(2)}) collective-permute-start(f32[16,8,128]{2,1,0:T(8,128)S(1)} %get-tuple-element.50), channel_id=1, source_target_pairs={{0,64},{64,128},{128,192},{192,0},{1,65},{65,129},{129,193},{193,1... | collective-permute-start | bytes 196616 | tf_op jit(solution)/shard_map/ppermute | solution.py:725
  79.3 10.1 %collective-permute-start.12 = (f32[48,8,128]{2,1,0:T(8,128)S(1)}, f32[48,8,128]{2,1,0:T(8,128)S(1)}, u32[]{:S(2)}, u32[]{:S(2)}) collective-permute-start(f32[48,8,128]{2,1,0:T(8,128)S(1)} %get-tuple-element.55), channel_id=1, source_target_pairs={{0,1},{1,2},{2,3},{3,0},{4,5},{5,6},{6,7},{7,4},{8,9},{9,10},{10,1... | collective-permute-start | bytes 589832 | tf_op jit(solution)/shard_map/ppermute | solution.py:725
  79.8 9.6 %collective-permute-start.11 = (f32[48,8,128]{2,1,0:T(8,128)S(1)}, f32[48,8,128]{2,1,0:T(8,128)S(1)}, u32[]{:S(2)}, u32[]{:S(2)}) collective-permute-start(f32[48,8,128]{2,1,0:T(8,128)S(1)} %get-tuple-element.54), channel_id=1, source_target_pairs={{1,0},{2,1},{3,2},{0,3},{5,4},{6,5},{7,6},{4,7},{9,8},{10,9},{11,1... | collective-permute-start | bytes 589832 | tf_op jit(solution)/shard_map/ppermute | solution.py:724
  94.1 6.7 %collective-permute-start.13 = (f32[3,8,8,128]{3,2,1,0:T(8,128)S(1)}, f32[3,8,8,128]{3,2,1,0:T(8,128)S(1)}, u32[]{:S(2)}, u32[]{:S(2)}) collective-permute-start(f32[3,8,8,128]{3,2,1,0:T(8,128)S(1)} %get-tuple-element.61), channel_id=1, source_target_pairs={{1,0},{2,1},{3,2},{0,3},{5,4},{6,5},{7,6},{4,7},{9,8},{10,9},{11,1... | collective-permute-start | bytes 294920 | tf_op jit(solution)/shard_map/ppermute | solution.py:875
  (1 other events, 0.8 us)

commit v6 on v5

--- a/solution.py
+++ b/solution.py
@@ -3,11 +3,12 @@
 from jax import lax
 from jax.experimental import pallas as pl
 from jax.experimental.pallas import tpu as pltpu
+from jax.sharding import Mesh
 from jax.sharding import PartitionSpec as P
 
 NS = 4
 FMAX = 8
-GRID_AXES = ("gx", "gy", "gz")
+GY = ("gy_hi", "gy_lo")
 
 sound_speed = 10.0
 buoyancy = 0.5
@@ -159,11 +160,12 @@
             to_right[k] = right
             return 0
 
-        def pair(i, _):
-            one(2 * i, 0)
-            return one(2 * i + 1, 0)
-
-        lax.fori_loop(0, LEVELS // 2, pair, 0)
+        def some(levels, _):
+            for k in levels:
+                one(k, 0)
+            return 0
+
+        sweep(0, LEVELS, 8, some)
 
     return kernel
 
@@ -290,7 +292,7 @@
             flat[n, l - REACH] = value
         return 0
 
-    sweep(REACH, LEVELS, 2, some)
+    sweep(REACH, LEVELS, 4, some)
 
 
 def rates(plan, ext, fields, write, around_own, most, flat=None):
@@ -322,8 +324,7 @@
     sweep(REACH + LEVELS, around_own, most, some, lows)
 
 
-def first_own(place_ref, own, above, below, from_right, from_left, *rest):
-    ext, flat = rest[-2:]
+def first_own(place_ref, own, above, below, from_right, from_left, ext, flat):
     place_own(FIRST, (own, above, below, from_right, from_left), ext)
 
     @pl.when(place_ref[0] == place_ref[1])
@@ -334,13 +335,14 @@
     flat_own(FIRST, ext, (C, PR), flat)
 
 
-def first_rates(place_ref, ext_in, flat, from_up, from_down, ext, rate):
+def first_rates(place_ref, ext_in, flat, from_up, from_down, *rest):
+    ext, rate = rest[-2:]
     place_halo(FIRST, from_up, from_down, ext, place_ref[0], place_ref[1])
 
     def write(n, l, value):
         rate[n, l] = value
 
-    rates(FIRST, ext, (C, PR), write, 4, 2, flat)
+    rates(FIRST, ext, (C, PR), write, 4, 4, flat)
 
 
 def acoustic(p, u, v, w, read_c, rate, step, first, count, place, last):
@@ -383,7 +385,7 @@
     low = first - 1
     w_low = wind_w(low, read_c(low), read_c(first), level(p[0](low)), level(p[0](first)))
     w[1](low, w_low)
-    sweep(first, count, 6, some, w_low)
+    sweep(first, count, 12, some, w_low)
 
 
 def access(ref, *lead):
@@ -417,9 +419,9 @@
     return level_flux(lambda m: tiles(m)[0:ROWS, 0:COLS], w(l)[0:ROWS, 0:COLS], l)
 
 
-def two_sections(place_ref, speed, start, rate0, s2, down, up, dt_out, s1, rate1, fast):
+def two_sections(place_ref, speed, other_speed, start, rate0, s2, down, up, dt_out, s1, rate1, fast):
     place, last = place_ref[0], place_ref[1]
-    dt = courant_goal / (1.0 + jnp.max(speed[...]))
+    dt = courant_goal / (1.0 + jnp.max(jnp.maximum(speed[...], other_speed[...])))
     dt_out[0] = dt
     third = dt * (1.0 / 3.0)
 
@@ -459,12 +461,12 @@
             s2[C, l - REACH] = value
         return low
 
-    sweep(REACH, LEVELS, 4, own_tracer, tracer_high(tiles, winds[2], REACH - 1))
+    sweep(REACH, LEVELS, 8, own_tracer, tracer_high(tiles, winds[2], REACH - 1))
 
     def write(n, l, value):
         rate1[l] = value
 
-    rates(SECTION, s1, (PR,), write, 1, 3)
+    rates(SECTION, s1, (PR,), write, 1, 6)
     step = half / (NS // 2)
     acoustic(
         (begin(start, PR), access(fast, 0)[1]),
@@ -678,8 +680,8 @@
     return [pl.BlockSpec(memory_space=pltpu.SMEM)] * n
 
 
-def anywhere(n):
-    return [pl.BlockSpec(memory_space=pl.ANY)] * n
+def far(n):
+    return [pl.BlockSpec(memory_space=pltpu.HBM)] * n
 
 
 def shaped(*dims):
@@ -708,8 +710,8 @@
     def run(*operands):
         return made(
             *(
-                pltpu.with_memory_space_constraint(value, pltpu.VMEM)
-                if spec.memory_space == pltpu.VMEM
+                pltpu.with_memory_space_constraint(value, spec.memory_space)
+                if spec.memory_space != pltpu.SMEM
                 else value
                 for spec, value in zip(ins, operands)
             )
@@ -727,12 +729,12 @@
 
 
 def exchange(plan, own, down, up, tokens=(), speed=None):
-    above, below = both_ways(down, "gy", up)
+    above, below = both_ways(down, GY, up)
     extra = [] if speed is None else [speed]
     to_left, to_right = call(
         pack_columns(plan, bool(extra)),
         "pack_columns",
-        vmem(3 + len(extra)) + anywhere(len(tokens)),
+        vmem(3 + len(extra)) + far(len(tokens)),
         [held(LEVELS, ROWS, COLS)] * 2,
     )(own, above, below, *extra, *tokens)
     from_right, from_left = both_ways(to_left, "gx", to_right)
@@ -741,7 +743,7 @@
         pack_levels(plan, bool(extra)),
         "pack_levels",
         vmem(5 + len(extra)),
-        [held(tiles, ROWS, COLS)] * 2 + [shaped(lax.axis_size("gy"), 1, COLS)] * len(extra),
+        [held(tiles, ROWS, COLS)] * 2 + [shaped(ROWS, COLS)] * len(extra),
     )(own, above, below, from_right, from_left, *extra)
     from_up, from_down = both_ways(to_down, "gz", to_up)
     return above, below, from_right, from_left, from_up, from_down, to_down, *speeds
@@ -781,7 +783,7 @@
                 out_specs=pl.BlockSpec(
                     (chunk, FMAX + 1, 3, ROWS, COLS), lambda i: (0, 0, 0, 0, 0)
                 ),
-                out_shape=shaped(chunk, FMAX + 1, 3, ROWS, COLS),
+                out_shape=pltpu.HBM((chunk, FMAX + 1, 3, ROWS, COLS), F32),
                 compiler_params=pltpu.CompilerParams(vmem_limit_bytes=12 << 20),
                 cost_estimate=pl.CostEstimate(
                     flops=200_000_000, bytes_accessed=0, transcendentals=0
@@ -808,29 +810,30 @@
     )(where, fields)
     pair = [(i, i ^ 1) for i in range(lax.axis_size("gx"))]
     speed = jnp.maximum(speed, lax.ppermute(speed, "gx", pair))
-    speed = jnp.broadcast_to(speed[0:1], (lax.axis_size("gz"), 1, COLS))
-    speed = jnp.max(lax.all_to_all(speed, "gz", 0, 0), axis=0)
+    plane = ("gy_hi", "gz")
+    speed = jnp.broadcast_to(speed[0:1], (lax.axis_size(plane), 1, COLS))
+    speed = jnp.max(lax.all_to_all(speed, plane, 0, 0), axis=0)
     *near, from_up, from_down, sent, speed = exchange(FIRST, own, fields, fields, (), speed)
-    early = drops(range(0, 2), sent)
-    speed = lax.all_to_all(speed, "gy", 0, 0)
+    other_speed = lax.ppermute(speed, "gy_lo", [(0, 1), (1, 0)])
+    by_depth = drops(range(0, 2), sent)
     ext = held(len(FIRST.tiles), DEPTH, ROWS, WIDE)
     start, flat = call(
         first_own,
         "first_own",
-        smem(1) + vmem(5) + anywhere(1 + len(early)),
+        smem(1) + vmem(5),
         [ext, held(2, LEVELS, 2 * ROWS, WIDE)],
-    )(where, own, *near, speed, *early)
+    )(where, own, *near)
     start, rate0 = call(
         first_rates,
         "first_rates",
-        smem(1) + vmem(4),
+        smem(1) + vmem(4) + far(len(by_depth)),
         [ext, held(2, DEPTH, 2 * ROWS, WIDE)],
         alias={1: 0},
-    )(where, start, flat, from_up, from_down)
+    )(where, start, flat, from_up, from_down, *by_depth)
     s2, down, up, dt = call(
         two_sections,
         "two_sections",
-        smem(1) + vmem(3),
+        smem(1) + vmem(4),
         [held(5, LEVELS, ROWS, COLS)] + [held(3, LEVELS, ROWS, COLS)] * 2 + [shaped(1)],
         scratch=[
             pltpu.VMEM((5, DEPTH, 2 * ROWS, WIDE), F32),
@@ -839,10 +842,10 @@
         ],
         out_specs=vmem(3) + smem(1),
         grant=10,
-    )(where, speed, start, rate0)
-    middle = drops(range(2, 6), s2)
+    )(where, speed, other_speed, start, rate0)
+    middle = drops(range(2, 7), s2)
     *near, from_up, from_down, sent = exchange(SECOND, s2, down, up, middle)
-    by_depth = early + middle + drops(range(6, 8), sent)
+    by_depth = by_depth + middle + drops(range(7, 8), sent)
     ext = held(len(SECOND.tiles), DEPTH, ROWS, WIDE)
     around_s2, flat, flat_tracer = call(
         second_own,
@@ -855,7 +858,7 @@
     _, tracer, landed, fallen, rate, warm = call(
         last_tracer,
         "last_tracer",
-        smem(2) + vmem(6) + anywhere(len(by_depth)),
+        smem(2) + vmem(6) + far(len(by_depth)),
         [
             ext,
             held(LEVELS, ROWS, COLS),
@@ -888,11 +891,16 @@
 
 
 def solution(mesh):
-    spread = P(None, "gz", "gy", "gx")
+    count = mesh.shape["gy"]
+    split = Mesh(
+        mesh.devices.reshape(mesh.shape["gx"], count // 2, 2, mesh.shape["gz"]),
+        ("gx", *GY, "gz"),
+    )
+    spread = P(None, "gz", GY, "gx")
     return jax.shard_map(
         per_device,
-        mesh=mesh,
-        in_specs=(spread, spread, spread, spread, P("gz", "gy", "gx"), spread),
+        mesh=split,
+        in_specs=(spread, spread, spread, spread, P("gz", GY, "gx"), spread),
         out_specs=(spread, spread),
         check_vma=False,
     )

time: 103 us -> 100 us (0.971)
  blocking collectives: 9.54 us -> 21 us
  starting transfers between devices: 28.6 us -> 21.7 us
  waiting for transfers between devices: 13.3 us -> 8.69 us
  local copies, waits for them, and re-layouts: 4.73 us -> 3.04 us
    all_to_all x1 -> x0, starting transfers between devices: 11.5 us -> none  [per_device(): speed = lax.all_to_all(speed, 'gy', 0, 0)]
    all_to_all x1, blocking collectives: 9.54 us -> 21 us  [per_device(): speed = jnp.max(lax.all_to_all(speed, plane, 0, 0), axis=0)]
    pallas_call x11, Pallas kernels: 28.9 us -> 22.9 us  [run(): made(*(pltpu.with_memory_space_constraint(value, spec.memory_space) if sp...]
    pallas_call x8, Pallas kernels: 15.3 us -> 20.9 us  [droplets(): pl.pallas_call(deposit, name='deposit', grid=(1,), in_specs=[whole, whole...]
    ppermute x0 -> x1, starting transfers between devices: none -> 2.99 us  [per_device(): other_speed = lax.ppermute(speed, 'gy_lo', [(0, 1), (1, 0)])]
    all_to_all x1 -> x0, waiting for transfers between devices: 2.46 us -> none  [per_device(): speed = lax.all_to_all(speed, 'gy', 0, 0)]
    ppermute x6, waiting for transfers between devices: 6.85 us -> 4.72 us  [both_ways(): lax.ppermute(up, axis, [(i, (i + 1) % count) for i in range(count)])]
    unnamed x21 -> x11, local copies, waits for them, and re-layouts: 4.72 us -> 3.03 us
  transfers between devices with their start and end apart: 15 -> 15, of which waited for: 7 -> 5; matrix products, arithmetic and copies ran while one was open for 1% -> 1% of each run, Pallas kernels for 27% -> 34%
where the time goes in v6:
time: 100 us; the launch traced here: 99.9 us
  Pallas kernels  44.5 us (44%)
  starting transfers between devices  21.7 us (22%)
  blocking collectives  21 us (21%)
  waiting for transfers between devices  8.69 us (9%)
  local copies, waits for them, and re-layouts  3.04 us (3%)
    pallas_call x11, Pallas kernels, run(): made(*(pltpu.with_memory_space_constraint(value, spec.memory_space) if sp...  22.9 us
    all_to_all x1, blocking collectives, per_device(): speed = jnp.max(lax.all_to_all(speed, plane, 0, 0), axis=0)  21 us
    pallas_call x8, Pallas kernels, droplets(): pl.pallas_call(deposit, name='deposit', grid=(1,), in_specs=[whole, whole...  20.9 us
    ppermute x6, starting transfers between devices, both_ways(): lax.ppermute(down, axis, [((i + 1) % count, i) for i in range(count)])  8.41 us
    ppermute x6, starting transfers between devices, both_ways(): lax.ppermute(up, axis, [(i, (i + 1) % count) for i in range(count)])  7.41 us
    ppermute x6, waiting for transfers between devices, both_ways(): lax.ppermute(up, axis, [(i, (i + 1) % count) for i in range(count)])  4.72 us
    unnamed x11, local copies, waits for them, and re-layouts  3.03 us
    ppermute x1, starting transfers between devices, per_device(): other_speed = lax.ppermute(speed, 'gy_lo', [(0, 1), (1, 0)])  2.99 us
  transfers between devices with their start and end apart: 15, of which 5 were waited for; matrix products, arithmetic and copies ran while one was open for 1% of the time, Pallas kernels for 34%

profile of v6, /device:TPU:4, one launch (start us, length us, event | category | flops | bytes accessed | tf_op | source)
XLA Modules:
  0.0 99.9 jit_solution(18440786801193379715)
XLA Ops:
  0.7 1.9 %collective-permute-start.1 = (f32[5,16,8,128]{3,2,1,0:T(8,128)}, f32[5,16,8,128]{3,2,1,0:T(8,128)S(1)}, u32[]{:S(2)}, u32[]{:S(2)}) collective-permute-start(f32[5,16,8,128]{3,2,1,0:T(8,128)} %fields.1), channel_id=1, source_target_pairs={{0,4},{4,8},{8,12},{12,16},{16,20},{20,24},{24,28},{28,32},{32,36}... | collective-permute-start | bytes 983048 | tf_op jit(solution)/shard_map/ppermute | solution.py:727
  2.6 1.7 %collective-permute-start = (f32[5,16,8,128]{3,2,1,0:T(8,128)}, f32[5,16,8,128]{3,2,1,0:T(8,128)S(1)}, u32[]{:S(2)}, u32[]{:S(2)}) collective-permute-start(f32[5,16,8,128]{3,2,1,0:T(8,128)} %fields.1), channel_id=1, source_target_pairs={{4,0},{8,4},{12,8},{16,12},{20,16},{24,20},{28,24},{32,28},{36,32}... | collective-permute-start | bytes 983048 | tf_op jit(solution)/shard_map/ppermute | solution.py:726
  7.3 21.0 %all_to_all.5 = f32[32,1,128]{2,1,0:T(1,128)S(1)} all-to-all(f32[32,1,128]{2,1,0:T(1,128)S(1)} %broadcast_in_dim.3), channel_id=1, replica_groups=mesh['gx'=4,'gy_hi'=8,'gy_lo'=2,'gz'=4] {'gy_hi','gz'}, dimensions={0} | all-to-all | bytes 32768 | tf_op jit(solution)/shard_map/all_to_all | solution.py:815
  31.0 2.2 %collective-permute-done.4.from_left = f32[16,8,128]{2,1,0:T(8,128)S(1)} collective-permute-done((f32[16,8,128]{2,1,0:T(8,128)S(1)}, f32[16,8,128]{2,1,0:T(8,128)S(1)}, u32[]{:S(2)}, u32[]{:S(2)}) %collective-permute-start.4) | collective-permute-done | bytes 65568 | tf_op jit(solution)/shard_map/ppermute | solution.py:727
  34.7 2.7 %collective-permute-start.6 = (f32[64,8,128]{2,1,0:T(8,128)}, f32[64,8,128]{2,1,0:T(8,128)}, u32[]{:S(2)}, u32[]{:S(2)}) collective-permute-start(f32[64,8,128]{2,1,0:T(8,128)} %get-tuple-element.39), channel_id=1, source_target_pairs={{1,0},{2,1},{3,2},{0,3},{5,4},{6,5},{7,6},{4,7},{9,8},{10,9},{11,1... | collective-permute-start | bytes 786440 | tf_op jit(solution)/shard_map/ppermute | solution.py:726
  38.5 3.0 %collective-permute-start.5 = (f32[8,128]{1,0:T(8,128)S(1)}, f32[8,128]{1,0:T(8,128)S(1)}, u32[]{:S(2)}, u32[]{:S(2)}) collective-permute-start(f32[8,128]{1,0:T(8,128)S(1)} %get-tuple-element.36.speed), channel_id=1, source_target_pairs={{0,4},{4,0},{1,5},{5,1},{2,6},{6,2},{3,7},{7,3},{8,12},{12,8},{9,1... | collective-permute-start | bytes 12296 | tf_op jit(solution)/shard_map/ppermute | solution.py:817
  42.4 2.6 %deposit.9.rest_1_ = f32[2,9,3,8,128]{4,3,2,1,0:T(8,128)} custom-call(f32[8,16,8,128]{3,2,1,0:T(8,128)S(1)} %copy-done, f32[8,16,8,128]{3,2,1,0:T(8,128)S(1)} %copy-done.1, s32[8,16,8,128]{3,2,1,0:T(8,128)S(1)} %copy-done.2, s32[16,8,128]{2,1,0:T(8,128)S(1)} %copy-done.3, s32[8,16,8,1]{3,2,1,0:T(8,128)S(1)} %copy.27.fall_depth), custom_call_target="tpu_custom_call" | custom-call | flops 200000000 | tf_op jit(solution)/shard_map/deposit/pallas_call | solution.py:772
  45.0 2.6 %deposit.8.rest_0_ = f32[2,9,3,8,128]{4,3,2,1,0:T(8,128)} custom-call(f32[8,16,8,128]{3,2,1,0:T(8,128)S(1)} %copy-done, f32[8,16,8,128]{3,2,1,0:T(8,128)S(1)} %copy-done.1, s32[8,16,8,128]{3,2,1,0:T(8,128)S(1)} %copy-done.2, s32[16,8,128]{2,1,0:T(8,128)S(1)} %copy-done.3, s32[8,16,8,1]{3,2,1,0:T(8,128)S(1)} %copy.27.fall_depth), custom_call_target="tpu_custom_call" | custom-call | flops 200000000 | tf_op jit(solution)/shard_map/deposit/pallas_call | solution.py:772
  47.6 3.5 %first_own.1 = (f32[13,30,8,256]{3,2,1,0:T(8,128)S(1)}, f32[2,16,16,256]{3,2,1,0:T(8,128)S(1)}) custom-call(s32[2]{0:T(128)S(1)} %pad_add_fusion.place_ref, f32[5,16,8,128]{3,2,1,0:T(8,128)S(1)} %get-tuple-element.32.own.initial, f32[5,16,8,128]{3,2,1,0:T(8,128)S(1)} %collective-permute-done.above, f32[5,16,8,128]{3,2,1,0:T(8,128)S(1)} %collective-permute-done.1.below, ...), custom_call_target="tpu_custom_call" | custom-call | tf_op jit(solution)/shard_map/first_own/pallas_call | solution.py:711
  51.1 2.8 %first_rates.1 = (f32[13,30,8,256]{3,2,1,0:T(8,128)S(1)}, f32[2,30,16,256]{3,2,1,0:T(8,128)S(1)}) custom-call(s32[2]{0:T(128)S(1)} %pad_add_fusion.place_ref, f32[13,30,8,256]{3,2,1,0:T(8,128)S(1)} %get-tuple-element.37.ext_in, f32[2,16,16,256]{3,2,1,0:T(8,128)S(1)} %get-tuple-element.38.flat, ...), custom_call_target="tpu_custom_call", output_to_operand_aliasing={{0}: (1, {})} | custom-call | tf_op jit(solution)/shard_map/first_rates/pallas_call | solution.py:711
  53.9 4.2 %two_sections.1 = (f32[5,16,8,128]{3,2,1,0:T(8,128)S(1)}, f32[3,16,8,128]{3,2,1,0:T(8,128)S(1)}, f32[3,16,8,128]{3,2,1,0:T(8,128)S(1)}, f32[1]{0:T(128)}) custom-call(s32[2]{0:T(128)S(1)} %pad_add_fusion.place_ref, f32[8,128]{1,0:T(8,128)S(1)} %get-tuple-element.36.speed, f32[8,128]{1,0:T(8,128)S(1)} %collective-permute-done.5.other_speed, ...), custom_call_target="tpu_custom_call" | custom-call | tf_op jit(solution)/shard_map/two_sections/pallas_call | solution.py:711
  58.8 3.8 %collective-permute-start.9 = (f32[3,16,8,128]{3,2,1,0:T(8,128)S(1)}, f32[3,16,8,128]{3,2,1,0:T(8,128)S(1)}, u32[]{:S(2)}, u32[]{:S(2)}) collective-permute-start(f32[3,16,8,128]{3,2,1,0:T(8,128)S(1)} %get-tuple-element.47), channel_id=1, source_target_pairs={{0,4},{4,8},{8,12},{12,16},{16,20},{20,24},{24,28},{28,32},{32,36}... | collective-permute-start | bytes 589832 | tf_op jit(solution)/shard_map/ppermute | solution.py:727
  62.6 2.6 %deposit.14.rest_4_.rest_6_ = f32[2,9,3,8,128]{4,3,2,1,0:T(8,128)} custom-call(f32[8,16,8,128]{3,2,1,0:T(8,128)S(1)} %copy-done, f32[8,16,8,128]{3,2,1,0:T(8,128)S(1)} %copy-done.1, s32[8,16,8,128]{3,2,1,0:T(8,128)S(1)} %copy-done.2, s32[16,8,128]{2,1,0:T(8,128)S(1)} %copy-done.3, s32[8,16,8,1]{3,2,1,0:T(8,128)S(1)} %copy.27.fall_depth), custom_call_target="tpu_custom_call" | custom-call | flops 200000000 | tf_op jit(solution)/shard_map/deposit/pallas_call | solution.py:772
  65.2 2.6 %deposit.13.rest_3_.rest_5_ = f32[2,9,3,8,128]{4,3,2,1,0:T(8,128)} custom-call(f32[8,16,8,128]{3,2,1,0:T(8,128)S(1)} %copy-done, f32[8,16,8,128]{3,2,1,0:T(8,128)S(1)} %copy-done.1, s32[8,16,8,128]{3,2,1,0:T(8,128)S(1)} %copy-done.2, s32[16,8,128]{2,1,0:T(8,128)S(1)} %copy-done.3, s32[8,16,8,1]{3,2,1,0:T(8,128)S(1)} %copy.27.fall_depth), custom_call_target="tpu_custom_call" | custom-call | flops 200000000 | tf_op jit(solution)/shard_map/deposit/pallas_call | solution.py:772
  67.8 2.6 %deposit.12.rest_2_.rest_4_ = f32[2,9,3,8,128]{4,3,2,1,0:T(8,128)} custom-call(f32[8,16,8,128]{3,2,1,0:T(8,128)S(1)} %copy-done, f32[8,16,8,128]{3,2,1,0:T(8,128)S(1)} %copy-done.1, s32[8,16,8,128]{3,2,1,0:T(8,128)S(1)} %copy-done.2, s32[16,8,128]{2,1,0:T(8,128)S(1)} %copy-done.3, s32[8,16,8,1]{3,2,1,0:T(8,128)S(1)} %copy.27.fall_depth), custom_call_target="tpu_custom_call" | custom-call | flops 200000000 | tf_op jit(solution)/shard_map/deposit/pallas_call | solution.py:772
  70.4 2.6 %deposit.11.rest_1_.rest_3_ = f32[2,9,3,8,128]{4,3,2,1,0:T(8,128)} custom-call(f32[8,16,8,128]{3,2,1,0:T(8,128)S(1)} %copy-done, f32[8,16,8,128]{3,2,1,0:T(8,128)S(1)} %copy-done.1, s32[8,16,8,128]{3,2,1,0:T(8,128)S(1)} %copy-done.2, s32[16,8,128]{2,1,0:T(8,128)S(1)} %copy-done.3, s32[8,16,8,1]{3,2,1,0:T(8,128)S(1)} %copy.27.fall_depth), custom_call_target="tpu_custom_call" | custom-call | flops 200000000 | tf_op jit(solution)/shard_map/deposit/pallas_call | solution.py:772
  73.0 2.6 %deposit.10.rest_0_.rest_2_ = f32[2,9,3,8,128]{4,3,2,1,0:T(8,128)} custom-call(f32[8,16,8,128]{3,2,1,0:T(8,128)S(1)} %copy-done, f32[8,16,8,128]{3,2,1,0:T(8,128)S(1)} %copy-done.1, s32[8,16,8,128]{3,2,1,0:T(8,128)S(1)} %copy-done.2, s32[16,8,128]{2,1,0:T(8,128)S(1)} %copy-done.3, s32[8,16,8,1]{3,2,1,0:T(8,128)S(1)} %copy.27.fall_depth), custom_call_target="tpu_custom_call" | custom-call | flops 200000000 | tf_op jit(solution)/shard_map/deposit/pallas_call | solution.py:772
  78.1 2.5 %collective-permute-done.11.from_left = f32[16,8,128]{2,1,0:T(8,128)S(1)} collective-permute-done((f32[16,8,128]{2,1,0:T(8,128)S(1)}, f32[16,8,128]{2,1,0:T(8,128)S(1)}, u32[]{:S(2)}, u32[]{:S(2)}) %collective-permute-start.11) | collective-permute-done | bytes 65568 | tf_op jit(solution)/shard_map/ppermute | solution.py:727
  80.7 3.2 %collective-permute-start.12 = (f32[48,8,128]{2,1,0:T(8,128)S(1)}, f32[48,8,128]{2,1,0:T(8,128)S(1)}, u32[]{:S(2)}, u32[]{:S(2)}) collective-permute-start(f32[48,8,128]{2,1,0:T(8,128)S(1)} %get-tuple-element.54), channel_id=1, source_target_pairs={{1,0},{2,1},{3,2},{0,3},{5,4},{6,5},{7,6},{4,7},{9,8},{10,9},{11,1... | collective-permute-start | bytes 589832 | tf_op jit(solution)/shard_map/ppermute | solution.py:726
  84.0 2.6 %deposit.15.rest_7_ = f32[2,9,3,8,128]{4,3,2,1,0:T(8,128)} custom-call(f32[8,16,8,128]{3,2,1,0:T(8,128)S(1)} %copy-done, f32[8,16,8,128]{3,2,1,0:T(8,128)S(1)} %copy-done.1, s32[8,16,8,128]{3,2,1,0:T(8,128)S(1)} %copy-done.2, s32[16,8,128]{2,1,0:T(8,128)S(1)} %copy-done.3, s32[8,16,8,1]{3,2,1,0:T(8,128)S(1)} %copy.27.fall_depth), custom_call_target="tpu_custom_call" | custom-call | flops 200000000 | tf_op jit(solution)/shard_map/deposit/pallas_call | solution.py:772
  86.6 2.4 %second_own.1 = (f32[11,30,8,256]{3,2,1,0:T(8,128)S(1)}, f32[1,16,16,256]{3,2,1,0:T(8,128)S(1)}, f32[16,8,128]{2,1,0:T(8,128)S(1)}) custom-call(f32[5,16,8,128]{3,2,1,0:T(8,128)S(1)} %get-tuple-element.45.own, f32[3,16,8,128]{3,2,1,0:T(8,128)S(1)} %collective-permute-done.8.above, f32[3,16,8,128]{3,2,1,0:T(8,128)S(1)} %collective-permute-done.9.below, ...), custom_call_target="tpu_custom_call" | custom-call | flops 1000000000 | tf_op jit(solution)/shard_map/second_own/pallas_call | solution.py:711
  89.0 3.1 %last_tracer.1 = (f32[11,30,8,256]{3,2,1,0:T(8,128)S(1)}, f32[16,8,128]{2,1,0:T(8,128)S(1)}, f32[3,16,8,128]{3,2,1,0:T(8,128)S(1)}, f32[3,8,8,128]{3,2,1,0:T(8,1...) custom-call(s32[2]{0:T(128)S(1)} %pad_add_fusion.place_ref, ...), custom_call_target="tpu_custom_call", output_to_operand_aliasing={{0}: (2, {})} | custom-call | tf_op jit(solution)/shard_map/last_tracer/pallas_call | solution.py:711
  92.1 2.8 %collective-permute-start.14 = (f32[3,8,8,128]{3,2,1,0:T(8,128)S(1)}, f32[3,8,8,128]{3,2,1,0:T(8,128)S(1)}, u32[]{:S(2)}, u32[]{:S(2)}) collective-permute-start(f32[3,8,8,128]{3,2,1,0:T(8,128)S(1)} %get-tuple-element.61), channel_id=1, source_target_pairs={{1,0},{2,1},{3,2},{0,3},{5,4},{6,5},{7,6},{4,7},{9,8},{10,9},{11,1... | collective-permute-start | bytes 294920 | tf_op jit(solution)/shard_map/ppermute | solution.py:878
  94.9 3.8 %last_section.1 = f32[5,16,8,128]{3,2,1,0:T(8,128)} custom-call(s32[2]{0:T(128)S(1)} %pad_add_fusion.place_ref, f32[1]{0:T(128)} %get-tuple-element.44.dt_ref, f32[30,16,256]{2,1,0:T(8,128)S(1)} %get-tuple-element.57.rate, f32[30,16,256]{2,1,0:T(8,128)S(1)} %get-tuple-element.58.warm, f32[13,30,8,256]{3,2,1,0:T(8,128)S(1)} %get-tuple-element.42.start, ...), custom_call_target="tpu_custom_call" | custom-call | flops 1000000000 | tf_op jit(solution)/shard_map/last_section/pallas_call | solution.py:711
  (43 shorter events, 13.7 us)
Async XLA Ops:
  0.6 40.9 %copy-start.2 = (s32[8,16,8,128]{3,2,1,0:T(8,128)S(1)}, s32[8,16,8,128]{3,2,1,0:T(8,128)}, u32[]{:S(2)}) copy-start(s32[8,16,8,128]{3,2,1,0:T(8,128)} %column.15) | copy-start | bytes 1572868
  0.6 40.9 %copy-start.1 = (f32[8,16,8,128]{3,2,1,0:T(8,128)S(1)}, f32[8,16,8,128]{3,2,1,0:T(8,128)}, u32[]{:S(2)}) copy-start(f32[8,16,8,128]{3,2,1,0:T(8,128)} %weight.15) | copy-start | bytes 1572868
  0.7 40.9 %copy-start = (f32[8,16,8,128]{3,2,1,0:T(8,128)S(1)}, f32[8,16,8,128]{3,2,1,0:T(8,128)}, u32[]{:S(2)}) copy-start(f32[8,16,8,128]{3,2,1,0:T(8,128)} %radius.15) | copy-start | bytes 1572868
  0.7 27.7 %collective-permute-start.1 = (f32[5,16,8,128]{3,2,1,0:T(8,128)}, f32[5,16,8,128]{3,2,1,0:T(8,128)S(1)}, u32[]{:S(2)}, u32[]{:S(2)}) collective-permute-start(f32[5,16,8,128]{3,2,1,0:T(8,128)} %fields.1), channel_id=1, source_target_pairs={{0,4},{4,8},{8,12},{12,16},{16,20},{20,24},{24,28},{28,32},{32,36}... | collective-permute-start | bytes 983048 | tf_op jit(solution)/shard_map/ppermute | solution.py:727
  2.6 25.8 %collective-permute-start = (f32[5,16,8,128]{3,2,1,0:T(8,128)}, f32[5,16,8,128]{3,2,1,0:T(8,128)S(1)}, u32[]{:S(2)}, u32[]{:S(2)}) collective-permute-start(f32[5,16,8,128]{3,2,1,0:T(8,128)} %fields.1), channel_id=1, source_target_pairs={{4,0},{8,4},{12,8},{16,12},{20,16},{24,20},{28,24},{32,28},{36,32}... | collective-permute-start | bytes 983048 | tf_op jit(solution)/shard_map/ppermute | solution.py:726
  4.3 1.0 copy-start.4
  6.0 1.3 %collective-permute-start.2 = (f32[8,128]{1,0:T(8,128)S(1)}, f32[8,128]{1,0:T(8,128)S(1)}, u32[]{:S(2)}, u32[]{:S(2)}) collective-permute-start(f32[8,128]{1,0:T(8,128)S(1)} %get-tuple-element.33), channel_id=1, source_target_pairs={{0,64},{64,0},{128,192},{192,128},{1,65},{65,1},{129,193},{193,129... | collective-permute-start | bytes 12296 | tf_op jit(solution)/shard_map/ppermute | solution.py:812
  29.1 2.0 %collective-permute-start.3 = (f32[16,8,128]{2,1,0:T(8,128)S(1)}, f32[16,8,128]{2,1,0:T(8,128)S(1)}, u32[]{:S(2)}, u32[]{:S(2)}) collective-permute-start(f32[16,8,128]{2,1,0:T(8,128)S(1)} %get-tuple-element.34), channel_id=1, source_target_pairs={{64,0},{128,64},{192,128},{0,192},{65,1},{129,65},{193,129},{1,193... | collective-permute-start | bytes 196616 | tf_op jit(solution)/shard_map/ppermute | solution.py:726
  29.1 4.1 %collective-permute-start.4 = (f32[16,8,128]{2,1,0:T(8,128)S(1)}, f32[16,8,128]{2,1,0:T(8,128)S(1)}, u32[]{:S(2)}, u32[]{:S(2)}) collective-permute-start(f32[16,8,128]{2,1,0:T(8,128)S(1)} %get-tuple-element.35), channel_id=1, source_target_pairs={{0,64},{64,128},{128,192},{192,0},{1,65},{65,129},{129,193},{193,1... | collective-permute-start | bytes 196616 | tf_op jit(solution)/shard_map/ppermute | solution.py:727
  34.1 17.0 %collective-permute-start.7 = (f32[64,8,128]{2,1,0:T(8,128)}, f32[64,8,128]{2,1,0:T(8,128)S(1)}, u32[]{:S(2)}, u32[]{:S(2)}) collective-permute-start(f32[64,8,128]{2,1,0:T(8,128)} %get-tuple-element.40), channel_id=1, source_target_pairs={{0,1},{1,2},{2,3},{3,0},{4,5},{5,6},{6,7},{7,4},{8,9},{9,10},{10,1... | collective-permute-start | bytes 786440 | tf_op jit(solution)/shard_map/ppermute | solution.py:727
  34.7 16.4 %collective-permute-start.6 = (f32[64,8,128]{2,1,0:T(8,128)}, f32[64,8,128]{2,1,0:T(8,128)}, u32[]{:S(2)}, u32[]{:S(2)}) collective-permute-start(f32[64,8,128]{2,1,0:T(8,128)} %get-tuple-element.39), channel_id=1, source_target_pairs={{1,0},{2,1},{3,2},{0,3},{5,4},{6,5},{7,6},{4,7},{9,8},{10,9},{11,1... | collective-permute-start | bytes 786440 | tf_op jit(solution)/shard_map/ppermute | solution.py:726
  38.5 15.4 %collective-permute-start.5 = (f32[8,128]{1,0:T(8,128)S(1)}, f32[8,128]{1,0:T(8,128)S(1)}, u32[]{:S(2)}, u32[]{:S(2)}) collective-permute-start(f32[8,128]{1,0:T(8,128)S(1)} %get-tuple-element.36.speed), channel_id=1, source_target_pairs={{0,4},{4,0},{1,5},{5,1},{2,6},{6,2},{3,7},{7,3},{8,12},{12,8},{9,1... | collective-permute-start | bytes 12296 | tf_op jit(solution)/shard_map/ppermute | solution.py:817
  41.5 0.8 copy-start.3
  58.1 17.6 %collective-permute-start.8 = (f32[3,16,8,128]{3,2,1,0:T(8,128)S(1)}, f32[3,16,8,128]{3,2,1,0:T(8,128)S(1)}, u32[]{:S(2)}, u32[]{:S(2)}) collective-permute-start(f32[3,16,8,128]{3,2,1,0:T(8,128)S(1)} %get-tuple-element.46), channel_id=1, source_target_pairs={{4,0},{8,4},{12,8},{16,12},{20,16},{24,20},{28,24},{32,28},{36,32}... | collective-permute-start | bytes 589832 | tf_op jit(solution)/shard_map/ppermute | solution.py:726
  58.8 16.9 %collective-permute-start.9 = (f32[3,16,8,128]{3,2,1,0:T(8,128)S(1)}, f32[3,16,8,128]{3,2,1,0:T(8,128)S(1)}, u32[]{:S(2)}, u32[]{:S(2)}) collective-permute-start(f32[3,16,8,128]{3,2,1,0:T(8,128)S(1)} %get-tuple-element.47), channel_id=1, source_target_pairs={{0,4},{4,8},{8,12},{12,16},{16,20},{20,24},{24,28},{28,32},{32,36}... | collective-permute-start | bytes 589832 | tf_op jit(solution)/shard_map/ppermute | solution.py:727
  76.1 2.0 %collective-permute-start.10 = (f32[16,8,128]{2,1,0:T(8,128)S(1)}, f32[16,8,128]{2,1,0:T(8,128)S(1)}, u32[]{:S(2)}, u32[]{:S(2)}) collective-permute-start(f32[16,8,128]{2,1,0:T(8,128)S(1)} %get-tuple-element.49), channel_id=1, source_target_pairs={{64,0},{128,64},{192,128},{0,192},{65,1},{129,65},{193,129},{1,193... | collective-permute-start | bytes 196616 | tf_op jit(solution)/shard_map/ppermute | solution.py:726
  76.2 4.4 %collective-permute-start.11 = (f32[16,8,128]{2,1,0:T(8,128)S(1)}, f32[16,8,128]{2,1,0:T(8,128)S(1)}, u32[]{:S(2)}, u32[]{:S(2)}) collective-permute-start(f32[16,8,128]{2,1,0:T(8,128)S(1)} %get-tuple-element.50), channel_id=1, source_target_pairs={{0,64},{64,128},{128,192},{192,0},{1,65},{65,129},{129,193},{193,1... | collective-permute-start | bytes 196616 | tf_op jit(solution)/shard_map/ppermute | solution.py:727
  80.6 8.3 %collective-permute-start.13 = (f32[48,8,128]{2,1,0:T(8,128)S(1)}, f32[48,8,128]{2,1,0:T(8,128)S(1)}, u32[]{:S(2)}, u32[]{:S(2)}) collective-permute-start(f32[48,8,128]{2,1,0:T(8,128)S(1)} %get-tuple-element.55), channel_id=1, source_target_pairs={{0,1},{1,2},{2,3},{3,0},{4,5},{5,6},{6,7},{7,4},{8,9},{9,10},{10,1... | collective-permute-start | bytes 589832 | tf_op jit(solution)/shard_map/ppermute | solution.py:727
  80.7 8.3 %collective-permute-start.12 = (f32[48,8,128]{2,1,0:T(8,128)S(1)}, f32[48,8,128]{2,1,0:T(8,128)S(1)}, u32[]{:S(2)}, u32[]{:S(2)}) collective-permute-start(f32[48,8,128]{2,1,0:T(8,128)S(1)} %get-tuple-element.54), channel_id=1, source_target_pairs={{1,0},{2,1},{3,2},{0,3},{5,4},{6,5},{7,6},{4,7},{9,8},{10,9},{11,1... | collective-permute-start | bytes 589832 | tf_op jit(solution)/shard_map/ppermute | solution.py:726
  92.1 6.5 %collective-permute-start.14 = (f32[3,8,8,128]{3,2,1,0:T(8,128)S(1)}, f32[3,8,8,128]{3,2,1,0:T(8,128)S(1)}, u32[]{:S(2)}, u32[]{:S(2)}) collective-permute-start(f32[3,8,8,128]{3,2,1,0:T(8,128)S(1)} %get-tuple-element.61), channel_id=1, source_target_pairs={{1,0},{2,1},{3,2},{0,3},{5,4},{6,5},{7,6},{4,7},{9,8},{10,9},{11,1... | collective-permute-start | bytes 294920 | tf_op jit(solution)/shard_map/ppermute | solution.py:878

commit v7 on v6

--- a/solution.py
+++ b/solution.py
@@ -335,8 +335,7 @@
     flat_own(FIRST, ext, (C, PR), flat)
 
 
-def first_rates(place_ref, ext_in, flat, from_up, from_down, *rest):
-    ext, rate = rest[-2:]
+def first_rates(place_ref, ext_in, flat, from_up, from_down, ext, rate):
     place_halo(FIRST, from_up, from_down, ext, place_ref[0], place_ref[1])
 
     def write(n, l, value):
@@ -535,11 +534,11 @@
 ):
     *chunks, ext, tracer, landed, fallen, rate, warm, factor, by_depth, sem = rest
     dt = dt_ref[0]
-    each = LEVELS // len(chunks)
-    copies = [
-        pltpu.make_async_copy(chunk, by_depth.at[pl.ds(n * each, each)], sem.at[n])
-        for n, chunk in enumerate(chunks)
-    ]
+    copies, first = [], 0
+    for n, chunk in enumerate(chunks):
+        there = by_depth.at[pl.ds(first, chunk.shape[0])]
+        copies.append(pltpu.make_async_copy(chunk, there, sem.at[n]))
+        first += chunk.shape[0]
     for copy in copies:
         copy.start()
     place_halo(SECOND, from_up, from_down, ext, place_ref[0], place_ref[1])
@@ -743,7 +742,7 @@
         pack_levels(plan, bool(extra)),
         "pack_levels",
         vmem(5 + len(extra)),
-        [held(tiles, ROWS, COLS)] * 2 + [shaped(ROWS, COLS)] * len(extra),
+        [held(tiles, ROWS, COLS)] * 2 + [held(ROWS, COLS)] * len(extra),
     )(own, above, below, from_right, from_left, *extra)
     from_up, from_down = both_ways(to_down, "gz", to_up)
     return above, below, from_right, from_left, from_up, from_down, to_down, *speeds
@@ -761,44 +760,42 @@
     speed[...] = jnp.broadcast_to(jnp.max(most), speed.shape)
 
 
-def droplets(radius, weight, column, counts, fall_depth, chunk, numbers, after=None):
-    slots = radius.shape[0]
-    if after is not None:
-        counts, _ = lax.optimization_barrier((counts, after))
-    made = []
-    for n in numbers:
-        whole = pl.BlockSpec((slots, chunk, ROWS, COLS), lambda i, n=n: (0, n, 0, 0))
-        made.append(
-            pl.pallas_call(
-                deposit,
-                name="deposit",
-                grid=(1,),
-                in_specs=[
-                    whole,
-                    whole,
-                    whole,
-                    pl.BlockSpec((chunk, ROWS, COLS), lambda i, n=n: (n, 0, 0)),
-                    pl.BlockSpec((slots, chunk, ROWS, 1), lambda i, n=n: (0, n, 0, 0)),
-                ],
-                out_specs=pl.BlockSpec(
-                    (chunk, FMAX + 1, 3, ROWS, COLS), lambda i: (0, 0, 0, 0, 0)
-                ),
-                out_shape=pltpu.HBM((chunk, FMAX + 1, 3, ROWS, COLS), F32),
-                compiler_params=pltpu.CompilerParams(vmem_limit_bytes=12 << 20),
-                cost_estimate=pl.CostEstimate(
-                    flops=200_000_000, bytes_accessed=0, transcendentals=0
-                ),
-            )(radius, weight, column, counts, fall_depth)
-        )
-    return made
+def droplets(radius, weight, column, counts, fall_depth, first, count, after):
+    slots, step = radius.shape[0], 2
+    counts, _ = lax.optimization_barrier((counts, after))
+    whole = pl.BlockSpec((slots, step, ROWS, COLS), lambda i: (0, first // step + i, 0, 0))
+    return pl.pallas_call(
+        deposit,
+        name="deposit",
+        grid=(count // step,),
+        in_specs=[
+            whole,
+            whole,
+            whole,
+            pl.BlockSpec((step, ROWS, COLS), lambda i: (first // step + i, 0, 0)),
+            pl.BlockSpec((slots, step, ROWS, 1), lambda i: (0, first // step + i, 0, 0)),
+        ],
+        out_specs=pl.BlockSpec((step, FMAX + 1, 3, ROWS, COLS), lambda i: (i, 0, 0, 0, 0)),
+        out_shape=pltpu.HBM((count, FMAX + 1, 3, ROWS, COLS), F32),
+        compiler_params=pltpu.CompilerParams(vmem_limit_bytes=12 << 20),
+        cost_estimate=pl.CostEstimate(
+            flops=100_000_000 * count, bytes_accessed=0, transcendentals=0
+        ),
+    )(
+        *(
+            pltpu.with_memory_space_constraint(value, pltpu.HBM)
+            for value in (radius, weight, column, counts)
+        ),
+        fall_depth,
+    )
 
 
 def per_device(fields, radius, weight, column, counts, fall_depth):
     place = lax.axis_index("gz")
     last = lax.axis_size("gz") - 1
     where = jnp.stack([place, jnp.int32(last)]).astype(jnp.int32)
-    def drops(numbers, after=None):
-        return droplets(radius, weight, column, counts, fall_depth, 2, numbers, after)
+    def drops(first, count, after):
+        return droplets(radius, weight, column, counts, fall_depth, first, count, after)
 
     own, speed = pl.pallas_call(
         prepare,
@@ -811,11 +808,11 @@
     pair = [(i, i ^ 1) for i in range(lax.axis_size("gx"))]
     speed = jnp.maximum(speed, lax.ppermute(speed, "gx", pair))
     plane = ("gy_hi", "gz")
+    early = drops(0, 6, speed)
     speed = jnp.broadcast_to(speed[0:1], (lax.axis_size(plane), 1, COLS))
     speed = jnp.max(lax.all_to_all(speed, plane, 0, 0), axis=0)
-    *near, from_up, from_down, sent, speed = exchange(FIRST, own, fields, fields, (), speed)
+    *near, from_up, from_down, _, speed = exchange(FIRST, own, fields, fields, [early], speed)
     other_speed = lax.ppermute(speed, "gy_lo", [(0, 1), (1, 0)])
-    by_depth = drops(range(0, 2), sent)
     ext = held(len(FIRST.tiles), DEPTH, ROWS, WIDE)
     start, flat = call(
         first_own,
@@ -826,10 +823,10 @@
     start, rate0 = call(
         first_rates,
         "first_rates",
-        smem(1) + vmem(4) + far(len(by_depth)),
+        smem(1) + vmem(4),
         [ext, held(2, DEPTH, 2 * ROWS, WIDE)],
         alias={1: 0},
-    )(where, start, flat, from_up, from_down, *by_depth)
+    )(where, start, flat, from_up, from_down)
     s2, down, up, dt = call(
         two_sections,
         "two_sections",
@@ -843,9 +840,9 @@
         out_specs=vmem(3) + smem(1),
         grant=10,
     )(where, speed, other_speed, start, rate0)
-    middle = drops(range(2, 7), s2)
-    *near, from_up, from_down, sent = exchange(SECOND, s2, down, up, middle)
-    by_depth = by_depth + middle + drops(range(7, 8), sent)
+    middle = drops(6, 8, s2)
+    *near, from_up, from_down, sent = exchange(SECOND, s2, down, up, [middle])
+    by_depth = [early, middle, drops(14, 2, sent)]
     ext = held(len(SECOND.tiles), DEPTH, ROWS, WIDE)
     around_s2, flat, flat_tracer = call(
         second_own,

time: 100 us -> 90.2 us (0.902); the launches traced: 99.9 us -> 89 us
  blocking collectives: 21 us -> 0 us
  starting transfers between devices: 21.7 us -> 31.2 us
  waiting for transfers between devices: 8.69 us -> 11.3 us
  Pallas kernels: 44.5 us -> 42.8 us
    all_to_all x1 -> x0, blocking collectives: 21 us -> none  [per_device(): speed = jnp.max(lax.all_to_all(speed, plane, 0, 0), axis=0)]
    all_to_all x0 -> x1, starting transfers between devices: none -> 11.5 us  [per_device(): speed = jnp.max(lax.all_to_all(speed, plane, 0, 0), axis=0)]
    all_to_all x0 -> x1, waiting for transfers between devices: none -> 2.27 us  [per_device(): speed = jnp.max(lax.all_to_all(speed, plane, 0, 0), axis=0)]
    ppermute x6, starting transfers between devices: 7.41 us -> 5.27 us  [both_ways(): lax.ppermute(up, axis, [(i, (i + 1) % count) for i in range(count)])]
    ppermute x6, waiting for transfers between devices: 4.72 us -> 6.18 us  [both_ways(): lax.ppermute(up, axis, [(i, (i + 1) % count) for i in range(count)])]
    ppermute x1, waiting for transfers between devices: 1.15 us -> 0.01 us  [per_device(): speed = jnp.maximum(speed, lax.ppermute(speed, 'gx', pair))]
    pallas_call x11, Pallas kernels: 22.9 us -> 21.8 us  [run(): made(*(pltpu.with_memory_space_constraint(value, spec.memory_space) if sp...]
    ppermute x6, starting transfers between devices: 8.41 us -> 9.42 us  [both_ways(): lax.ppermute(down, axis, [((i + 1) % count, i) for i in range(count)])]
  transfers between devices with their start and end apart: 15 -> 16, of which waited for: 5 -> 6; matrix products, arithmetic and copies ran while one was open for 1% -> 2% of each run, Pallas kernels for 34% -> 37%
where the time goes in v7:
time: 90.2 us; the launch traced here: 89 us
  Pallas kernels  42.8 us (47%)
  starting transfers between devices  31.2 us (35%)
  waiting for transfers between devices  11.3 us (13%)
  local copies, waits for them, and re-layouts  2.8 us (3%)
    pallas_call x11, Pallas kernels, run(): made(*(pltpu.with_memory_space_constraint(value, spec.memory_space) if sp...  21.8 us
    pallas_call x3, Pallas kernels, droplets(): pl.pallas_call(deposit, name='deposit', grid=(count // step,), in_specs=[...  20.3 us
    all_to_all x1, starting transfers between devices, per_device(): speed = jnp.max(lax.all_to_all(speed, plane, 0, 0), axis=0)  11.5 us
    ppermute x6, starting transfers between devices, both_ways(): lax.ppermute(down, axis, [((i + 1) % count, i) for i in range(count)])  9.42 us
    ppermute x6, waiting for transfers between devices, both_ways(): lax.ppermute(up, axis, [(i, (i + 1) % count) for i in range(count)])  6.18 us
    ppermute x6, starting transfers between devices, both_ways(): lax.ppermute(up, axis, [(i, (i + 1) % count) for i in range(count)])  5.27 us
    ppermute x1, starting transfers between devices, per_device(): other_speed = lax.ppermute(speed, 'gy_lo', [(0, 1), (1, 0)])  2.91 us
    ppermute x6, waiting for transfers between devices, both_ways(): lax.ppermute(down, axis, [((i + 1) % count, i) for i in range(count)])  2.88 us
  transfers between devices with their start and end apart: 16, of which 6 were waited for; matrix products, arithmetic and copies ran while one was open for 2% of the time, Pallas kernels for 37%

profile of v7, /device:TPU:4, one launch (start us, length us, event | category | flops | bytes accessed | tf_op | source)
XLA Modules:
  0.0 89.0 jit_solution(12249431621968658751)
XLA Ops:
  0.6 1.9 %collective-permute-start.1 = (f32[5,16,8,128]{3,2,1,0:T(8,128)}, f32[5,16,8,128]{3,2,1,0:T(8,128)S(1)}, u32[]{:S(2)}, u32[]{:S(2)}) collective-permute-start(f32[5,16,8,128]{3,2,1,0:T(8,128)} %fields.1), channel_id=1, source_target_pairs={{0,4},{4,8},{8,12},{12,16},{16,20},{20,24},{24,28},{28,32},{32,36}... | collective-permute-start | bytes 983048 | tf_op jit(solution)/shard_map/ppermute | solution.py:726
  2.6 1.7 %collective-permute-start = (f32[5,16,8,128]{3,2,1,0:T(8,128)}, f32[5,16,8,128]{3,2,1,0:T(8,128)S(1)}, u32[]{:S(2)}, u32[]{:S(2)}) collective-permute-start(f32[5,16,8,128]{3,2,1,0:T(8,128)} %fields.1), channel_id=1, source_target_pairs={{4,0},{8,4},{12,8},{16,12},{20,16},{24,20},{28,24},{32,28},{36,32}... | collective-permute-start | bytes 983048 | tf_op jit(solution)/shard_map/ppermute | solution.py:725
  7.9 11.5 %all-to-all-start = ((f32[32,1,128]{2,1,0:T(1,128)}), f32[32,1,128]{2,1,0:T(1,128)S(1)}, u32[]{:S(2)}, u32[]{:S(2)}) async-start(f32[32,1,128]{2,1,0:T(1,128)} %broadcast_in_dim.3), calls=%async_computation | async-start | bytes 32768 | tf_op jit(solution)/shard_map/all_to_all | solution.py:813
  19.4 7.4 %deposit.3.rest_1_.rest_0_ = f32[6,9,3,8,128]{4,3,2,1,0:T(8,128)} custom-call(f32[8,16,8,128]{3,2,1,0:T(8,128)} %radius.5, f32[8,16,8,128]{3,2,1,0:T(8,128)} %weight.5, s32[8,16,8,128]{3,2,1,0:T(8,128)} %column.5, s32[16,8,128]{2,1,0:T(8,128)} %counts.2, s32[8,16,8,1]{3,2,1,0:T(8,128)S(1)} %copy.17.fall_depth), custom_call_target="tpu_custom_call" | custom-call | flops 600000000 | tf_op jit(solution)/shard_map/deposit/pallas_call | solution.py:767
  26.8 2.3 %all-to-all-done = f32[32,1,128]{2,1,0:T(1,128)S(1)} async-done(((f32[32,1,128]{2,1,0:T(1,128)}), f32[32,1,128]{2,1,0:T(1,128)S(1)}, u32[]{:S(2)}, u32[]{:S(2)}) %all-to-all-start) | async-done | bytes 16416 | tf_op jit(solution)/shard_map/all_to_all | solution.py:813
  30.4 1.4 %collective-permute-done.3.from_right = f32[16,8,128]{2,1,0:T(8,128)S(1)} collective-permute-done((f32[16,8,128]{2,1,0:T(8,128)S(1)}, f32[16,8,128]{2,1,0:T(8,128)S(1)}, u32[]{:S(2)}, u32[]{:S(2)}) %collective-permute-start.3) | collective-permute-done | bytes 65568 | tf_op jit(solution)/shard_map/ppermute | solution.py:725
  31.8 2.2 %collective-permute-done.4.from_left = f32[16,8,128]{2,1,0:T(8,128)S(1)} collective-permute-done((f32[16,8,128]{2,1,0:T(8,128)S(1)}, f32[16,8,128]{2,1,0:T(8,128)S(1)}, u32[]{:S(2)}, u32[]{:S(2)}) %collective-permute-start.4) | collective-permute-done | bytes 65568 | tf_op jit(solution)/shard_map/ppermute | solution.py:726
  34.2 1.3 %collective-permute-start.6 = (f32[64,8,128]{2,1,0:T(8,128)S(1)}, f32[64,8,128]{2,1,0:T(8,128)S(1)}, u32[]{:S(2)}, u32[]{:S(2)}) collective-permute-start(f32[64,8,128]{2,1,0:T(8,128)S(1)} %get-tuple-element.40), channel_id=1, source_target_pairs={{1,0},{2,1},{3,2},{0,3},{5,4},{6,5},{7,6},{4,7},{9,8},{10,9},{11,1... | collective-permute-start | bytes 786440 | tf_op jit(solution)/shard_map/ppermute | solution.py:725
  36.3 2.9 %collective-permute-start.5 = (f32[8,128]{1,0:T(8,128)S(1)}, f32[8,128]{1,0:T(8,128)S(1)}, u32[]{:S(2)}, u32[]{:S(2)}) collective-permute-start(f32[8,128]{1,0:T(8,128)S(1)} %get-tuple-element.37.speed), channel_id=1, source_target_pairs={{0,4},{4,0},{1,5},{5,1},{2,6},{6,2},{3,7},{7,3},{8,12},{12,8},{9,1... | collective-permute-start | bytes 12296 | tf_op jit(solution)/shard_map/ppermute | solution.py:815
  39.2 3.5 %first_own.1 = (f32[13,30,8,256]{3,2,1,0:T(8,128)S(1)}, f32[2,16,16,256]{3,2,1,0:T(8,128)S(1)}) custom-call(s32[2]{0:T(128)S(1)} %pad_add_fusion.place_ref, f32[5,16,8,128]{3,2,1,0:T(8,128)S(1)} %get-tuple-element.32.own.initial, f32[5,16,8,128]{3,2,1,0:T(8,128)S(1)} %collective-permute-done.above, f32[5,16,8,128]{3,2,1,0:T(8,128)S(1)} %collective-permute-done.1.below, ...), custom_call_target="tpu_custom_call" | custom-call | tf_op jit(solution)/shard_map/first_own/pallas_call | solution.py:710
  42.7 1.6 %collective-permute-done.7.from_down = f32[64,8,128]{2,1,0:T(8,128)S(1)} collective-permute-done((f32[64,8,128]{2,1,0:T(8,128)S(1)}, f32[64,8,128]{2,1,0:T(8,128)S(1)}, u32[]{:S(2)}, u32[]{:S(2)}) %collective-permute-start.7) | collective-permute-done | bytes 262176 | tf_op jit(solution)/shard_map/ppermute | solution.py:726
  44.3 2.4 %first_rates.1 = (f32[13,30,8,256]{3,2,1,0:T(8,128)S(1)}, f32[2,30,16,256]{3,2,1,0:T(8,128)S(1)}) custom-call(s32[2]{0:T(128)S(1)} %pad_add_fusion.place_ref, f32[13,30,8,256]{3,2,1,0:T(8,128)S(1)} %get-tuple-element.38.ext_in, f32[2,16,16,256]{3,2,1,0:T(8,128)S(1)} %get-tuple-element.39.flat, ...), custom_call_target="tpu_custom_call", output_to_operand_aliasing={{0}: (1, {})} | custom-call | tf_op jit(solution)/shard_map/first_rates/pallas_call | solution.py:710
  46.7 4.2 %two_sections.1 = (f32[5,16,8,128]{3,2,1,0:T(8,128)S(1)}, f32[3,16,8,128]{3,2,1,0:T(8,128)S(1)}, f32[3,16,8,128]{3,2,1,0:T(8,128)S(1)}, f32[1]{0:T(128)}) custom-call(s32[2]{0:T(128)S(1)} %pad_add_fusion.place_ref, f32[8,128]{1,0:T(8,128)S(1)} %get-tuple-element.37.speed, f32[8,128]{1,0:T(8,128)S(1)} %collective-permute-done.5.other_speed, ...), custom_call_target="tpu_custom_call" | custom-call | tf_op jit(solution)/shard_map/two_sections/pallas_call | solution.py:710
  50.9 3.0 %collective-permute-start.8 = (f32[3,16,8,128]{3,2,1,0:T(8,128)S(1)}, f32[3,16,8,128]{3,2,1,0:T(8,128)S(1)}, u32[]{:S(2)}, u32[]{:S(2)}) collective-permute-start(f32[3,16,8,128]{3,2,1,0:T(8,128)S(1)} %get-tuple-element.46), channel_id=1, source_target_pairs={{4,0},{8,4},{12,8},{16,12},{20,16},{24,20},{28,24},{32,28},{36,32}... | collective-permute-start | bytes 589832 | tf_op jit(solution)/shard_map/ppermute | solution.py:725
  53.9 1.5 %collective-permute-start.9 = (f32[3,16,8,128]{3,2,1,0:T(8,128)S(1)}, f32[3,16,8,128]{3,2,1,0:T(8,128)S(1)}, u32[]{:S(2)}, u32[]{:S(2)}) collective-permute-start(f32[3,16,8,128]{3,2,1,0:T(8,128)S(1)} %get-tuple-element.47), channel_id=1, source_target_pairs={{0,4},{4,8},{8,12},{12,16},{16,20},{20,24},{24,28},{28,32},{32,36}... | collective-permute-start | bytes 589832 | tf_op jit(solution)/shard_map/ppermute | solution.py:726
  55.4 9.4 %deposit.4.rest_0_.rest_1_ = f32[8,9,3,8,128]{4,3,2,1,0:T(8,128)} custom-call(f32[8,16,8,128]{3,2,1,0:T(8,128)} %radius.5, f32[8,16,8,128]{3,2,1,0:T(8,128)} %weight.5, s32[8,16,8,128]{3,2,1,0:T(8,128)} %column.5, s32[16,8,128]{2,1,0:T(8,128)} %counts.2, s32[8,16,8,1]{3,2,1,0:T(8,128)S(1)} %copy.17.fall_depth), custom_call_target="tpu_custom_call" | custom-call | flops 800000000 | tf_op jit(solution)/shard_map/deposit/pallas_call | solution.py:767
  65.8 1.5 %collective-permute-done.10.from_right = f32[16,8,128]{2,1,0:T(8,128)S(1)} collective-permute-done((f32[16,8,128]{2,1,0:T(8,128)S(1)}, f32[16,8,128]{2,1,0:T(8,128)S(1)}, u32[]{:S(2)}, u32[]{:S(2)}) %collective-permute-start.10) | collective-permute-done | bytes 65568 | tf_op jit(solution)/shard_map/ppermute | solution.py:725
  67.3 2.4 %collective-permute-done.11.from_left = f32[16,8,128]{2,1,0:T(8,128)S(1)} collective-permute-done((f32[16,8,128]{2,1,0:T(8,128)S(1)}, f32[16,8,128]{2,1,0:T(8,128)S(1)}, u32[]{:S(2)}, u32[]{:S(2)}) %collective-permute-start.11) | collective-permute-done | bytes 65568 | tf_op jit(solution)/shard_map/ppermute | solution.py:726
  69.8 3.2 %collective-permute-start.12 = (f32[48,8,128]{2,1,0:T(8,128)S(1)}, f32[48,8,128]{2,1,0:T(8,128)S(1)}, u32[]{:S(2)}, u32[]{:S(2)}) collective-permute-start(f32[48,8,128]{2,1,0:T(8,128)S(1)} %get-tuple-element.54), channel_id=1, source_target_pairs={{1,0},{2,1},{3,2},{0,3},{5,4},{6,5},{7,6},{4,7},{9,8},{10,9},{11,1... | collective-permute-start | bytes 589832 | tf_op jit(solution)/shard_map/ppermute | solution.py:725
  73.0 3.5 %deposit.5.rest_2_ = f32[2,9,3,8,128]{4,3,2,1,0:T(8,128)} custom-call(f32[8,16,8,128]{3,2,1,0:T(8,128)} %radius.5, f32[8,16,8,128]{3,2,1,0:T(8,128)} %weight.5, s32[8,16,8,128]{3,2,1,0:T(8,128)} %column.5, s32[16,8,128]{2,1,0:T(8,128)} %counts.2, s32[8,16,8,1]{3,2,1,0:T(8,128)S(1)} %copy.17.fall_depth), custom_call_target="tpu_custom_call" | custom-call | flops 200000000 | tf_op jit(solution)/shard_map/deposit/pallas_call | solution.py:767
  76.5 2.4 %second_own.1 = (f32[11,30,8,256]{3,2,1,0:T(8,128)S(1)}, f32[1,16,16,256]{3,2,1,0:T(8,128)S(1)}, f32[16,8,128]{2,1,0:T(8,128)S(1)}) custom-call(f32[5,16,8,128]{3,2,1,0:T(8,128)S(1)} %get-tuple-element.45.own, f32[3,16,8,128]{3,2,1,0:T(8,128)S(1)} %collective-permute-done.8.above, f32[3,16,8,128]{3,2,1,0:T(8,128)S(1)} %collective-permute-done.9.below, ...), custom_call_target="tpu_custom_call" | custom-call | flops 1000000000 | tf_op jit(solution)/shard_map/second_own/pallas_call | solution.py:710
  79.0 3.0 %last_tracer.1 = (f32[11,30,8,256]{3,2,1,0:T(8,128)S(1)}, f32[16,8,128]{2,1,0:T(8,128)S(1)}, f32[3,16,8,128]{3,2,1,0:T(8,128)S(1)}, f32[3,8,8,128]{3,2,1,0:T(8,1...) custom-call(s32[2]{0:T(128)S(1)} %pad_add_fusion.place_ref, ...), custom_call_target="tpu_custom_call", output_to_operand_aliasing={{0}: (2, {})} | custom-call | tf_op jit(solution)/shard_map/last_tracer/pallas_call | solution.py:710
  82.0 2.0 %collective-permute-start.14 = (f32[3,8,8,128]{3,2,1,0:T(8,128)S(1)}, f32[3,8,8,128]{3,2,1,0:T(8,128)S(1)}, u32[]{:S(2)}, u32[]{:S(2)}) collective-permute-start(f32[3,8,8,128]{3,2,1,0:T(8,128)S(1)} %get-tuple-element.61), channel_id=1, source_target_pairs={{1,0},{2,1},{3,2},{0,3},{5,4},{6,5},{7,6},{4,7},{9,8},{10,9},{11,1... | collective-permute-start | bytes 294920 | tf_op jit(solution)/shard_map/ppermute | solution.py:875
  84.0 3.8 %last_section.1 = f32[5,16,8,128]{3,2,1,0:T(8,128)} custom-call(s32[2]{0:T(128)S(1)} %pad_add_fusion.place_ref, f32[1]{0:T(128)} %get-tuple-element.44.dt_ref, f32[30,16,256]{2,1,0:T(8,128)S(1)} %get-tuple-element.57.rate, f32[30,16,256]{2,1,0:T(8,128)S(1)} %get-tuple-element.58.warm, f32[13,30,8,256]{3,2,1,0:T(8,128)S(1)} %get-tuple-element.42.start, ...), custom_call_target="tpu_custom_call" | custom-call | flops 1000000000 | tf_op jit(solution)/shard_map/last_section/pallas_call | solution.py:710
  (31 shorter events, 8.3 us)
Async XLA Ops:
  0.6 28.5 %collective-permute-start.1 = (f32[5,16,8,128]{3,2,1,0:T(8,128)}, f32[5,16,8,128]{3,2,1,0:T(8,128)S(1)}, u32[]{:S(2)}, u32[]{:S(2)}) collective-permute-start(f32[5,16,8,128]{3,2,1,0:T(8,128)} %fields.1), channel_id=1, source_target_pairs={{0,4},{4,8},{8,12},{12,16},{16,20},{20,24},{24,28},{28,32},{32,36}... | collective-permute-start | bytes 983048 | tf_op jit(solution)/shard_map/ppermute | solution.py:726
  2.6 26.6 %collective-permute-start = (f32[5,16,8,128]{3,2,1,0:T(8,128)}, f32[5,16,8,128]{3,2,1,0:T(8,128)S(1)}, u32[]{:S(2)}, u32[]{:S(2)}) collective-permute-start(f32[5,16,8,128]{3,2,1,0:T(8,128)} %fields.1), channel_id=1, source_target_pairs={{4,0},{8,4},{12,8},{16,12},{20,16},{24,20},{28,24},{32,28},{36,32}... | collective-permute-start | bytes 983048 | tf_op jit(solution)/shard_map/ppermute | solution.py:725
  4.3 1.0 %copy-start = (f32[5,16,8,128]{3,2,1,0:T(8,128)S(1)}, f32[5,16,8,128]{3,2,1,0:T(8,128)}, u32[]{:S(2)}) copy-start(f32[5,16,8,128]{3,2,1,0:T(8,128)} %fields.1) | copy-start | bytes 983044
  6.0 1.3 %collective-permute-start.2 = (f32[8,128]{1,0:T(8,128)S(1)}, f32[8,128]{1,0:T(8,128)S(1)}, u32[]{:S(2)}, u32[]{:S(2)}) collective-permute-start(f32[8,128]{1,0:T(8,128)S(1)} %get-tuple-element.33), channel_id=1, source_target_pairs={{0,64},{64,0},{128,192},{192,128},{1,65},{65,1},{129,193},{193,129... | collective-permute-start | bytes 12296 | tf_op jit(solution)/shard_map/ppermute | solution.py:809
  7.9 21.2 %all-to-all-start = ((f32[32,1,128]{2,1,0:T(1,128)}), f32[32,1,128]{2,1,0:T(1,128)S(1)}, u32[]{:S(2)}, u32[]{:S(2)}) async-start(f32[32,1,128]{2,1,0:T(1,128)} %broadcast_in_dim.3), calls=%async_computation | async-start | bytes 32768 | tf_op jit(solution)/shard_map/all_to_all | solution.py:813
  29.8 2.0 %collective-permute-start.3 = (f32[16,8,128]{2,1,0:T(8,128)S(1)}, f32[16,8,128]{2,1,0:T(8,128)S(1)}, u32[]{:S(2)}, u32[]{:S(2)}) collective-permute-start(f32[16,8,128]{2,1,0:T(8,128)S(1)} %get-tuple-element.35), channel_id=1, source_target_pairs={{64,0},{128,64},{192,128},{0,192},{65,1},{129,65},{193,129},{1,193... | collective-permute-start | bytes 196616 | tf_op jit(solution)/shard_map/ppermute | solution.py:725
  29.9 4.1 %collective-permute-start.4 = (f32[16,8,128]{2,1,0:T(8,128)S(1)}, f32[16,8,128]{2,1,0:T(8,128)S(1)}, u32[]{:S(2)}, u32[]{:S(2)}) collective-permute-start(f32[16,8,128]{2,1,0:T(8,128)S(1)} %get-tuple-element.36), channel_id=1, source_target_pairs={{0,64},{64,128},{128,192},{192,0},{1,65},{65,129},{129,193},{193,1... | collective-permute-start | bytes 196616 | tf_op jit(solution)/shard_map/ppermute | solution.py:726
  34.2 8.5 %collective-permute-start.6 = (f32[64,8,128]{2,1,0:T(8,128)S(1)}, f32[64,8,128]{2,1,0:T(8,128)S(1)}, u32[]{:S(2)}, u32[]{:S(2)}) collective-permute-start(f32[64,8,128]{2,1,0:T(8,128)S(1)} %get-tuple-element.40), channel_id=1, source_target_pairs={{1,0},{2,1},{3,2},{0,3},{5,4},{6,5},{7,6},{4,7},{9,8},{10,9},{11,1... | collective-permute-start | bytes 786440 | tf_op jit(solution)/shard_map/ppermute | solution.py:725
  35.5 8.8 %collective-permute-start.7 = (f32[64,8,128]{2,1,0:T(8,128)S(1)}, f32[64,8,128]{2,1,0:T(8,128)S(1)}, u32[]{:S(2)}, u32[]{:S(2)}) collective-permute-start(f32[64,8,128]{2,1,0:T(8,128)S(1)} %get-tuple-element.41), channel_id=1, source_target_pairs={{0,1},{1,2},{2,3},{3,0},{4,5},{5,6},{6,7},{7,4},{8,9},{9,10},{10,1... | collective-permute-start | bytes 786440 | tf_op jit(solution)/shard_map/ppermute | solution.py:726
  36.3 10.4 %collective-permute-start.5 = (f32[8,128]{1,0:T(8,128)S(1)}, f32[8,128]{1,0:T(8,128)S(1)}, u32[]{:S(2)}, u32[]{:S(2)}) collective-permute-start(f32[8,128]{1,0:T(8,128)S(1)} %get-tuple-element.37.speed), channel_id=1, source_target_pairs={{0,4},{4,0},{1,5},{5,1},{2,6},{6,2},{3,7},{7,3},{8,12},{12,8},{9,1... | collective-permute-start | bytes 12296 | tf_op jit(solution)/shard_map/ppermute | solution.py:815
  50.9 13.9 %collective-permute-start.8 = (f32[3,16,8,128]{3,2,1,0:T(8,128)S(1)}, f32[3,16,8,128]{3,2,1,0:T(8,128)S(1)}, u32[]{:S(2)}, u32[]{:S(2)}) collective-permute-start(f32[3,16,8,128]{3,2,1,0:T(8,128)S(1)} %get-tuple-element.46), channel_id=1, source_target_pairs={{4,0},{8,4},{12,8},{16,12},{20,16},{24,20},{28,24},{32,28},{36,32}... | collective-permute-start | bytes 589832 | tf_op jit(solution)/shard_map/ppermute | solution.py:725
  53.9 10.9 %collective-permute-start.9 = (f32[3,16,8,128]{3,2,1,0:T(8,128)S(1)}, f32[3,16,8,128]{3,2,1,0:T(8,128)S(1)}, u32[]{:S(2)}, u32[]{:S(2)}) collective-permute-start(f32[3,16,8,128]{3,2,1,0:T(8,128)S(1)} %get-tuple-element.47), channel_id=1, source_target_pairs={{0,4},{4,8},{8,12},{12,16},{16,20},{20,24},{24,28},{28,32},{32,36}... | collective-permute-start | bytes 589832 | tf_op jit(solution)/shard_map/ppermute | solution.py:726
  65.3 2.1 %collective-permute-start.10 = (f32[16,8,128]{2,1,0:T(8,128)S(1)}, f32[16,8,128]{2,1,0:T(8,128)S(1)}, u32[]{:S(2)}, u32[]{:S(2)}) collective-permute-start(f32[16,8,128]{2,1,0:T(8,128)S(1)} %get-tuple-element.49), channel_id=1, source_target_pairs={{64,0},{128,64},{192,128},{0,192},{65,1},{129,65},{193,129},{1,193... | collective-permute-start | bytes 196616 | tf_op jit(solution)/shard_map/ppermute | solution.py:725
  65.4 4.3 %collective-permute-start.11 = (f32[16,8,128]{2,1,0:T(8,128)S(1)}, f32[16,8,128]{2,1,0:T(8,128)S(1)}, u32[]{:S(2)}, u32[]{:S(2)}) collective-permute-start(f32[16,8,128]{2,1,0:T(8,128)S(1)} %get-tuple-element.50), channel_id=1, source_target_pairs={{0,64},{64,128},{128,192},{192,0},{1,65},{65,129},{129,193},{193,1... | collective-permute-start | bytes 196616 | tf_op jit(solution)/shard_map/ppermute | solution.py:726
  69.7 9.2 %collective-permute-start.13 = (f32[48,8,128]{2,1,0:T(8,128)S(1)}, f32[48,8,128]{2,1,0:T(8,128)S(1)}, u32[]{:S(2)}, u32[]{:S(2)}) collective-permute-start(f32[48,8,128]{2,1,0:T(8,128)S(1)} %get-tuple-element.55), channel_id=1, source_target_pairs={{0,1},{1,2},{2,3},{3,0},{4,5},{5,6},{6,7},{7,4},{8,9},{9,10},{10,1... | collective-permute-start | bytes 589832 | tf_op jit(solution)/shard_map/ppermute | solution.py:726
  69.8 9.2 %collective-permute-start.12 = (f32[48,8,128]{2,1,0:T(8,128)S(1)}, f32[48,8,128]{2,1,0:T(8,128)S(1)}, u32[]{:S(2)}, u32[]{:S(2)}) collective-permute-start(f32[48,8,128]{2,1,0:T(8,128)S(1)} %get-tuple-element.54), channel_id=1, source_target_pairs={{1,0},{2,1},{3,2},{0,3},{5,4},{6,5},{7,6},{4,7},{9,8},{10,9},{11,1... | collective-permute-start | bytes 589832 | tf_op jit(solution)/shard_map/ppermute | solution.py:725
  82.0 5.8 %collective-permute-start.14 = (f32[3,8,8,128]{3,2,1,0:T(8,128)S(1)}, f32[3,8,8,128]{3,2,1,0:T(8,128)S(1)}, u32[]{:S(2)}, u32[]{:S(2)}) collective-permute-start(f32[3,8,8,128]{3,2,1,0:T(8,128)S(1)} %get-tuple-element.61), channel_id=1, source_target_pairs={{1,0},{2,1},{3,2},{0,3},{5,4},{6,5},{7,6},{4,7},{9,8},{10,9},{11,1... | collective-permute-start | bytes 294920 | tf_op jit(solution)/shard_map/ppermute | solution.py:875

commit v8 on v7

--- a/solution.py
+++ b/solution.py
@@ -115,9 +115,9 @@
     {
         C: [THREE] + [TWO] * 4 + [ONE],
         PR: [THREE] * 2 + [TWO] * 4 + [ONE],
-        U: [TWO] * 4,
+        U: [TWO] * 3 + [ONE],
         V: [TWO] * 4,
-        W: [TWO] * 4 + [ONE],
+        W: [TWO] * 3 + [ONE] * 2,
     },
 )
 SECOND = Plan(
@@ -333,15 +333,6 @@
             ext[FIRST.at[W, part], REACH + LEVELS - 1] = jnp.zeros((ROWS, WIDE), F32)
 
     flat_own(FIRST, ext, (C, PR), flat)
-
-
-def first_rates(place_ref, ext_in, flat, from_up, from_down, ext, rate):
-    place_halo(FIRST, from_up, from_down, ext, place_ref[0], place_ref[1])
-
-    def write(n, l, value):
-        rate[n, l] = value
-
-    rates(FIRST, ext, (C, PR), write, 4, 4, flat)
 
 
 def acoustic(p, u, v, w, read_c, rate, step, first, count, place, last):
@@ -418,8 +409,17 @@
     return level_flux(lambda m: tiles(m)[0:ROWS, 0:COLS], w(l)[0:ROWS, 0:COLS], l)
 
 
-def two_sections(place_ref, speed, other_speed, start, rate0, s2, down, up, dt_out, s1, rate1, fast):
+def two_sections(
+    place_ref, speed, other_speed, start_in, flat, from_up, from_down, *rest
+):
+    start, s2, down, up, dt_out, rate0, s1, rate1, fast = rest[-9:]
     place, last = place_ref[0], place_ref[1]
+    place_halo(FIRST, from_up, from_down, start, place, last)
+
+    def write0(n, l, value):
+        rate0[n, l] = value
+
+    rates(FIRST, start, (C, PR), write0, 4, 4, flat)
     dt = courant_goal / (1.0 + jnp.max(jnp.maximum(speed[...], other_speed[...])))
     dt_out[0] = dt
     third = dt * (1.0 / 3.0)
@@ -811,8 +811,9 @@
     early = drops(0, 6, speed)
     speed = jnp.broadcast_to(speed[0:1], (lax.axis_size(plane), 1, COLS))
     speed = jnp.max(lax.all_to_all(speed, plane, 0, 0), axis=0)
-    *near, from_up, from_down, _, speed = exchange(FIRST, own, fields, fields, [early], speed)
+    *near, from_up, from_down, sent, speed = exchange(FIRST, own, fields, fields, [early], speed)
     other_speed = lax.ppermute(speed, "gy_lo", [(0, 1), (1, 0)])
+    second = drops(6, 2, sent)
     ext = held(len(FIRST.tiles), DEPTH, ROWS, WIDE)
     start, flat = call(
         first_own,
@@ -820,29 +821,24 @@
         smem(1) + vmem(5),
         [ext, held(2, LEVELS, 2 * ROWS, WIDE)],
     )(where, own, *near)
-    start, rate0 = call(
-        first_rates,
-        "first_rates",
-        smem(1) + vmem(4),
-        [ext, held(2, DEPTH, 2 * ROWS, WIDE)],
-        alias={1: 0},
-    )(where, start, flat, from_up, from_down)
-    s2, down, up, dt = call(
+    start, s2, down, up, dt = call(
         two_sections,
         "two_sections",
-        smem(1) + vmem(4),
-        [held(5, LEVELS, ROWS, COLS)] + [held(3, LEVELS, ROWS, COLS)] * 2 + [shaped(1)],
+        smem(1) + vmem(6) + far(1),
+        [ext, held(5, LEVELS, ROWS, COLS)] + [held(3, LEVELS, ROWS, COLS)] * 2 + [shaped(1)],
         scratch=[
+            pltpu.VMEM((2, DEPTH, 2 * ROWS, WIDE), F32),
             pltpu.VMEM((5, DEPTH, 2 * ROWS, WIDE), F32),
             pltpu.VMEM((DEPTH, 2 * ROWS, WIDE), F32),
             pltpu.VMEM((4, DEPTH, 2 * ROWS, WIDE), F32),
         ],
-        out_specs=vmem(3) + smem(1),
-        grant=10,
-    )(where, speed, other_speed, start, rate0)
-    middle = drops(6, 8, s2)
-    *near, from_up, from_down, sent = exchange(SECOND, s2, down, up, [middle])
-    by_depth = [early, middle, drops(14, 2, sent)]
+        out_specs=vmem(4) + smem(1),
+        grant=12,
+        alias={3: 0},
+    )(where, speed, other_speed, start, flat, from_up, from_down, second)
+    middle = drops(8, 8, s2)
+    *near, from_up, from_down, _ = exchange(SECOND, s2, down, up, [middle])
+    by_depth = [early, second, middle]
     ext = held(len(SECOND.tiles), DEPTH, ROWS, WIDE)
     around_s2, flat, flat_tracer = call(
         second_own,

time: 90.2 us -> 89.9 us (level)
  waiting for transfers between devices: 11.3 us -> 14.2 us
  starting transfers between devices: 31.2 us -> 29.4 us
    ppermute x6, starting transfers between devices: 9.42 us -> 5.27 us  [both_ways(): lax.ppermute(down, axis, [((i + 1) % count, i) for i in range(count)])]
    ppermute x6, starting transfers between devices: 5.27 us -> 9.41 us  [both_ways(): lax.ppermute(up, axis, [(i, (i + 1) % count) for i in range(count)])]
    ppermute x6, waiting for transfers between devices: 2.88 us -> 5.2 us  [both_ways(): lax.ppermute(down, axis, [((i + 1) % count, i) for i in range(count)])]
    ppermute x1, starting transfers between devices: 2 us -> 0.28 us  [per_device(): lax.ppermute(fallen, 'gz', [((i + 1) % count, i) for i in range(count)])]
    pallas_call x11 -> x10, Pallas kernels: 21.8 us -> 21.2 us  [run(): made(*(pltpu.with_memory_space_constraint(value, spec.memory_space) if sp...]
  transfers between devices with their start and end apart: 16 -> 16, of which waited for: 6 -> 8; matrix products, arithmetic and copies ran while one was open for 2% -> 2% of each run, Pallas kernels for 37% -> 34%
where the time goes in v8:
time: 89.9 us; the launch traced here: 89.4 us
  Pallas kernels  42.1 us (47%)
  starting transfers between devices  29.4 us (33%)
  waiting for transfers between devices  14.2 us (16%)
  local copies, waits for them, and re-layouts  2.8 us (3%)
    pallas_call x10, Pallas kernels, run(): made(*(pltpu.with_memory_space_constraint(value, spec.memory_space) if sp...  21.2 us
    pallas_call x3, Pallas kernels, droplets(): pl.pallas_call(deposit, name='deposit', grid=(count // step,), in_specs=[...  20.3 us
    all_to_all x1, starting transfers between devices, per_device(): speed = jnp.max(lax.all_to_all(speed, plane, 0, 0), axis=0)  11.5 us
    ppermute x6, starting transfers between devices, both_ways(): lax.ppermute(up, axis, [(i, (i + 1) % count) for i in range(count)])  9.41 us
    ppermute x6, waiting for transfers between devices, both_ways(): lax.ppermute(up, axis, [(i, (i + 1) % count) for i in range(count)])  6.02 us
    ppermute x6, starting transfers between devices, both_ways(): lax.ppermute(down, axis, [((i + 1) % count, i) for i in range(count)])  5.27 us
    ppermute x6, waiting for transfers between devices, both_ways(): lax.ppermute(down, axis, [((i + 1) % count, i) for i in range(count)])  5.2 us
    ppermute x1, starting transfers between devices, per_device(): other_speed = lax.ppermute(speed, 'gy_lo', [(0, 1), (1, 0)])  2.91 us
  transfers between devices with their start and end apart: 16, of which 8 were waited for; matrix products, arithmetic and copies ran while one was open for 2% of the time, Pallas kernels for 34%

profile of v8, /device:TPU:4, one launch (start us, length us, event | category | flops | bytes accessed | tf_op | source)
XLA Modules:
  0.0 89.4 jit_solution(9746028734176637675)
XLA Ops:
  0.6 1.9 %collective-permute-start.1 = (f32[5,16,8,128]{3,2,1,0:T(8,128)}, f32[5,16,8,128]{3,2,1,0:T(8,128)S(1)}, u32[]{:S(2)}, u32[]{:S(2)}) collective-permute-start(f32[5,16,8,128]{3,2,1,0:T(8,128)} %fields.1), channel_id=1, source_target_pairs={{0,4},{4,8},{8,12},{12,16},{16,20},{20,24},{24,28},{28,32},{32,36}... | collective-permute-start | bytes 983048 | tf_op jit(solution)/shard_map/ppermute | solution.py:726
  2.6 1.7 %collective-permute-start = (f32[5,16,8,128]{3,2,1,0:T(8,128)}, f32[5,16,8,128]{3,2,1,0:T(8,128)S(1)}, u32[]{:S(2)}, u32[]{:S(2)}) collective-permute-start(f32[5,16,8,128]{3,2,1,0:T(8,128)} %fields.1), channel_id=1, source_target_pairs={{4,0},{8,4},{12,8},{16,12},{20,16},{24,20},{28,24},{32,28},{36,32}... | collective-permute-start | bytes 983048 | tf_op jit(solution)/shard_map/ppermute | solution.py:725
  6.1 1.2 %copy.17.fall_depth = s32[8,16,8,1]{3,2,1,0:T(8,128)S(1)} copy(s32[8,16,8,1]{1,3,2,0:T(1,128)} %param.11) | data formatting | bytes 8192 | tf_op args[5]
  7.9 11.5 %all-to-all-start = ((f32[32,1,128]{2,1,0:T(1,128)}), f32[32,1,128]{2,1,0:T(1,128)S(1)}, u32[]{:S(2)}, u32[]{:S(2)}) async-start(f32[32,1,128]{2,1,0:T(1,128)} %broadcast_in_dim.3), calls=%async_computation | async-start | bytes 32768 | tf_op jit(solution)/shard_map/all_to_all | solution.py:813
  19.4 7.4 %deposit.3.rest_1_.rest_0_ = f32[6,9,3,8,128]{4,3,2,1,0:T(8,128)} custom-call(f32[8,16,8,128]{3,2,1,0:T(8,128)} %radius.5, f32[8,16,8,128]{3,2,1,0:T(8,128)} %weight.5, s32[8,16,8,128]{3,2,1,0:T(8,128)} %column.5, s32[16,8,128]{2,1,0:T(8,128)} %counts.2, s32[8,16,8,1]{3,2,1,0:T(8,128)S(1)} %copy.17.fall_depth), custom_call_target="tpu_custom_call" | custom-call | flops 600000000 | tf_op jit(solution)/shard_map/deposit/pallas_call | solution.py:767
  26.8 2.3 %all-to-all-done = f32[32,1,128]{2,1,0:T(1,128)S(1)} async-done(((f32[32,1,128]{2,1,0:T(1,128)}), f32[32,1,128]{2,1,0:T(1,128)S(1)}, u32[]{:S(2)}, u32[]{:S(2)}) %all-to-all-start) | async-done | bytes 16416 | tf_op jit(solution)/shard_map/all_to_all | solution.py:813
  30.4 1.4 %collective-permute-done.3.from_right = f32[16,8,128]{2,1,0:T(8,128)S(1)} collective-permute-done((f32[16,8,128]{2,1,0:T(8,128)S(1)}, f32[16,8,128]{2,1,0:T(8,128)S(1)}, u32[]{:S(2)}, u32[]{:S(2)}) %collective-permute-start.3) | collective-permute-done | bytes 65568 | tf_op jit(solution)/shard_map/ppermute | solution.py:725
  31.8 2.2 %collective-permute-done.4.from_left = f32[16,8,128]{2,1,0:T(8,128)S(1)} collective-permute-done((f32[16,8,128]{2,1,0:T(8,128)S(1)}, f32[16,8,128]{2,1,0:T(8,128)S(1)}, u32[]{:S(2)}, u32[]{:S(2)}) %collective-permute-start.4) | collective-permute-done | bytes 65568 | tf_op jit(solution)/shard_map/ppermute | solution.py:726
  34.9 2.7 %collective-permute-start.6 = (f32[62,8,128]{2,1,0:T(8,128)S(1)}, f32[62,8,128]{2,1,0:T(8,128)S(1)}, u32[]{:S(2)}, u32[]{:S(2)}) collective-permute-start(f32[62,8,128]{2,1,0:T(8,128)S(1)} %get-tuple-element.39), channel_id=1, source_target_pairs={{1,0},{2,1},{3,2},{0,3},{5,4},{6,5},{7,6},{4,7},{9,8},{10,9},{11,1... | collective-permute-start | bytes 761864 | tf_op jit(solution)/shard_map/ppermute | solution.py:725
  37.5 2.9 %collective-permute-start.5 = (f32[8,128]{1,0:T(8,128)S(1)}, f32[8,128]{1,0:T(8,128)S(1)}, u32[]{:S(2)}, u32[]{:S(2)}) collective-permute-start(f32[8,128]{1,0:T(8,128)S(1)} %get-tuple-element.36.speed), channel_id=1, source_target_pairs={{0,4},{4,0},{1,5},{5,1},{2,6},{6,2},{3,7},{7,3},{8,12},{12,8},{9,1... | collective-permute-start | bytes 12296 | tf_op jit(solution)/shard_map/ppermute | solution.py:815
  40.4 3.5 %deposit.4.rest_0_.rest_1_ = f32[2,9,3,8,128]{4,3,2,1,0:T(8,128)} custom-call(f32[8,16,8,128]{3,2,1,0:T(8,128)} %radius.5, f32[8,16,8,128]{3,2,1,0:T(8,128)} %weight.5, s32[8,16,8,128]{3,2,1,0:T(8,128)} %column.5, s32[16,8,128]{2,1,0:T(8,128)} %counts.2, s32[8,16,8,1]{3,2,1,0:T(8,128)S(1)} %copy.17.fall_depth), custom_call_target="tpu_custom_call" | custom-call | flops 200000000 | tf_op jit(solution)/shard_map/deposit/pallas_call | solution.py:767
  43.9 3.5 %first_own.1 = (f32[13,30,8,256]{3,2,1,0:T(8,128)S(1)}, f32[2,16,16,256]{3,2,1,0:T(8,128)S(1)}) custom-call(s32[2]{0:T(128)S(1)} %pad_add_fusion.place_ref, f32[5,16,8,128]{3,2,1,0:T(8,128)S(1)} %get-tuple-element.31.own.initial, f32[5,16,8,128]{3,2,1,0:T(8,128)S(1)} %collective-permute-done.above, f32[5,16,8,128]{3,2,1,0:T(8,128)S(1)} %collective-permute-done.1.below, ...), custom_call_target="tpu_custom_call" | custom-call | tf_op jit(solution)/shard_map/first_own/pallas_call | solution.py:710
  47.5 5.9 %two_sections.1 = (f32[13,30,8,256]{3,2,1,0:T(8,128)S(1)}, f32[5,16,8,128]{3,2,1,0:T(8,128)S(1)}, f32[3,16,8,128]{3,2,1,0:T(8,128)S(1)}, f32[3,16,8,128]{3,2,1,0:T(8,128)S(1)}, f32[1]{0:T(128)}) custom-call(s32[2]{0:T(128)S(1)} %pad_add_fusion.place_ref, f32[8,128]{1,0:T(8,128)S(1)} %get-tuple-element.36.speed, ...), custom_call_target="tpu_custom_call", output_to_operand_aliasing={{0}: (3, {})} | custom-call | tf_op jit(solution)/shard_map/two_sections/pallas_call | solution.py:710
  54.0 3.8 %collective-permute-start.9 = (f32[3,16,8,128]{3,2,1,0:T(8,128)S(1)}, f32[3,16,8,128]{3,2,1,0:T(8,128)S(1)}, u32[]{:S(2)}, u32[]{:S(2)}) collective-permute-start(f32[3,16,8,128]{3,2,1,0:T(8,128)S(1)} %get-tuple-element.45), channel_id=1, source_target_pairs={{0,4},{4,8},{8,12},{12,16},{16,20},{20,24},{24,28},{28,32},{32,36}... | collective-permute-start | bytes 589832 | tf_op jit(solution)/shard_map/ppermute | solution.py:726
  57.9 9.4 %deposit.5.rest_0_.rest_2_ = f32[8,9,3,8,128]{4,3,2,1,0:T(8,128)} custom-call(f32[8,16,8,128]{3,2,1,0:T(8,128)} %radius.5, f32[8,16,8,128]{3,2,1,0:T(8,128)} %weight.5, s32[8,16,8,128]{3,2,1,0:T(8,128)} %column.5, s32[16,8,128]{2,1,0:T(8,128)} %counts.2, s32[8,16,8,1]{3,2,1,0:T(8,128)S(1)} %copy.17.fall_depth), custom_call_target="tpu_custom_call" | custom-call | flops 800000000 | tf_op jit(solution)/shard_map/deposit/pallas_call | solution.py:767
  68.3 1.4 %collective-permute-done.10.from_right = f32[16,8,128]{2,1,0:T(8,128)S(1)} collective-permute-done((f32[16,8,128]{2,1,0:T(8,128)S(1)}, f32[16,8,128]{2,1,0:T(8,128)S(1)}, u32[]{:S(2)}, u32[]{:S(2)}) %collective-permute-start.10) | collective-permute-done | bytes 65568 | tf_op jit(solution)/shard_map/ppermute | solution.py:725
  69.7 2.5 %collective-permute-done.11.from_left = f32[16,8,128]{2,1,0:T(8,128)S(1)} collective-permute-done((f32[16,8,128]{2,1,0:T(8,128)S(1)}, f32[16,8,128]{2,1,0:T(8,128)S(1)}, u32[]{:S(2)}, u32[]{:S(2)}) %collective-permute-start.11) | collective-permute-done | bytes 65568 | tf_op jit(solution)/shard_map/ppermute | solution.py:726
  72.3 2.0 %collective-permute-start.13 = (f32[48,8,128]{2,1,0:T(8,128)S(1)}, f32[48,8,128]{2,1,0:T(8,128)S(1)}, u32[]{:S(2)}, u32[]{:S(2)}) collective-permute-start(f32[48,8,128]{2,1,0:T(8,128)S(1)} %get-tuple-element.53), channel_id=1, source_target_pairs={{0,1},{1,2},{2,3},{3,0},{4,5},{5,6},{6,7},{7,4},{8,9},{9,10},{10,1... | collective-permute-start | bytes 589832 | tf_op jit(solution)/shard_map/ppermute | solution.py:726
  74.3 2.4 %second_own.1 = (f32[11,30,8,256]{3,2,1,0:T(8,128)S(1)}, f32[1,16,16,256]{3,2,1,0:T(8,128)S(1)}, f32[16,8,128]{2,1,0:T(8,128)S(1)}) custom-call(f32[5,16,8,128]{3,2,1,0:T(8,128)S(1)} %get-tuple-element.43.own, f32[3,16,8,128]{3,2,1,0:T(8,128)S(1)} %collective-permute-done.8.above, f32[3,16,8,128]{3,2,1,0:T(8,128)S(1)} %collective-permute-done.9.below, ...), custom_call_target="tpu_custom_call" | custom-call | flops 1000000000 | tf_op jit(solution)/shard_map/second_own/pallas_call | solution.py:710
  76.8 2.4 %collective-permute-done.12.from_up = f32[48,8,128]{2,1,0:T(8,128)S(1)} collective-permute-done((f32[48,8,128]{2,1,0:T(8,128)S(1)}, f32[48,8,128]{2,1,0:T(8,128)S(1)}, u32[]{:S(2)}, u32[]{:S(2)}) %collective-permute-start.12) | collective-permute-done | bytes 196640 | tf_op jit(solution)/shard_map/ppermute | solution.py:725
  79.1 1.3 %collective-permute-done.13.from_down = f32[48,8,128]{2,1,0:T(8,128)S(1)} collective-permute-done((f32[48,8,128]{2,1,0:T(8,128)S(1)}, f32[48,8,128]{2,1,0:T(8,128)S(1)}, u32[]{:S(2)}, u32[]{:S(2)}) %collective-permute-start.13) | collective-permute-done | bytes 196640 | tf_op jit(solution)/shard_map/ppermute | solution.py:726
  80.4 3.1 %last_tracer.1 = (f32[11,30,8,256]{3,2,1,0:T(8,128)S(1)}, f32[16,8,128]{2,1,0:T(8,128)S(1)}, f32[3,16,8,128]{3,2,1,0:T(8,128)S(1)}, f32[3,8,8,128]{3,2,1,0:T(8,1...) custom-call(s32[2]{0:T(128)S(1)} %pad_add_fusion.place_ref, ...), custom_call_target="tpu_custom_call", output_to_operand_aliasing={{0}: (2, {})} | custom-call | tf_op jit(solution)/shard_map/last_tracer/pallas_call | solution.py:710
  83.8 3.8 %last_section.1 = f32[5,16,8,128]{3,2,1,0:T(8,128)} custom-call(s32[2]{0:T(128)S(1)} %pad_add_fusion.place_ref, f32[1]{0:T(128)} %get-tuple-element.42.dt_ref, f32[30,16,256]{2,1,0:T(8,128)S(1)} %get-tuple-element.54.rate, f32[30,16,256]{2,1,0:T(8,128)S(1)} %get-tuple-element.55.warm, f32[13,30,8,256]{3,2,1,0:T(8,128)S(1)} %get-tuple-element.56.start, ...), custom_call_target="tpu_custom_call" | custom-call | flops 1000000000 | tf_op jit(solution)/shard_map/last_section/pallas_call | solution.py:710
  88.2 1.2 %land.1 = f32[3,16,8,128]{3,2,1,0:T(8,128)} custom-call(s32[2]{0:T(128)S(1)} %pad_add_fusion.place_ref, f32[3,16,8,128]{3,2,1,0:T(8,128)S(1)} %get-tuple-element.58.landed, f32[3,8,8,128]{3,2,1,0:T(8,128)S(1)} %collective-permute-done.14.arrived), custom_call_target="tpu_custom_call" | custom-call | tf_op jit(solution)/shard_map/land/pallas_call | solution.py:710
  (30 shorter events, 7.4 us)
Async XLA Ops:
  0.6 28.5 %collective-permute-start.1 = (f32[5,16,8,128]{3,2,1,0:T(8,128)}, f32[5,16,8,128]{3,2,1,0:T(8,128)S(1)}, u32[]{:S(2)}, u32[]{:S(2)}) collective-permute-start(f32[5,16,8,128]{3,2,1,0:T(8,128)} %fields.1), channel_id=1, source_target_pairs={{0,4},{4,8},{8,12},{12,16},{16,20},{20,24},{24,28},{28,32},{32,36}... | collective-permute-start | bytes 983048 | tf_op jit(solution)/shard_map/ppermute | solution.py:726
  2.6 26.6 %collective-permute-start = (f32[5,16,8,128]{3,2,1,0:T(8,128)}, f32[5,16,8,128]{3,2,1,0:T(8,128)S(1)}, u32[]{:S(2)}, u32[]{:S(2)}) collective-permute-start(f32[5,16,8,128]{3,2,1,0:T(8,128)} %fields.1), channel_id=1, source_target_pairs={{4,0},{8,4},{12,8},{16,12},{20,16},{24,20},{28,24},{32,28},{36,32}... | collective-permute-start | bytes 983048 | tf_op jit(solution)/shard_map/ppermute | solution.py:725
  4.3 1.0 %copy-start = (f32[5,16,8,128]{3,2,1,0:T(8,128)S(1)}, f32[5,16,8,128]{3,2,1,0:T(8,128)}, u32[]{:S(2)}) copy-start(f32[5,16,8,128]{3,2,1,0:T(8,128)} %fields.1) | copy-start | bytes 983044
  6.0 1.3 %collective-permute-start.2 = (f32[8,128]{1,0:T(8,128)S(1)}, f32[8,128]{1,0:T(8,128)S(1)}, u32[]{:S(2)}, u32[]{:S(2)}) collective-permute-start(f32[8,128]{1,0:T(8,128)S(1)} %get-tuple-element.32), channel_id=1, source_target_pairs={{0,64},{64,0},{128,192},{192,128},{1,65},{65,1},{129,193},{193,129... | collective-permute-start | bytes 12296 | tf_op jit(solution)/shard_map/ppermute | solution.py:809
  7.9 21.2 %all-to-all-start = ((f32[32,1,128]{2,1,0:T(1,128)}), f32[32,1,128]{2,1,0:T(1,128)S(1)}, u32[]{:S(2)}, u32[]{:S(2)}) async-start(f32[32,1,128]{2,1,0:T(1,128)} %broadcast_in_dim.3), calls=%async_computation | async-start | bytes 32768 | tf_op jit(solution)/shard_map/all_to_all | solution.py:813
  29.8 2.0 %collective-permute-start.3 = (f32[16,8,128]{2,1,0:T(8,128)S(1)}, f32[16,8,128]{2,1,0:T(8,128)S(1)}, u32[]{:S(2)}, u32[]{:S(2)}) collective-permute-start(f32[16,8,128]{2,1,0:T(8,128)S(1)} %get-tuple-element.34), channel_id=1, source_target_pairs={{64,0},{128,64},{192,128},{0,192},{65,1},{129,65},{193,129},{1,193... | collective-permute-start | bytes 196616 | tf_op jit(solution)/shard_map/ppermute | solution.py:725
  29.9 4.1 %collective-permute-start.4 = (f32[16,8,128]{2,1,0:T(8,128)S(1)}, f32[16,8,128]{2,1,0:T(8,128)S(1)}, u32[]{:S(2)}, u32[]{:S(2)}) collective-permute-start(f32[16,8,128]{2,1,0:T(8,128)S(1)} %get-tuple-element.35), channel_id=1, source_target_pairs={{0,64},{64,128},{128,192},{192,0},{1,65},{65,129},{129,193},{193,1... | collective-permute-start | bytes 196616 | tf_op jit(solution)/shard_map/ppermute | solution.py:726
  34.2 13.2 %collective-permute-start.7 = (f32[62,8,128]{2,1,0:T(8,128)S(1)}, f32[62,8,128]{2,1,0:T(8,128)S(1)}, u32[]{:S(2)}, u32[]{:S(2)}) collective-permute-start(f32[62,8,128]{2,1,0:T(8,128)S(1)} %get-tuple-element.40), channel_id=1, source_target_pairs={{0,1},{1,2},{2,3},{3,0},{4,5},{5,6},{6,7},{7,4},{8,9},{9,10},{10,1... | collective-permute-start | bytes 761864 | tf_op jit(solution)/shard_map/ppermute | solution.py:726
  34.9 12.6 %collective-permute-start.6 = (f32[62,8,128]{2,1,0:T(8,128)S(1)}, f32[62,8,128]{2,1,0:T(8,128)S(1)}, u32[]{:S(2)}, u32[]{:S(2)}) collective-permute-start(f32[62,8,128]{2,1,0:T(8,128)S(1)} %get-tuple-element.39), channel_id=1, source_target_pairs={{1,0},{2,1},{3,2},{0,3},{5,4},{6,5},{7,6},{4,7},{9,8},{10,9},{11,1... | collective-permute-start | bytes 761864 | tf_op jit(solution)/shard_map/ppermute | solution.py:725
  37.5 9.9 %collective-permute-start.5 = (f32[8,128]{1,0:T(8,128)S(1)}, f32[8,128]{1,0:T(8,128)S(1)}, u32[]{:S(2)}, u32[]{:S(2)}) collective-permute-start(f32[8,128]{1,0:T(8,128)S(1)} %get-tuple-element.36.speed), channel_id=1, source_target_pairs={{0,4},{4,0},{1,5},{5,1},{2,6},{6,2},{3,7},{7,3},{8,12},{12,8},{9,1... | collective-permute-start | bytes 12296 | tf_op jit(solution)/shard_map/ppermute | solution.py:815
  53.4 13.9 %collective-permute-start.8 = (f32[3,16,8,128]{3,2,1,0:T(8,128)S(1)}, f32[3,16,8,128]{3,2,1,0:T(8,128)S(1)}, u32[]{:S(2)}, u32[]{:S(2)}) collective-permute-start(f32[3,16,8,128]{3,2,1,0:T(8,128)S(1)} %get-tuple-element.44), channel_id=1, source_target_pairs={{4,0},{8,4},{12,8},{16,12},{20,16},{24,20},{28,24},{32,28},{36,32}... | collective-permute-start | bytes 589832 | tf_op jit(solution)/shard_map/ppermute | solution.py:725
  54.0 13.2 %collective-permute-start.9 = (f32[3,16,8,128]{3,2,1,0:T(8,128)S(1)}, f32[3,16,8,128]{3,2,1,0:T(8,128)S(1)}, u32[]{:S(2)}, u32[]{:S(2)}) collective-permute-start(f32[3,16,8,128]{3,2,1,0:T(8,128)S(1)} %get-tuple-element.45), channel_id=1, source_target_pairs={{0,4},{4,8},{8,12},{12,16},{16,20},{20,24},{24,28},{28,32},{32,36}... | collective-permute-start | bytes 589832 | tf_op jit(solution)/shard_map/ppermute | solution.py:726
  67.7 2.0 %collective-permute-start.10 = (f32[16,8,128]{2,1,0:T(8,128)S(1)}, f32[16,8,128]{2,1,0:T(8,128)S(1)}, u32[]{:S(2)}, u32[]{:S(2)}) collective-permute-start(f32[16,8,128]{2,1,0:T(8,128)S(1)} %get-tuple-element.47), channel_id=1, source_target_pairs={{64,0},{128,64},{192,128},{0,192},{65,1},{129,65},{193,129},{1,193... | collective-permute-start | bytes 196616 | tf_op jit(solution)/shard_map/ppermute | solution.py:725
  67.8 4.4 %collective-permute-start.11 = (f32[16,8,128]{2,1,0:T(8,128)S(1)}, f32[16,8,128]{2,1,0:T(8,128)S(1)}, u32[]{:S(2)}, u32[]{:S(2)}) collective-permute-start(f32[16,8,128]{2,1,0:T(8,128)S(1)} %get-tuple-element.48), channel_id=1, source_target_pairs={{0,64},{64,128},{128,192},{192,0},{1,65},{65,129},{129,193},{193,1... | collective-permute-start | bytes 196616 | tf_op jit(solution)/shard_map/ppermute | solution.py:726
  72.2 6.9 %collective-permute-start.12 = (f32[48,8,128]{2,1,0:T(8,128)S(1)}, f32[48,8,128]{2,1,0:T(8,128)S(1)}, u32[]{:S(2)}, u32[]{:S(2)}) collective-permute-start(f32[48,8,128]{2,1,0:T(8,128)S(1)} %get-tuple-element.52), channel_id=1, source_target_pairs={{1,0},{2,1},{3,2},{0,3},{5,4},{6,5},{7,6},{4,7},{9,8},{10,9},{11,1... | collective-permute-start | bytes 589832 | tf_op jit(solution)/shard_map/ppermute | solution.py:725
  72.3 8.1 %collective-permute-start.13 = (f32[48,8,128]{2,1,0:T(8,128)S(1)}, f32[48,8,128]{2,1,0:T(8,128)S(1)}, u32[]{:S(2)}, u32[]{:S(2)}) collective-permute-start(f32[48,8,128]{2,1,0:T(8,128)S(1)} %get-tuple-element.53), channel_id=1, source_target_pairs={{0,1},{1,2},{2,3},{3,0},{4,5},{5,6},{6,7},{7,4},{8,9},{9,10},{10,1... | collective-permute-start | bytes 589832 | tf_op jit(solution)/shard_map/ppermute | solution.py:726
  83.5 4.7 %collective-permute-start.14 = (f32[3,8,8,128]{3,2,1,0:T(8,128)S(1)}, f32[3,8,8,128]{3,2,1,0:T(8,128)S(1)}, u32[]{:S(2)}, u32[]{:S(2)}) collective-permute-start(f32[3,8,8,128]{3,2,1,0:T(8,128)S(1)} %get-tuple-element.59), channel_id=1, source_target_pairs={{1,0},{2,1},{3,2},{0,3},{5,4},{6,5},{7,6},{4,7},{9,8},{10,9},{11,1... | collective-permute-start | bytes 294920 | tf_op jit(solution)/shard_map/ppermute | solution.py:871

commit v9 on v8

--- a/solution.py
+++ b/solution.py
@@ -117,7 +117,7 @@
         PR: [THREE] * 2 + [TWO] * 4 + [ONE],
         U: [TWO] * 3 + [ONE],
         V: [TWO] * 4,
-        W: [TWO] * 3 + [ONE] * 2,
+        W: [TWO] * 4 + [ONE],
     },
 )
 SECOND = Plan(
@@ -410,9 +410,23 @@
 
 
 def two_sections(
-    place_ref, speed, other_speed, start_in, flat, from_up, from_down, *rest
+    place_ref,
+    speed,
+    other_speed,
+    start_in,
+    flat,
+    from_up,
+    from_down,
+    start,
+    s2,
+    down,
+    up,
+    dt_out,
+    rate0,
+    s1,
+    rate1,
+    fast,
 ):
-    start, s2, down, up, dt_out, rate0, s1, rate1, fast = rest[-9:]
     place, last = place_ref[0], place_ref[1]
     place_halo(FIRST, from_up, from_down, start, place, last)
 
@@ -808,12 +822,11 @@
     pair = [(i, i ^ 1) for i in range(lax.axis_size("gx"))]
     speed = jnp.maximum(speed, lax.ppermute(speed, "gx", pair))
     plane = ("gy_hi", "gz")
-    early = drops(0, 6, speed)
+    early = drops(0, 8, speed)
     speed = jnp.broadcast_to(speed[0:1], (lax.axis_size(plane), 1, COLS))
     speed = jnp.max(lax.all_to_all(speed, plane, 0, 0), axis=0)
-    *near, from_up, from_down, sent, speed = exchange(FIRST, own, fields, fields, [early], speed)
+    *near, from_up, from_down, _, speed = exchange(FIRST, own, fields, fields, [early], speed)
     other_speed = lax.ppermute(speed, "gy_lo", [(0, 1), (1, 0)])
-    second = drops(6, 2, sent)
     ext = held(len(FIRST.tiles), DEPTH, ROWS, WIDE)
     start, flat = call(
         first_own,
@@ -824,7 +837,7 @@
     start, s2, down, up, dt = call(
         two_sections,
         "two_sections",
-        smem(1) + vmem(6) + far(1),
+        smem(1) + vmem(6),
         [ext, held(5, LEVELS, ROWS, COLS)] + [held(3, LEVELS, ROWS, COLS)] * 2 + [shaped(1)],
         scratch=[
             pltpu.VMEM((2, DEPTH, 2 * ROWS, WIDE), F32),
@@ -835,10 +848,10 @@
         out_specs=vmem(4) + smem(1),
         grant=12,
         alias={3: 0},
-    )(where, speed, other_speed, start, flat, from_up, from_down, second)
-    middle = drops(8, 8, s2)
-    *near, from_up, from_down, _ = exchange(SECOND, s2, down, up, [middle])
-    by_depth = [early, second, middle]
+    )(where, speed, other_speed, start, flat, from_up, from_down)
+    middle = drops(8, 6, s2)
+    *near, from_up, from_down, sent = exchange(SECOND, s2, down, up, [middle])
+    by_depth = [early, middle, drops(14, 2, sent)]
     ext = held(len(SECOND.tiles), DEPTH, ROWS, WIDE)
     around_s2, flat, flat_tracer = call(
         second_own,

time: 89.9 us -> 90.2 us (level); the launches traced: 89.4 us -> 88.6 us
  waiting for transfers between devices: 14.2 us -> 9.97 us
  starting transfers between devices: 29.4 us -> 32.7 us
    ppermute x6, starting transfers between devices: 5.27 us -> 13.1 us  [both_ways(): lax.ppermute(down, axis, [((i + 1) % count, i) for i in range(count)])]
    ppermute x6, starting transfers between devices: 9.41 us -> 4.21 us  [both_ways(): lax.ppermute(up, axis, [(i, (i + 1) % count) for i in range(count)])]
    all_to_all x1, waiting for transfers between devices: 2.28 us -> 0.3 us  [per_device(): speed = jnp.max(lax.all_to_all(speed, plane, 0, 0), axis=0)]
    ppermute x6, waiting for transfers between devices: 6.02 us -> 5.03 us  [both_ways(): lax.ppermute(up, axis, [(i, (i + 1) % count) for i in range(count)])]
  transfers between devices with their start and end apart: 16 -> 16, of which waited for: 8 -> 6; matrix products, arithmetic and copies ran while one was open for 2% -> 2% of each run, Pallas kernels for 34% -> 35%
where the time goes in v9:
time: 90.2 us; the launch traced here: 88.6 us
  Pallas kernels  42.2 us (47%)
  starting transfers between devices  32.7 us (36%)
  waiting for transfers between devices  9.97 us (11%)
  local copies, waits for them, and re-layouts  2.8 us (3%)
    pallas_call x10, Pallas kernels, run(): made(*(pltpu.with_memory_space_constraint(value, spec.memory_space) if sp...  21.2 us
    pallas_call x3, Pallas kernels, droplets(): pl.pallas_call(deposit, name='deposit', grid=(count // step,), in_specs=[...  20.3 us
    ppermute x6, starting transfers between devices, both_ways(): lax.ppermute(down, axis, [((i + 1) % count, i) for i in range(count)])  13.1 us
    all_to_all x1, starting transfers between devices, per_device(): speed = jnp.max(lax.all_to_all(speed, plane, 0, 0), axis=0)  11.5 us
    ppermute x6, waiting for transfers between devices, both_ways(): lax.ppermute(up, axis, [(i, (i + 1) % count) for i in range(count)])  5.03 us
    ppermute x6, waiting for transfers between devices, both_ways(): lax.ppermute(down, axis, [((i + 1) % count, i) for i in range(count)])  4.64 us
    ppermute x6, starting transfers between devices, both_ways(): lax.ppermute(up, axis, [(i, (i + 1) % count) for i in range(count)])  4.21 us
    ppermute x1, starting transfers between devices, per_device(): other_speed = lax.ppermute(speed, 'gy_lo', [(0, 1), (1, 0)])  2.83 us
  transfers between devices with their start and end apart: 16, of which 6 were waited for; matrix products, arithmetic and copies ran while one was open for 2% of the time, Pallas kernels for 35%

profile of v9, /device:TPU:4, one launch (start us, length us, event | category | flops | bytes accessed | tf_op | source)
XLA Modules:
  0.0 88.6 jit_solution(14399577387559338288)
XLA Ops:
  0.6 1.9 %collective-permute-start.1 = (f32[5,16,8,128]{3,2,1,0:T(8,128)}, f32[5,16,8,128]{3,2,1,0:T(8,128)S(1)}, u32[]{:S(2)}, u32[]{:S(2)}) collective-permute-start(f32[5,16,8,128]{3,2,1,0:T(8,128)} %fields.1), channel_id=1, source_target_pairs={{0,4},{4,8},{8,12},{12,16},{16,20},{20,24},{24,28},{28,32},{32,36}... | collective-permute-start | bytes 983048 | tf_op jit(solution)/shard_map/ppermute | solution.py:740
  2.6 1.7 %collective-permute-start = (f32[5,16,8,128]{3,2,1,0:T(8,128)}, f32[5,16,8,128]{3,2,1,0:T(8,128)S(1)}, u32[]{:S(2)}, u32[]{:S(2)}) collective-permute-start(f32[5,16,8,128]{3,2,1,0:T(8,128)} %fields.1), channel_id=1, source_target_pairs={{4,0},{8,4},{12,8},{16,12},{20,16},{24,20},{28,24},{32,28},{36,32}... | collective-permute-start | bytes 983048 | tf_op jit(solution)/shard_map/ppermute | solution.py:739
  6.1 1.2 %copy.17.fall_depth = s32[8,16,8,1]{3,2,1,0:T(8,128)S(1)} copy(s32[8,16,8,1]{1,3,2,0:T(1,128)} %param.11) | data formatting | bytes 8192 | tf_op args[5]
  7.9 11.5 %all-to-all-start = ((f32[32,1,128]{2,1,0:T(1,128)}), f32[32,1,128]{2,1,0:T(1,128)S(1)}, u32[]{:S(2)}, u32[]{:S(2)}) async-start(f32[32,1,128]{2,1,0:T(1,128)} %broadcast_in_dim.3), calls=%async_computation | async-start | bytes 32768 | tf_op jit(solution)/shard_map/all_to_all | solution.py:827
  19.4 9.4 %deposit.3.rest_1_.rest_0_ = f32[8,9,3,8,128]{4,3,2,1,0:T(8,128)} custom-call(f32[8,16,8,128]{3,2,1,0:T(8,128)} %radius.5, f32[8,16,8,128]{3,2,1,0:T(8,128)} %weight.5, s32[8,16,8,128]{3,2,1,0:T(8,128)} %column.5, s32[16,8,128]{2,1,0:T(8,128)} %counts.2, s32[8,16,8,1]{3,2,1,0:T(8,128)S(1)} %copy.17.fall_depth), custom_call_target="tpu_custom_call" | custom-call | flops 800000000 | tf_op jit(solution)/shard_map/deposit/pallas_call | solution.py:781
  30.6 2.2 %collective-permute-done.3.from_right = f32[16,8,128]{2,1,0:T(8,128)S(1)} collective-permute-done((f32[16,8,128]{2,1,0:T(8,128)S(1)}, f32[16,8,128]{2,1,0:T(8,128)S(1)}, u32[]{:S(2)}, u32[]{:S(2)}) %collective-permute-start.3) | collective-permute-done | bytes 65568 | tf_op jit(solution)/shard_map/ppermute | solution.py:739
  32.9 1.5 %collective-permute-done.4.from_left = f32[16,8,128]{2,1,0:T(8,128)S(1)} collective-permute-done((f32[16,8,128]{2,1,0:T(8,128)S(1)}, f32[16,8,128]{2,1,0:T(8,128)S(1)}, u32[]{:S(2)}, u32[]{:S(2)}) %collective-permute-start.4) | collective-permute-done | bytes 65568 | tf_op jit(solution)/shard_map/ppermute | solution.py:740
  34.5 2.8 %collective-permute-start.6 = (f32[63,8,128]{2,1,0:T(8,128)S(1)}, f32[63,8,128]{2,1,0:T(8,128)S(1)}, u32[]{:S(2)}, u32[]{:S(2)}) collective-permute-start(f32[63,8,128]{2,1,0:T(8,128)S(1)} %get-tuple-element.39), channel_id=1, source_target_pairs={{1,0},{2,1},{3,2},{0,3},{5,4},{6,5},{7,6},{4,7},{9,8},{10,9},{11,1... | collective-permute-start | bytes 774152 | tf_op jit(solution)/shard_map/ppermute | solution.py:739
  37.4 2.8 %collective-permute-start.5 = (f32[8,128]{1,0:T(8,128)S(1)}, f32[8,128]{1,0:T(8,128)S(1)}, u32[]{:S(2)}, u32[]{:S(2)}) collective-permute-start(f32[8,128]{1,0:T(8,128)S(1)} %get-tuple-element.36.speed), channel_id=1, source_target_pairs={{0,4},{4,0},{1,5},{5,1},{2,6},{6,2},{3,7},{7,3},{8,12},{12,8},{9,1... | collective-permute-start | bytes 12296 | tf_op jit(solution)/shard_map/ppermute | solution.py:829
  40.2 3.5 %first_own.1 = (f32[13,30,8,256]{3,2,1,0:T(8,128)S(1)}, f32[2,16,16,256]{3,2,1,0:T(8,128)S(1)}) custom-call(s32[2]{0:T(128)S(1)} %pad_add_fusion.place_ref, f32[5,16,8,128]{3,2,1,0:T(8,128)S(1)} %get-tuple-element.31.own.initial, f32[5,16,8,128]{3,2,1,0:T(8,128)S(1)} %collective-permute-done.above, f32[5,16,8,128]{3,2,1,0:T(8,128)S(1)} %collective-permute-done.1.below, ...), custom_call_target="tpu_custom_call" | custom-call | tf_op jit(solution)/shard_map/first_own/pallas_call | solution.py:724
  43.7 2.2 %collective-permute-done.7.from_down = f32[63,8,128]{2,1,0:T(8,128)S(1)} collective-permute-done((f32[63,8,128]{2,1,0:T(8,128)S(1)}, f32[63,8,128]{2,1,0:T(8,128)S(1)}, u32[]{:S(2)}, u32[]{:S(2)}) %collective-permute-start.7) | collective-permute-done | bytes 258080 | tf_op jit(solution)/shard_map/ppermute | solution.py:740
  45.9 6.0 %two_sections.1 = (f32[13,30,8,256]{3,2,1,0:T(8,128)S(1)}, f32[5,16,8,128]{3,2,1,0:T(8,128)S(1)}, f32[3,16,8,128]{3,2,1,0:T(8,128)S(1)}, f32[3,16,8,128]{3,2,1,0:T(8,128)S(1)}, f32[1]{0:T(128)}) custom-call(s32[2]{0:T(128)S(1)} %pad_add_fusion.place_ref, f32[8,128]{1,0:T(8,128)S(1)} %get-tuple-element.36.speed, ...), custom_call_target="tpu_custom_call", output_to_operand_aliasing={{0}: (3, {})} | custom-call | tf_op jit(solution)/shard_map/two_sections/pallas_call | solution.py:724
  51.9 2.3 %collective-permute-start.8 = (f32[3,16,8,128]{3,2,1,0:T(8,128)S(1)}, f32[3,16,8,128]{3,2,1,0:T(8,128)S(1)}, u32[]{:S(2)}, u32[]{:S(2)}) collective-permute-start(f32[3,16,8,128]{3,2,1,0:T(8,128)S(1)} %get-tuple-element.43), channel_id=1, source_target_pairs={{4,0},{8,4},{12,8},{16,12},{20,16},{24,20},{28,24},{32,28},{36,32}... | collective-permute-start | bytes 589832 | tf_op jit(solution)/shard_map/ppermute | solution.py:739
  54.2 2.2 %collective-permute-start.9 = (f32[3,16,8,128]{3,2,1,0:T(8,128)S(1)}, f32[3,16,8,128]{3,2,1,0:T(8,128)S(1)}, u32[]{:S(2)}, u32[]{:S(2)}) collective-permute-start(f32[3,16,8,128]{3,2,1,0:T(8,128)S(1)} %get-tuple-element.44), channel_id=1, source_target_pairs={{0,4},{4,8},{8,12},{12,16},{16,20},{20,24},{24,28},{28,32},{32,36}... | collective-permute-start | bytes 589832 | tf_op jit(solution)/shard_map/ppermute | solution.py:740
  56.4 7.4 %deposit.4.rest_0_.rest_1_ = f32[6,9,3,8,128]{4,3,2,1,0:T(8,128)} custom-call(f32[8,16,8,128]{3,2,1,0:T(8,128)} %radius.5, f32[8,16,8,128]{3,2,1,0:T(8,128)} %weight.5, s32[8,16,8,128]{3,2,1,0:T(8,128)} %column.5, s32[16,8,128]{2,1,0:T(8,128)} %counts.2, s32[8,16,8,1]{3,2,1,0:T(8,128)S(1)} %copy.17.fall_depth), custom_call_target="tpu_custom_call" | custom-call | flops 600000000 | tf_op jit(solution)/shard_map/deposit/pallas_call | solution.py:781
  64.3 2.3 %collective-permute-start.10 = (f32[16,8,128]{2,1,0:T(8,128)S(1)}, f32[16,8,128]{2,1,0:T(8,128)S(1)}, u32[]{:S(2)}, u32[]{:S(2)}) collective-permute-start(f32[16,8,128]{2,1,0:T(8,128)S(1)} %get-tuple-element.46), channel_id=1, source_target_pairs={{64,0},{128,64},{192,128},{0,192},{65,1},{129,65},{193,129},{1,193... | collective-permute-start | bytes 196616 | tf_op jit(solution)/shard_map/ppermute | solution.py:739
  66.6 2.4 %collective-permute-done.10.from_right = f32[16,8,128]{2,1,0:T(8,128)S(1)} collective-permute-done((f32[16,8,128]{2,1,0:T(8,128)S(1)}, f32[16,8,128]{2,1,0:T(8,128)S(1)}, u32[]{:S(2)}, u32[]{:S(2)}) %collective-permute-start.10) | collective-permute-done | bytes 65568 | tf_op jit(solution)/shard_map/ppermute | solution.py:739
  69.0 1.3 %collective-permute-done.11.from_left = f32[16,8,128]{2,1,0:T(8,128)S(1)} collective-permute-done((f32[16,8,128]{2,1,0:T(8,128)S(1)}, f32[16,8,128]{2,1,0:T(8,128)S(1)}, u32[]{:S(2)}, u32[]{:S(2)}) %collective-permute-start.11) | collective-permute-done | bytes 65568 | tf_op jit(solution)/shard_map/ppermute | solution.py:740
  70.4 3.2 %collective-permute-start.12 = (f32[48,8,128]{2,1,0:T(8,128)S(1)}, f32[48,8,128]{2,1,0:T(8,128)S(1)}, u32[]{:S(2)}, u32[]{:S(2)}) collective-permute-start(f32[48,8,128]{2,1,0:T(8,128)S(1)} %get-tuple-element.51), channel_id=1, source_target_pairs={{1,0},{2,1},{3,2},{0,3},{5,4},{6,5},{7,6},{4,7},{9,8},{10,9},{11,1... | collective-permute-start | bytes 589832 | tf_op jit(solution)/shard_map/ppermute | solution.py:739
  73.6 3.5 %deposit.5.rest_2_ = f32[2,9,3,8,128]{4,3,2,1,0:T(8,128)} custom-call(f32[8,16,8,128]{3,2,1,0:T(8,128)} %radius.5, f32[8,16,8,128]{3,2,1,0:T(8,128)} %weight.5, s32[8,16,8,128]{3,2,1,0:T(8,128)} %column.5, s32[16,8,128]{2,1,0:T(8,128)} %counts.2, s32[8,16,8,1]{3,2,1,0:T(8,128)S(1)} %copy.17.fall_depth), custom_call_target="tpu_custom_call" | custom-call | flops 200000000 | tf_op jit(solution)/shard_map/deposit/pallas_call | solution.py:781
  77.1 2.4 %second_own.1 = (f32[11,30,8,256]{3,2,1,0:T(8,128)S(1)}, f32[1,16,16,256]{3,2,1,0:T(8,128)S(1)}, f32[16,8,128]{2,1,0:T(8,128)S(1)}) custom-call(f32[5,16,8,128]{3,2,1,0:T(8,128)S(1)} %get-tuple-element.42.own, f32[3,16,8,128]{3,2,1,0:T(8,128)S(1)} %collective-permute-done.8.above, f32[3,16,8,128]{3,2,1,0:T(8,128)S(1)} %collective-permute-done.9.below, ...), custom_call_target="tpu_custom_call" | custom-call | flops 1000000000 | tf_op jit(solution)/shard_map/second_own/pallas_call | solution.py:724
  79.5 3.0 %last_tracer.1 = (f32[11,30,8,256]{3,2,1,0:T(8,128)S(1)}, f32[16,8,128]{2,1,0:T(8,128)S(1)}, f32[3,16,8,128]{3,2,1,0:T(8,128)S(1)}, f32[3,8,8,128]{3,2,1,0:T(8,1...) custom-call(s32[2]{0:T(128)S(1)} %pad_add_fusion.place_ref, ...), custom_call_target="tpu_custom_call", output_to_operand_aliasing={{0}: (2, {})} | custom-call | tf_op jit(solution)/shard_map/last_tracer/pallas_call | solution.py:724
  83.6 3.8 %last_section.1 = f32[5,16,8,128]{3,2,1,0:T(8,128)} custom-call(s32[2]{0:T(128)S(1)} %pad_add_fusion.place_ref, f32[1]{0:T(128)} %get-tuple-element.41.dt_ref, f32[30,16,256]{2,1,0:T(8,128)S(1)} %get-tuple-element.54.rate, f32[30,16,256]{2,1,0:T(8,128)S(1)} %get-tuple-element.55.warm, f32[13,30,8,256]{3,2,1,0:T(8,128)S(1)} %get-tuple-element.56.start, ...), custom_call_target="tpu_custom_call" | custom-call | flops 1000000000 | tf_op jit(solution)/shard_map/last_section/pallas_call | solution.py:724
  87.3 1.2 %land.1 = f32[3,16,8,128]{3,2,1,0:T(8,128)} custom-call(s32[2]{0:T(128)S(1)} %pad_add_fusion.place_ref, f32[3,16,8,128]{3,2,1,0:T(8,128)S(1)} %get-tuple-element.58.landed, f32[3,8,8,128]{3,2,1,0:T(8,128)S(1)} %collective-permute-done.14.arrived), custom_call_target="tpu_custom_call" | custom-call | tf_op jit(solution)/shard_map/land/pallas_call | solution.py:724
  (30 shorter events, 6.0 us)
Async XLA Ops:
  0.6 28.5 %collective-permute-start.1 = (f32[5,16,8,128]{3,2,1,0:T(8,128)}, f32[5,16,8,128]{3,2,1,0:T(8,128)S(1)}, u32[]{:S(2)}, u32[]{:S(2)}) collective-permute-start(f32[5,16,8,128]{3,2,1,0:T(8,128)} %fields.1), channel_id=1, source_target_pairs={{0,4},{4,8},{8,12},{12,16},{16,20},{20,24},{24,28},{28,32},{32,36}... | collective-permute-start | bytes 983048 | tf_op jit(solution)/shard_map/ppermute | solution.py:740
  2.6 26.6 %collective-permute-start = (f32[5,16,8,128]{3,2,1,0:T(8,128)}, f32[5,16,8,128]{3,2,1,0:T(8,128)S(1)}, u32[]{:S(2)}, u32[]{:S(2)}) collective-permute-start(f32[5,16,8,128]{3,2,1,0:T(8,128)} %fields.1), channel_id=1, source_target_pairs={{4,0},{8,4},{12,8},{16,12},{20,16},{24,20},{28,24},{32,28},{36,32}... | collective-permute-start | bytes 983048 | tf_op jit(solution)/shard_map/ppermute | solution.py:739
  4.3 1.0 %copy-start = (f32[5,16,8,128]{3,2,1,0:T(8,128)S(1)}, f32[5,16,8,128]{3,2,1,0:T(8,128)}, u32[]{:S(2)}) copy-start(f32[5,16,8,128]{3,2,1,0:T(8,128)} %fields.1) | copy-start | bytes 983044
  6.0 1.3 %collective-permute-start.2 = (f32[8,128]{1,0:T(8,128)S(1)}, f32[8,128]{1,0:T(8,128)S(1)}, u32[]{:S(2)}, u32[]{:S(2)}) collective-permute-start(f32[8,128]{1,0:T(8,128)S(1)} %get-tuple-element.32), channel_id=1, source_target_pairs={{0,64},{64,0},{128,192},{192,128},{1,65},{65,1},{129,193},{193,129... | collective-permute-start | bytes 12296 | tf_op jit(solution)/shard_map/ppermute | solution.py:823
  7.9 21.2 %all-to-all-start = ((f32[32,1,128]{2,1,0:T(1,128)}), f32[32,1,128]{2,1,0:T(1,128)S(1)}, u32[]{:S(2)}, u32[]{:S(2)}) async-start(f32[32,1,128]{2,1,0:T(1,128)} %broadcast_in_dim.3), calls=%async_computation | async-start | bytes 32768 | tf_op jit(solution)/shard_map/all_to_all | solution.py:827
  29.8 3.0 %collective-permute-start.3 = (f32[16,8,128]{2,1,0:T(8,128)S(1)}, f32[16,8,128]{2,1,0:T(8,128)S(1)}, u32[]{:S(2)}, u32[]{:S(2)}) collective-permute-start(f32[16,8,128]{2,1,0:T(8,128)S(1)} %get-tuple-element.34), channel_id=1, source_target_pairs={{64,0},{128,64},{192,128},{0,192},{65,1},{129,65},{193,129},{1,193... | collective-permute-start | bytes 196616 | tf_op jit(solution)/shard_map/ppermute | solution.py:739
  30.6 3.8 %collective-permute-start.4 = (f32[16,8,128]{2,1,0:T(8,128)S(1)}, f32[16,8,128]{2,1,0:T(8,128)S(1)}, u32[]{:S(2)}, u32[]{:S(2)}) collective-permute-start(f32[16,8,128]{2,1,0:T(8,128)S(1)} %get-tuple-element.35), channel_id=1, source_target_pairs={{0,64},{64,128},{128,192},{192,0},{1,65},{65,129},{129,193},{193,1... | collective-permute-start | bytes 196616 | tf_op jit(solution)/shard_map/ppermute | solution.py:740
  34.5 9.1 %collective-permute-start.6 = (f32[63,8,128]{2,1,0:T(8,128)S(1)}, f32[63,8,128]{2,1,0:T(8,128)S(1)}, u32[]{:S(2)}, u32[]{:S(2)}) collective-permute-start(f32[63,8,128]{2,1,0:T(8,128)S(1)} %get-tuple-element.39), channel_id=1, source_target_pairs={{1,0},{2,1},{3,2},{0,3},{5,4},{6,5},{7,6},{4,7},{9,8},{10,9},{11,1... | collective-permute-start | bytes 774152 | tf_op jit(solution)/shard_map/ppermute | solution.py:739
  37.3 8.5 %collective-permute-start.7 = (f32[63,8,128]{2,1,0:T(8,128)S(1)}, f32[63,8,128]{2,1,0:T(8,128)S(1)}, u32[]{:S(2)}, u32[]{:S(2)}) collective-permute-start(f32[63,8,128]{2,1,0:T(8,128)S(1)} %get-tuple-element.40), channel_id=1, source_target_pairs={{0,1},{1,2},{2,3},{3,0},{4,5},{5,6},{6,7},{7,4},{8,9},{9,10},{10,1... | collective-permute-start | bytes 774152 | tf_op jit(solution)/shard_map/ppermute | solution.py:740
  37.4 6.3 %collective-permute-start.5 = (f32[8,128]{1,0:T(8,128)S(1)}, f32[8,128]{1,0:T(8,128)S(1)}, u32[]{:S(2)}, u32[]{:S(2)}) collective-permute-start(f32[8,128]{1,0:T(8,128)S(1)} %get-tuple-element.36.speed), channel_id=1, source_target_pairs={{0,4},{4,0},{1,5},{5,1},{2,6},{6,2},{3,7},{7,3},{8,12},{12,8},{9,1... | collective-permute-start | bytes 12296 | tf_op jit(solution)/shard_map/ppermute | solution.py:829
  51.9 11.9 %collective-permute-start.8 = (f32[3,16,8,128]{3,2,1,0:T(8,128)S(1)}, f32[3,16,8,128]{3,2,1,0:T(8,128)S(1)}, u32[]{:S(2)}, u32[]{:S(2)}) collective-permute-start(f32[3,16,8,128]{3,2,1,0:T(8,128)S(1)} %get-tuple-element.43), channel_id=1, source_target_pairs={{4,0},{8,4},{12,8},{16,12},{20,16},{24,20},{28,24},{32,28},{36,32}... | collective-permute-start | bytes 589832 | tf_op jit(solution)/shard_map/ppermute | solution.py:739
  54.2 9.6 %collective-permute-start.9 = (f32[3,16,8,128]{3,2,1,0:T(8,128)S(1)}, f32[3,16,8,128]{3,2,1,0:T(8,128)S(1)}, u32[]{:S(2)}, u32[]{:S(2)}) collective-permute-start(f32[3,16,8,128]{3,2,1,0:T(8,128)S(1)} %get-tuple-element.44), channel_id=1, source_target_pairs={{0,4},{4,8},{8,12},{12,16},{16,20},{20,24},{24,28},{28,32},{32,36}... | collective-permute-start | bytes 589832 | tf_op jit(solution)/shard_map/ppermute | solution.py:740
  64.3 4.7 %collective-permute-start.10 = (f32[16,8,128]{2,1,0:T(8,128)S(1)}, f32[16,8,128]{2,1,0:T(8,128)S(1)}, u32[]{:S(2)}, u32[]{:S(2)}) collective-permute-start(f32[16,8,128]{2,1,0:T(8,128)S(1)} %get-tuple-element.46), channel_id=1, source_target_pairs={{64,0},{128,64},{192,128},{0,192},{65,1},{129,65},{193,129},{1,193... | collective-permute-start | bytes 196616 | tf_op jit(solution)/shard_map/ppermute | solution.py:739
  66.6 3.7 %collective-permute-start.11 = (f32[16,8,128]{2,1,0:T(8,128)S(1)}, f32[16,8,128]{2,1,0:T(8,128)S(1)}, u32[]{:S(2)}, u32[]{:S(2)}) collective-permute-start(f32[16,8,128]{2,1,0:T(8,128)S(1)} %get-tuple-element.47), channel_id=1, source_target_pairs={{0,64},{64,128},{128,192},{192,0},{1,65},{65,129},{129,193},{193,1... | collective-permute-start | bytes 196616 | tf_op jit(solution)/shard_map/ppermute | solution.py:740
  70.3 9.2 %collective-permute-start.13 = (f32[48,8,128]{2,1,0:T(8,128)S(1)}, f32[48,8,128]{2,1,0:T(8,128)S(1)}, u32[]{:S(2)}, u32[]{:S(2)}) collective-permute-start(f32[48,8,128]{2,1,0:T(8,128)S(1)} %get-tuple-element.52), channel_id=1, source_target_pairs={{0,1},{1,2},{2,3},{3,0},{4,5},{5,6},{6,7},{7,4},{8,9},{9,10},{10,1... | collective-permute-start | bytes 589832 | tf_op jit(solution)/shard_map/ppermute | solution.py:740
  70.4 9.1 %collective-permute-start.12 = (f32[48,8,128]{2,1,0:T(8,128)S(1)}, f32[48,8,128]{2,1,0:T(8,128)S(1)}, u32[]{:S(2)}, u32[]{:S(2)}) collective-permute-start(f32[48,8,128]{2,1,0:T(8,128)S(1)} %get-tuple-element.51), channel_id=1, source_target_pairs={{1,0},{2,1},{3,2},{0,3},{5,4},{6,5},{7,6},{4,7},{9,8},{10,9},{11,1... | collective-permute-start | bytes 589832 | tf_op jit(solution)/shard_map/ppermute | solution.py:739
  82.6 4.8 %collective-permute-start.14 = (f32[3,8,8,128]{3,2,1,0:T(8,128)S(1)}, f32[3,8,8,128]{3,2,1,0:T(8,128)S(1)}, u32[]{:S(2)}, u32[]{:S(2)}) collective-permute-start(f32[3,8,8,128]{3,2,1,0:T(8,128)S(1)} %get-tuple-element.59), channel_id=1, source_target_pairs={{1,0},{2,1},{3,2},{0,3},{5,4},{6,5},{7,6},{4,7},{9,8},{10,9},{11,1... | collective-permute-start | bytes 294920 | tf_op jit(solution)/shard_map/ppermute | solution.py:884

commit v10 on v9

--- a/solution.py
+++ b/solution.py
@@ -762,16 +762,24 @@
     return above, below, from_right, from_left, from_up, from_down, to_down, *speeds
 
 
-def prepare(place_ref, fields, own, speed):
-    own[...] = fields[...]
+def prepare(place_ref, fields, speed, winds, sem):
+    copy = pltpu.make_async_copy(fields.at[pl.ds(U, 3)], winds, sem)
+    copy.start()
+    copy.wait()
     keep = jnp.where(place_ref[0] == place_ref[1], 0.0, 1.0).astype(F32)
     most = jnp.zeros((ROWS, COLS), F32)
     for k in range(LEVELS):
-        w = jnp.abs(fields[W, k])
+        w = jnp.abs(winds[2, k])
         if k == LEVELS - 1:
             w = w * keep
-        most = jnp.maximum(most, jnp.abs(fields[U, k]) + jnp.abs(fields[V, k]) + w)
+        most = jnp.maximum(most, jnp.abs(winds[0, k]) + jnp.abs(winds[1, k]) + w)
     speed[...] = jnp.broadcast_to(jnp.max(most), speed.shape)
+
+
+def hold(fields, own, sem):
+    copy = pltpu.make_async_copy(fields, own, sem)
+    copy.start()
+    copy.wait()
 
 
 def droplets(radius, weight, column, counts, fall_depth, first, count, after):
@@ -811,19 +819,24 @@
     def drops(first, count, after):
         return droplets(radius, weight, column, counts, fall_depth, first, count, after)
 
-    own, speed = pl.pallas_call(
+    plane = ("gy_hi", "gz")
+    (speed,) = call(
         prepare,
-        name="prepare",
-        in_specs=smem(1) + vmem(1),
-        out_specs=tuple(vmem(2)),
-        out_shape=(held(5, LEVELS, ROWS, COLS), shaped(ROWS, COLS)),
-        compiler_params=pltpu.CompilerParams(vmem_limit_bytes=4 << 20),
+        "prepare",
+        smem(1) + far(1),
+        [shaped(lax.axis_size(plane), 1, COLS)],
+        scratch=[pltpu.VMEM((3, LEVELS, ROWS, COLS), F32), pltpu.SemaphoreType.DMA],
     )(where, fields)
     pair = [(i, i ^ 1) for i in range(lax.axis_size("gx"))]
     speed = jnp.maximum(speed, lax.ppermute(speed, "gx", pair))
-    plane = ("gy_hi", "gz")
-    early = drops(0, 8, speed)
-    speed = jnp.broadcast_to(speed[0:1], (lax.axis_size(plane), 1, COLS))
+    (own,) = call(
+        hold,
+        "hold",
+        far(1),
+        [held(5, LEVELS, ROWS, COLS)],
+        scratch=[pltpu.SemaphoreType.DMA],
+    )(lax.optimization_barrier((fields, speed))[0])
+    early = drops(0, 8, own)
     speed = jnp.max(lax.all_to_all(speed, plane, 0, 0), axis=0)
     *near, from_up, from_down, _, speed = exchange(FIRST, own, fields, fields, [early], speed)
     other_speed = lax.ppermute(speed, "gy_lo", [(0, 1), (1, 0)])

time: 90.2 us -> 91.2 us (1.011)
  Pallas kernels: 42.2 us -> 44.1 us
  local copies, waits for them, and re-layouts: 2.8 us -> 1.21 us
    pallas_call x10 -> x12, Pallas kernels: 21.2 us -> 23.8 us  [run(): made(*(pltpu.with_memory_space_constraint(value, spec.memory_space) if sp...]
    unnamed x3 -> x1, local copies, waits for them, and re-layouts: 2.18 us -> 1.21 us
  transfers between devices with their start and end apart: 16 -> 16, of which waited for: 6 -> 5; matrix products, arithmetic and copies ran while one was open for 2% -> 2% of each run, Pallas kernels for 35% -> 36%
where the time goes in v10:
time: 91.2 us; the launch traced here: 89.6 us
  Pallas kernels  44.1 us (48%)
  starting transfers between devices  33 us (36%)
  waiting for transfers between devices  9.67 us (11%)
  local copies, waits for them, and re-layouts  1.21 us (1%)
    pallas_call x12, Pallas kernels, run(): made(*(pltpu.with_memory_space_constraint(value, spec.memory_space) if sp...  23.8 us
    pallas_call x3, Pallas kernels, droplets(): pl.pallas_call(deposit, name='deposit', grid=(count // step,), in_specs=[...  20.3 us
    ppermute x6, starting transfers between devices, both_ways(): lax.ppermute(down, axis, [((i + 1) % count, i) for i in range(count)])  13.4 us
    all_to_all x1, starting transfers between devices, per_device(): speed = jnp.max(lax.all_to_all(speed, plane, 0, 0), axis=0)  11.5 us
    ppermute x6, waiting for transfers between devices, both_ways(): lax.ppermute(up, axis, [(i, (i + 1) % count) for i in range(count)])  5.03 us
    ppermute x6, waiting for transfers between devices, both_ways(): lax.ppermute(down, axis, [((i + 1) % count, i) for i in range(count)])  4.63 us
    ppermute x6, starting transfers between devices, both_ways(): lax.ppermute(up, axis, [(i, (i + 1) % count) for i in range(count)])  4.21 us
    ppermute x1, starting transfers between devices, per_device(): other_speed = lax.ppermute(speed, 'gy_lo', [(0, 1), (1, 0)])  2.83 us
  transfers between devices with their start and end apart: 16, of which 5 were waited for; matrix products, arithmetic and copies ran while one was open for 2% of the time, Pallas kernels for 36%

profile of v10, /device:TPU:4, one launch (start us, length us, event | category | flops | bytes accessed | tf_op | source)
XLA Modules:
  0.0 89.6 jit_solution(15185688182457948383)
XLA Ops:
  0.6 1.9 %collective-permute-start.2 = (f32[5,16,8,128]{3,2,1,0:T(8,128)}, f32[5,16,8,128]{3,2,1,0:T(8,128)S(1)}, u32[]{:S(2)}, u32[]{:S(2)}) collective-permute-start(f32[5,16,8,128]{3,2,1,0:T(8,128)} %fields.2), channel_id=1, source_target_pairs={{0,4},{4,8},{8,12},{12,16},{16,20},{20,24},{24,28},{28,32},{32,36}... | collective-permute-start | bytes 983048 | tf_op jit(solution)/shard_map/ppermute | solution.py:740
  2.6 1.7 %collective-permute-start.1 = (f32[5,16,8,128]{3,2,1,0:T(8,128)}, f32[5,16,8,128]{3,2,1,0:T(8,128)S(1)}, u32[]{:S(2)}, u32[]{:S(2)}) collective-permute-start(f32[5,16,8,128]{3,2,1,0:T(8,128)} %fields.2), channel_id=1, source_target_pairs={{4,0},{8,4},{12,8},{16,12},{20,16},{24,20},{28,24},{32,28},{36,32}... | collective-permute-start | bytes 983048 | tf_op jit(solution)/shard_map/ppermute | solution.py:739
  4.3 1.6 %prepare.1 = f32[32,1,128]{2,1,0:T(1,128)S(1)} custom-call(s32[2]{0:T(128)S(1)} %pad_add_fusion.place_ref, f32[5,16,8,128]{3,2,1,0:T(8,128)} %fields.2), custom_call_target="tpu_custom_call" | custom-call | tf_op jit(solution)/shard_map/prepare/pallas_call | solution.py:724
  7.9 11.5 %all-to-all-start = ((f32[32,1,128]{2,1,0:T(1,128)}), f32[32,1,128]{2,1,0:T(1,128)S(1)}, u32[]{:S(2)}, u32[]{:S(2)}) async-start(f32[32,1,128]{2,1,0:T(1,128)} %max.3), calls=%async_computation | async-start | bytes 32768 | tf_op jit(solution)/shard_map/all_to_all | solution.py:840
  20.4 9.4 %deposit.3.rest_1_.rest_0_ = f32[8,9,3,8,128]{4,3,2,1,0:T(8,128)} custom-call(f32[8,16,8,128]{3,2,1,0:T(8,128)} %radius.5, f32[8,16,8,128]{3,2,1,0:T(8,128)} %weight.5, s32[8,16,8,128]{3,2,1,0:T(8,128)} %column.5, s32[16,8,128]{2,1,0:T(8,128)} %counts.2, s32[8,16,8,1]{3,2,1,0:T(8,128)S(1)} %copy.10.fall_depth), custom_call_target="tpu_custom_call" | custom-call | flops 800000000 | tf_op jit(solution)/shard_map/deposit/pallas_call | solution.py:789
  31.6 2.2 %collective-permute-done.3.from_right = f32[16,8,128]{2,1,0:T(8,128)S(1)} collective-permute-done((f32[16,8,128]{2,1,0:T(8,128)S(1)}, f32[16,8,128]{2,1,0:T(8,128)S(1)}, u32[]{:S(2)}, u32[]{:S(2)}) %collective-permute-start.3) | collective-permute-done | bytes 65568 | tf_op jit(solution)/shard_map/ppermute | solution.py:739
  33.8 1.5 %collective-permute-done.4.from_left = f32[16,8,128]{2,1,0:T(8,128)S(1)} collective-permute-done((f32[16,8,128]{2,1,0:T(8,128)S(1)}, f32[16,8,128]{2,1,0:T(8,128)S(1)}, u32[]{:S(2)}, u32[]{:S(2)}) %collective-permute-start.4) | collective-permute-done | bytes 65568 | tf_op jit(solution)/shard_map/ppermute | solution.py:740
  35.5 2.8 %collective-permute-start.6 = (f32[63,8,128]{2,1,0:T(8,128)S(1)}, f32[63,8,128]{2,1,0:T(8,128)S(1)}, u32[]{:S(2)}, u32[]{:S(2)}) collective-permute-start(f32[63,8,128]{2,1,0:T(8,128)S(1)} %get-tuple-element.37), channel_id=1, source_target_pairs={{1,0},{2,1},{3,2},{0,3},{5,4},{6,5},{7,6},{4,7},{9,8},{10,9},{11,1... | collective-permute-start | bytes 774152 | tf_op jit(solution)/shard_map/ppermute | solution.py:739
  38.3 2.8 %collective-permute-start.5 = (f32[8,128]{1,0:T(8,128)S(1)}, f32[8,128]{1,0:T(8,128)S(1)}, u32[]{:S(2)}, u32[]{:S(2)}) collective-permute-start(f32[8,128]{1,0:T(8,128)S(1)} %get-tuple-element.34.speed), channel_id=1, source_target_pairs={{0,4},{4,0},{1,5},{5,1},{2,6},{6,2},{3,7},{7,3},{8,12},{12,8},{9,1... | collective-permute-start | bytes 12296 | tf_op jit(solution)/shard_map/ppermute | solution.py:842
  41.1 3.5 %first_own.1 = (f32[13,30,8,256]{3,2,1,0:T(8,128)S(1)}, f32[2,16,16,256]{3,2,1,0:T(8,128)S(1)}) custom-call(s32[2]{0:T(128)S(1)} %pad_add_fusion.place_ref, f32[5,16,8,128]{3,2,1,0:T(8,128)S(1)} %hold.1.own.initial, f32[5,16,8,128]{3,2,1,0:T(8,128)S(1)} %collective-permute-done.1.above, f32[5,16,8,128]{3,2,1,0:T(8,128)S(1)} %collective-permute-done.2.below, ...), custom_call_target="tpu_custom_call" | custom-call | tf_op jit(solution)/shard_map/first_own/pallas_call | solution.py:724
  44.7 2.2 %collective-permute-done.7.from_down = f32[63,8,128]{2,1,0:T(8,128)S(1)} collective-permute-done((f32[63,8,128]{2,1,0:T(8,128)S(1)}, f32[63,8,128]{2,1,0:T(8,128)S(1)}, u32[]{:S(2)}, u32[]{:S(2)}) %collective-permute-start.7) | collective-permute-done | bytes 258080 | tf_op jit(solution)/shard_map/ppermute | solution.py:740
  46.9 6.0 %two_sections.1 = (f32[13,30,8,256]{3,2,1,0:T(8,128)S(1)}, f32[5,16,8,128]{3,2,1,0:T(8,128)S(1)}, f32[3,16,8,128]{3,2,1,0:T(8,128)S(1)}, f32[3,16,8,128]{3,2,1,0:T(8,128)S(1)}, f32[1]{0:T(128)}) custom-call(s32[2]{0:T(128)S(1)} %pad_add_fusion.place_ref, f32[8,128]{1,0:T(8,128)S(1)} %get-tuple-element.34.speed, ...), custom_call_target="tpu_custom_call", output_to_operand_aliasing={{0}: (3, {})} | custom-call | tf_op jit(solution)/shard_map/two_sections/pallas_call | solution.py:724
  52.8 2.3 %collective-permute-start.8 = (f32[3,16,8,128]{3,2,1,0:T(8,128)S(1)}, f32[3,16,8,128]{3,2,1,0:T(8,128)S(1)}, u32[]{:S(2)}, u32[]{:S(2)}) collective-permute-start(f32[3,16,8,128]{3,2,1,0:T(8,128)S(1)} %get-tuple-element.41), channel_id=1, source_target_pairs={{4,0},{8,4},{12,8},{16,12},{20,16},{24,20},{28,24},{32,28},{36,32}... | collective-permute-start | bytes 589832 | tf_op jit(solution)/shard_map/ppermute | solution.py:739
  55.1 2.2 %collective-permute-start.9 = (f32[3,16,8,128]{3,2,1,0:T(8,128)S(1)}, f32[3,16,8,128]{3,2,1,0:T(8,128)S(1)}, u32[]{:S(2)}, u32[]{:S(2)}) collective-permute-start(f32[3,16,8,128]{3,2,1,0:T(8,128)S(1)} %get-tuple-element.42), channel_id=1, source_target_pairs={{0,4},{4,8},{8,12},{12,16},{16,20},{20,24},{24,28},{28,32},{32,36}... | collective-permute-start | bytes 589832 | tf_op jit(solution)/shard_map/ppermute | solution.py:740
  57.3 7.4 %deposit.4.rest_0_.rest_1_ = f32[6,9,3,8,128]{4,3,2,1,0:T(8,128)} custom-call(f32[8,16,8,128]{3,2,1,0:T(8,128)} %radius.5, f32[8,16,8,128]{3,2,1,0:T(8,128)} %weight.5, s32[8,16,8,128]{3,2,1,0:T(8,128)} %column.5, s32[16,8,128]{2,1,0:T(8,128)} %counts.2, s32[8,16,8,1]{3,2,1,0:T(8,128)S(1)} %copy.10.fall_depth), custom_call_target="tpu_custom_call" | custom-call | flops 600000000 | tf_op jit(solution)/shard_map/deposit/pallas_call | solution.py:789
  65.2 2.3 %collective-permute-start.10 = (f32[16,8,128]{2,1,0:T(8,128)S(1)}, f32[16,8,128]{2,1,0:T(8,128)S(1)}, u32[]{:S(2)}, u32[]{:S(2)}) collective-permute-start(f32[16,8,128]{2,1,0:T(8,128)S(1)} %get-tuple-element.44), channel_id=1, source_target_pairs={{64,0},{128,64},{192,128},{0,192},{65,1},{129,65},{193,129},{1,193... | collective-permute-start | bytes 196616 | tf_op jit(solution)/shard_map/ppermute | solution.py:739
  67.5 2.4 %collective-permute-done.10.from_right = f32[16,8,128]{2,1,0:T(8,128)S(1)} collective-permute-done((f32[16,8,128]{2,1,0:T(8,128)S(1)}, f32[16,8,128]{2,1,0:T(8,128)S(1)}, u32[]{:S(2)}, u32[]{:S(2)}) %collective-permute-start.10) | collective-permute-done | bytes 65568 | tf_op jit(solution)/shard_map/ppermute | solution.py:739
  69.9 1.3 %collective-permute-done.11.from_left = f32[16,8,128]{2,1,0:T(8,128)S(1)} collective-permute-done((f32[16,8,128]{2,1,0:T(8,128)S(1)}, f32[16,8,128]{2,1,0:T(8,128)S(1)}, u32[]{:S(2)}, u32[]{:S(2)}) %collective-permute-start.11) | collective-permute-done | bytes 65568 | tf_op jit(solution)/shard_map/ppermute | solution.py:740
  71.3 3.2 %collective-permute-start.12 = (f32[48,8,128]{2,1,0:T(8,128)S(1)}, f32[48,8,128]{2,1,0:T(8,128)S(1)}, u32[]{:S(2)}, u32[]{:S(2)}) collective-permute-start(f32[48,8,128]{2,1,0:T(8,128)S(1)} %get-tuple-element.49), channel_id=1, source_target_pairs={{1,0},{2,1},{3,2},{0,3},{5,4},{6,5},{7,6},{4,7},{9,8},{10,9},{11,1... | collective-permute-start | bytes 589832 | tf_op jit(solution)/shard_map/ppermute | solution.py:739
  74.6 3.5 %deposit.5.rest_2_ = f32[2,9,3,8,128]{4,3,2,1,0:T(8,128)} custom-call(f32[8,16,8,128]{3,2,1,0:T(8,128)} %radius.5, f32[8,16,8,128]{3,2,1,0:T(8,128)} %weight.5, s32[8,16,8,128]{3,2,1,0:T(8,128)} %column.5, s32[16,8,128]{2,1,0:T(8,128)} %counts.2, s32[8,16,8,1]{3,2,1,0:T(8,128)S(1)} %copy.10.fall_depth), custom_call_target="tpu_custom_call" | custom-call | flops 200000000 | tf_op jit(solution)/shard_map/deposit/pallas_call | solution.py:789
  78.1 2.4 %second_own.1 = (f32[11,30,8,256]{3,2,1,0:T(8,128)S(1)}, f32[1,16,16,256]{3,2,1,0:T(8,128)S(1)}, f32[16,8,128]{2,1,0:T(8,128)S(1)}) custom-call(f32[5,16,8,128]{3,2,1,0:T(8,128)S(1)} %get-tuple-element.40.own, f32[3,16,8,128]{3,2,1,0:T(8,128)S(1)} %collective-permute-done.8.above, f32[3,16,8,128]{3,2,1,0:T(8,128)S(1)} %collective-permute-done.9.below, ...), custom_call_target="tpu_custom_call" | custom-call | flops 1000000000 | tf_op jit(solution)/shard_map/second_own/pallas_call | solution.py:724
  80.5 3.0 %last_tracer.1 = (f32[11,30,8,256]{3,2,1,0:T(8,128)S(1)}, f32[16,8,128]{2,1,0:T(8,128)S(1)}, f32[3,16,8,128]{3,2,1,0:T(8,128)S(1)}, f32[3,8,8,128]{3,2,1,0:T(8,1...) custom-call(s32[2]{0:T(128)S(1)} %pad_add_fusion.place_ref, ...), custom_call_target="tpu_custom_call", output_to_operand_aliasing={{0}: (2, {})} | custom-call | tf_op jit(solution)/shard_map/last_tracer/pallas_call | solution.py:724
  84.6 3.8 %last_section.1 = f32[5,16,8,128]{3,2,1,0:T(8,128)} custom-call(s32[2]{0:T(128)S(1)} %pad_add_fusion.place_ref, f32[1]{0:T(128)} %get-tuple-element.39.dt_ref, f32[30,16,256]{2,1,0:T(8,128)S(1)} %get-tuple-element.52.rate, f32[30,16,256]{2,1,0:T(8,128)S(1)} %get-tuple-element.53.warm, f32[13,30,8,256]{3,2,1,0:T(8,128)S(1)} %get-tuple-element.54.start, ...), custom_call_target="tpu_custom_call" | custom-call | flops 1000000000 | tf_op jit(solution)/shard_map/last_section/pallas_call | solution.py:724
  88.3 1.2 %land.1 = f32[3,16,8,128]{3,2,1,0:T(8,128)} custom-call(s32[2]{0:T(128)S(1)} %pad_add_fusion.place_ref, f32[3,16,8,128]{3,2,1,0:T(8,128)S(1)} %get-tuple-element.56.landed, f32[3,8,8,128]{3,2,1,0:T(8,128)S(1)} %collective-permute-done.14.arrived), custom_call_target="tpu_custom_call" | custom-call | tf_op jit(solution)/shard_map/land/pallas_call | solution.py:724
  (27 shorter events, 6.6 us)
Async XLA Ops:
  0.6 29.2 %collective-permute-start.2 = (f32[5,16,8,128]{3,2,1,0:T(8,128)}, f32[5,16,8,128]{3,2,1,0:T(8,128)S(1)}, u32[]{:S(2)}, u32[]{:S(2)}) collective-permute-start(f32[5,16,8,128]{3,2,1,0:T(8,128)} %fields.2), channel_id=1, source_target_pairs={{0,4},{4,8},{8,12},{12,16},{16,20},{20,24},{24,28},{28,32},{32,36}... | collective-permute-start | bytes 983048 | tf_op jit(solution)/shard_map/ppermute | solution.py:740
  2.6 27.3 %collective-permute-start.1 = (f32[5,16,8,128]{3,2,1,0:T(8,128)}, f32[5,16,8,128]{3,2,1,0:T(8,128)S(1)}, u32[]{:S(2)}, u32[]{:S(2)}) collective-permute-start(f32[5,16,8,128]{3,2,1,0:T(8,128)} %fields.2), channel_id=1, source_target_pairs={{4,0},{8,4},{12,8},{16,12},{20,16},{24,20},{28,24},{32,28},{36,32}... | collective-permute-start | bytes 983048 | tf_op jit(solution)/shard_map/ppermute | solution.py:739
  5.9 1.3 %collective-permute-start = (f32[32,1,128]{2,1,0:T(1,128)S(1)}, f32[32,1,128]{2,1,0:T(1,128)S(1)}, u32[]{:S(2)}, u32[]{:S(2)}) collective-permute-start(f32[32,1,128]{2,1,0:T(1,128)S(1)} %prepare.1), channel_id=1, source_target_pairs={{0,64},{64,0},{128,192},{192,128},{1,65},{65,1},{129,193},{193,129... | collective-permute-start | bytes 49160 | tf_op jit(solution)/shard_map/ppermute | solution.py:831
  7.9 21.9 %all-to-all-start = ((f32[32,1,128]{2,1,0:T(1,128)}), f32[32,1,128]{2,1,0:T(1,128)S(1)}, u32[]{:S(2)}, u32[]{:S(2)}) async-start(f32[32,1,128]{2,1,0:T(1,128)} %max.3), calls=%async_computation | async-start | bytes 32768 | tf_op jit(solution)/shard_map/all_to_all | solution.py:840
  30.5 3.3 %collective-permute-start.3 = (f32[16,8,128]{2,1,0:T(8,128)S(1)}, f32[16,8,128]{2,1,0:T(8,128)S(1)}, u32[]{:S(2)}, u32[]{:S(2)}) collective-permute-start(f32[16,8,128]{2,1,0:T(8,128)S(1)} %get-tuple-element.32), channel_id=1, source_target_pairs={{64,0},{128,64},{192,128},{0,192},{65,1},{129,65},{193,129},{1,193... | collective-permute-start | bytes 196616 | tf_op jit(solution)/shard_map/ppermute | solution.py:739
  31.6 3.8 %collective-permute-start.4 = (f32[16,8,128]{2,1,0:T(8,128)S(1)}, f32[16,8,128]{2,1,0:T(8,128)S(1)}, u32[]{:S(2)}, u32[]{:S(2)}) collective-permute-start(f32[16,8,128]{2,1,0:T(8,128)S(1)} %get-tuple-element.33), channel_id=1, source_target_pairs={{0,64},{64,128},{128,192},{192,0},{1,65},{65,129},{129,193},{193,1... | collective-permute-start | bytes 196616 | tf_op jit(solution)/shard_map/ppermute | solution.py:740
  35.5 9.1 %collective-permute-start.6 = (f32[63,8,128]{2,1,0:T(8,128)S(1)}, f32[63,8,128]{2,1,0:T(8,128)S(1)}, u32[]{:S(2)}, u32[]{:S(2)}) collective-permute-start(f32[63,8,128]{2,1,0:T(8,128)S(1)} %get-tuple-element.37), channel_id=1, source_target_pairs={{1,0},{2,1},{3,2},{0,3},{5,4},{6,5},{7,6},{4,7},{9,8},{10,9},{11,1... | collective-permute-start | bytes 774152 | tf_op jit(solution)/shard_map/ppermute | solution.py:739
  38.3 8.5 %collective-permute-start.7 = (f32[63,8,128]{2,1,0:T(8,128)S(1)}, f32[63,8,128]{2,1,0:T(8,128)S(1)}, u32[]{:S(2)}, u32[]{:S(2)}) collective-permute-start(f32[63,8,128]{2,1,0:T(8,128)S(1)} %get-tuple-element.38), channel_id=1, source_target_pairs={{0,1},{1,2},{2,3},{3,0},{4,5},{5,6},{6,7},{7,4},{8,9},{9,10},{10,1... | collective-permute-start | bytes 774152 | tf_op jit(solution)/shard_map/ppermute | solution.py:740
  38.3 6.3 %collective-permute-start.5 = (f32[8,128]{1,0:T(8,128)S(1)}, f32[8,128]{1,0:T(8,128)S(1)}, u32[]{:S(2)}, u32[]{:S(2)}) collective-permute-start(f32[8,128]{1,0:T(8,128)S(1)} %get-tuple-element.34.speed), channel_id=1, source_target_pairs={{0,4},{4,0},{1,5},{5,1},{2,6},{6,2},{3,7},{7,3},{8,12},{12,8},{9,1... | collective-permute-start | bytes 12296 | tf_op jit(solution)/shard_map/ppermute | solution.py:842
  52.8 11.9 %collective-permute-start.8 = (f32[3,16,8,128]{3,2,1,0:T(8,128)S(1)}, f32[3,16,8,128]{3,2,1,0:T(8,128)S(1)}, u32[]{:S(2)}, u32[]{:S(2)}) collective-permute-start(f32[3,16,8,128]{3,2,1,0:T(8,128)S(1)} %get-tuple-element.41), channel_id=1, source_target_pairs={{4,0},{8,4},{12,8},{16,12},{20,16},{24,20},{28,24},{32,28},{36,32}... | collective-permute-start | bytes 589832 | tf_op jit(solution)/shard_map/ppermute | solution.py:739
  55.1 9.6 %collective-permute-start.9 = (f32[3,16,8,128]{3,2,1,0:T(8,128)S(1)}, f32[3,16,8,128]{3,2,1,0:T(8,128)S(1)}, u32[]{:S(2)}, u32[]{:S(2)}) collective-permute-start(f32[3,16,8,128]{3,2,1,0:T(8,128)S(1)} %get-tuple-element.42), channel_id=1, source_target_pairs={{0,4},{4,8},{8,12},{12,16},{16,20},{20,24},{24,28},{28,32},{32,36}... | collective-permute-start | bytes 589832 | tf_op jit(solution)/shard_map/ppermute | solution.py:740
  65.2 4.7 %collective-permute-start.10 = (f32[16,8,128]{2,1,0:T(8,128)S(1)}, f32[16,8,128]{2,1,0:T(8,128)S(1)}, u32[]{:S(2)}, u32[]{:S(2)}) collective-permute-start(f32[16,8,128]{2,1,0:T(8,128)S(1)} %get-tuple-element.44), channel_id=1, source_target_pairs={{64,0},{128,64},{192,128},{0,192},{65,1},{129,65},{193,129},{1,193... | collective-permute-start | bytes 196616 | tf_op jit(solution)/shard_map/ppermute | solution.py:739
  67.5 3.7 %collective-permute-start.11 = (f32[16,8,128]{2,1,0:T(8,128)S(1)}, f32[16,8,128]{2,1,0:T(8,128)S(1)}, u32[]{:S(2)}, u32[]{:S(2)}) collective-permute-start(f32[16,8,128]{2,1,0:T(8,128)S(1)} %get-tuple-element.45), channel_id=1, source_target_pairs={{0,64},{64,128},{128,192},{192,0},{1,65},{65,129},{129,193},{193,1... | collective-permute-start | bytes 196616 | tf_op jit(solution)/shard_map/ppermute | solution.py:740
  71.3 9.2 %collective-permute-start.13 = (f32[48,8,128]{2,1,0:T(8,128)S(1)}, f32[48,8,128]{2,1,0:T(8,128)S(1)}, u32[]{:S(2)}, u32[]{:S(2)}) collective-permute-start(f32[48,8,128]{2,1,0:T(8,128)S(1)} %get-tuple-element.50), channel_id=1, source_target_pairs={{0,1},{1,2},{2,3},{3,0},{4,5},{5,6},{6,7},{7,4},{8,9},{9,10},{10,1... | collective-permute-start | bytes 589832 | tf_op jit(solution)/shard_map/ppermute | solution.py:740
  71.3 9.1 %collective-permute-start.12 = (f32[48,8,128]{2,1,0:T(8,128)S(1)}, f32[48,8,128]{2,1,0:T(8,128)S(1)}, u32[]{:S(2)}, u32[]{:S(2)}) collective-permute-start(f32[48,8,128]{2,1,0:T(8,128)S(1)} %get-tuple-element.49), channel_id=1, source_target_pairs={{1,0},{2,1},{3,2},{0,3},{5,4},{6,5},{7,6},{4,7},{9,8},{10,9},{11,1... | collective-permute-start | bytes 589832 | tf_op jit(solution)/shard_map/ppermute | solution.py:739
  83.5 4.8 %collective-permute-start.14 = (f32[3,8,8,128]{3,2,1,0:T(8,128)S(1)}, f32[3,8,8,128]{3,2,1,0:T(8,128)S(1)}, u32[]{:S(2)}, u32[]{:S(2)}) collective-permute-start(f32[3,8,8,128]{3,2,1,0:T(8,128)S(1)} %get-tuple-element.57), channel_id=1, source_target_pairs={{1,0},{2,1},{3,2},{0,3},{5,4},{6,5},{7,6},{4,7},{9,8},{10,9},{11,1... | collective-permute-start | bytes 294920 | tf_op jit(solution)/shard_map/ppermute | solution.py:897

commit v11 on v9

--- a/solution.py
+++ b/solution.py
@@ -849,9 +849,9 @@
         grant=12,
         alias={3: 0},
     )(where, speed, other_speed, start, flat, from_up, from_down)
-    middle = drops(8, 6, s2)
-    *near, from_up, from_down, sent = exchange(SECOND, s2, down, up, [middle])
-    by_depth = [early, middle, drops(14, 2, sent)]
+    middle = drops(8, 8, s2)
+    *near, from_up, from_down, _ = exchange(SECOND, s2, down, up, [middle])
+    by_depth = [early, middle]
     ext = held(len(SECOND.tiles), DEPTH, ROWS, WIDE)
     around_s2, flat, flat_tracer = call(
         second_own,

time: 90.2 us -> 89.4 us (level); the launches traced: 88.6 us -> 88.9 us
  waiting for transfers between devices: 9.97 us -> 15.5 us
  starting transfers between devices: 32.7 us -> 29.2 us
  Pallas kernels: 42.2 us -> 40.6 us
    ppermute x6, starting transfers between devices: 13.1 us -> 9.23 us  [both_ways(): lax.ppermute(down, axis, [((i + 1) % count, i) for i in range(count)])]
    ppermute x6, waiting for transfers between devices: 5.03 us -> 8.18 us  [both_ways(): lax.ppermute(up, axis, [(i, (i + 1) % count) for i in range(count)])]
    ppermute x6, waiting for transfers between devices: 4.64 us -> 6.46 us  [both_ways(): lax.ppermute(down, axis, [((i + 1) % count, i) for i in range(count)])]
    pallas_call x3 -> x2, Pallas kernels: 20.3 us -> 18.8 us  [droplets(): pl.pallas_call(deposit, name='deposit', grid=(count // step,), in_specs=[...]
    ppermute x6, starting transfers between devices: 4.21 us -> 5.18 us  [both_ways(): lax.ppermute(up, axis, [(i, (i + 1) % count) for i in range(count)])]
  transfers between devices with their start and end apart: 16 -> 16, of which waited for: 6 -> 9; matrix products, arithmetic and copies ran while one was open for 2% -> 2% of each run, Pallas kernels for 35% -> 33%
where the time goes in v11:
time: 89.4 us; the launch traced here: 88.9 us
  Pallas kernels  40.6 us (45%)
  starting transfers between devices  29.2 us (33%)
  waiting for transfers between devices  15.5 us (17%)
  local copies, waits for them, and re-layouts  2.8 us (3%)
    pallas_call x10, Pallas kernels, run(): made(*(pltpu.with_memory_space_constraint(value, spec.memory_space) if sp...  21.1 us
    pallas_call x2, Pallas kernels, droplets(): pl.pallas_call(deposit, name='deposit', grid=(count // step,), in_specs=[...  18.8 us
    all_to_all x1, starting transfers between devices, per_device(): speed = jnp.max(lax.all_to_all(speed, plane, 0, 0), axis=0)  11.5 us
    ppermute x6, starting transfers between devices, both_ways(): lax.ppermute(down, axis, [((i + 1) % count, i) for i in range(count)])  9.23 us
    ppermute x6, waiting for transfers between devices, both_ways(): lax.ppermute(up, axis, [(i, (i + 1) % count) for i in range(count)])  8.18 us
    ppermute x6, waiting for transfers between devices, both_ways(): lax.ppermute(down, axis, [((i + 1) % count, i) for i in range(count)])  6.46 us
    ppermute x6, starting transfers between devices, both_ways(): lax.ppermute(up, axis, [(i, (i + 1) % count) for i in range(count)])  5.18 us
    ppermute x1, starting transfers between devices, per_device(): other_speed = lax.ppermute(speed, 'gy_lo', [(0, 1), (1, 0)])  2.83 us
  transfers between devices with their start and end apart: 16, of which 9 were waited for; matrix products, arithmetic and copies ran while one was open for 2% of the time, Pallas kernels for 33%

profile of v11, /device:TPU:4, one launch (start us, length us, event | category | flops | bytes accessed | tf_op | source)
XLA Modules:
  0.0 88.9 jit_solution(14155275444317741621)
XLA Ops:
  0.6 1.9 %collective-permute-start.1 = (f32[5,16,8,128]{3,2,1,0:T(8,128)}, f32[5,16,8,128]{3,2,1,0:T(8,128)S(1)}, u32[]{:S(2)}, u32[]{:S(2)}) collective-permute-start(f32[5,16,8,128]{3,2,1,0:T(8,128)} %fields.1), channel_id=1, source_target_pairs={{0,4},{4,8},{8,12},{12,16},{16,20},{20,24},{24,28},{28,32},{32,36}... | collective-permute-start | bytes 983048 | tf_op jit(solution)/shard_map/ppermute | solution.py:740
  2.6 1.7 %collective-permute-start = (f32[5,16,8,128]{3,2,1,0:T(8,128)}, f32[5,16,8,128]{3,2,1,0:T(8,128)S(1)}, u32[]{:S(2)}, u32[]{:S(2)}) collective-permute-start(f32[5,16,8,128]{3,2,1,0:T(8,128)} %fields.1), channel_id=1, source_target_pairs={{4,0},{8,4},{12,8},{16,12},{20,16},{24,20},{28,24},{32,28},{36,32}... | collective-permute-start | bytes 983048 | tf_op jit(solution)/shard_map/ppermute | solution.py:739
  6.1 1.2 %copy.15.fall_depth = s32[8,16,8,1]{3,2,1,0:T(8,128)S(1)} copy(s32[8,16,8,1]{1,3,2,0:T(1,128)} %param.11) | data formatting | bytes 8192 | tf_op args[5]
  7.9 11.5 %all-to-all-start = ((f32[32,1,128]{2,1,0:T(1,128)}), f32[32,1,128]{2,1,0:T(1,128)S(1)}, u32[]{:S(2)}, u32[]{:S(2)}) async-start(f32[32,1,128]{2,1,0:T(1,128)} %broadcast_in_dim.3), calls=%async_computation | async-start | bytes 32768 | tf_op jit(solution)/shard_map/all_to_all | solution.py:827
  19.4 9.4 %deposit.2.rest_1_.rest_0_ = f32[8,9,3,8,128]{4,3,2,1,0:T(8,128)} custom-call(f32[8,16,8,128]{3,2,1,0:T(8,128)} %radius.3, f32[8,16,8,128]{3,2,1,0:T(8,128)} %weight.3, s32[8,16,8,128]{3,2,1,0:T(8,128)} %column.3, s32[16,8,128]{2,1,0:T(8,128)} %counts.1, s32[8,16,8,1]{3,2,1,0:T(8,128)S(1)} %copy.15.fall_depth), custom_call_target="tpu_custom_call" | custom-call | flops 800000000 | tf_op jit(solution)/shard_map/deposit/pallas_call | solution.py:781
  30.6 2.2 %collective-permute-done.3.from_right = f32[16,8,128]{2,1,0:T(8,128)S(1)} collective-permute-done((f32[16,8,128]{2,1,0:T(8,128)S(1)}, f32[16,8,128]{2,1,0:T(8,128)S(1)}, u32[]{:S(2)}, u32[]{:S(2)}) %collective-permute-start.3) | collective-permute-done | bytes 65568 | tf_op jit(solution)/shard_map/ppermute | solution.py:739
  32.9 1.5 %collective-permute-done.4.from_left = f32[16,8,128]{2,1,0:T(8,128)S(1)} collective-permute-done((f32[16,8,128]{2,1,0:T(8,128)S(1)}, f32[16,8,128]{2,1,0:T(8,128)S(1)}, u32[]{:S(2)}, u32[]{:S(2)}) %collective-permute-start.4) | collective-permute-done | bytes 65568 | tf_op jit(solution)/shard_map/ppermute | solution.py:740
  34.5 2.8 %collective-permute-start.6 = (f32[63,8,128]{2,1,0:T(8,128)S(1)}, f32[63,8,128]{2,1,0:T(8,128)S(1)}, u32[]{:S(2)}, u32[]{:S(2)}) collective-permute-start(f32[63,8,128]{2,1,0:T(8,128)S(1)} %get-tuple-element.38), channel_id=1, source_target_pairs={{1,0},{2,1},{3,2},{0,3},{5,4},{6,5},{7,6},{4,7},{9,8},{10,9},{11,1... | collective-permute-start | bytes 774152 | tf_op jit(solution)/shard_map/ppermute | solution.py:739
  37.4 2.8 %collective-permute-start.5 = (f32[8,128]{1,0:T(8,128)S(1)}, f32[8,128]{1,0:T(8,128)S(1)}, u32[]{:S(2)}, u32[]{:S(2)}) collective-permute-start(f32[8,128]{1,0:T(8,128)S(1)} %get-tuple-element.35.speed), channel_id=1, source_target_pairs={{0,4},{4,0},{1,5},{5,1},{2,6},{6,2},{3,7},{7,3},{8,12},{12,8},{9,1... | collective-permute-start | bytes 12296 | tf_op jit(solution)/shard_map/ppermute | solution.py:829
  40.2 3.5 %first_own.1 = (f32[13,30,8,256]{3,2,1,0:T(8,128)S(1)}, f32[2,16,16,256]{3,2,1,0:T(8,128)S(1)}) custom-call(s32[2]{0:T(128)S(1)} %pad_add_fusion.place_ref, f32[5,16,8,128]{3,2,1,0:T(8,128)S(1)} %get-tuple-element.30.own.initial, f32[5,16,8,128]{3,2,1,0:T(8,128)S(1)} %collective-permute-done.above, f32[5,16,8,128]{3,2,1,0:T(8,128)S(1)} %collective-permute-done.1.below, ...), custom_call_target="tpu_custom_call" | custom-call | tf_op jit(solution)/shard_map/first_own/pallas_call | solution.py:724
  43.7 2.2 %collective-permute-done.7.from_down = f32[63,8,128]{2,1,0:T(8,128)S(1)} collective-permute-done((f32[63,8,128]{2,1,0:T(8,128)S(1)}, f32[63,8,128]{2,1,0:T(8,128)S(1)}, u32[]{:S(2)}, u32[]{:S(2)}) %collective-permute-start.7) | collective-permute-done | bytes 258080 | tf_op jit(solution)/shard_map/ppermute | solution.py:740
  45.9 6.0 %two_sections.1 = (f32[13,30,8,256]{3,2,1,0:T(8,128)S(1)}, f32[5,16,8,128]{3,2,1,0:T(8,128)S(1)}, f32[3,16,8,128]{3,2,1,0:T(8,128)S(1)}, f32[3,16,8,128]{3,2,1,0:T(8,128)S(1)}, f32[1]{0:T(128)}) custom-call(s32[2]{0:T(128)S(1)} %pad_add_fusion.place_ref, f32[8,128]{1,0:T(8,128)S(1)} %get-tuple-element.35.speed, ...), custom_call_target="tpu_custom_call", output_to_operand_aliasing={{0}: (3, {})} | custom-call | tf_op jit(solution)/shard_map/two_sections/pallas_call | solution.py:724
  51.9 2.3 %collective-permute-start.8 = (f32[3,16,8,128]{3,2,1,0:T(8,128)S(1)}, f32[3,16,8,128]{3,2,1,0:T(8,128)S(1)}, u32[]{:S(2)}, u32[]{:S(2)}) collective-permute-start(f32[3,16,8,128]{3,2,1,0:T(8,128)S(1)} %get-tuple-element.42), channel_id=1, source_target_pairs={{4,0},{8,4},{12,8},{16,12},{20,16},{24,20},{28,24},{32,28},{36,32}... | collective-permute-start | bytes 589832 | tf_op jit(solution)/shard_map/ppermute | solution.py:739
  54.2 2.2 %collective-permute-start.9 = (f32[3,16,8,128]{3,2,1,0:T(8,128)S(1)}, f32[3,16,8,128]{3,2,1,0:T(8,128)S(1)}, u32[]{:S(2)}, u32[]{:S(2)}) collective-permute-start(f32[3,16,8,128]{3,2,1,0:T(8,128)S(1)} %get-tuple-element.43), channel_id=1, source_target_pairs={{0,4},{4,8},{8,12},{12,16},{16,20},{20,24},{24,28},{28,32},{32,36}... | collective-permute-start | bytes 589832 | tf_op jit(solution)/shard_map/ppermute | solution.py:740
  56.4 9.4 %deposit.3.rest_0_.rest_1_ = f32[8,9,3,8,128]{4,3,2,1,0:T(8,128)} custom-call(f32[8,16,8,128]{3,2,1,0:T(8,128)} %radius.3, f32[8,16,8,128]{3,2,1,0:T(8,128)} %weight.3, s32[8,16,8,128]{3,2,1,0:T(8,128)} %column.3, s32[16,8,128]{2,1,0:T(8,128)} %counts.1, s32[8,16,8,1]{3,2,1,0:T(8,128)S(1)} %copy.15.fall_depth), custom_call_target="tpu_custom_call" | custom-call | flops 800000000 | tf_op jit(solution)/shard_map/deposit/pallas_call | solution.py:781
  66.8 1.7 %collective-permute-done.10.from_right = f32[16,8,128]{2,1,0:T(8,128)S(1)} collective-permute-done((f32[16,8,128]{2,1,0:T(8,128)S(1)}, f32[16,8,128]{2,1,0:T(8,128)S(1)}, u32[]{:S(2)}, u32[]{:S(2)}) %collective-permute-start.10) | collective-permute-done | bytes 65568 | tf_op jit(solution)/shard_map/ppermute | solution.py:739
  68.6 2.4 %collective-permute-done.11.from_left = f32[16,8,128]{2,1,0:T(8,128)S(1)} collective-permute-done((f32[16,8,128]{2,1,0:T(8,128)S(1)}, f32[16,8,128]{2,1,0:T(8,128)S(1)}, u32[]{:S(2)}, u32[]{:S(2)}) %collective-permute-start.11) | collective-permute-done | bytes 65568 | tf_op jit(solution)/shard_map/ppermute | solution.py:740
  71.0 1.2 %collective-permute-start.12 = (f32[48,8,128]{2,1,0:T(8,128)S(1)}, f32[48,8,128]{2,1,0:T(8,128)S(1)}, u32[]{:S(2)}, u32[]{:S(2)}) collective-permute-start(f32[48,8,128]{2,1,0:T(8,128)S(1)} %get-tuple-element.50), channel_id=1, source_target_pairs={{1,0},{2,1},{3,2},{0,3},{5,4},{6,5},{7,6},{4,7},{9,8},{10,9},{11,1... | collective-permute-start | bytes 589832 | tf_op jit(solution)/shard_map/ppermute | solution.py:739
  73.1 2.4 %second_own.1 = (f32[11,30,8,256]{3,2,1,0:T(8,128)S(1)}, f32[1,16,16,256]{3,2,1,0:T(8,128)S(1)}, f32[16,8,128]{2,1,0:T(8,128)S(1)}) custom-call(f32[5,16,8,128]{3,2,1,0:T(8,128)S(1)} %get-tuple-element.41.own, f32[3,16,8,128]{3,2,1,0:T(8,128)S(1)} %collective-permute-done.8.above, f32[3,16,8,128]{3,2,1,0:T(8,128)S(1)} %collective-permute-done.9.below, ...), custom_call_target="tpu_custom_call" | custom-call | flops 1000000000 | tf_op jit(solution)/shard_map/second_own/pallas_call | solution.py:724
  75.5 2.5 %collective-permute-done.12.from_up = f32[48,8,128]{2,1,0:T(8,128)S(1)} collective-permute-done((f32[48,8,128]{2,1,0:T(8,128)S(1)}, f32[48,8,128]{2,1,0:T(8,128)S(1)}, u32[]{:S(2)}, u32[]{:S(2)}) %collective-permute-start.12) | collective-permute-done | bytes 196640 | tf_op jit(solution)/shard_map/ppermute | solution.py:739
  78.0 2.1 %collective-permute-done.13.from_down = f32[48,8,128]{2,1,0:T(8,128)S(1)} collective-permute-done((f32[48,8,128]{2,1,0:T(8,128)S(1)}, f32[48,8,128]{2,1,0:T(8,128)S(1)}, u32[]{:S(2)}, u32[]{:S(2)}) %collective-permute-start.13) | collective-permute-done | bytes 196640 | tf_op jit(solution)/shard_map/ppermute | solution.py:740
  80.0 2.9 %last_tracer.1 = (f32[11,30,8,256]{3,2,1,0:T(8,128)S(1)}, f32[16,8,128]{2,1,0:T(8,128)S(1)}, f32[3,16,8,128]{3,2,1,0:T(8,128)S(1)}, f32[3,8,8,128]{3,2,1,0:T(8,1...) custom-call(s32[2]{0:T(128)S(1)} %pad_add_fusion.place_ref, ...), custom_call_target="tpu_custom_call", output_to_operand_aliasing={{0}: (2, {})} | custom-call | tf_op jit(solution)/shard_map/last_tracer/pallas_call | solution.py:724
  83.3 3.8 %last_section.1 = f32[5,16,8,128]{3,2,1,0:T(8,128)} custom-call(s32[2]{0:T(128)S(1)} %pad_add_fusion.place_ref, f32[1]{0:T(128)} %get-tuple-element.40.dt_ref, f32[30,16,256]{2,1,0:T(8,128)S(1)} %get-tuple-element.52.rate, f32[30,16,256]{2,1,0:T(8,128)S(1)} %get-tuple-element.53.warm, f32[13,30,8,256]{3,2,1,0:T(8,128)S(1)} %get-tuple-element.54.start, ...), custom_call_target="tpu_custom_call" | custom-call | flops 1000000000 | tf_op jit(solution)/shard_map/last_section/pallas_call | solution.py:724
  87.7 1.2 %land.1 = f32[3,16,8,128]{3,2,1,0:T(8,128)} custom-call(s32[2]{0:T(128)S(1)} %pad_add_fusion.place_ref, f32[3,16,8,128]{3,2,1,0:T(8,128)S(1)} %get-tuple-element.56.landed, f32[3,8,8,128]{3,2,1,0:T(8,128)S(1)} %collective-permute-done.14.arrived), custom_call_target="tpu_custom_call" | custom-call | tf_op jit(solution)/shard_map/land/pallas_call | solution.py:724
  (29 shorter events, 7.3 us)
Async XLA Ops:
  0.6 28.5 %collective-permute-start.1 = (f32[5,16,8,128]{3,2,1,0:T(8,128)}, f32[5,16,8,128]{3,2,1,0:T(8,128)S(1)}, u32[]{:S(2)}, u32[]{:S(2)}) collective-permute-start(f32[5,16,8,128]{3,2,1,0:T(8,128)} %fields.1), channel_id=1, source_target_pairs={{0,4},{4,8},{8,12},{12,16},{16,20},{20,24},{24,28},{28,32},{32,36}... | collective-permute-start | bytes 983048 | tf_op jit(solution)/shard_map/ppermute | solution.py:740
  2.6 26.6 %collective-permute-start = (f32[5,16,8,128]{3,2,1,0:T(8,128)}, f32[5,16,8,128]{3,2,1,0:T(8,128)S(1)}, u32[]{:S(2)}, u32[]{:S(2)}) collective-permute-start(f32[5,16,8,128]{3,2,1,0:T(8,128)} %fields.1), channel_id=1, source_target_pairs={{4,0},{8,4},{12,8},{16,12},{20,16},{24,20},{28,24},{32,28},{36,32}... | collective-permute-start | bytes 983048 | tf_op jit(solution)/shard_map/ppermute | solution.py:739
  4.3 1.0 %copy-start = (f32[5,16,8,128]{3,2,1,0:T(8,128)S(1)}, f32[5,16,8,128]{3,2,1,0:T(8,128)}, u32[]{:S(2)}) copy-start(f32[5,16,8,128]{3,2,1,0:T(8,128)} %fields.1) | copy-start | bytes 983044
  6.0 1.3 %collective-permute-start.2 = (f32[8,128]{1,0:T(8,128)S(1)}, f32[8,128]{1,0:T(8,128)S(1)}, u32[]{:S(2)}, u32[]{:S(2)}) collective-permute-start(f32[8,128]{1,0:T(8,128)S(1)} %get-tuple-element.31), channel_id=1, source_target_pairs={{0,64},{64,0},{128,192},{192,128},{1,65},{65,1},{129,193},{193,129... | collective-permute-start | bytes 12296 | tf_op jit(solution)/shard_map/ppermute | solution.py:823
  7.9 21.2 %all-to-all-start = ((f32[32,1,128]{2,1,0:T(1,128)}), f32[32,1,128]{2,1,0:T(1,128)S(1)}, u32[]{:S(2)}, u32[]{:S(2)}) async-start(f32[32,1,128]{2,1,0:T(1,128)} %broadcast_in_dim.3), calls=%async_computation | async-start | bytes 32768 | tf_op jit(solution)/shard_map/all_to_all | solution.py:827
  29.8 3.0 %collective-permute-start.3 = (f32[16,8,128]{2,1,0:T(8,128)S(1)}, f32[16,8,128]{2,1,0:T(8,128)S(1)}, u32[]{:S(2)}, u32[]{:S(2)}) collective-permute-start(f32[16,8,128]{2,1,0:T(8,128)S(1)} %get-tuple-element.33), channel_id=1, source_target_pairs={{64,0},{128,64},{192,128},{0,192},{65,1},{129,65},{193,129},{1,193... | collective-permute-start | bytes 196616 | tf_op jit(solution)/shard_map/ppermute | solution.py:739
  30.6 3.8 %collective-permute-start.4 = (f32[16,8,128]{2,1,0:T(8,128)S(1)}, f32[16,8,128]{2,1,0:T(8,128)S(1)}, u32[]{:S(2)}, u32[]{:S(2)}) collective-permute-start(f32[16,8,128]{2,1,0:T(8,128)S(1)} %get-tuple-element.34), channel_id=1, source_target_pairs={{0,64},{64,128},{128,192},{192,0},{1,65},{65,129},{129,193},{193,1... | collective-permute-start | bytes 196616 | tf_op jit(solution)/shard_map/ppermute | solution.py:740
  34.5 9.1 %collective-permute-start.6 = (f32[63,8,128]{2,1,0:T(8,128)S(1)}, f32[63,8,128]{2,1,0:T(8,128)S(1)}, u32[]{:S(2)}, u32[]{:S(2)}) collective-permute-start(f32[63,8,128]{2,1,0:T(8,128)S(1)} %get-tuple-element.38), channel_id=1, source_target_pairs={{1,0},{2,1},{3,2},{0,3},{5,4},{6,5},{7,6},{4,7},{9,8},{10,9},{11,1... | collective-permute-start | bytes 774152 | tf_op jit(solution)/shard_map/ppermute | solution.py:739
  37.3 8.5 %collective-permute-start.7 = (f32[63,8,128]{2,1,0:T(8,128)S(1)}, f32[63,8,128]{2,1,0:T(8,128)S(1)}, u32[]{:S(2)}, u32[]{:S(2)}) collective-permute-start(f32[63,8,128]{2,1,0:T(8,128)S(1)} %get-tuple-element.39), channel_id=1, source_target_pairs={{0,1},{1,2},{2,3},{3,0},{4,5},{5,6},{6,7},{7,4},{8,9},{9,10},{10,1... | collective-permute-start | bytes 774152 | tf_op jit(solution)/shard_map/ppermute | solution.py:740
  37.4 6.3 %collective-permute-start.5 = (f32[8,128]{1,0:T(8,128)S(1)}, f32[8,128]{1,0:T(8,128)S(1)}, u32[]{:S(2)}, u32[]{:S(2)}) collective-permute-start(f32[8,128]{1,0:T(8,128)S(1)} %get-tuple-element.35.speed), channel_id=1, source_target_pairs={{0,4},{4,0},{1,5},{5,1},{2,6},{6,2},{3,7},{7,3},{8,12},{12,8},{9,1... | collective-permute-start | bytes 12296 | tf_op jit(solution)/shard_map/ppermute | solution.py:829
  51.9 13.9 %collective-permute-start.8 = (f32[3,16,8,128]{3,2,1,0:T(8,128)S(1)}, f32[3,16,8,128]{3,2,1,0:T(8,128)S(1)}, u32[]{:S(2)}, u32[]{:S(2)}) collective-permute-start(f32[3,16,8,128]{3,2,1,0:T(8,128)S(1)} %get-tuple-element.42), channel_id=1, source_target_pairs={{4,0},{8,4},{12,8},{16,12},{20,16},{24,20},{28,24},{32,28},{36,32}... | collective-permute-start | bytes 589832 | tf_op jit(solution)/shard_map/ppermute | solution.py:739
  54.2 11.6 %collective-permute-start.9 = (f32[3,16,8,128]{3,2,1,0:T(8,128)S(1)}, f32[3,16,8,128]{3,2,1,0:T(8,128)S(1)}, u32[]{:S(2)}, u32[]{:S(2)}) collective-permute-start(f32[3,16,8,128]{3,2,1,0:T(8,128)S(1)} %get-tuple-element.43), channel_id=1, source_target_pairs={{0,4},{4,8},{8,12},{12,16},{16,20},{20,24},{24,28},{28,32},{32,36}... | collective-permute-start | bytes 589832 | tf_op jit(solution)/shard_map/ppermute | solution.py:740
  66.2 2.3 %collective-permute-start.10 = (f32[16,8,128]{2,1,0:T(8,128)S(1)}, f32[16,8,128]{2,1,0:T(8,128)S(1)}, u32[]{:S(2)}, u32[]{:S(2)}) collective-permute-start(f32[16,8,128]{2,1,0:T(8,128)S(1)} %get-tuple-element.45), channel_id=1, source_target_pairs={{64,0},{128,64},{192,128},{0,192},{65,1},{129,65},{193,129},{1,193... | collective-permute-start | bytes 196616 | tf_op jit(solution)/shard_map/ppermute | solution.py:739
  66.7 4.3 %collective-permute-start.11 = (f32[16,8,128]{2,1,0:T(8,128)S(1)}, f32[16,8,128]{2,1,0:T(8,128)S(1)}, u32[]{:S(2)}, u32[]{:S(2)}) collective-permute-start(f32[16,8,128]{2,1,0:T(8,128)S(1)} %get-tuple-element.46), channel_id=1, source_target_pairs={{0,64},{64,128},{128,192},{192,0},{1,65},{65,129},{129,193},{193,1... | collective-permute-start | bytes 196616 | tf_op jit(solution)/shard_map/ppermute | solution.py:740
  71.0 7.0 %collective-permute-start.12 = (f32[48,8,128]{2,1,0:T(8,128)S(1)}, f32[48,8,128]{2,1,0:T(8,128)S(1)}, u32[]{:S(2)}, u32[]{:S(2)}) collective-permute-start(f32[48,8,128]{2,1,0:T(8,128)S(1)} %get-tuple-element.50), channel_id=1, source_target_pairs={{1,0},{2,1},{3,2},{0,3},{5,4},{6,5},{7,6},{4,7},{9,8},{10,9},{11,1... | collective-permute-start | bytes 589832 | tf_op jit(solution)/shard_map/ppermute | solution.py:739
  72.2 7.9 %collective-permute-start.13 = (f32[48,8,128]{2,1,0:T(8,128)S(1)}, f32[48,8,128]{2,1,0:T(8,128)S(1)}, u32[]{:S(2)}, u32[]{:S(2)}) collective-permute-start(f32[48,8,128]{2,1,0:T(8,128)S(1)} %get-tuple-element.51), channel_id=1, source_target_pairs={{0,1},{1,2},{2,3},{3,0},{4,5},{5,6},{6,7},{7,4},{8,9},{9,10},{10,1... | collective-permute-start | bytes 589832 | tf_op jit(solution)/shard_map/ppermute | solution.py:740
  83.0 4.7 %collective-permute-start.14 = (f32[3,8,8,128]{3,2,1,0:T(8,128)S(1)}, f32[3,8,8,128]{3,2,1,0:T(8,128)S(1)}, u32[]{:S(2)}, u32[]{:S(2)}) collective-permute-start(f32[3,8,8,128]{3,2,1,0:T(8,128)S(1)} %get-tuple-element.57), channel_id=1, source_target_pairs={{1,0},{2,1},{3,2},{0,3},{5,4},{6,5},{7,6},{4,7},{9,8},{10,9},{11,1... | collective-permute-start | bytes 294920 | tf_op jit(solution)/shard_map/ppermute | solution.py:884
